TPU v7x, 256 devices: a whole 4x4x8 slice. The times are simulated.
256 devices in a mesh: lon: 64 (over x, z, core), lat: 4 (over y).
Axes of the slice: x: 4, y: 4, z: 8, core: 2. Of those that a mesh axis runs over, the one named last changes fastest.
Arguments:
- state: float32 [2048, 64, 1024], P('lon', None, 'lat'), may hold values from -6 to 6
Outputs:
- spectrum: float32 [2, 1024, 64, 1024], P(None, 'lon', None, 'lat')
All inputs are finite; a program needn't handle non-finite values.
Results may differ from a plain program's by a relative error of at most 0.00011.
Values sent between devices are 32-bit elements; how exact they have to be, the bound alone decides.
No kernel may reach another device: no remote copies, remote signals or barrier semaphores. Data moves between devices by JAX's collectives and lax.ppermute only.
A program may use at most 64 MiB of HBM per device.

v0:
```python
import math

import jax
import jax.numpy as jnp
from jax import lax
from jax.sharding import PartitionSpec as P


def phase_angle(first_index, second_index, period):
    product = first_index * second_index % period
    return product.astype(jnp.float32) * (2.0 * math.pi / period)


def factored_spectrum(gathered, factor):
    lon_count, width = gathered.shape
    bit_total = lon_count.bit_length() - 1
    outer = 2 ** (bit_total // 2)
    inner = lon_count // outer
    kept = inner // 2
    blocks = gathered.reshape(outer, inner, width)
    angle_first = phase_angle(
        lax.broadcasted_iota(jnp.int32, (outer, outer), 0),
        lax.broadcasted_iota(jnp.int32, (outer, outer), 1),
        outer,
    )
    first_re = jnp.einsum(
        "an,nbr->abr", jnp.cos(angle_first), blocks, precision=lax.Precision.HIGHEST
    )
    first_im = jnp.einsum(
        "an,nbr->abr", -jnp.sin(angle_first), blocks, precision=lax.Precision.HIGHEST
    )
    angle_turn = phase_angle(
        lax.broadcasted_iota(jnp.int32, (outer, inner), 0),
        lax.broadcasted_iota(jnp.int32, (outer, inner), 1),
        lon_count,
    )[:, :, None]
    cos_turn = jnp.cos(angle_turn)
    sin_turn = jnp.sin(angle_turn)
    turned_re = first_re * cos_turn + first_im * sin_turn
    turned_im = first_im * cos_turn - first_re * sin_turn
    angle_second = phase_angle(
        lax.broadcasted_iota(jnp.int32, (kept, inner), 0),
        lax.broadcasted_iota(jnp.int32, (kept, inner), 1),
        inner,
    )
    cos_second = jnp.cos(angle_second) * factor
    sin_second = jnp.sin(angle_second) * factor
    out_re = jnp.einsum(
        "cb,abr->car", cos_second, turned_re, precision=lax.Precision.HIGHEST
    ) + jnp.einsum("cb,abr->car", sin_second, turned_im, precision=lax.Precision.HIGHEST)
    out_im = jnp.einsum(
        "cb,abr->car", cos_second, turned_im, precision=lax.Precision.HIGHEST
    ) - jnp.einsum("cb,abr->car", sin_second, turned_re, precision=lax.Precision.HIGHEST)
    return jnp.stack([out_re, out_im]).reshape(2, kept * outer, width)


def local(state):
    lon_dev, fields, lat_dev = state.shape
    devices = lax.axis_size("lon")
    columns = state.reshape(lon_dev, fields * lat_dev)
    factor = 1.0 / math.sqrt(lon_dev * devices)
    gathered = lax.all_to_all(columns, "lon", split_axis=1, concat_axis=0, tiled=True)
    spectrum = factored_spectrum(gathered, factor)
    shares = lax.all_to_all(spectrum, "lon", split_axis=1, concat_axis=2, tiled=True)
    return shares.reshape(2, shares.shape[1], fields, lat_dev)


def solution(mesh):
    return jax.shard_map(
        local,
        mesh=mesh,
        in_specs=(P("lon", None, "lat"),),
        out_specs=P(None, "lon", None, "lat"),
        check_vma=False,
    )
```

profile of v0, /device:TPU:1, one launch (start us, length us, event | category | flops | bytes accessed | tf_op | source)
XLA Modules:
  0.0 147.2 jit_solution(2070723789590345443)
XLA Ops:
  0.0 4.1 %copy.20 = f32[32,64,256]{2,0,1:T(8,128)} copy(f32[32,64,256]{2,1,0:T(8,128)} %param.1) | data formatting | bytes 4194304 | tf_op args[0]
  4.1 13.2 %all-to-all-start = ((f32[32,64,256]{2,0,1:T(8,128)}), f32[32,64,256]{2,0,1:T(8,128)S(1)}, u32[]{:S(2)}, u32[]{:S(2)}) async-start(f32[32,64,256]{2,0,1:T(8,128)} %copy.20), calls=%async_computation | async-start | bytes 4194304 | tf_op jit(solution)/shard_map/all_to_all | solution.py:62
  17.3 0.1 fusion.55
  17.4 0.1 copy.22
  17.5 0.1 fusion.54
  17.5 0.1 copy.24
  17.6 50.7 %all-to-all-done = f32[32,64,256]{2,0,1:T(8,128)S(1)} async-done(((f32[32,64,256]{2,0,1:T(8,128)}), f32[32,64,256]{2,0,1:T(8,128)S(1)}, u32[]{:S(2)}, u32[]{:S(2)}) %all-to-all-start) | async-done | bytes 2097184 | tf_op jit(solution)/shard_map/all_to_all | solution.py:62
  68.3 3.0 %fusion.10 = f32[32,64,256]{2,0,1:T(8,128)S(1)} fusion(f32[32,64,256]{2,1,0:T(8,128)S(1)} %bitcast.26), kind=kOutput, calls=%fused_computation.13 | convolution fusion | flops 201340928 | bytes 4194304 | tf_op jit(solution)/shard_map/an,nbr->abr/dot_general | solution.py:26
  71.3 3.6 %multiply_add_fusion = (f32[32,64,256]{2,0,1:T(8,128)S(1)}, f32[32,64,256]{2,0,1:T(8,128)S(1)}) fusion(f32[32,64,256]{2,0,1:T(8,128)S(1)} %fusion.10, f32[32,64]{0,1:T(8,128)S(1)} %copy.24, f32[32,64]{0,1:T(8,128)S(1)} %copy.22, f32[32,64,256]{2,1,0:T(8,128)S(1)} %bitcast.27), kind=kOutput, calls=%fused_computation.2 | convolution fusion | flops 204487680 | bytes 8404992 | tf_op jit(solution)/shard_map/an,nbr->abr/dot_general | solution.py:29
  74.9 2.4 %fusion = f32[32,32,256]{2,0,1:T(8,128)S(1)} fusion(f32[32,64,256]{2,0,1:T(8,128)S(1)} %get-tuple-element.6), kind=kOutput, calls=%fused_computation.3 | convolution fusion | flops 201357312 | bytes 3145728 | tf_op jit(solution)/shard_map/cb,abr->car/dot_general | solution.py:51
  77.3 2.4 %fusion.2 = f32[32,32,256]{2,0,1:T(8,128)S(1)} fusion(f32[32,64,256]{2,0,1:T(8,128)S(1)} %get-tuple-element.6), kind=kOutput, calls=%fused_computation.5 | convolution fusion | flops 201357312 | bytes 3145728 | tf_op jit(solution)/shard_map/cb,abr->car/dot_general | solution.py:50
  79.7 2.6 %fusion.12 = f32[32,32,256]{2,0,1:T(8,128)S(1)} fusion(f32[32,32,256]{2,0,1:T(8,128)S(1)} %fusion.2, f32[32,64,256]{2,0,1:T(8,128)S(1)} %get-tuple-element.5), kind=kOutput, calls=%fused_computation.15 | convolution fusion | flops 201619456 | bytes 4194304 | tf_op jit(solution)/shard_map/cb,abr->car/dot_general | solution.py:48
  82.2 2.4 %fusion.15 = f32[32,32,256]{2,0,1:T(8,128)S(1)} fusion(f32[32,32,256]{2,0,1:T(8,128)S(1)} %fusion, f32[32,64,256]{2,0,1:T(8,128)S(1)} %get-tuple-element.5), kind=kOutput, calls=%fused_computation.16 | convolution fusion | flops 201619456 | bytes 4194304 | tf_op jit(solution)/shard_map/cb,abr->car/dot_general | solution.py:53
  84.6 0.6 copy.30
  85.2 0.6 copy.27
  85.8 0.1 pad_maximum_fusion
  86.0 1.6 %copy.31 = f32[2,1024,256]{2,0,1:T(2,128)S(1)} copy(f32[2,1024,256]{2,1,0:T(8,128)S(1)} %pad_maximum_fusion) | data formatting | bytes 4194304 | tf_op jit(solution)/shard_map/stack | solution.py:54
  87.6 56.8 %all_to_all.28 = f32[2,1024,256]{2,0,1:T(2,128)S(1)} all-to-all(f32[2,1024,256]{2,0,1:T(2,128)S(1)} %copy.31), channel_id=1, replica_groups=mesh['lon'=64,'lat'=4] {'lon'}, dimensions={1} | all-to-all | bytes 4194304 | tf_op jit(solution)/shard_map/all_to_all | solution.py:64
  144.4 0.2 copy.32
  144.6 2.5 %copy.33 = f32[2,16,64,256]{3,2,1,0:T(8,128)} copy(f32[2,16,64,256]{3,1,2,0:T(8,128)S(1)} %bitcast.28) | data formatting | bytes 4194304 | tf_op jit(solution)/shard_map/all_to_all | solution.py:64
Async XLA Ops:
  4.1 64.2 %all-to-all-start = ((f32[32,64,256]{2,0,1:T(8,128)}), f32[32,64,256]{2,0,1:T(8,128)S(1)}, u32[]{:S(2)}, u32[]{:S(2)}) async-start(f32[32,64,256]{2,0,1:T(8,128)} %copy.20), calls=%async_computation | async-start | bytes 4194304 | tf_op jit(solution)/shard_map/all_to_all | solution.py:62
where the time goes:
time: 147 us
  blocking collectives  56.8 us (39%)
  waiting for transfers between devices  50.7 us (34%)
  matrix products  16.2 us (11%)
  starting transfers between devices  13.2 us (9%)
  local copies, waits for them, and re-layouts  9.82 us (7%)
    all_to_all x1, blocking collectives, local(): lax.all_to_all(spectrum, 'lon', split_axis=1, concat_axis=2, tiled=True)  56.8 us
    all_to_all x1, waiting for transfers between devices, local(): lax.all_to_all(columns, 'lon', split_axis=1, concat_axis=0, tiled=True)  50.7 us
    all_to_all x1, starting transfers between devices, local(): lax.all_to_all(columns, 'lon', split_axis=1, concat_axis=0, tiled=True)  13.2 us
    unnamed x1, local copies, waits for them, and re-layouts  4.13 us
    dot_general x1, matrix products, factored_spectrum(): jnp.einsum('an,nbr->abr', -jnp.sin(angle_first), blocks, precision=lax.Pr...  3.57 us
    dot_general x1, matrix products, factored_spectrum(): jnp.einsum('an,nbr->abr', jnp.cos(angle_first), blocks, precision=lax.Pre...  3.02 us
  transfers between devices with their start and end apart: 1, of which 1 were waited for; matrix products, arithmetic and copies ran while one was open for 0% of the time, Pallas kernels for 0%

commit v1 on v0

v1 whole, which is shorter than its diff:
```python
import math

import jax
import jax.numpy as jnp
from jax import lax
from jax.experimental import pallas as pl
from jax.experimental.pallas import tpu as pltpu
from jax.sharding import PartitionSpec as P

NLON = 2048
RADIX = 16
INNER = NLON // RADIX
PEERS = 64
HALF = RADIX // 2


def split_bf16(v):
    high = v.astype(jnp.bfloat16)
    low = (v - high.astype(jnp.float32)).astype(jnp.bfloat16)
    return high, low


def phase(rows, cols):
    turn = (rows * cols) % NLON
    turn = jnp.where(turn >= NLON // 2, turn - NLON, turn)
    return turn.astype(jnp.float32) * (2.0 * math.pi / NLON)


def twiddle_matrices(scale):
    shape = (HALF, 2, PEERS, INNER)
    pair = lax.broadcasted_iota(jnp.int32, shape, 0)
    mirror = lax.broadcasted_iota(jnp.int32, shape, 1)
    outer = lax.broadcasted_iota(jnp.int32, shape, 2)
    inner = lax.broadcasted_iota(jnp.int32, shape, 3)
    first = jnp.where(mirror == 0, pair, jnp.where(pair == 0, HALF, RADIX - pair))
    angle = phase(inner, first + RADIX * outer)
    c = jnp.cos(angle) * scale
    s = jnp.sin(angle) * scale
    real_only = pair == 0
    zero = jnp.zeros_like(c)
    plain = mirror == 0
    re_a = jnp.where(real_only, jnp.where(plain, c, zero), c)
    im_a = jnp.where(real_only, jnp.where(plain, -s, zero), -s)
    re_b = jnp.where(real_only, jnp.where(plain, zero, c), jnp.where(plain, s, -s))
    im_b = jnp.where(real_only, jnp.where(plain, zero, -s), jnp.where(plain, c, -c))
    re = jnp.concatenate([re_a, re_b], axis=-1)
    im = jnp.concatenate([im_a, im_b], axis=-1)
    full = jnp.stack([re, im], axis=2)
    full = full.reshape(HALF, 4 * PEERS, 2 * INNER)
    high = lax.reduce_precision(full, 8, 7)
    return high.astype(jnp.bfloat16), (full - high).astype(jnp.bfloat16)


def fft_real16(x):
    def fft_complex8(z):
        def fft4(a):
            (ar, ai), (br, bi), (cr, ci), (dr, di) = a
            sr, si = ar + cr, ai + ci
            tr, ti = ar - cr, ai - ci
            ur, ui = br + dr, bi + di
            vr, vi = br - dr, bi - di
            return [(sr + ur, si + ui), (tr + vi, ti - vr), (sr - ur, si - ui), (tr - vi, ti + vr)]

        even = fft4(z[0::2])
        odd = fft4(z[1::2])
        h = math.sqrt(0.5)
        out = [None] * 8
        for k in range(4):
            er, ei = even[k]
            pr, pi = odd[k]
            if k == 1:
                pr, pi = (pr + pi) * h, (pi - pr) * h
            elif k == 2:
                pr, pi = pi, -pr
            elif k == 3:
                pr, pi = (pi - pr) * h, -(pr + pi) * h
            out[k] = (er + pr, ei + pi)
            out[k + 4] = (er - pr, ei - pi)
        return out

    z = fft_complex8([(x[2 * i], x[2 * i + 1]) for i in range(8)])
    out = [(z[0][0] + z[0][1], None)]
    for k in range(1, 8):
        zr, zi = z[k]
        wr, wi = z[8 - k]
        er, ei = (zr + wr) * 0.5, (zi - wi) * 0.5
        pr, pi = (zi + wi) * 0.5, (wr - zr) * 0.5
        c, s = math.cos(2 * math.pi * k / 16), math.sin(2 * math.pi * k / 16)
        out.append((er + c * pr + s * pi, ei + c * pi - s * pr))
    out.append((z[0][0] - z[0][1], None))
    return out


def relayout_in_kernel(x_ref, o_ref):
    o_ref[...] = jnp.swapaxes(x_ref[...], 0, 1)


def relayout_in(state):
    lon_dev, fields, lat_dev = state.shape
    return pl.pallas_call(
        relayout_in_kernel,
        grid=(fields // 8,),
        in_specs=[pl.BlockSpec((lon_dev, 8, lat_dev), lambda i: (0, i, 0))],
        out_specs=pl.BlockSpec((8, lon_dev, lat_dev), lambda i: (i, 0, 0)),
        out_shape=jax.ShapeDtypeStruct((fields, lon_dev, lat_dev), jnp.float32),
        name="relayout_in",
    )(state)


def fft_kernel(x_ref, wh_ref, wl_ref, o_ref, yh_ref, yl_ref, r_ref):
    width = x_ref.shape[1]

    def butterfly(i, carry):
        rows = 16 if width == 128 else 8
        base = i * rows
        x = [x_ref[pl.ds(n2 * INNER + base, rows), :] for n2 in range(RADIX)]
        y = fft_real16(x)
        for k in range(HALF):
            parts = (y[0][0], y[HALF][0]) if k == 0 else y[k]
            for j, part in enumerate(parts):
                yh_ref[k, pl.ds(j * INNER + base, rows), :] = part
        return carry

    lax.fori_loop(0, INNER // (16 if width == 128 else 8), butterfly, 0)
    for k in range(HALF):
        yh, yl = split_bf16(yh_ref[k])
        wh = wh_ref[k]
        r = jnp.dot(wh, yh, preferred_element_type=jnp.float32)
        r = r + jnp.dot(wh, yl, preferred_element_type=jnp.float32)
        r = r + jnp.dot(wl_ref[k], yh, preferred_element_type=jnp.float32)
        r_ref[0, k] = r[:PEERS]
        r_ref[1, k] = r[PEERS : 2 * PEERS]
        mirror = HALF if k == 0 else RADIX - k
        r_ref[0, mirror] = r[2 * PEERS : 3 * PEERS]
        r_ref[1, mirror] = r[3 * PEERS :]
    for part in range(2):
        for block in range(2):
            o_ref[:, part * RADIX + block * 8 : part * RADIX + block * 8 + 8, :] = jnp.swapaxes(
                r_ref[part, block * 8 : block * 8 + 8], 0, 1
            )


def fft_call(gathered, wh, wl):
    width = gathered.shape[1]
    vmem = pl.BlockSpec(memory_space=pltpu.VMEM)
    return pl.pallas_call(
        fft_kernel,
        in_specs=[vmem, vmem, vmem],
        out_specs=vmem,
        out_shape=jax.ShapeDtypeStruct((PEERS, 2 * RADIX, width), jnp.float32),
        scratch_shapes=[
            pltpu.VMEM((HALF, 2 * INNER, width), jnp.float32),
            pltpu.VMEM((8, 128), jnp.float32),
            pltpu.VMEM((2, RADIX, PEERS, width), jnp.float32),
        ],
        name="fft",
    )(gathered, wh, wl)


def relayout_out_kernel(x_ref, o_ref):
    lat = x_ref.shape[2]
    o_ref[...] = jnp.swapaxes(x_ref[...], 0, 1).reshape(2, RADIX, 8, lat)


def relayout_out(x):
    fields, rows, lat_dev = x.shape
    return pl.pallas_call(
        relayout_out_kernel,
        grid=(fields // 8,),
        in_specs=[pl.BlockSpec((8, rows, lat_dev), lambda i: (i, 0, 0))],
        out_specs=pl.BlockSpec((2, RADIX, 8, lat_dev), lambda i: (0, 0, i, 0)),
        out_shape=jax.ShapeDtypeStruct((2, RADIX, fields, lat_dev), jnp.float32),
        name="relayout_out",
    )(x)


def local(state):
    lon_dev, fields, lat_dev = state.shape
    wh, wl = twiddle_matrices(1.0 / math.sqrt(NLON))
    sent = relayout_in(state)
    gathered = lax.all_to_all(sent, "lon", split_axis=0, concat_axis=0, tiled=True)
    spectrum = fft_call(gathered.reshape(NLON, lat_dev), wh, wl)
    shares = lax.all_to_all(spectrum, "lon", split_axis=0, concat_axis=0, tiled=True)
    return relayout_out(shares)


def solution(mesh):
    return jax.shard_map(
        local,
        mesh=mesh,
        in_specs=(P("lon", None, "lat"),),
        out_specs=P(None, "lon", None, "lat"),
        check_vma=False,
    )
```

time: 147 us -> 140 us (0.952)
  Pallas kernels: 0 us -> 17.3 us
  matrix products: 16.2 us -> 0 us
  local copies, waits for them, and re-layouts: 9.82 us -> 1.32 us
  other arithmetic: 0.31 us -> 4.55 us
  waiting for transfers between devices: 50.7 us -> 46.6 us
    pallas_call x0 -> x3, Pallas kernels: none -> 17.3 us  [the longest x1 5.76 us: fft_call(): pl.pallas_call(fft_kernel, in_specs=[vmem, vmem, vmem], out_specs=vmem, o...]
    dot_general x6 -> x0, matrix products: 16.2 us -> none  [the longest x1 3.57 us: factored_spectrum(): jnp.einsum('an,nbr->abr', -jnp.sin(angle_first), blocks, precision=lax.Pr...]
    all_to_all x1, waiting for transfers between devices: 50.7 us -> 46.6 us  [local(): lax.all_to_all(sent, 'lon', split_axis=0, concat_axis=0, tiled=True)]
    unnamed x1 -> x2, local copies, waits for them, and re-layouts: 4.13 us -> 1.32 us
    all_to_all x2 -> x0, local copies, waits for them, and re-layouts: 2.7 us -> none  [local(): lax.all_to_all(spectrum, 'lon', split_axis=1, concat_axis=2, tiled=True)]
    select_n x0 -> x1, other arithmetic: none -> 2.49 us  [twiddle_matrices(): re_a = jnp.where(real_only, jnp.where(plain, c, zero), c)]
    convert_element_type x0 -> x1, other arithmetic: none -> 1.71 us  [twiddle_matrices(): return (high.astype(jnp.bfloat16), (full - high).astype(jnp.bfloat16))]
    another operation x1 -> x0, local copies, waits for them, and re-layouts: 1.62 us -> none  [factored_spectrum(): return jnp.stack([out_re, out_im]).reshape(2, kept * outer, width)]
  transfers between devices with their start and end apart: 1 -> 1, of which waited for: 1 -> 1; matrix products, arithmetic and copies ran while one was open for 0% -> 3% of each run, Pallas kernels for 0% -> 0%
where the time goes in v1:
time: 140 us
  blocking collectives  57.1 us (41%)
  waiting for transfers between devices  46.6 us (33%)
  Pallas kernels  17.3 us (12%)
  starting transfers between devices  13 us (9%)
  other arithmetic  4.55 us (3%)
    all_to_all x1, blocking collectives, local(): lax.all_to_all(spectrum, 'lon', split_axis=0, concat_axis=0, tiled=True)  57.1 us
    all_to_all x1, waiting for transfers between devices, local(): lax.all_to_all(sent, 'lon', split_axis=0, concat_axis=0, tiled=True)  46.6 us
    all_to_all x1, starting transfers between devices, local(): lax.all_to_all(sent, 'lon', split_axis=0, concat_axis=0, tiled=True)  13 us
    pallas_call x1, Pallas kernels, fft_call(): pl.pallas_call(fft_kernel, in_specs=[vmem, vmem, vmem], out_specs=vmem, o...  5.76 us
    pallas_call x1, Pallas kernels, relayout_in(): pl.pallas_call(relayout_in_kernel, grid=(fields // 8,), in_specs=[pl.Bloc...  5.76 us
    pallas_call x1, Pallas kernels, relayout_out(): pl.pallas_call(relayout_out_kernel, grid=(fields // 8,), in_specs=[pl.Blo...  5.75 us
  transfers between devices with their start and end apart: 1, of which 1 were waited for; matrix products, arithmetic and copies ran while one was open for 3% of the time, Pallas kernels for 0%

profile of v1, /device:TPU:1, one launch (start us, length us, event | category | flops | bytes accessed | tf_op | source)
XLA Modules:
  0.0 139.9 jit_solution(6474237030023138308)
XLA Ops:
  0.0 5.8 %relayout_in.1 = f32[64,32,256]{2,1,0:T(8,128)} custom-call(f32[32,64,256]{2,1,0:T(8,128)} %x_ref.1), custom_call_target="tpu_custom_call" | custom-call | tf_op jit(solution)/shard_map/relayout_in/pallas_call | solution.py:100
  5.8 13.0 %all-to-all-start = ((f32[64,32,256]{2,1,0:T(8,128)}), f32[64,32,256]{2,1,0:T(8,128)S(1)}, u32[]{:S(2)}, u32[]{:S(2)}) async-start(f32[64,32,256]{2,1,0:T(8,128)} %relayout_in.1), calls=%async_computation | async-start | bytes 4194304 | tf_op jit(solution)/shard_map/all_to_all | solution.py:181
  18.8 2.5 %select_select_fusion.1 = (f32[8,2,64,128]{3,2,1,0:T(8,128)S(1)}, f32[8,2,64,128]{3,2,1,0:T(8,128)S(1)}, f32[8,2,64,128]{3,2,1,0:T(8,128)S(1)}, f32[8,2,64,128]{3,2,1,0:T(8,128)S(1)}) fusion(pred[2]{0:T(512)(128)(4,1)S(1)} %iota_compare_fusion.1, pred[8]{0:T(512)(128)(4,1)S(1)} %iota_compare_fusion, s32[64]{0:T(128)S(1)} %iota_multiply_fusion, ...), kind=kLoop, calls=%fused_computation.9 | loop fusion | flops 4456448 | bytes 2097450 | tf_op jit(solution)/shard_map/jit(_where)/select_n | solution.py:42
  21.3 0.2 maximum_bitcast_fusion
  21.5 0.2 pad_maximum_fusion
  21.6 1.7 %fusion = (bf16[8,256,256]{2,1,0:T(8,128)(2,1)}, bf16[8,256,256]{2,1,0:T(8,128)(2,1)}) fusion(f32[8,2,2,64,256]{4,3,2,1,0:T(8,128)S(1)} %pad_maximum_fusion), kind=kLoop, calls=%fused_computation.2 | loop fusion | flops 2097152 | bytes 4194304 | tf_op jit(solution)/shard_map/convert_element_type | solution.py:51
  23.3 46.6 %all-to-all-done = f32[64,32,256]{2,1,0:T(8,128)S(1)} async-done(((f32[64,32,256]{2,1,0:T(8,128)}), f32[64,32,256]{2,1,0:T(8,128)S(1)}, u32[]{:S(2)}, u32[]{:S(2)}) %all-to-all-start) | async-done | bytes 2097184 | tf_op jit(solution)/shard_map/all_to_all | solution.py:181
  69.9 0.0 copy-start
  69.9 1.3 copy-done
  71.3 5.8 %fft.1 = f32[64,32,256]{2,1,0:T(8,128)} custom-call(f32[2048,256]{1,0:T(8,128)} %bitcast.10, bf16[8,256,256]{2,1,0:T(8,128)(2,1)} %get-tuple-element.6.wh_ref, bf16[8,256,256]{2,1,0:T(8,128)(2,1)} %get-tuple-element.5.wl_ref), custom_call_target="tpu_custom_call" | custom-call | tf_op jit(solution)/shard_map/fft/pallas_call | solution.py:146
  77.0 57.1 %all_to_all.10.x_ref = f32[64,32,256]{2,1,0:T(8,128)} all-to-all(f32[64,32,256]{2,1,0:T(8,128)} %fft.1), channel_id=1, replica_groups=mesh['lon'=64,'lat'=4] {'lon'}, dimensions={0} | all-to-all | bytes 4194304 | tf_op jit(solution)/shard_map/all_to_all | solution.py:183
  134.2 5.8 %relayout_out.1 = f32[2,16,64,256]{3,2,1,0:T(8,128)} custom-call(f32[64,32,256]{2,1,0:T(8,128)} %all_to_all.10.x_ref), custom_call_target="tpu_custom_call" | custom-call | tf_op jit(solution)/shard_map/relayout_out/pallas_call | solution.py:167
  (4 shorter events, 0.0 us)
Async XLA Ops:
  5.8 64.2 %all-to-all-start = ((f32[64,32,256]{2,1,0:T(8,128)}), f32[64,32,256]{2,1,0:T(8,128)S(1)}, u32[]{:S(2)}, u32[]{:S(2)}) async-start(f32[64,32,256]{2,1,0:T(8,128)} %relayout_in.1), calls=%async_computation | async-start | bytes 4194304 | tf_op jit(solution)/shard_map/all_to_all | solution.py:181
  69.9 1.3 copy-start

commit v2 on v1

v2 whole, which is shorter than its diff:
```python
import math

import jax
import jax.numpy as jnp
from jax import lax
from jax.experimental import pallas as pl
from jax.experimental.pallas import tpu as pltpu
from jax.sharding import PartitionSpec as P


NLON = 2048
RADIX = 16
INNER = NLON // RADIX
PEERS = 64
HALF = RADIX // 2
NX, NZ, NC = 4, 8, 2
LON = 32
KEPT = 2 * RADIX
FIELDS = 64
LANES = 128
VMEM = pl.BlockSpec(memory_space=pltpu.VMEM)
HBM = pl.BlockSpec(memory_space=pltpu.HBM)
SMEM = pl.BlockSpec(memory_space=pltpu.SMEM)
PARAMS = pltpu.CompilerParams(vmem_limit_bytes=16 * 1024 * 1024)


def f32(*shape):
    return jax.ShapeDtypeStruct(shape, jnp.float32)


def split_bf16(v):
    high = v.astype(jnp.bfloat16)
    low = (v - high.astype(jnp.float32)).astype(jnp.bfloat16)
    return high, low


def phase(rows, cols):
    turn = (rows * cols) % NLON
    turn = jnp.where(turn >= NLON // 2, turn - NLON, turn)
    return turn.astype(jnp.float32) * (2.0 * math.pi / NLON)


def twiddle_matrices(scale):
    shape = (HALF, 2, PEERS, INNER)
    pair = lax.broadcasted_iota(jnp.int32, shape, 0)
    mirror = lax.broadcasted_iota(jnp.int32, shape, 1)
    outer = lax.broadcasted_iota(jnp.int32, shape, 2)
    inner = lax.broadcasted_iota(jnp.int32, shape, 3)
    first = jnp.where(mirror == 0, pair, jnp.where(pair == 0, HALF, RADIX - pair))
    angle = phase(inner, first + RADIX * outer)
    c = jnp.cos(angle) * scale
    s = jnp.sin(angle) * scale
    real_only = pair == 0
    zero = jnp.zeros_like(c)
    plain = mirror == 0
    re_a = jnp.where(real_only, jnp.where(plain, c, zero), c)
    im_a = jnp.where(real_only, jnp.where(plain, -s, zero), -s)
    re_b = jnp.where(real_only, jnp.where(plain, zero, c), jnp.where(plain, s, -s))
    im_b = jnp.where(real_only, jnp.where(plain, zero, -s), jnp.where(plain, c, -c))
    re = jnp.concatenate([re_a, re_b], axis=-1)
    im = jnp.concatenate([im_a, im_b], axis=-1)
    full = jnp.stack([re, im], axis=2)
    full = full.reshape(HALF, 4 * PEERS, 2 * INNER)
    high = lax.reduce_precision(full, 8, 7)
    return high.astype(jnp.bfloat16), (full - high).astype(jnp.bfloat16)


def fft_real16(x):
    def fft_complex8(z):
        def fft4(a):
            (ar, ai), (br, bi), (cr, ci), (dr, di) = a
            sr, si = ar + cr, ai + ci
            tr, ti = ar - cr, ai - ci
            ur, ui = br + dr, bi + di
            vr, vi = br - dr, bi - di
            return [(sr + ur, si + ui), (tr + vi, ti - vr), (sr - ur, si - ui), (tr - vi, ti + vr)]

        even = fft4(z[0::2])
        odd = fft4(z[1::2])
        h = math.sqrt(0.5)
        out = [None] * 8
        for k in range(4):
            er, ei = even[k]
            pr, pi = odd[k]
            if k == 1:
                pr, pi = (pr + pi) * h, (pi - pr) * h
            elif k == 2:
                pr, pi = pi, -pr
            elif k == 3:
                pr, pi = (pi - pr) * h, -(pr + pi) * h
            out[k] = (er + pr, ei + pi)
            out[k + 4] = (er - pr, ei - pi)
        return out

    z = fft_complex8([(x[2 * i], x[2 * i + 1]) for i in range(8)])
    out = [(z[0][0] + z[0][1], None)]
    for k in range(1, 8):
        zr, zi = z[k]
        wr, wi = z[8 - k]
        er, ei = (zr + wr) * 0.5, (zi - wi) * 0.5
        pr, pi = (zi + wi) * 0.5, (wr - zr) * 0.5
        c, s = math.cos(2 * math.pi * k / 16), math.sin(2 * math.pi * k / 16)
        out.append((er + c * pr + s * pi, ei + c * pi - s * pr))
    out.append((z[0][0] - z[0][1], None))
    return out


PAD_R = PEERS + 8


def fft_core(x_ref, wh_ref, wl_ref, y_ref, r_ref):
    def butterfly(i, carry):
        base = pl.multiple_of(i * 8, 8)
        x = [x_ref[pl.ds(n2 * INNER + base, 8), :] for n2 in range(RADIX)]
        y = fft_real16(x)
        for k in range(HALF):
            parts = (y[0][0], y[HALF][0]) if k == 0 else y[k]
            for j, part in enumerate(parts):
                y_ref[k, pl.ds(j * INNER + base, 8), :] = part
        return carry

    lax.fori_loop(0, INNER // 8, butterfly, 0)
    for k in range(HALF):
        yh, yl = split_bf16(y_ref[k])
        wh = wh_ref[k]
        r = jnp.dot(wh, yh, preferred_element_type=jnp.float32)
        r = r + jnp.dot(wh, yl, preferred_element_type=jnp.float32)
        r = r + jnp.dot(wl_ref[k], yh, preferred_element_type=jnp.float32)
        mirror = HALF if k == 0 else RADIX - k
        for q, row in enumerate((k, RADIX + k, mirror, RADIX + mirror)):
            r_ref[pl.ds(row * PAD_R, PEERS), :] = r[q * PEERS : (q + 1) * PEERS]


PIECES = 4


def send_pieces(body, count, buf_ref, o_ref, sem):
    step = count // PIECES
    copies = []
    for piece in range(PIECES):
        lax.fori_loop(piece * step, (piece + 1) * step, body, 0, unroll=4)
        rows = pl.ds(piece * step, step)
        copy = pltpu.make_async_copy(buf_ref.at[rows], o_ref.at[rows], sem.at[piece])
        copy.start()
        copies.append(copy)
    for copy in copies:
        copy.wait()


FFT_SCRATCH = [
    pltpu.VMEM((HALF, 2 * INNER, LANES), jnp.float32),
    pltpu.VMEM((KEPT * PAD_R, LANES), jnp.float32),
]


def mode_rows(r_ref, k1, eight):
    return r_ref[pl.ds(eight * 8 * PAD_R + k1, 8, stride=PAD_R), :]


def fft_a_kernel(x_ref, wh_ref, wl_ref, o_ref, y_ref, r_ref, buf_ref, sem):
    fft_core(x_ref, wh_ref, wl_ref, y_ref, r_ref)

    def peer(k1, carry):
        for eight in range(KEPT // 8):
            buf_ref[k1, eight * 8 : eight * 8 + 8, :] = mode_rows(r_ref, k1, eight)
        return carry

    send_pieces(peer, PEERS, buf_ref, o_ref, sem)


def fft_a(gathered, wh, wl):
    return pl.pallas_call(
        fft_a_kernel,
        in_specs=[VMEM] * 3,
        out_specs=HBM,
        out_shape=f32(PEERS, KEPT, LANES),
        scratch_shapes=FFT_SCRATCH
        + [pltpu.VMEM((PEERS, KEPT, LANES), jnp.float32), pltpu.SemaphoreType.DMA((PIECES,))],
        compiler_params=PARAMS,
        name="fft_a",
    )(gathered, wh, wl)


def fft_p_kernel(pos_ref, *refs):
    g_refs, (wh_ref, wl_ref), o_refs = refs[:8], refs[8:10], refs[10:18]
    x_ref, y_ref, r_ref = refs[18:]
    x, z, c = pos_ref[0], pos_ref[1], pos_ref[2]
    for dx in range(NX):
        for dc in range(NC):
            start = ((x + NX - dx) % NX) * (NLON // NX) + ((c + dc) % NC) * LON
            for zz in range(NZ):
                row = pl.multiple_of(start + zz * NC * LON, LON)
                x_ref[pl.ds(row, LON), :] = g_refs[dx * NC + dc][zz * LON : (zz + 1) * LON, :]
    fft_core(x_ref, wh_ref, wl_ref, y_ref, r_ref)
    for dz in range(NZ):
        target = (z + dz) % NZ
        for xx in range(NX):
            for cc in range(NC):
                k1 = xx * NZ * NC + target * NC + cc
                for eight in range(KEPT // 8):
                    row = (xx * NC + cc) * KEPT + eight * 8
                    o_refs[dz][row : row + 8, :] = mode_rows(r_ref, k1, eight)


def fft_p(pos, blocks, wh, wl):
    return pl.pallas_call(
        fft_p_kernel,
        in_specs=[SMEM] + [VMEM] * 10,
        out_specs=[VMEM] * NZ,
        out_shape=[f32(NX * NC * KEPT, LANES)] * NZ,
        scratch_shapes=[pltpu.VMEM((NLON, LANES), jnp.float32)] + FFT_SCRATCH,
        compiler_params=PARAMS,
        name="fft_p",
    )(pos, *blocks, wh, wl)


def split_z_kernel(pos_ref, s_ref, *refs):
    o_refs, sem = refs[:NZ], refs[NZ]
    z = pos_ref[1]
    copies = []
    for dz in range(NZ):
        field = pl.multiple_of(((z + dz) % NZ) * 8, 8)
        copies.append(
            pltpu.make_async_copy(s_ref.at[:, pl.ds(field, 8), pl.ds(0, LANES)], o_refs[dz], sem.at[dz])
        )
    for copy in copies:
        copy.start()
    for copy in copies:
        copy.wait()


def split_z(pos, state):
    return pl.pallas_call(
        split_z_kernel,
        in_specs=[SMEM, HBM],
        out_specs=[VMEM] * NZ,
        out_shape=[f32(LON, 8, LANES)] * NZ,
        scratch_shapes=[pltpu.SemaphoreType.DMA((NZ,))],
        compiler_params=PARAMS,
        name="split_z",
    )(pos, state)


def spread_x_kernel(pos_ref, *refs):
    b_refs, o_refs = refs[:NZ], refs[NZ:]
    x, z, c = pos_ref[0], pos_ref[1], pos_ref[2]
    for dx in range(NX):
        for dc in range(NC):
            field = ((x + dx) % NX) * NC + (c + dc) % NC
            for dz in range(NZ):
                row = pl.multiple_of(((z + NZ - dz) % NZ) * LON, LON)
                o_refs[dx * NC + dc][pl.ds(row, LON), :] = b_refs[dz][pl.ds(field, LON, stride=8), :]


def spread_x(pos, blocks):
    return pl.pallas_call(
        spread_x_kernel,
        in_specs=[SMEM] + [VMEM] * NZ,
        out_specs=[VMEM] * (NX * NC),
        out_shape=[f32(NZ * LON, LANES)] * (NX * NC),
        compiler_params=PARAMS,
        name="spread_x",
    )(pos, *blocks)


def spread_out_kernel(pos_ref, *refs):
    h_refs, o_refs = refs[:NZ], refs[NZ:]
    x, z, c = pos_ref[0], pos_ref[1], pos_ref[2]
    for dx in range(NX):
        for dc in range(NC):
            source = pl.multiple_of((((x + dx) % NX) * NC + (c + dc) % NC) * KEPT, KEPT)
            for dz in range(NZ):
                row = pl.multiple_of(((z + NZ - dz) % NZ) * KEPT, KEPT)
                o_refs[dx * NC + dc][pl.ds(row, KEPT), :] = h_refs[dz][pl.ds(source, KEPT), :]


def spread_out(pos, blocks):
    return pl.pallas_call(
        spread_out_kernel,
        in_specs=[SMEM] + [VMEM] * NZ,
        out_specs=[VMEM] * (NX * NC),
        out_shape=[f32(NZ * KEPT, LANES)] * (NX * NC),
        compiler_params=PARAMS,
        name="spread_out",
    )(pos, *blocks)


PAD_F = FIELDS + 8


def relayout_a_kernel(s_ref, o_ref, x_ref, buf_ref, sem, out_sem):
    copies = [
        pltpu.make_async_copy(
            s_ref.at[n, :, pl.ds(LANES, LANES)], x_ref.at[pl.ds(n * PAD_F, FIELDS), :], sem.at[n]
        )
        for n in range(LON)
    ]
    for copy in copies:
        copy.start()
    for copy in copies:
        copy.wait()

    def field(f, carry):
        for eight in range(LON // 8):
            buf_ref[f, eight * 8 : eight * 8 + 8, :] = x_ref[pl.ds(eight * 8 * PAD_F + f, 8, stride=PAD_F), :]
        return carry

    send_pieces(field, FIELDS, buf_ref, o_ref, out_sem)


def relayout_a(state):
    return pl.pallas_call(
        relayout_a_kernel,
        in_specs=[HBM],
        out_specs=HBM,
        out_shape=f32(FIELDS, LON, LANES),
        scratch_shapes=[
            pltpu.VMEM((LON * PAD_F, LANES), jnp.float32),
            pltpu.VMEM((FIELDS, LON, LANES), jnp.float32),
            pltpu.SemaphoreType.DMA((LON,)),
            pltpu.SemaphoreType.DMA((PIECES,)),
        ],
        compiler_params=PARAMS,
        name="relayout_a",
    )(state)


PAD_K = KEPT + 8


def store_half(x_ref, buf_ref, o_ref, sem, lane):
    copies = []
    step = KEPT // PIECES
    for piece in range(PIECES):
        for kept in range(piece * step, (piece + 1) * step):
            for eight in range(FIELDS // 8):
                buf_ref[kept, eight * 8 : eight * 8 + 8, :] = x_ref[pl.ds(eight * 8 * PAD_K + kept, 8, stride=PAD_K), :]
        copy = pltpu.make_async_copy(
            buf_ref.at[pl.ds(piece * step, step)],
            o_ref.at[pl.ds(piece * step, step), :, pl.ds(lane, LANES)],
            sem.at[piece],
        )
        copy.start()
        copies.append(copy)
    for copy in copies:
        copy.wait()


STORE_SCRATCH = [
    pltpu.VMEM((FIELDS * PAD_K, LANES), jnp.float32),
    pltpu.VMEM((KEPT, FIELDS, LANES), jnp.float32),
    pltpu.SemaphoreType.DMA((PIECES,)),
]


def store_p_kernel(pos_ref, *refs):
    q_refs, o_ref = refs[:8], refs[8]
    x_ref, buf_ref, sem = refs[9:]
    x, c = pos_ref[0], pos_ref[2]
    for dx in range(NX):
        for dc in range(NC):
            base = ((x + NX - dx) % NX) * NC + (c + dc) % NC
            for zz in range(NZ):
                row = pl.multiple_of((base + zz * NX * NC) * PAD_K, 8)
                x_ref[pl.ds(row, KEPT), :] = q_refs[dx * NC + dc][zz * KEPT : (zz + 1) * KEPT, :]
    store_half(x_ref, buf_ref, o_ref, sem, 0)


def store_p(pos, blocks):
    return pl.pallas_call(
        store_p_kernel,
        in_specs=[SMEM] + [VMEM] * 8,
        out_specs=HBM,
        out_shape=f32(KEPT, FIELDS, 2 * LANES),
        scratch_shapes=STORE_SCRATCH,
        compiler_params=PARAMS,
        name="store_p",
    )(pos, *blocks)


def store_a_kernel(prior_ref, q_ref, o_ref, x_ref, buf_ref, sem):
    del prior_ref

    def field(f, carry):
        x_ref[pl.ds(pl.multiple_of(f * PAD_K, 8), KEPT), :] = q_ref[f]
        return carry

    lax.fori_loop(0, FIELDS, field, 0, unroll=8)
    store_half(x_ref, buf_ref, o_ref, sem, LANES)


def store_a(prior, shares):
    return pl.pallas_call(
        store_a_kernel,
        in_specs=[HBM, VMEM],
        out_specs=HBM,
        out_shape=f32(KEPT, FIELDS, 2 * LANES),
        scratch_shapes=STORE_SCRATCH,
        input_output_aliases={0: 0},
        compiler_params=PARAMS,
        name="store_a",
    )(prior, shares)


def shifts(dx, dz, dc):
    def at(x, z, c):
        return (x % NX) * NZ * NC + (z % NZ) * NC + c % NC

    return [
        (at(x, z, c), at(x + dx, z + dz, c + dc)) for x in range(NX) for z in range(NZ) for c in range(NC)
    ]


Z_ORDER = (4, 3, 5, 2, 6, 1, 7)


def exchange_z(blocks):
    out = [None] * NZ
    out[0] = blocks[0]
    for dz in Z_ORDER:
        out[dz] = lax.ppermute(blocks[dz], "lon", shifts(0, dz, 0))
    return out


def exchange_xc(blocks):
    out = [None] * (NX * NC)
    out[0] = blocks[0]
    for dx in (2, 1, 3, 0):
        for dc in range(NC):
            if dx or dc:
                out[dx * NC + dc] = lax.ppermute(blocks[dx * NC + dc], "lon", shifts(dx, 0, dc))
    return out


def local(state):
    device = lax.axis_index("lon")
    pos = jnp.stack([device // (NZ * NC), (device // NC) % NZ, device % NC]).astype(jnp.int32)
    wh, wl = twiddle_matrices(1.0 / math.sqrt(NLON))
    pieces = split_z(pos, state)
    pieces = exchange_z(pieces)
    sent = relayout_a(state)
    gathered = lax.all_to_all(sent, "lon", split_axis=0, concat_axis=0, tiled=True)
    pieces = spread_x(pos, [b.reshape(LON * 8, LANES) for b in pieces])
    pieces = exchange_xc(pieces)
    pieces = fft_p(pos, pieces, wh, wl)
    pieces = exchange_z(pieces)
    spectrum = fft_a(gathered.reshape(NLON, LANES), wh, wl)
    shares = lax.all_to_all(spectrum, "lon", split_axis=0, concat_axis=0, tiled=True)
    pieces = spread_out(pos, pieces)
    pieces = exchange_xc(pieces)
    out = store_p(pos, pieces)
    out = store_a(out, shares)
    return out.reshape(2, RADIX, FIELDS, 2 * LANES)


def solution(mesh):
    return jax.shard_map(
        local,
        mesh=mesh,
        in_specs=(P("lon", None, "lat"),),
        out_specs=P(None, "lon", None, "lat"),
        check_vma=False,
    )
```

time: 140 us -> 178 us (1.27)
  blocking collectives: 57.1 us -> 0 us
  starting transfers between devices: 13 us -> 67.9 us
  waiting for transfers between devices: 46.6 us -> 91.4 us
  Pallas kernels: 17.3 us -> 10.8 us
  local copies, waits for them, and re-layouts: 1.32 us -> 4.16 us
    ppermute x0 -> x28, waiting for transfers between devices: none -> 66.2 us  [the longest x14 49.6 us: exchange_z(): out[dz] = lax.ppermute(blocks[dz], 'lon', shifts(0, dz, 0))]
    all_to_all x1 -> x0, blocking collectives: 57.1 us -> none  [local(): lax.all_to_all(spectrum, 'lon', split_axis=0, concat_axis=0, tiled=True)]
    ppermute x0 -> x28, starting transfers between devices: none -> 48.7 us  [the longest x14 28.5 us: exchange_z(): out[dz] = lax.ppermute(blocks[dz], 'lon', shifts(0, dz, 0))]
    all_to_all x1, waiting for transfers between devices: 46.6 us -> 25.2 us  [local(): lax.all_to_all(sent, 'lon', split_axis=0, concat_axis=0, tiled=True)]
    pallas_call x3 -> x8, Pallas kernels: 17.3 us -> 10.8 us  [the longest x1 2.32 us: fft_p(): pl.pallas_call(fft_p_kernel, in_specs=[SMEM] + [VMEM] * 10, out_specs=[VM...]
    all_to_all x0 -> x1, starting transfers between devices: none -> 6.2 us  [local(): lax.all_to_all(spectrum, 'lon', split_axis=0, concat_axis=0, tiled=True)]
    unnamed x2 -> x6, local copies, waits for them, and re-layouts: 1.32 us -> 4.16 us
  transfers between devices with their start and end apart: 1 -> 30, of which waited for: 1 -> 15; matrix products, arithmetic and copies ran while one was open for 3% -> 2% of each run, Pallas kernels for 0% -> 4%
where the time goes in v2:
time: 178 us
  waiting for transfers between devices  91.4 us (51%)
  starting transfers between devices  67.9 us (38%)
  Pallas kernels  10.8 us (6%)
  local copies, waits for them, and re-layouts  4.16 us (2%)
  other arithmetic  3.31 us (2%)
    ppermute x14, waiting for transfers between devices, exchange_z(): out[dz] = lax.ppermute(blocks[dz], 'lon', shifts(0, dz, 0))  49.6 us
    ppermute x14, starting transfers between devices, exchange_z(): out[dz] = lax.ppermute(blocks[dz], 'lon', shifts(0, dz, 0))  28.5 us
    all_to_all x1, waiting for transfers between devices, local(): lax.all_to_all(sent, 'lon', split_axis=0, concat_axis=0, tiled=True)  25.2 us
    ppermute x14, starting transfers between devices, exchange_xc(): lax.ppermute(blocks[dx * NC + dc], 'lon', shifts(dx, 0, dc))  20.2 us
    ppermute x14, waiting for transfers between devices, exchange_xc(): lax.ppermute(blocks[dx * NC + dc], 'lon', shifts(dx, 0, dc))  16.6 us
    all_to_all x1, starting transfers between devices, local(): lax.all_to_all(sent, 'lon', split_axis=0, concat_axis=0, tiled=True)  13 us
    all_to_all x1, starting transfers between devices, local(): lax.all_to_all(spectrum, 'lon', split_axis=0, concat_axis=0, tiled=True)  6.2 us
    unnamed x6, local copies, waits for them, and re-layouts  4.16 us
  transfers between devices with their start and end apart: 30, of which 15 were waited for; matrix products, arithmetic and copies ran while one was open for 2% of the time, Pallas kernels for 4%

profile of v2, /device:TPU:1, one launch (start us, length us, event | category | flops | bytes accessed | tf_op | source)
XLA Modules:
  0.0 178.0 jit_solution(14540416728200572378)
XLA Ops:
  3.1 13.0 %all-to-all-start = ((f32[64,32,128]{2,1,0:T(8,128)}), f32[64,32,128]{2,1,0:T(8,128)S(1)}, u32[]{:S(2)}, u32[]{:S(2)}) async-start(f32[64,32,128]{2,1,0:T(8,128)} %relayout_a.1), calls=%async_computation | async-start | bytes 2097152 | tf_op jit(solution)/shard_map/all_to_all | solution.py:442
  16.2 2.5 %select_select_fusion.1 = (f32[8,2,64,128]{3,2,1,0:T(8,128)S(1)}, f32[8,2,64,128]{3,2,1,0:T(8,128)S(1)}, f32[8,2,64,128]{3,2,1,0:T(8,128)S(1)}, f32[8,2,64,128]{3,2,1,0:T(8,128)S(1)}) fusion(pred[2]{0:T(512)(128)(4,1)S(1)} %iota_compare_fusion.1, pred[8]{0:T(512)(128)(4,1)S(1)} %iota_compare_fusion, s32[64]{0:T(128)S(1)} %iota_multiply_fusion, ...), kind=kLoop, calls=%fused_computation.9 | loop fusion | flops 4456448 | bytes 2097450 | tf_op jit(solution)/shard_map/jit(_where)/select_n | solution.py:56
  19.4 25.2 %all-to-all-done = f32[64,32,128]{2,1,0:T(8,128)S(1)} async-done(((f32[64,32,128]{2,1,0:T(8,128)}), f32[64,32,128]{2,1,0:T(8,128)S(1)}, u32[]{:S(2)}, u32[]{:S(2)}) %all-to-all-start) | async-done | bytes 1048608 | tf_op jit(solution)/shard_map/all_to_all | solution.py:442
  47.5 6.2 %all-to-all-start.1 = ((f32[64,32,128]{2,1,0:T(8,128)}), f32[64,32,128]{2,1,0:T(8,128)S(1)}, u32[]{:S(2)}, u32[]{:S(2)}) async-start(f32[64,32,128]{2,1,0:T(8,128)} %copy-done.2), calls=%async_computation.1 | async-start | bytes 2097152 | tf_op jit(solution)/shard_map/all_to_all | solution.py:448
  59.7 2.4 %collective-permute-start.2 = (f32[32,8,128]{2,1,0:T(8,128)S(1)}, f32[32,8,128]{2,1,0:T(8,128)S(1)}, u32[]{:S(2)}, u32[]{:S(2)}) collective-permute-start(f32[32,8,128]{2,1,0:T(8,128)S(1)} %get-tuple-element.40), channel_id=1, source_target_pairs={{0,24},{4,28},{8,32},{12,36},{16,40},{20,44},{24,48},{28,52},{32,5... | collective-permute-start | bytes 393224 | tf_op jit(solution)/shard_map/ppermute | solution.py:421
  64.2 2.4 %collective-permute-start.4 = (f32[32,8,128]{2,1,0:T(8,128)S(1)}, f32[32,8,128]{2,1,0:T(8,128)S(1)}, u32[]{:S(2)}, u32[]{:S(2)}) collective-permute-start(f32[32,8,128]{2,1,0:T(8,128)S(1)} %get-tuple-element.42), channel_id=1, source_target_pairs={{0,40},{4,44},{8,48},{12,52},{16,56},{20,60},{24,0},{28,4},{32,8},... | collective-permute-start | bytes 393224 | tf_op jit(solution)/shard_map/ppermute | solution.py:421
  66.6 15.3 %collective-permute-done = f32[32,8,128]{2,1,0:T(8,128)S(1)} collective-permute-done((f32[32,8,128]{2,1,0:T(8,128)S(1)}, f32[32,8,128]{2,1,0:T(8,128)S(1)}, u32[]{:S(2)}, u32[]{:S(2)}) %collective-permute-start) | collective-permute-done | bytes 131104 | tf_op jit(solution)/shard_map/ppermute | solution.py:421
  81.9 2.3 %collective-permute-start.5 = (f32[32,8,128]{2,1,0:T(8,128)S(1)}, f32[32,8,128]{2,1,0:T(8,128)S(1)}, u32[]{:S(2)}, u32[]{:S(2)}) collective-permute-start(f32[32,8,128]{2,1,0:T(8,128)S(1)} %get-tuple-element.43), channel_id=1, source_target_pairs={{0,48},{4,52},{8,56},{12,60},{16,0},{20,4},{24,8},{28,12},{32,16},... | collective-permute-start | bytes 393224 | tf_op jit(solution)/shard_map/ppermute | solution.py:421
  84.1 2.8 %collective-permute-done.1 = f32[32,8,128]{2,1,0:T(8,128)S(1)} collective-permute-done((f32[32,8,128]{2,1,0:T(8,128)S(1)}, f32[32,8,128]{2,1,0:T(8,128)S(1)}, u32[]{:S(2)}, u32[]{:S(2)}) %collective-permute-start.1) | collective-permute-done | bytes 131104 | tf_op jit(solution)/shard_map/ppermute | solution.py:421
  86.9 2.3 %collective-permute-start.6 = (f32[32,8,128]{2,1,0:T(8,128)S(1)}, f32[32,8,128]{2,1,0:T(8,128)S(1)}, u32[]{:S(2)}, u32[]{:S(2)}) collective-permute-start(f32[32,8,128]{2,1,0:T(8,128)S(1)} %get-tuple-element.44), channel_id=1, source_target_pairs={{0,56},{4,60},{8,0},{12,4},{16,8},{20,12},{24,16},{28,20},{32,24},... | collective-permute-start | bytes 393224 | tf_op jit(solution)/shard_map/ppermute | solution.py:421
  89.3 8.8 %collective-permute-done.2 = f32[32,8,128]{2,1,0:T(8,128)S(1)} collective-permute-done((f32[32,8,128]{2,1,0:T(8,128)S(1)}, f32[32,8,128]{2,1,0:T(8,128)S(1)}, u32[]{:S(2)}, u32[]{:S(2)}) %collective-permute-start.2) | collective-permute-done | bytes 131104 | tf_op jit(solution)/shard_map/ppermute | solution.py:421
  98.1 4.9 %collective-permute-done.3 = f32[32,8,128]{2,1,0:T(8,128)S(1)} collective-permute-done((f32[32,8,128]{2,1,0:T(8,128)S(1)}, f32[32,8,128]{2,1,0:T(8,128)S(1)}, u32[]{:S(2)}, u32[]{:S(2)}) %collective-permute-start.3) | collective-permute-done | bytes 131104 | tf_op jit(solution)/shard_map/ppermute | solution.py:421
  103.9 2.5 %collective-permute-start.7 = (f32[256,128]{1,0:T(8,128)S(1)}, f32[256,128]{1,0:T(8,128)S(1)}, u32[]{:S(2)}, u32[]{:S(2)}) collective-permute-start(f32[256,128]{1,0:T(8,128)S(1)} %get-tuple-element.46), channel_id=1, source_target_pairs={{0,4},{4,0},{8,12},{12,8},{16,20},{20,16},{24,28},{28,24},{32,36},... | collective-permute-start | bytes 393224 | tf_op jit(solution)/shard_map/ppermute | solution.py:431
  107.3 3.2 %collective-permute-start.10 = (f32[256,128]{1,0:T(8,128)S(1)}, f32[256,128]{1,0:T(8,128)S(1)}, u32[]{:S(2)}, u32[]{:S(2)}) collective-permute-start(f32[256,128]{1,0:T(8,128)S(1)} %get-tuple-element.49), channel_id=1, source_target_pairs={{0,128},{4,132},{8,136},{12,140},{16,144},{20,148},{24,152},{28,15... | collective-permute-start | bytes 393224 | tf_op jit(solution)/shard_map/ppermute | solution.py:431
  114.3 6.9 %collective-permute-done.9.refs_3_ = f32[256,128]{1,0:T(8,128)S(1)} collective-permute-done((f32[256,128]{1,0:T(8,128)S(1)}, f32[256,128]{1,0:T(8,128)S(1)}, u32[]{:S(2)}, u32[]{:S(2)}) %collective-permute-start.9) | collective-permute-done | bytes 131104 | tf_op jit(solution)/shard_map/ppermute | solution.py:431
  121.9 2.3 %fft_p.1 = (f32[256,128]{1,0:T(8,128)S(1)}, f32[256,128]{1,0:T(8,128)S(1)}, f32[256,128]{1,0:T(8,128)S(1)}, f32[256,128]{1,0:T(8,128)S(1)}, f32[256,128]{1,0:T(8...) custom-call(s32[3]{0:T(128)S(1)} %pad_add_fusion.pos_ref, ...), custom_call_target="tpu_custom_call" | custom-call | tf_op jit(solution)/shard_map/fft_p/pallas_call | solution.py:206
  128.4 3.3 %collective-permute-start.17 = (f32[256,128]{1,0:T(8,128)S(1)}, f32[256,128]{1,0:T(8,128)S(1)}, u32[]{:S(2)}, u32[]{:S(2)}) collective-permute-start(f32[256,128]{1,0:T(8,128)S(1)} %get-tuple-element.57), channel_id=1, source_target_pairs={{0,32},{4,36},{8,40},{12,44},{16,48},{20,52},{24,56},{28,60},{32,0... | collective-permute-start | bytes 393224 | tf_op jit(solution)/shard_map/ppermute | solution.py:421
  134.4 4.6 %collective-permute-start.20 = (f32[256,128]{1,0:T(8,128)S(1)}, f32[256,128]{1,0:T(8,128)S(1)}, u32[]{:S(2)}, u32[]{:S(2)}) collective-permute-start(f32[256,128]{1,0:T(8,128)S(1)} %get-tuple-element.60), channel_id=1, source_target_pairs={{0,56},{4,60},{8,0},{12,4},{16,8},{20,12},{24,16},{28,20},{32,24},... | collective-permute-start | bytes 393224 | tf_op jit(solution)/shard_map/ppermute | solution.py:421
  138.9 9.8 %collective-permute-done.16.refs_3_ = f32[256,128]{1,0:T(8,128)S(1)} collective-permute-done((f32[256,128]{1,0:T(8,128)S(1)}, f32[256,128]{1,0:T(8,128)S(1)}, u32[]{:S(2)}, u32[]{:S(2)}) %collective-permute-start.16) | collective-permute-done | bytes 131104 | tf_op jit(solution)/shard_map/ppermute | solution.py:421
  148.7 4.1 %collective-permute-done.19.refs_6_ = f32[256,128]{1,0:T(8,128)S(1)} collective-permute-done((f32[256,128]{1,0:T(8,128)S(1)}, f32[256,128]{1,0:T(8,128)S(1)}, u32[]{:S(2)}, u32[]{:S(2)}) %collective-permute-start.19) | collective-permute-done | bytes 131104 | tf_op jit(solution)/shard_map/ppermute | solution.py:421
  152.8 2.7 %collective-permute-done.20.refs_7_ = f32[256,128]{1,0:T(8,128)S(1)} collective-permute-done((f32[256,128]{1,0:T(8,128)S(1)}, f32[256,128]{1,0:T(8,128)S(1)}, u32[]{:S(2)}, u32[]{:S(2)}) %collective-permute-start.20) | collective-permute-done | bytes 131104 | tf_op jit(solution)/shard_map/ppermute | solution.py:421
  162.8 2.5 %collective-permute-start.26 = (f32[256,128]{1,0:T(8,128)S(1)}, f32[256,128]{1,0:T(8,128)S(1)}, u32[]{:S(2)}, u32[]{:S(2)}) collective-permute-start(f32[256,128]{1,0:T(8,128)S(1)} %get-tuple-element.67), channel_id=1, source_target_pairs={{0,192},{4,196},{8,200},{12,204},{16,208},{20,212},{24,216},{28,22... | collective-permute-start | bytes 393224 | tf_op jit(solution)/shard_map/ppermute | solution.py:431
  166.3 3.3 %collective-permute-done.24.refs_4_ = f32[256,128]{1,0:T(8,128)S(1)} collective-permute-done((f32[256,128]{1,0:T(8,128)S(1)}, f32[256,128]{1,0:T(8,128)S(1)}, u32[]{:S(2)}, u32[]{:S(2)}) %collective-permute-start.24) | collective-permute-done | bytes 131104 | tf_op jit(solution)/shard_map/ppermute | solution.py:431
  169.5 3.3 %collective-permute-done.25.refs_5_ = f32[256,128]{1,0:T(8,128)S(1)} collective-permute-done((f32[256,128]{1,0:T(8,128)S(1)}, f32[256,128]{1,0:T(8,128)S(1)}, u32[]{:S(2)}, u32[]{:S(2)}) %collective-permute-start.25) | collective-permute-done | bytes 131104 | tf_op jit(solution)/shard_map/ppermute | solution.py:431
  (59 shorter events, 41.1 us)
Async XLA Ops:
  3.1 41.5 %all-to-all-start = ((f32[64,32,128]{2,1,0:T(8,128)}), f32[64,32,128]{2,1,0:T(8,128)S(1)}, u32[]{:S(2)}, u32[]{:S(2)}) async-start(f32[64,32,128]{2,1,0:T(8,128)} %relayout_a.1), calls=%async_computation | async-start | bytes 2097152 | tf_op jit(solution)/shard_map/all_to_all | solution.py:442
  47.5 129.2 %all-to-all-start.1 = ((f32[64,32,128]{2,1,0:T(8,128)}), f32[64,32,128]{2,1,0:T(8,128)S(1)}, u32[]{:S(2)}, u32[]{:S(2)}) async-start(f32[64,32,128]{2,1,0:T(8,128)} %copy-done.2), calls=%async_computation.1 | async-start | bytes 2097152 | tf_op jit(solution)/shard_map/all_to_all | solution.py:448
  56.2 25.7 %collective-permute-start = (f32[32,8,128]{2,1,0:T(8,128)S(1)}, f32[32,8,128]{2,1,0:T(8,128)S(1)}, u32[]{:S(2)}, u32[]{:S(2)}) collective-permute-start(f32[32,8,128]{2,1,0:T(8,128)S(1)} %get-tuple-element.38), channel_id=1, source_target_pairs={{0,8},{4,12},{8,16},{12,20},{16,24},{20,28},{24,32},{28,36},{32,40... | collective-permute-start | bytes 393224 | tf_op jit(solution)/shard_map/ppermute | solution.py:421
  57.6 29.3 %collective-permute-start.1 = (f32[32,8,128]{2,1,0:T(8,128)S(1)}, f32[32,8,128]{2,1,0:T(8,128)S(1)}, u32[]{:S(2)}, u32[]{:S(2)}) collective-permute-start(f32[32,8,128]{2,1,0:T(8,128)S(1)} %get-tuple-element.39), channel_id=1, source_target_pairs={{0,16},{4,20},{8,24},{12,28},{16,32},{20,36},{24,40},{28,44},{32,4... | collective-permute-start | bytes 393224 | tf_op jit(solution)/shard_map/ppermute | solution.py:421
  59.7 38.4 %collective-permute-start.2 = (f32[32,8,128]{2,1,0:T(8,128)S(1)}, f32[32,8,128]{2,1,0:T(8,128)S(1)}, u32[]{:S(2)}, u32[]{:S(2)}) collective-permute-start(f32[32,8,128]{2,1,0:T(8,128)S(1)} %get-tuple-element.40), channel_id=1, source_target_pairs={{0,24},{4,28},{8,32},{12,36},{16,40},{20,44},{24,48},{28,52},{32,5... | collective-permute-start | bytes 393224 | tf_op jit(solution)/shard_map/ppermute | solution.py:421
  62.1 40.9 %collective-permute-start.3 = (f32[32,8,128]{2,1,0:T(8,128)S(1)}, f32[32,8,128]{2,1,0:T(8,128)S(1)}, u32[]{:S(2)}, u32[]{:S(2)}) collective-permute-start(f32[32,8,128]{2,1,0:T(8,128)S(1)} %get-tuple-element.41), channel_id=1, source_target_pairs={{0,32},{4,36},{8,40},{12,44},{16,48},{20,52},{24,56},{28,60},{32,0... | collective-permute-start | bytes 393224 | tf_op jit(solution)/shard_map/ppermute | solution.py:421
  64.2 38.8 %collective-permute-start.4 = (f32[32,8,128]{2,1,0:T(8,128)S(1)}, f32[32,8,128]{2,1,0:T(8,128)S(1)}, u32[]{:S(2)}, u32[]{:S(2)}) collective-permute-start(f32[32,8,128]{2,1,0:T(8,128)S(1)} %get-tuple-element.42), channel_id=1, source_target_pairs={{0,40},{4,44},{8,48},{12,52},{16,56},{20,60},{24,0},{28,4},{32,8},... | collective-permute-start | bytes 393224 | tf_op jit(solution)/shard_map/ppermute | solution.py:421
  81.9 21.1 %collective-permute-start.5 = (f32[32,8,128]{2,1,0:T(8,128)S(1)}, f32[32,8,128]{2,1,0:T(8,128)S(1)}, u32[]{:S(2)}, u32[]{:S(2)}) collective-permute-start(f32[32,8,128]{2,1,0:T(8,128)S(1)} %get-tuple-element.43), channel_id=1, source_target_pairs={{0,48},{4,52},{8,56},{12,60},{16,0},{20,4},{24,8},{28,12},{32,16},... | collective-permute-start | bytes 393224 | tf_op jit(solution)/shard_map/ppermute | solution.py:421
  86.9 16.0 %collective-permute-start.6 = (f32[32,8,128]{2,1,0:T(8,128)S(1)}, f32[32,8,128]{2,1,0:T(8,128)S(1)}, u32[]{:S(2)}, u32[]{:S(2)}) collective-permute-start(f32[32,8,128]{2,1,0:T(8,128)S(1)} %get-tuple-element.44), channel_id=1, source_target_pairs={{0,56},{4,60},{8,0},{12,4},{16,8},{20,12},{24,16},{28,20},{32,24},... | collective-permute-start | bytes 393224 | tf_op jit(solution)/shard_map/ppermute | solution.py:421
  106.4 14.9 %collective-permute-start.9 = (f32[256,128]{1,0:T(8,128)S(1)}, f32[256,128]{1,0:T(8,128)S(1)}, u32[]{:S(2)}, u32[]{:S(2)}) collective-permute-start(f32[256,128]{1,0:T(8,128)S(1)} %get-tuple-element.48), channel_id=1, source_target_pairs={{0,68},{4,64},{8,76},{12,72},{16,84},{20,80},{24,92},{28,88},{32,1... | collective-permute-start | bytes 393224 | tf_op jit(solution)/shard_map/ppermute | solution.py:431
  107.3 13.9 %collective-permute-start.10 = (f32[256,128]{1,0:T(8,128)S(1)}, f32[256,128]{1,0:T(8,128)S(1)}, u32[]{:S(2)}, u32[]{:S(2)}) collective-permute-start(f32[256,128]{1,0:T(8,128)S(1)} %get-tuple-element.49), channel_id=1, source_target_pairs={{0,128},{4,132},{8,136},{12,140},{16,144},{20,148},{24,152},{28,15... | collective-permute-start | bytes 393224 | tf_op jit(solution)/shard_map/ppermute | solution.py:431
  110.5 10.8 %collective-permute-start.11 = (f32[256,128]{1,0:T(8,128)S(1)}, f32[256,128]{1,0:T(8,128)S(1)}, u32[]{:S(2)}, u32[]{:S(2)}) collective-permute-start(f32[256,128]{1,0:T(8,128)S(1)} %get-tuple-element.50), channel_id=1, source_target_pairs={{0,132},{4,128},{8,140},{12,136},{16,148},{20,144},{24,156},{28,15... | collective-permute-start | bytes 393224 | tf_op jit(solution)/shard_map/ppermute | solution.py:431
  110.6 10.7 %collective-permute-start.12 = (f32[256,128]{1,0:T(8,128)S(1)}, f32[256,128]{1,0:T(8,128)S(1)}, u32[]{:S(2)}, u32[]{:S(2)}) collective-permute-start(f32[256,128]{1,0:T(8,128)S(1)} %get-tuple-element.51), channel_id=1, source_target_pairs={{0,192},{4,196},{8,200},{12,204},{16,208},{20,212},{24,216},{28,22... | collective-permute-start | bytes 393224 | tf_op jit(solution)/shard_map/ppermute | solution.py:431
  124.2 9.6 %collective-permute-start.14 = (f32[256,128]{1,0:T(8,128)S(1)}, f32[256,128]{1,0:T(8,128)S(1)}, u32[]{:S(2)}, u32[]{:S(2)}) collective-permute-start(f32[256,128]{1,0:T(8,128)S(1)} %get-tuple-element.54), channel_id=1, source_target_pairs={{0,8},{4,12},{8,16},{12,20},{16,24},{20,28},{24,32},{28,36},{32,40... | collective-permute-start | bytes 393224 | tf_op jit(solution)/shard_map/ppermute | solution.py:421
  124.3 10.0 %collective-permute-start.15 = (f32[256,128]{1,0:T(8,128)S(1)}, f32[256,128]{1,0:T(8,128)S(1)}, u32[]{:S(2)}, u32[]{:S(2)}) collective-permute-start(f32[256,128]{1,0:T(8,128)S(1)} %get-tuple-element.55), channel_id=1, source_target_pairs={{0,16},{4,20},{8,24},{12,28},{16,32},{20,36},{24,40},{28,44},{32,4... | collective-permute-start | bytes 393224 | tf_op jit(solution)/shard_map/ppermute | solution.py:421
  126.3 22.5 %collective-permute-start.16 = (f32[256,128]{1,0:T(8,128)S(1)}, f32[256,128]{1,0:T(8,128)S(1)}, u32[]{:S(2)}, u32[]{:S(2)}) collective-permute-start(f32[256,128]{1,0:T(8,128)S(1)} %get-tuple-element.56), channel_id=1, source_target_pairs={{0,24},{4,28},{8,32},{12,36},{16,40},{20,44},{24,48},{28,52},{32,5... | collective-permute-start | bytes 393224 | tf_op jit(solution)/shard_map/ppermute | solution.py:421
  128.4 20.3 %collective-permute-start.17 = (f32[256,128]{1,0:T(8,128)S(1)}, f32[256,128]{1,0:T(8,128)S(1)}, u32[]{:S(2)}, u32[]{:S(2)}) collective-permute-start(f32[256,128]{1,0:T(8,128)S(1)} %get-tuple-element.57), channel_id=1, source_target_pairs={{0,32},{4,36},{8,40},{12,44},{16,48},{20,52},{24,56},{28,60},{32,0... | collective-permute-start | bytes 393224 | tf_op jit(solution)/shard_map/ppermute | solution.py:421
  131.7 17.0 %collective-permute-start.18 = (f32[256,128]{1,0:T(8,128)S(1)}, f32[256,128]{1,0:T(8,128)S(1)}, u32[]{:S(2)}, u32[]{:S(2)}) collective-permute-start(f32[256,128]{1,0:T(8,128)S(1)} %get-tuple-element.58), channel_id=1, source_target_pairs={{0,40},{4,44},{8,48},{12,52},{16,56},{20,60},{24,0},{28,4},{32,8},... | collective-permute-start | bytes 393224 | tf_op jit(solution)/shard_map/ppermute | solution.py:421
  133.9 19.0 %collective-permute-start.19 = (f32[256,128]{1,0:T(8,128)S(1)}, f32[256,128]{1,0:T(8,128)S(1)}, u32[]{:S(2)}, u32[]{:S(2)}) collective-permute-start(f32[256,128]{1,0:T(8,128)S(1)} %get-tuple-element.59), channel_id=1, source_target_pairs={{0,48},{4,52},{8,56},{12,60},{16,0},{20,4},{24,8},{28,12},{32,16},... | collective-permute-start | bytes 393224 | tf_op jit(solution)/shard_map/ppermute | solution.py:421
  134.4 21.2 %collective-permute-start.20 = (f32[256,128]{1,0:T(8,128)S(1)}, f32[256,128]{1,0:T(8,128)S(1)}, u32[]{:S(2)}, u32[]{:S(2)}) collective-permute-start(f32[256,128]{1,0:T(8,128)S(1)} %get-tuple-element.60), channel_id=1, source_target_pairs={{0,56},{4,60},{8,0},{12,4},{16,8},{20,12},{24,16},{28,20},{32,24},... | collective-permute-start | bytes 393224 | tf_op jit(solution)/shard_map/ppermute | solution.py:421
  159.6 9.9 %collective-permute-start.24 = (f32[256,128]{1,0:T(8,128)S(1)}, f32[256,128]{1,0:T(8,128)S(1)}, u32[]{:S(2)}, u32[]{:S(2)}) collective-permute-start(f32[256,128]{1,0:T(8,128)S(1)} %get-tuple-element.65), channel_id=1, source_target_pairs={{0,128},{4,132},{8,136},{12,140},{16,144},{20,148},{24,152},{28,15... | collective-permute-start | bytes 393224 | tf_op jit(solution)/shard_map/ppermute | solution.py:431
  161.2 11.6 %collective-permute-start.25 = (f32[256,128]{1,0:T(8,128)S(1)}, f32[256,128]{1,0:T(8,128)S(1)}, u32[]{:S(2)}, u32[]{:S(2)}) collective-permute-start(f32[256,128]{1,0:T(8,128)S(1)} %get-tuple-element.66), channel_id=1, source_target_pairs={{0,132},{4,128},{8,140},{12,136},{16,148},{20,144},{24,156},{28,15... | collective-permute-start | bytes 393224 | tf_op jit(solution)/shard_map/ppermute | solution.py:431
  162.8 10.0 %collective-permute-start.26 = (f32[256,128]{1,0:T(8,128)S(1)}, f32[256,128]{1,0:T(8,128)S(1)}, u32[]{:S(2)}, u32[]{:S(2)}) collective-permute-start(f32[256,128]{1,0:T(8,128)S(1)} %get-tuple-element.67), channel_id=1, source_target_pairs={{0,192},{4,196},{8,200},{12,204},{16,208},{20,212},{24,216},{28,22... | collective-permute-start | bytes 393224 | tf_op jit(solution)/shard_map/ppermute | solution.py:431
  165.3 9.7 %collective-permute-start.27 = (f32[256,128]{1,0:T(8,128)S(1)}, f32[256,128]{1,0:T(8,128)S(1)}, u32[]{:S(2)}, u32[]{:S(2)}) collective-permute-start(f32[256,128]{1,0:T(8,128)S(1)} %get-tuple-element.68), channel_id=1, source_target_pairs={{0,196},{4,192},{8,204},{12,200},{16,212},{20,208},{24,220},{28,21... | collective-permute-start | bytes 393224 | tf_op jit(solution)/shard_map/ppermute | solution.py:431
  (9 other events, 48.6 us)

commit v3 on v2

--- a/solution.py
+++ b/solution.py
@@ -184,7 +184,7 @@
 def fft_p_kernel(pos_ref, *refs):
     g_refs, (wh_ref, wl_ref), o_refs = refs[:8], refs[8:10], refs[10:18]
     x_ref, y_ref, r_ref = refs[18:]
-    x, z, c = pos_ref[0], pos_ref[1], pos_ref[2]
+    x, c = pos_ref[0], pos_ref[2]
     for dx in range(NX):
         for dc in range(NC):
             start = ((x + NX - dx) % NX) * (NLON // NX) + ((c + dc) % NC) * LON
@@ -192,22 +192,21 @@
                 row = pl.multiple_of(start + zz * NC * LON, LON)
                 x_ref[pl.ds(row, LON), :] = g_refs[dx * NC + dc][zz * LON : (zz + 1) * LON, :]
     fft_core(x_ref, wh_ref, wl_ref, y_ref, r_ref)
-    for dz in range(NZ):
-        target = (z + dz) % NZ
-        for xx in range(NX):
-            for cc in range(NC):
-                k1 = xx * NZ * NC + target * NC + cc
+    for dx in range(NX):
+        for dc in range(NC):
+            target = ((x + dx) % NX) * NZ * NC + (c + dc) % NC
+            for zz in range(NZ):
                 for eight in range(KEPT // 8):
-                    row = (xx * NC + cc) * KEPT + eight * 8
-                    o_refs[dz][row : row + 8, :] = mode_rows(r_ref, k1, eight)
+                    row = zz * KEPT + eight * 8
+                    o_refs[dx * NC + dc][row : row + 8, :] = mode_rows(r_ref, target + zz * NC, eight)
 
 
 def fft_p(pos, blocks, wh, wl):
     return pl.pallas_call(
         fft_p_kernel,
         in_specs=[SMEM] + [VMEM] * 10,
-        out_specs=[VMEM] * NZ,
-        out_shape=[f32(NX * NC * KEPT, LANES)] * NZ,
+        out_specs=[VMEM] * (NX * NC),
+        out_shape=[f32(NZ * KEPT, LANES)] * (NX * NC),
         scratch_shapes=[pltpu.VMEM((NLON, LANES), jnp.float32)] + FFT_SCRATCH,
         compiler_params=PARAMS,
         name="fft_p",
@@ -264,22 +263,22 @@
 
 
 def spread_out_kernel(pos_ref, *refs):
-    h_refs, o_refs = refs[:NZ], refs[NZ:]
+    q_refs, o_refs = refs[:8], refs[8:]
     x, z, c = pos_ref[0], pos_ref[1], pos_ref[2]
-    for dx in range(NX):
-        for dc in range(NC):
-            source = pl.multiple_of((((x + dx) % NX) * NC + (c + dc) % NC) * KEPT, KEPT)
-            for dz in range(NZ):
-                row = pl.multiple_of(((z + NZ - dz) % NZ) * KEPT, KEPT)
-                o_refs[dx * NC + dc][pl.ds(row, KEPT), :] = h_refs[dz][pl.ds(source, KEPT), :]
+    for dz in range(NZ):
+        source = pl.multiple_of(((z + dz) % NZ) * KEPT, KEPT)
+        for dx in range(NX):
+            for dc in range(NC):
+                row = pl.multiple_of((((x + NX - dx) % NX) * NC + (c + dc) % NC) * KEPT, KEPT)
+                o_refs[dz][pl.ds(row, KEPT), :] = q_refs[dx * NC + dc][pl.ds(source, KEPT), :]
 
 
 def spread_out(pos, blocks):
     return pl.pallas_call(
         spread_out_kernel,
-        in_specs=[SMEM] + [VMEM] * NZ,
-        out_specs=[VMEM] * (NX * NC),
-        out_shape=[f32(NZ * KEPT, LANES)] * (NX * NC),
+        in_specs=[SMEM] + [VMEM] * (NX * NC),
+        out_specs=[VMEM] * NZ,
+        out_shape=[f32(NX * NC * KEPT, LANES)] * NZ,
         compiler_params=PARAMS,
         name="spread_out",
     )(pos, *blocks)
@@ -353,34 +352,33 @@
 ]
 
 
-def store_p_kernel(pos_ref, *refs):
-    q_refs, o_ref = refs[:8], refs[8]
-    x_ref, buf_ref, sem = refs[9:]
-    x, c = pos_ref[0], pos_ref[2]
-    for dx in range(NX):
-        for dc in range(NC):
-            base = ((x + NX - dx) % NX) * NC + (c + dc) % NC
-            for zz in range(NZ):
-                row = pl.multiple_of((base + zz * NX * NC) * PAD_K, 8)
-                x_ref[pl.ds(row, KEPT), :] = q_refs[dx * NC + dc][zz * KEPT : (zz + 1) * KEPT, :]
+def store_p_kernel(pos_ref, prior_ref, *refs):
+    del prior_ref
+    h_refs, o_ref = refs[:NZ], refs[NZ]
+    x_ref, buf_ref, sem = refs[NZ + 1 :]
+    z = pos_ref[1]
+    for dz in range(NZ):
+        base = ((z + NZ - dz) % NZ) * 8 * PAD_K
+        for s in range(8):
+            row = pl.multiple_of(base + s * PAD_K, 8)
+            x_ref[pl.ds(row, KEPT), :] = h_refs[dz][s * KEPT : (s + 1) * KEPT, :]
     store_half(x_ref, buf_ref, o_ref, sem, 0)
 
 
-def store_p(pos, blocks):
+def store_p(pos, prior, blocks):
     return pl.pallas_call(
         store_p_kernel,
-        in_specs=[SMEM] + [VMEM] * 8,
+        in_specs=[SMEM, HBM] + [VMEM] * NZ,
         out_specs=HBM,
         out_shape=f32(KEPT, FIELDS, 2 * LANES),
         scratch_shapes=STORE_SCRATCH,
+        input_output_aliases={1: 0},
         compiler_params=PARAMS,
         name="store_p",
-    )(pos, *blocks)
-
-
-def store_a_kernel(prior_ref, q_ref, o_ref, x_ref, buf_ref, sem):
-    del prior_ref
-
+    )(pos, prior, *blocks)
+
+
+def store_a_kernel(q_ref, o_ref, x_ref, buf_ref, sem):
     def field(f, carry):
         x_ref[pl.ds(pl.multiple_of(f * PAD_K, 8), KEPT), :] = q_ref[f]
         return carry
@@ -389,17 +387,16 @@
     store_half(x_ref, buf_ref, o_ref, sem, LANES)
 
 
-def store_a(prior, shares):
+def store_a(shares):
     return pl.pallas_call(
         store_a_kernel,
-        in_specs=[HBM, VMEM],
+        in_specs=[VMEM],
         out_specs=HBM,
         out_shape=f32(KEPT, FIELDS, 2 * LANES),
         scratch_shapes=STORE_SCRATCH,
-        input_output_aliases={0: 0},
         compiler_params=PARAMS,
         name="store_a",
-    )(prior, shares)
+    )(shares)
 
 
 def shifts(dx, dz, dc):
@@ -411,14 +408,16 @@
     ]
 
 
-Z_ORDER = (4, 3, 5, 2, 6, 1, 7)
+Z_FAR = (4, 3, 5)
+Z_NEAR = (2, 6, 1, 7)
 
 
 def exchange_z(blocks):
     out = [None] * NZ
     out[0] = blocks[0]
-    for dz in Z_ORDER:
-        out[dz] = lax.ppermute(blocks[dz], "lon", shifts(0, dz, 0))
+    for group in (Z_FAR, Z_NEAR):
+        for dz in group:
+            out[dz] = lax.ppermute(blocks[dz], "lon", shifts(0, dz, 0))
     return out
 
 
@@ -442,14 +441,14 @@
     gathered = lax.all_to_all(sent, "lon", split_axis=0, concat_axis=0, tiled=True)
     pieces = spread_x(pos, [b.reshape(LON * 8, LANES) for b in pieces])
     pieces = exchange_xc(pieces)
-    pieces = fft_p(pos, pieces, wh, wl)
-    pieces = exchange_z(pieces)
     spectrum = fft_a(gathered.reshape(NLON, LANES), wh, wl)
     shares = lax.all_to_all(spectrum, "lon", split_axis=0, concat_axis=0, tiled=True)
+    pieces = fft_p(pos, pieces, wh, wl)
+    pieces = exchange_xc(pieces)
     pieces = spread_out(pos, pieces)
-    pieces = exchange_xc(pieces)
-    out = store_p(pos, pieces)
-    out = store_a(out, shares)
+    pieces = exchange_z(pieces)
+    out = store_a(shares)
+    out = store_p(pos, out, pieces)
     return out.reshape(2, RADIX, FIELDS, 2 * LANES)
 
 

time: 178 us -> 174 us (0.978)
  waiting for transfers between devices: 91.4 us -> 87.5 us
    ppermute x14, waiting for transfers between devices: 16.6 us -> 14.1 us  [exchange_xc(): lax.ppermute(blocks[dx * NC + dc], 'lon', shifts(dx, 0, dc))]
  transfers between devices with their start and end apart: 30 -> 30, of which waited for: 15 -> 16; matrix products, arithmetic and copies ran while one was open for 2% -> 2% of each run, Pallas kernels for 4% -> 3%
where the time goes in v3:
time: 174 us; the launch traced here: 173 us
  waiting for transfers between devices  87.5 us (50%)
  starting transfers between devices  66.8 us (38%)
  Pallas kernels  10.8 us (6%)
  local copies, waits for them, and re-layouts  4.15 us (2%)
  other arithmetic  3.31 us (2%)
    ppermute x14, waiting for transfers between devices, exchange_z(): out[dz] = lax.ppermute(blocks[dz], 'lon', shifts(0, dz, 0))  48.2 us
    ppermute x14, starting transfers between devices, exchange_z(): out[dz] = lax.ppermute(blocks[dz], 'lon', shifts(0, dz, 0))  28.3 us
    all_to_all x1, waiting for transfers between devices, local(): lax.all_to_all(sent, 'lon', split_axis=0, concat_axis=0, tiled=True)  25.2 us
    ppermute x14, starting transfers between devices, exchange_xc(): lax.ppermute(blocks[dx * NC + dc], 'lon', shifts(dx, 0, dc))  19.3 us
    ppermute x14, waiting for transfers between devices, exchange_xc(): lax.ppermute(blocks[dx * NC + dc], 'lon', shifts(dx, 0, dc))  14.1 us
    all_to_all x1, starting transfers between devices, local(): lax.all_to_all(sent, 'lon', split_axis=0, concat_axis=0, tiled=True)  13 us
    all_to_all x1, starting transfers between devices, local(): lax.all_to_all(spectrum, 'lon', split_axis=0, concat_axis=0, tiled=True)  6.2 us
    unnamed x6, local copies, waits for them, and re-layouts  4.15 us
  transfers between devices with their start and end apart: 30, of which 16 were waited for; matrix products, arithmetic and copies ran while one was open for 2% of the time, Pallas kernels for 3%

profile of v3, /device:TPU:1, one launch (start us, length us, event | category | flops | bytes accessed | tf_op | source)
XLA Modules:
  0.0 173.0 jit_solution(588258906698841373)
XLA Ops:
  3.1 13.0 %all-to-all-start = ((f32[64,32,128]{2,1,0:T(8,128)}), f32[64,32,128]{2,1,0:T(8,128)S(1)}, u32[]{:S(2)}, u32[]{:S(2)}) async-start(f32[64,32,128]{2,1,0:T(8,128)} %relayout_a.1), calls=%async_computation | async-start | bytes 2097152 | tf_op jit(solution)/shard_map/all_to_all | solution.py:441
  16.2 2.5 %select_select_fusion.1 = (f32[8,2,64,128]{3,2,1,0:T(8,128)S(1)}, f32[8,2,64,128]{3,2,1,0:T(8,128)S(1)}, f32[8,2,64,128]{3,2,1,0:T(8,128)S(1)}, f32[8,2,64,128]{3,2,1,0:T(8,128)S(1)}) fusion(pred[2]{0:T(512)(128)(4,1)S(1)} %iota_compare_fusion.1, pred[8]{0:T(512)(128)(4,1)S(1)} %iota_compare_fusion, s32[64]{0:T(128)S(1)} %iota_multiply_fusion, ...), kind=kLoop, calls=%fused_computation.9 | loop fusion | flops 4456448 | bytes 2097450 | tf_op jit(solution)/shard_map/jit(_where)/select_n | solution.py:56
  19.4 25.2 %all-to-all-done = f32[64,32,128]{2,1,0:T(8,128)S(1)} async-done(((f32[64,32,128]{2,1,0:T(8,128)}), f32[64,32,128]{2,1,0:T(8,128)S(1)}, u32[]{:S(2)}, u32[]{:S(2)}) %all-to-all-start) | async-done | bytes 1048608 | tf_op jit(solution)/shard_map/all_to_all | solution.py:441
  47.5 6.2 %all-to-all-start.1 = ((f32[64,32,128]{2,1,0:T(8,128)}), f32[64,32,128]{2,1,0:T(8,128)S(1)}, u32[]{:S(2)}, u32[]{:S(2)}) async-start(f32[64,32,128]{2,1,0:T(8,128)} %copy-done.2), calls=%async_computation.1 | async-start | bytes 2097152 | tf_op jit(solution)/shard_map/all_to_all | solution.py:445
  56.2 2.3 %collective-permute-start.1 = (f32[32,8,128]{2,1,0:T(8,128)S(1)}, f32[32,8,128]{2,1,0:T(8,128)S(1)}, u32[]{:S(2)}, u32[]{:S(2)}) collective-permute-start(f32[32,8,128]{2,1,0:T(8,128)S(1)} %get-tuple-element.39), channel_id=1, source_target_pairs={{0,16},{4,20},{8,24},{12,28},{16,32},{20,36},{24,40},{28,44},{32,4... | collective-permute-start | bytes 393224 | tf_op jit(solution)/shard_map/ppermute | solution.py:420
  58.5 3.3 %collective-permute-start.2 = (f32[32,8,128]{2,1,0:T(8,128)S(1)}, f32[32,8,128]{2,1,0:T(8,128)S(1)}, u32[]{:S(2)}, u32[]{:S(2)}) collective-permute-start(f32[32,8,128]{2,1,0:T(8,128)S(1)} %get-tuple-element.40), channel_id=1, source_target_pairs={{0,24},{4,28},{8,32},{12,36},{16,40},{20,44},{24,48},{28,52},{32,5... | collective-permute-start | bytes 393224 | tf_op jit(solution)/shard_map/ppermute | solution.py:420
  63.0 3.3 %collective-permute-start.4 = (f32[32,8,128]{2,1,0:T(8,128)S(1)}, f32[32,8,128]{2,1,0:T(8,128)S(1)}, u32[]{:S(2)}, u32[]{:S(2)}) collective-permute-start(f32[32,8,128]{2,1,0:T(8,128)S(1)} %get-tuple-element.42), channel_id=1, source_target_pairs={{0,40},{4,44},{8,48},{12,52},{16,56},{20,60},{24,0},{28,4},{32,8},... | collective-permute-start | bytes 393224 | tf_op jit(solution)/shard_map/ppermute | solution.py:420
  66.3 3.3 %collective-permute-start.5 = (f32[32,8,128]{2,1,0:T(8,128)S(1)}, f32[32,8,128]{2,1,0:T(8,128)S(1)}, u32[]{:S(2)}, u32[]{:S(2)}) collective-permute-start(f32[32,8,128]{2,1,0:T(8,128)S(1)} %get-tuple-element.43), channel_id=1, source_target_pairs={{0,48},{4,52},{8,56},{12,60},{16,0},{20,4},{24,8},{28,12},{32,16},... | collective-permute-start | bytes 393224 | tf_op jit(solution)/shard_map/ppermute | solution.py:420
  69.6 14.7 %collective-permute-done.1 = f32[32,8,128]{2,1,0:T(8,128)S(1)} collective-permute-done((f32[32,8,128]{2,1,0:T(8,128)S(1)}, f32[32,8,128]{2,1,0:T(8,128)S(1)}, u32[]{:S(2)}, u32[]{:S(2)}) %collective-permute-start.1) | collective-permute-done | bytes 131104 | tf_op jit(solution)/shard_map/ppermute | solution.py:420
  86.3 9.0 %collective-permute-done.2 = f32[32,8,128]{2,1,0:T(8,128)S(1)} collective-permute-done((f32[32,8,128]{2,1,0:T(8,128)S(1)}, f32[32,8,128]{2,1,0:T(8,128)S(1)}, u32[]{:S(2)}, u32[]{:S(2)}) %collective-permute-start.2) | collective-permute-done | bytes 131104 | tf_op jit(solution)/shard_map/ppermute | solution.py:420
  95.4 4.7 %collective-permute-done.3 = f32[32,8,128]{2,1,0:T(8,128)S(1)} collective-permute-done((f32[32,8,128]{2,1,0:T(8,128)S(1)}, f32[32,8,128]{2,1,0:T(8,128)S(1)}, u32[]{:S(2)}, u32[]{:S(2)}) %collective-permute-start.3) | collective-permute-done | bytes 131104 | tf_op jit(solution)/shard_map/ppermute | solution.py:420
  100.5 2.2 %collective-permute-done = f32[32,8,128]{2,1,0:T(8,128)S(1)} collective-permute-done((f32[32,8,128]{2,1,0:T(8,128)S(1)}, f32[32,8,128]{2,1,0:T(8,128)S(1)}, u32[]{:S(2)}, u32[]{:S(2)}) %collective-permute-start) | collective-permute-done | bytes 131104 | tf_op jit(solution)/shard_map/ppermute | solution.py:420
  103.6 3.1 %collective-permute-start.10 = (f32[256,128]{1,0:T(8,128)S(1)}, f32[256,128]{1,0:T(8,128)S(1)}, u32[]{:S(2)}, u32[]{:S(2)}) collective-permute-start(f32[256,128]{1,0:T(8,128)S(1)} %get-tuple-element.49), channel_id=1, source_target_pairs={{0,128},{4,132},{8,136},{12,140},{16,144},{20,148},{24,152},{28,15... | collective-permute-start | bytes 393224 | tf_op jit(solution)/shard_map/ppermute | solution.py:430
  107.9 2.6 %collective-permute-start.12 = (f32[256,128]{1,0:T(8,128)S(1)}, f32[256,128]{1,0:T(8,128)S(1)}, u32[]{:S(2)}, u32[]{:S(2)}) collective-permute-start(f32[256,128]{1,0:T(8,128)S(1)} %get-tuple-element.51), channel_id=1, source_target_pairs={{0,192},{4,196},{8,200},{12,204},{16,208},{20,212},{24,216},{28,22... | collective-permute-start | bytes 393224 | tf_op jit(solution)/shard_map/ppermute | solution.py:430
  116.0 3.6 %collective-permute-done.13.refs_7_ = f32[256,128]{1,0:T(8,128)S(1)} collective-permute-done((f32[256,128]{1,0:T(8,128)S(1)}, f32[256,128]{1,0:T(8,128)S(1)}, u32[]{:S(2)}, u32[]{:S(2)}) %collective-permute-start.13) | collective-permute-done | bytes 131104 | tf_op jit(solution)/shard_map/ppermute | solution.py:430
  120.7 2.3 %fft_p.1 = (f32[256,128]{1,0:T(8,128)S(1)}, f32[256,128]{1,0:T(8,128)S(1)}, f32[256,128]{1,0:T(8,128)S(1)}, f32[256,128]{1,0:T(8,128)S(1)}, f32[256,128]{1,0:T(8...) custom-call(s32[3]{0:T(128)S(1)} %pad_add_fusion.pos_ref, ...), custom_call_target="tpu_custom_call" | custom-call | tf_op jit(solution)/shard_map/fft_p/pallas_call | solution.py:205
  125.3 2.6 %collective-permute-start.17 = (f32[256,128]{1,0:T(8,128)S(1)}, f32[256,128]{1,0:T(8,128)S(1)}, u32[]{:S(2)}, u32[]{:S(2)}) collective-permute-start(f32[256,128]{1,0:T(8,128)S(1)} %get-tuple-element.57), channel_id=1, source_target_pairs={{0,128},{4,132},{8,136},{12,140},{16,144},{20,148},{24,152},{28,15... | collective-permute-start | bytes 393224 | tf_op jit(solution)/shard_map/ppermute | solution.py:430
  131.7 6.9 %collective-permute-done.16.refs_3_ = f32[256,128]{1,0:T(8,128)S(1)} collective-permute-done((f32[256,128]{1,0:T(8,128)S(1)}, f32[256,128]{1,0:T(8,128)S(1)}, u32[]{:S(2)}, u32[]{:S(2)}) %collective-permute-start.16) | collective-permute-done | bytes 131104 | tf_op jit(solution)/shard_map/ppermute | solution.py:430
  140.1 2.6 %collective-permute-start.22 = (f32[256,128]{1,0:T(8,128)S(1)}, f32[256,128]{1,0:T(8,128)S(1)}, u32[]{:S(2)}, u32[]{:S(2)}) collective-permute-start(f32[256,128]{1,0:T(8,128)S(1)} %get-tuple-element.63), channel_id=1, source_target_pairs={{0,16},{4,20},{8,24},{12,28},{16,32},{20,36},{24,40},{28,44},{32,4... | collective-permute-start | bytes 393224 | tf_op jit(solution)/shard_map/ppermute | solution.py:420
  142.8 2.1 %collective-permute-start.23 = (f32[256,128]{1,0:T(8,128)S(1)}, f32[256,128]{1,0:T(8,128)S(1)}, u32[]{:S(2)}, u32[]{:S(2)}) collective-permute-start(f32[256,128]{1,0:T(8,128)S(1)} %get-tuple-element.64), channel_id=1, source_target_pairs={{0,24},{4,28},{8,32},{12,36},{16,40},{20,44},{24,48},{28,52},{32,5... | collective-permute-start | bytes 393224 | tf_op jit(solution)/shard_map/ppermute | solution.py:420
  145.8 3.5 %collective-permute-start.25 = (f32[256,128]{1,0:T(8,128)S(1)}, f32[256,128]{1,0:T(8,128)S(1)}, u32[]{:S(2)}, u32[]{:S(2)}) collective-permute-start(f32[256,128]{1,0:T(8,128)S(1)} %get-tuple-element.66), channel_id=1, source_target_pairs={{0,40},{4,44},{8,48},{12,52},{16,56},{20,60},{24,0},{28,4},{32,8},... | collective-permute-start | bytes 393224 | tf_op jit(solution)/shard_map/ppermute | solution.py:420
  149.3 2.4 %collective-permute-start.26 = (f32[256,128]{1,0:T(8,128)S(1)}, f32[256,128]{1,0:T(8,128)S(1)}, u32[]{:S(2)}, u32[]{:S(2)}) collective-permute-start(f32[256,128]{1,0:T(8,128)S(1)} %get-tuple-element.67), channel_id=1, source_target_pairs={{0,48},{4,52},{8,56},{12,60},{16,0},{20,4},{24,8},{28,12},{32,16},... | collective-permute-start | bytes 393224 | tf_op jit(solution)/shard_map/ppermute | solution.py:420
  154.0 9.4 %collective-permute-done.23.refs_3_ = f32[256,128]{1,0:T(8,128)S(1)} collective-permute-done((f32[256,128]{1,0:T(8,128)S(1)}, f32[256,128]{1,0:T(8,128)S(1)}, u32[]{:S(2)}, u32[]{:S(2)}) %collective-permute-start.23) | collective-permute-done | bytes 131104 | tf_op jit(solution)/shard_map/ppermute | solution.py:420
  164.5 5.5 %collective-permute-done.26.refs_6_ = f32[256,128]{1,0:T(8,128)S(1)} collective-permute-done((f32[256,128]{1,0:T(8,128)S(1)}, f32[256,128]{1,0:T(8,128)S(1)}, u32[]{:S(2)}, u32[]{:S(2)}) %collective-permute-start.26) | collective-permute-done | bytes 131104 | tf_op jit(solution)/shard_map/ppermute | solution.py:420
  (59 shorter events, 36.1 us)
Async XLA Ops:
  3.1 41.5 %all-to-all-start = ((f32[64,32,128]{2,1,0:T(8,128)}), f32[64,32,128]{2,1,0:T(8,128)S(1)}, u32[]{:S(2)}, u32[]{:S(2)}) async-start(f32[64,32,128]{2,1,0:T(8,128)} %relayout_a.1), calls=%async_computation | async-start | bytes 2097152 | tf_op jit(solution)/shard_map/all_to_all | solution.py:441
  47.5 105.5 %all-to-all-start.1 = ((f32[64,32,128]{2,1,0:T(8,128)}), f32[64,32,128]{2,1,0:T(8,128)S(1)}, u32[]{:S(2)}, u32[]{:S(2)}) async-start(f32[64,32,128]{2,1,0:T(8,128)} %copy-done.2), calls=%async_computation.1 | async-start | bytes 2097152 | tf_op jit(solution)/shard_map/all_to_all | solution.py:445
  56.2 28.1 %collective-permute-start.1 = (f32[32,8,128]{2,1,0:T(8,128)S(1)}, f32[32,8,128]{2,1,0:T(8,128)S(1)}, u32[]{:S(2)}, u32[]{:S(2)}) collective-permute-start(f32[32,8,128]{2,1,0:T(8,128)S(1)} %get-tuple-element.39), channel_id=1, source_target_pairs={{0,16},{4,20},{8,24},{12,28},{16,32},{20,36},{24,40},{28,44},{32,4... | collective-permute-start | bytes 393224 | tf_op jit(solution)/shard_map/ppermute | solution.py:420
  58.5 36.8 %collective-permute-start.2 = (f32[32,8,128]{2,1,0:T(8,128)S(1)}, f32[32,8,128]{2,1,0:T(8,128)S(1)}, u32[]{:S(2)}, u32[]{:S(2)}) collective-permute-start(f32[32,8,128]{2,1,0:T(8,128)S(1)} %get-tuple-element.40), channel_id=1, source_target_pairs={{0,24},{4,28},{8,32},{12,36},{16,40},{20,44},{24,48},{28,52},{32,5... | collective-permute-start | bytes 393224 | tf_op jit(solution)/shard_map/ppermute | solution.py:420
  61.8 38.3 %collective-permute-start.3 = (f32[32,8,128]{2,1,0:T(8,128)S(1)}, f32[32,8,128]{2,1,0:T(8,128)S(1)}, u32[]{:S(2)}, u32[]{:S(2)}) collective-permute-start(f32[32,8,128]{2,1,0:T(8,128)S(1)} %get-tuple-element.41), channel_id=1, source_target_pairs={{0,32},{4,36},{8,40},{12,44},{16,48},{20,52},{24,56},{28,60},{32,0... | collective-permute-start | bytes 393224 | tf_op jit(solution)/shard_map/ppermute | solution.py:420
  63.0 37.1 %collective-permute-start.4 = (f32[32,8,128]{2,1,0:T(8,128)S(1)}, f32[32,8,128]{2,1,0:T(8,128)S(1)}, u32[]{:S(2)}, u32[]{:S(2)}) collective-permute-start(f32[32,8,128]{2,1,0:T(8,128)S(1)} %get-tuple-element.42), channel_id=1, source_target_pairs={{0,40},{4,44},{8,48},{12,52},{16,56},{20,60},{24,0},{28,4},{32,8},... | collective-permute-start | bytes 393224 | tf_op jit(solution)/shard_map/ppermute | solution.py:420
  66.3 33.8 %collective-permute-start.5 = (f32[32,8,128]{2,1,0:T(8,128)S(1)}, f32[32,8,128]{2,1,0:T(8,128)S(1)}, u32[]{:S(2)}, u32[]{:S(2)}) collective-permute-start(f32[32,8,128]{2,1,0:T(8,128)S(1)} %get-tuple-element.43), channel_id=1, source_target_pairs={{0,48},{4,52},{8,56},{12,60},{16,0},{20,4},{24,8},{28,12},{32,16},... | collective-permute-start | bytes 393224 | tf_op jit(solution)/shard_map/ppermute | solution.py:420
  84.3 16.2 %collective-permute-start.6 = (f32[32,8,128]{2,1,0:T(8,128)S(1)}, f32[32,8,128]{2,1,0:T(8,128)S(1)}, u32[]{:S(2)}, u32[]{:S(2)}) collective-permute-start(f32[32,8,128]{2,1,0:T(8,128)S(1)} %get-tuple-element.44), channel_id=1, source_target_pairs={{0,56},{4,60},{8,0},{12,4},{16,8},{20,12},{24,16},{28,20},{32,24},... | collective-permute-start | bytes 393224 | tf_op jit(solution)/shard_map/ppermute | solution.py:420
  107.9 8.0 %collective-permute-start.12 = (f32[256,128]{1,0:T(8,128)S(1)}, f32[256,128]{1,0:T(8,128)S(1)}, u32[]{:S(2)}, u32[]{:S(2)}) collective-permute-start(f32[256,128]{1,0:T(8,128)S(1)} %get-tuple-element.51), channel_id=1, source_target_pairs={{0,192},{4,196},{8,200},{12,204},{16,208},{20,212},{24,216},{28,22... | collective-permute-start | bytes 393224 | tf_op jit(solution)/shard_map/ppermute | solution.py:430
  110.5 9.0 %collective-permute-start.13 = (f32[256,128]{1,0:T(8,128)S(1)}, f32[256,128]{1,0:T(8,128)S(1)}, u32[]{:S(2)}, u32[]{:S(2)}) collective-permute-start(f32[256,128]{1,0:T(8,128)S(1)} %get-tuple-element.52), channel_id=1, source_target_pairs={{0,196},{4,192},{8,204},{12,200},{16,212},{20,208},{24,220},{28,21... | collective-permute-start | bytes 393224 | tf_op jit(solution)/shard_map/ppermute | solution.py:430
  110.5 9.0 %collective-permute-start.7 = (f32[256,128]{1,0:T(8,128)S(1)}, f32[256,128]{1,0:T(8,128)S(1)}, u32[]{:S(2)}, u32[]{:S(2)}) collective-permute-start(f32[256,128]{1,0:T(8,128)S(1)} %get-tuple-element.46), channel_id=1, source_target_pairs={{0,4},{4,0},{8,12},{12,8},{16,20},{20,16},{24,28},{28,24},{32,36},... | collective-permute-start | bytes 393224 | tf_op jit(solution)/shard_map/ppermute | solution.py:430
  111.4 8.1 %collective-permute-start.8 = (f32[256,128]{1,0:T(8,128)S(1)}, f32[256,128]{1,0:T(8,128)S(1)}, u32[]{:S(2)}, u32[]{:S(2)}) collective-permute-start(f32[256,128]{1,0:T(8,128)S(1)} %get-tuple-element.47), channel_id=1, source_target_pairs={{0,64},{4,68},{8,72},{12,76},{16,80},{20,84},{24,88},{28,92},{32,9... | collective-permute-start | bytes 393224 | tf_op jit(solution)/shard_map/ppermute | solution.py:430
  123.8 14.9 %collective-permute-start.16 = (f32[256,128]{1,0:T(8,128)S(1)}, f32[256,128]{1,0:T(8,128)S(1)}, u32[]{:S(2)}, u32[]{:S(2)}) collective-permute-start(f32[256,128]{1,0:T(8,128)S(1)} %get-tuple-element.56), channel_id=1, source_target_pairs={{0,68},{4,64},{8,76},{12,72},{16,84},{20,80},{24,92},{28,88},{32,1... | collective-permute-start | bytes 393224 | tf_op jit(solution)/shard_map/ppermute | solution.py:430
  125.3 13.3 %collective-permute-start.17 = (f32[256,128]{1,0:T(8,128)S(1)}, f32[256,128]{1,0:T(8,128)S(1)}, u32[]{:S(2)}, u32[]{:S(2)}) collective-permute-start(f32[256,128]{1,0:T(8,128)S(1)} %get-tuple-element.57), channel_id=1, source_target_pairs={{0,128},{4,132},{8,136},{12,140},{16,144},{20,148},{24,152},{28,15... | collective-permute-start | bytes 393224 | tf_op jit(solution)/shard_map/ppermute | solution.py:430
  127.9 10.8 %collective-permute-start.18 = (f32[256,128]{1,0:T(8,128)S(1)}, f32[256,128]{1,0:T(8,128)S(1)}, u32[]{:S(2)}, u32[]{:S(2)}) collective-permute-start(f32[256,128]{1,0:T(8,128)S(1)} %get-tuple-element.58), channel_id=1, source_target_pairs={{0,132},{4,128},{8,140},{12,136},{16,148},{20,144},{24,156},{28,15... | collective-permute-start | bytes 393224 | tf_op jit(solution)/shard_map/ppermute | solution.py:430
  128.3 10.4 %collective-permute-start.19 = (f32[256,128]{1,0:T(8,128)S(1)}, f32[256,128]{1,0:T(8,128)S(1)}, u32[]{:S(2)}, u32[]{:S(2)}) collective-permute-start(f32[256,128]{1,0:T(8,128)S(1)} %get-tuple-element.59), channel_id=1, source_target_pairs={{0,192},{4,196},{8,200},{12,204},{16,208},{20,212},{24,216},{28,22... | collective-permute-start | bytes 393224 | tf_op jit(solution)/shard_map/ppermute | solution.py:430
  130.0 9.3 %collective-permute-start.20 = (f32[256,128]{1,0:T(8,128)S(1)}, f32[256,128]{1,0:T(8,128)S(1)}, u32[]{:S(2)}, u32[]{:S(2)}) collective-permute-start(f32[256,128]{1,0:T(8,128)S(1)} %get-tuple-element.60), channel_id=1, source_target_pairs={{0,196},{4,192},{8,204},{12,200},{16,212},{20,208},{24,220},{28,21... | collective-permute-start | bytes 393224 | tf_op jit(solution)/shard_map/ppermute | solution.py:430
  140.0 9.3 %collective-permute-start.21 = (f32[256,128]{1,0:T(8,128)S(1)}, f32[256,128]{1,0:T(8,128)S(1)}, u32[]{:S(2)}, u32[]{:S(2)}) collective-permute-start(f32[256,128]{1,0:T(8,128)S(1)} %get-tuple-element.62), channel_id=1, source_target_pairs={{0,8},{4,12},{8,16},{12,20},{16,24},{20,28},{24,32},{28,36},{32,40... | collective-permute-start | bytes 393224 | tf_op jit(solution)/shard_map/ppermute | solution.py:420
  140.1 11.6 %collective-permute-start.22 = (f32[256,128]{1,0:T(8,128)S(1)}, f32[256,128]{1,0:T(8,128)S(1)}, u32[]{:S(2)}, u32[]{:S(2)}) collective-permute-start(f32[256,128]{1,0:T(8,128)S(1)} %get-tuple-element.63), channel_id=1, source_target_pairs={{0,16},{4,20},{8,24},{12,28},{16,32},{20,36},{24,40},{28,44},{32,4... | collective-permute-start | bytes 393224 | tf_op jit(solution)/shard_map/ppermute | solution.py:420
  142.8 20.7 %collective-permute-start.23 = (f32[256,128]{1,0:T(8,128)S(1)}, f32[256,128]{1,0:T(8,128)S(1)}, u32[]{:S(2)}, u32[]{:S(2)}) collective-permute-start(f32[256,128]{1,0:T(8,128)S(1)} %get-tuple-element.64), channel_id=1, source_target_pairs={{0,24},{4,28},{8,32},{12,36},{16,40},{20,44},{24,48},{28,52},{32,5... | collective-permute-start | bytes 393224 | tf_op jit(solution)/shard_map/ppermute | solution.py:420
  144.8 19.7 %collective-permute-start.24 = (f32[256,128]{1,0:T(8,128)S(1)}, f32[256,128]{1,0:T(8,128)S(1)}, u32[]{:S(2)}, u32[]{:S(2)}) collective-permute-start(f32[256,128]{1,0:T(8,128)S(1)} %get-tuple-element.65), channel_id=1, source_target_pairs={{0,32},{4,36},{8,40},{12,44},{16,48},{20,52},{24,56},{28,60},{32,0... | collective-permute-start | bytes 393224 | tf_op jit(solution)/shard_map/ppermute | solution.py:420
  145.8 18.7 %collective-permute-start.25 = (f32[256,128]{1,0:T(8,128)S(1)}, f32[256,128]{1,0:T(8,128)S(1)}, u32[]{:S(2)}, u32[]{:S(2)}) collective-permute-start(f32[256,128]{1,0:T(8,128)S(1)} %get-tuple-element.66), channel_id=1, source_target_pairs={{0,40},{4,44},{8,48},{12,52},{16,56},{20,60},{24,0},{28,4},{32,8},... | collective-permute-start | bytes 393224 | tf_op jit(solution)/shard_map/ppermute | solution.py:420
  149.3 20.7 %collective-permute-start.26 = (f32[256,128]{1,0:T(8,128)S(1)}, f32[256,128]{1,0:T(8,128)S(1)}, u32[]{:S(2)}, u32[]{:S(2)}) collective-permute-start(f32[256,128]{1,0:T(8,128)S(1)} %get-tuple-element.67), channel_id=1, source_target_pairs={{0,48},{4,52},{8,56},{12,60},{16,0},{20,4},{24,8},{28,12},{32,16},... | collective-permute-start | bytes 393224 | tf_op jit(solution)/shard_map/ppermute | solution.py:420
  151.7 19.5 %collective-permute-start.27 = (f32[256,128]{1,0:T(8,128)S(1)}, f32[256,128]{1,0:T(8,128)S(1)}, u32[]{:S(2)}, u32[]{:S(2)}) collective-permute-start(f32[256,128]{1,0:T(8,128)S(1)} %get-tuple-element.68), channel_id=1, source_target_pairs={{0,56},{4,60},{8,0},{12,4},{16,8},{20,12},{24,16},{28,20},{32,24},... | collective-permute-start | bytes 393224 | tf_op jit(solution)/shard_map/ppermute | solution.py:420
  (9 other events, 44.9 us)

commit v4 on v2

--- a/solution.py
+++ b/solution.py
@@ -422,13 +422,14 @@
     return out
 
 
+X_ORDER = ((2, 0), (2, 1), (1, 0), (3, 0), (1, 1), (3, 1), (0, 1))
+
+
 def exchange_xc(blocks):
     out = [None] * (NX * NC)
     out[0] = blocks[0]
-    for dx in (2, 1, 3, 0):
-        for dc in range(NC):
-            if dx or dc:
-                out[dx * NC + dc] = lax.ppermute(blocks[dx * NC + dc], "lon", shifts(dx, 0, dc))
+    for dx, dc in X_ORDER:
+        out[dx * NC + dc] = lax.ppermute(blocks[dx * NC + dc], "lon", shifts(dx, 0, dc))
     return out
 
 

time: 178 us -> 178 us (level)
  no operation moved by 1% of the time
where the time goes in v4:
time: 178 us
  waiting for transfers between devices  91.4 us (51%)
  starting transfers between devices  67.9 us (38%)
  Pallas kernels  10.8 us (6%)
  local copies, waits for them, and re-layouts  4.16 us (2%)
  other arithmetic  3.31 us (2%)
    ppermute x14, waiting for transfers between devices, exchange_z(): out[dz] = lax.ppermute(blocks[dz], 'lon', shifts(0, dz, 0))  49.6 us
    ppermute x14, starting transfers between devices, exchange_z(): out[dz] = lax.ppermute(blocks[dz], 'lon', shifts(0, dz, 0))  28.5 us
    all_to_all x1, waiting for transfers between devices, local(): lax.all_to_all(sent, 'lon', split_axis=0, concat_axis=0, tiled=True)  25.2 us
    ppermute x14, starting transfers between devices, exchange_xc(): lax.ppermute(blocks[dx * NC + dc], 'lon', shifts(dx, 0, dc))  20.2 us
    ppermute x14, waiting for transfers between devices, exchange_xc(): lax.ppermute(blocks[dx * NC + dc], 'lon', shifts(dx, 0, dc))  16.6 us
    all_to_all x1, starting transfers between devices, local(): lax.all_to_all(sent, 'lon', split_axis=0, concat_axis=0, tiled=True)  13 us
    all_to_all x1, starting transfers between devices, local(): lax.all_to_all(spectrum, 'lon', split_axis=0, concat_axis=0, tiled=True)  6.2 us
    unnamed x6, local copies, waits for them, and re-layouts  4.16 us
  transfers between devices with their start and end apart: 30, of which 15 were waited for; matrix products, arithmetic and copies ran while one was open for 2% of the time, Pallas kernels for 4%

profile of v4, /device:TPU:1, one launch (start us, length us, event | category | flops | bytes accessed | tf_op | source)
XLA Modules:
  0.0 178.0 jit_solution(14540416728200572378)
XLA Ops:
  3.1 13.0 %all-to-all-start = ((f32[64,32,128]{2,1,0:T(8,128)}), f32[64,32,128]{2,1,0:T(8,128)S(1)}, u32[]{:S(2)}, u32[]{:S(2)}) async-start(f32[64,32,128]{2,1,0:T(8,128)} %relayout_a.1), calls=%async_computation | async-start | bytes 2097152 | tf_op jit(solution)/shard_map/all_to_all | solution.py:443
  16.2 2.5 %select_select_fusion.1 = (f32[8,2,64,128]{3,2,1,0:T(8,128)S(1)}, f32[8,2,64,128]{3,2,1,0:T(8,128)S(1)}, f32[8,2,64,128]{3,2,1,0:T(8,128)S(1)}, f32[8,2,64,128]{3,2,1,0:T(8,128)S(1)}) fusion(pred[2]{0:T(512)(128)(4,1)S(1)} %iota_compare_fusion.1, pred[8]{0:T(512)(128)(4,1)S(1)} %iota_compare_fusion, s32[64]{0:T(128)S(1)} %iota_multiply_fusion, ...), kind=kLoop, calls=%fused_computation.9 | loop fusion | flops 4456448 | bytes 2097450 | tf_op jit(solution)/shard_map/jit(_where)/select_n | solution.py:56
  19.4 25.2 %all-to-all-done = f32[64,32,128]{2,1,0:T(8,128)S(1)} async-done(((f32[64,32,128]{2,1,0:T(8,128)}), f32[64,32,128]{2,1,0:T(8,128)S(1)}, u32[]{:S(2)}, u32[]{:S(2)}) %all-to-all-start) | async-done | bytes 1048608 | tf_op jit(solution)/shard_map/all_to_all | solution.py:443
  47.5 6.2 %all-to-all-start.1 = ((f32[64,32,128]{2,1,0:T(8,128)}), f32[64,32,128]{2,1,0:T(8,128)S(1)}, u32[]{:S(2)}, u32[]{:S(2)}) async-start(f32[64,32,128]{2,1,0:T(8,128)} %copy-done.2), calls=%async_computation.1 | async-start | bytes 2097152 | tf_op jit(solution)/shard_map/all_to_all | solution.py:449
  59.7 2.4 %collective-permute-start.2 = (f32[32,8,128]{2,1,0:T(8,128)S(1)}, f32[32,8,128]{2,1,0:T(8,128)S(1)}, u32[]{:S(2)}, u32[]{:S(2)}) collective-permute-start(f32[32,8,128]{2,1,0:T(8,128)S(1)} %get-tuple-element.40), channel_id=1, source_target_pairs={{0,24},{4,28},{8,32},{12,36},{16,40},{20,44},{24,48},{28,52},{32,5... | collective-permute-start | bytes 393224 | tf_op jit(solution)/shard_map/ppermute | solution.py:421
  64.2 2.4 %collective-permute-start.4 = (f32[32,8,128]{2,1,0:T(8,128)S(1)}, f32[32,8,128]{2,1,0:T(8,128)S(1)}, u32[]{:S(2)}, u32[]{:S(2)}) collective-permute-start(f32[32,8,128]{2,1,0:T(8,128)S(1)} %get-tuple-element.42), channel_id=1, source_target_pairs={{0,40},{4,44},{8,48},{12,52},{16,56},{20,60},{24,0},{28,4},{32,8},... | collective-permute-start | bytes 393224 | tf_op jit(solution)/shard_map/ppermute | solution.py:421
  66.6 15.3 %collective-permute-done = f32[32,8,128]{2,1,0:T(8,128)S(1)} collective-permute-done((f32[32,8,128]{2,1,0:T(8,128)S(1)}, f32[32,8,128]{2,1,0:T(8,128)S(1)}, u32[]{:S(2)}, u32[]{:S(2)}) %collective-permute-start) | collective-permute-done | bytes 131104 | tf_op jit(solution)/shard_map/ppermute | solution.py:421
  81.9 2.3 %collective-permute-start.5 = (f32[32,8,128]{2,1,0:T(8,128)S(1)}, f32[32,8,128]{2,1,0:T(8,128)S(1)}, u32[]{:S(2)}, u32[]{:S(2)}) collective-permute-start(f32[32,8,128]{2,1,0:T(8,128)S(1)} %get-tuple-element.43), channel_id=1, source_target_pairs={{0,48},{4,52},{8,56},{12,60},{16,0},{20,4},{24,8},{28,12},{32,16},... | collective-permute-start | bytes 393224 | tf_op jit(solution)/shard_map/ppermute | solution.py:421
  84.1 2.8 %collective-permute-done.1 = f32[32,8,128]{2,1,0:T(8,128)S(1)} collective-permute-done((f32[32,8,128]{2,1,0:T(8,128)S(1)}, f32[32,8,128]{2,1,0:T(8,128)S(1)}, u32[]{:S(2)}, u32[]{:S(2)}) %collective-permute-start.1) | collective-permute-done | bytes 131104 | tf_op jit(solution)/shard_map/ppermute | solution.py:421
  86.9 2.3 %collective-permute-start.6 = (f32[32,8,128]{2,1,0:T(8,128)S(1)}, f32[32,8,128]{2,1,0:T(8,128)S(1)}, u32[]{:S(2)}, u32[]{:S(2)}) collective-permute-start(f32[32,8,128]{2,1,0:T(8,128)S(1)} %get-tuple-element.44), channel_id=1, source_target_pairs={{0,56},{4,60},{8,0},{12,4},{16,8},{20,12},{24,16},{28,20},{32,24},... | collective-permute-start | bytes 393224 | tf_op jit(solution)/shard_map/ppermute | solution.py:421
  89.3 8.8 %collective-permute-done.2 = f32[32,8,128]{2,1,0:T(8,128)S(1)} collective-permute-done((f32[32,8,128]{2,1,0:T(8,128)S(1)}, f32[32,8,128]{2,1,0:T(8,128)S(1)}, u32[]{:S(2)}, u32[]{:S(2)}) %collective-permute-start.2) | collective-permute-done | bytes 131104 | tf_op jit(solution)/shard_map/ppermute | solution.py:421
  98.1 4.9 %collective-permute-done.3 = f32[32,8,128]{2,1,0:T(8,128)S(1)} collective-permute-done((f32[32,8,128]{2,1,0:T(8,128)S(1)}, f32[32,8,128]{2,1,0:T(8,128)S(1)}, u32[]{:S(2)}, u32[]{:S(2)}) %collective-permute-start.3) | collective-permute-done | bytes 131104 | tf_op jit(solution)/shard_map/ppermute | solution.py:421
  103.9 2.5 %collective-permute-start.7 = (f32[256,128]{1,0:T(8,128)S(1)}, f32[256,128]{1,0:T(8,128)S(1)}, u32[]{:S(2)}, u32[]{:S(2)}) collective-permute-start(f32[256,128]{1,0:T(8,128)S(1)} %get-tuple-element.46), channel_id=1, source_target_pairs={{0,4},{4,0},{8,12},{12,8},{16,20},{20,16},{24,28},{28,24},{32,36},... | collective-permute-start | bytes 393224 | tf_op jit(solution)/shard_map/ppermute | solution.py:432
  107.3 3.2 %collective-permute-start.10 = (f32[256,128]{1,0:T(8,128)S(1)}, f32[256,128]{1,0:T(8,128)S(1)}, u32[]{:S(2)}, u32[]{:S(2)}) collective-permute-start(f32[256,128]{1,0:T(8,128)S(1)} %get-tuple-element.49), channel_id=1, source_target_pairs={{0,128},{4,132},{8,136},{12,140},{16,144},{20,148},{24,152},{28,15... | collective-permute-start | bytes 393224 | tf_op jit(solution)/shard_map/ppermute | solution.py:432
  114.3 6.9 %collective-permute-done.9.refs_3_ = f32[256,128]{1,0:T(8,128)S(1)} collective-permute-done((f32[256,128]{1,0:T(8,128)S(1)}, f32[256,128]{1,0:T(8,128)S(1)}, u32[]{:S(2)}, u32[]{:S(2)}) %collective-permute-start.9) | collective-permute-done | bytes 131104 | tf_op jit(solution)/shard_map/ppermute | solution.py:432
  121.9 2.3 %fft_p.1 = (f32[256,128]{1,0:T(8,128)S(1)}, f32[256,128]{1,0:T(8,128)S(1)}, f32[256,128]{1,0:T(8,128)S(1)}, f32[256,128]{1,0:T(8,128)S(1)}, f32[256,128]{1,0:T(8...) custom-call(s32[3]{0:T(128)S(1)} %pad_add_fusion.pos_ref, ...), custom_call_target="tpu_custom_call" | custom-call | tf_op jit(solution)/shard_map/fft_p/pallas_call | solution.py:206
  128.4 3.3 %collective-permute-start.17 = (f32[256,128]{1,0:T(8,128)S(1)}, f32[256,128]{1,0:T(8,128)S(1)}, u32[]{:S(2)}, u32[]{:S(2)}) collective-permute-start(f32[256,128]{1,0:T(8,128)S(1)} %get-tuple-element.57), channel_id=1, source_target_pairs={{0,32},{4,36},{8,40},{12,44},{16,48},{20,52},{24,56},{28,60},{32,0... | collective-permute-start | bytes 393224 | tf_op jit(solution)/shard_map/ppermute | solution.py:421
  134.4 4.6 %collective-permute-start.20 = (f32[256,128]{1,0:T(8,128)S(1)}, f32[256,128]{1,0:T(8,128)S(1)}, u32[]{:S(2)}, u32[]{:S(2)}) collective-permute-start(f32[256,128]{1,0:T(8,128)S(1)} %get-tuple-element.60), channel_id=1, source_target_pairs={{0,56},{4,60},{8,0},{12,4},{16,8},{20,12},{24,16},{28,20},{32,24},... | collective-permute-start | bytes 393224 | tf_op jit(solution)/shard_map/ppermute | solution.py:421
  138.9 9.8 %collective-permute-done.16.refs_3_ = f32[256,128]{1,0:T(8,128)S(1)} collective-permute-done((f32[256,128]{1,0:T(8,128)S(1)}, f32[256,128]{1,0:T(8,128)S(1)}, u32[]{:S(2)}, u32[]{:S(2)}) %collective-permute-start.16) | collective-permute-done | bytes 131104 | tf_op jit(solution)/shard_map/ppermute | solution.py:421
  148.7 4.1 %collective-permute-done.19.refs_6_ = f32[256,128]{1,0:T(8,128)S(1)} collective-permute-done((f32[256,128]{1,0:T(8,128)S(1)}, f32[256,128]{1,0:T(8,128)S(1)}, u32[]{:S(2)}, u32[]{:S(2)}) %collective-permute-start.19) | collective-permute-done | bytes 131104 | tf_op jit(solution)/shard_map/ppermute | solution.py:421
  152.8 2.7 %collective-permute-done.20.refs_7_ = f32[256,128]{1,0:T(8,128)S(1)} collective-permute-done((f32[256,128]{1,0:T(8,128)S(1)}, f32[256,128]{1,0:T(8,128)S(1)}, u32[]{:S(2)}, u32[]{:S(2)}) %collective-permute-start.20) | collective-permute-done | bytes 131104 | tf_op jit(solution)/shard_map/ppermute | solution.py:421
  162.8 2.5 %collective-permute-start.26 = (f32[256,128]{1,0:T(8,128)S(1)}, f32[256,128]{1,0:T(8,128)S(1)}, u32[]{:S(2)}, u32[]{:S(2)}) collective-permute-start(f32[256,128]{1,0:T(8,128)S(1)} %get-tuple-element.67), channel_id=1, source_target_pairs={{0,192},{4,196},{8,200},{12,204},{16,208},{20,212},{24,216},{28,22... | collective-permute-start | bytes 393224 | tf_op jit(solution)/shard_map/ppermute | solution.py:432
  166.3 3.3 %collective-permute-done.24.refs_4_ = f32[256,128]{1,0:T(8,128)S(1)} collective-permute-done((f32[256,128]{1,0:T(8,128)S(1)}, f32[256,128]{1,0:T(8,128)S(1)}, u32[]{:S(2)}, u32[]{:S(2)}) %collective-permute-start.24) | collective-permute-done | bytes 131104 | tf_op jit(solution)/shard_map/ppermute | solution.py:432
  169.5 3.3 %collective-permute-done.25.refs_5_ = f32[256,128]{1,0:T(8,128)S(1)} collective-permute-done((f32[256,128]{1,0:T(8,128)S(1)}, f32[256,128]{1,0:T(8,128)S(1)}, u32[]{:S(2)}, u32[]{:S(2)}) %collective-permute-start.25) | collective-permute-done | bytes 131104 | tf_op jit(solution)/shard_map/ppermute | solution.py:432
  (59 shorter events, 41.1 us)
Async XLA Ops:
  3.1 41.5 %all-to-all-start = ((f32[64,32,128]{2,1,0:T(8,128)}), f32[64,32,128]{2,1,0:T(8,128)S(1)}, u32[]{:S(2)}, u32[]{:S(2)}) async-start(f32[64,32,128]{2,1,0:T(8,128)} %relayout_a.1), calls=%async_computation | async-start | bytes 2097152 | tf_op jit(solution)/shard_map/all_to_all | solution.py:443
  47.5 129.2 %all-to-all-start.1 = ((f32[64,32,128]{2,1,0:T(8,128)}), f32[64,32,128]{2,1,0:T(8,128)S(1)}, u32[]{:S(2)}, u32[]{:S(2)}) async-start(f32[64,32,128]{2,1,0:T(8,128)} %copy-done.2), calls=%async_computation.1 | async-start | bytes 2097152 | tf_op jit(solution)/shard_map/all_to_all | solution.py:449
  56.2 25.7 %collective-permute-start = (f32[32,8,128]{2,1,0:T(8,128)S(1)}, f32[32,8,128]{2,1,0:T(8,128)S(1)}, u32[]{:S(2)}, u32[]{:S(2)}) collective-permute-start(f32[32,8,128]{2,1,0:T(8,128)S(1)} %get-tuple-element.38), channel_id=1, source_target_pairs={{0,8},{4,12},{8,16},{12,20},{16,24},{20,28},{24,32},{28,36},{32,40... | collective-permute-start | bytes 393224 | tf_op jit(solution)/shard_map/ppermute | solution.py:421
  57.6 29.3 %collective-permute-start.1 = (f32[32,8,128]{2,1,0:T(8,128)S(1)}, f32[32,8,128]{2,1,0:T(8,128)S(1)}, u32[]{:S(2)}, u32[]{:S(2)}) collective-permute-start(f32[32,8,128]{2,1,0:T(8,128)S(1)} %get-tuple-element.39), channel_id=1, source_target_pairs={{0,16},{4,20},{8,24},{12,28},{16,32},{20,36},{24,40},{28,44},{32,4... | collective-permute-start | bytes 393224 | tf_op jit(solution)/shard_map/ppermute | solution.py:421
  59.7 38.4 %collective-permute-start.2 = (f32[32,8,128]{2,1,0:T(8,128)S(1)}, f32[32,8,128]{2,1,0:T(8,128)S(1)}, u32[]{:S(2)}, u32[]{:S(2)}) collective-permute-start(f32[32,8,128]{2,1,0:T(8,128)S(1)} %get-tuple-element.40), channel_id=1, source_target_pairs={{0,24},{4,28},{8,32},{12,36},{16,40},{20,44},{24,48},{28,52},{32,5... | collective-permute-start | bytes 393224 | tf_op jit(solution)/shard_map/ppermute | solution.py:421
  62.1 40.9 %collective-permute-start.3 = (f32[32,8,128]{2,1,0:T(8,128)S(1)}, f32[32,8,128]{2,1,0:T(8,128)S(1)}, u32[]{:S(2)}, u32[]{:S(2)}) collective-permute-start(f32[32,8,128]{2,1,0:T(8,128)S(1)} %get-tuple-element.41), channel_id=1, source_target_pairs={{0,32},{4,36},{8,40},{12,44},{16,48},{20,52},{24,56},{28,60},{32,0... | collective-permute-start | bytes 393224 | tf_op jit(solution)/shard_map/ppermute | solution.py:421
  64.2 38.8 %collective-permute-start.4 = (f32[32,8,128]{2,1,0:T(8,128)S(1)}, f32[32,8,128]{2,1,0:T(8,128)S(1)}, u32[]{:S(2)}, u32[]{:S(2)}) collective-permute-start(f32[32,8,128]{2,1,0:T(8,128)S(1)} %get-tuple-element.42), channel_id=1, source_target_pairs={{0,40},{4,44},{8,48},{12,52},{16,56},{20,60},{24,0},{28,4},{32,8},... | collective-permute-start | bytes 393224 | tf_op jit(solution)/shard_map/ppermute | solution.py:421
  81.9 21.1 %collective-permute-start.5 = (f32[32,8,128]{2,1,0:T(8,128)S(1)}, f32[32,8,128]{2,1,0:T(8,128)S(1)}, u32[]{:S(2)}, u32[]{:S(2)}) collective-permute-start(f32[32,8,128]{2,1,0:T(8,128)S(1)} %get-tuple-element.43), channel_id=1, source_target_pairs={{0,48},{4,52},{8,56},{12,60},{16,0},{20,4},{24,8},{28,12},{32,16},... | collective-permute-start | bytes 393224 | tf_op jit(solution)/shard_map/ppermute | solution.py:421
  86.9 16.0 %collective-permute-start.6 = (f32[32,8,128]{2,1,0:T(8,128)S(1)}, f32[32,8,128]{2,1,0:T(8,128)S(1)}, u32[]{:S(2)}, u32[]{:S(2)}) collective-permute-start(f32[32,8,128]{2,1,0:T(8,128)S(1)} %get-tuple-element.44), channel_id=1, source_target_pairs={{0,56},{4,60},{8,0},{12,4},{16,8},{20,12},{24,16},{28,20},{32,24},... | collective-permute-start | bytes 393224 | tf_op jit(solution)/shard_map/ppermute | solution.py:421
  106.4 14.9 %collective-permute-start.9 = (f32[256,128]{1,0:T(8,128)S(1)}, f32[256,128]{1,0:T(8,128)S(1)}, u32[]{:S(2)}, u32[]{:S(2)}) collective-permute-start(f32[256,128]{1,0:T(8,128)S(1)} %get-tuple-element.48), channel_id=1, source_target_pairs={{0,68},{4,64},{8,76},{12,72},{16,84},{20,80},{24,92},{28,88},{32,1... | collective-permute-start | bytes 393224 | tf_op jit(solution)/shard_map/ppermute | solution.py:432
  107.3 13.9 %collective-permute-start.10 = (f32[256,128]{1,0:T(8,128)S(1)}, f32[256,128]{1,0:T(8,128)S(1)}, u32[]{:S(2)}, u32[]{:S(2)}) collective-permute-start(f32[256,128]{1,0:T(8,128)S(1)} %get-tuple-element.49), channel_id=1, source_target_pairs={{0,128},{4,132},{8,136},{12,140},{16,144},{20,148},{24,152},{28,15... | collective-permute-start | bytes 393224 | tf_op jit(solution)/shard_map/ppermute | solution.py:432
  110.5 10.8 %collective-permute-start.11 = (f32[256,128]{1,0:T(8,128)S(1)}, f32[256,128]{1,0:T(8,128)S(1)}, u32[]{:S(2)}, u32[]{:S(2)}) collective-permute-start(f32[256,128]{1,0:T(8,128)S(1)} %get-tuple-element.50), channel_id=1, source_target_pairs={{0,132},{4,128},{8,140},{12,136},{16,148},{20,144},{24,156},{28,15... | collective-permute-start | bytes 393224 | tf_op jit(solution)/shard_map/ppermute | solution.py:432
  110.6 10.7 %collective-permute-start.12 = (f32[256,128]{1,0:T(8,128)S(1)}, f32[256,128]{1,0:T(8,128)S(1)}, u32[]{:S(2)}, u32[]{:S(2)}) collective-permute-start(f32[256,128]{1,0:T(8,128)S(1)} %get-tuple-element.51), channel_id=1, source_target_pairs={{0,192},{4,196},{8,200},{12,204},{16,208},{20,212},{24,216},{28,22... | collective-permute-start | bytes 393224 | tf_op jit(solution)/shard_map/ppermute | solution.py:432
  124.2 9.6 %collective-permute-start.14 = (f32[256,128]{1,0:T(8,128)S(1)}, f32[256,128]{1,0:T(8,128)S(1)}, u32[]{:S(2)}, u32[]{:S(2)}) collective-permute-start(f32[256,128]{1,0:T(8,128)S(1)} %get-tuple-element.54), channel_id=1, source_target_pairs={{0,8},{4,12},{8,16},{12,20},{16,24},{20,28},{24,32},{28,36},{32,40... | collective-permute-start | bytes 393224 | tf_op jit(solution)/shard_map/ppermute | solution.py:421
  124.3 10.0 %collective-permute-start.15 = (f32[256,128]{1,0:T(8,128)S(1)}, f32[256,128]{1,0:T(8,128)S(1)}, u32[]{:S(2)}, u32[]{:S(2)}) collective-permute-start(f32[256,128]{1,0:T(8,128)S(1)} %get-tuple-element.55), channel_id=1, source_target_pairs={{0,16},{4,20},{8,24},{12,28},{16,32},{20,36},{24,40},{28,44},{32,4... | collective-permute-start | bytes 393224 | tf_op jit(solution)/shard_map/ppermute | solution.py:421
  126.3 22.5 %collective-permute-start.16 = (f32[256,128]{1,0:T(8,128)S(1)}, f32[256,128]{1,0:T(8,128)S(1)}, u32[]{:S(2)}, u32[]{:S(2)}) collective-permute-start(f32[256,128]{1,0:T(8,128)S(1)} %get-tuple-element.56), channel_id=1, source_target_pairs={{0,24},{4,28},{8,32},{12,36},{16,40},{20,44},{24,48},{28,52},{32,5... | collective-permute-start | bytes 393224 | tf_op jit(solution)/shard_map/ppermute | solution.py:421
  128.4 20.3 %collective-permute-start.17 = (f32[256,128]{1,0:T(8,128)S(1)}, f32[256,128]{1,0:T(8,128)S(1)}, u32[]{:S(2)}, u32[]{:S(2)}) collective-permute-start(f32[256,128]{1,0:T(8,128)S(1)} %get-tuple-element.57), channel_id=1, source_target_pairs={{0,32},{4,36},{8,40},{12,44},{16,48},{20,52},{24,56},{28,60},{32,0... | collective-permute-start | bytes 393224 | tf_op jit(solution)/shard_map/ppermute | solution.py:421
  131.7 17.0 %collective-permute-start.18 = (f32[256,128]{1,0:T(8,128)S(1)}, f32[256,128]{1,0:T(8,128)S(1)}, u32[]{:S(2)}, u32[]{:S(2)}) collective-permute-start(f32[256,128]{1,0:T(8,128)S(1)} %get-tuple-element.58), channel_id=1, source_target_pairs={{0,40},{4,44},{8,48},{12,52},{16,56},{20,60},{24,0},{28,4},{32,8},... | collective-permute-start | bytes 393224 | tf_op jit(solution)/shard_map/ppermute | solution.py:421
  133.9 19.0 %collective-permute-start.19 = (f32[256,128]{1,0:T(8,128)S(1)}, f32[256,128]{1,0:T(8,128)S(1)}, u32[]{:S(2)}, u32[]{:S(2)}) collective-permute-start(f32[256,128]{1,0:T(8,128)S(1)} %get-tuple-element.59), channel_id=1, source_target_pairs={{0,48},{4,52},{8,56},{12,60},{16,0},{20,4},{24,8},{28,12},{32,16},... | collective-permute-start | bytes 393224 | tf_op jit(solution)/shard_map/ppermute | solution.py:421
  134.4 21.2 %collective-permute-start.20 = (f32[256,128]{1,0:T(8,128)S(1)}, f32[256,128]{1,0:T(8,128)S(1)}, u32[]{:S(2)}, u32[]{:S(2)}) collective-permute-start(f32[256,128]{1,0:T(8,128)S(1)} %get-tuple-element.60), channel_id=1, source_target_pairs={{0,56},{4,60},{8,0},{12,4},{16,8},{20,12},{24,16},{28,20},{32,24},... | collective-permute-start | bytes 393224 | tf_op jit(solution)/shard_map/ppermute | solution.py:421
  159.6 9.9 %collective-permute-start.24 = (f32[256,128]{1,0:T(8,128)S(1)}, f32[256,128]{1,0:T(8,128)S(1)}, u32[]{:S(2)}, u32[]{:S(2)}) collective-permute-start(f32[256,128]{1,0:T(8,128)S(1)} %get-tuple-element.65), channel_id=1, source_target_pairs={{0,128},{4,132},{8,136},{12,140},{16,144},{20,148},{24,152},{28,15... | collective-permute-start | bytes 393224 | tf_op jit(solution)/shard_map/ppermute | solution.py:432
  161.2 11.6 %collective-permute-start.25 = (f32[256,128]{1,0:T(8,128)S(1)}, f32[256,128]{1,0:T(8,128)S(1)}, u32[]{:S(2)}, u32[]{:S(2)}) collective-permute-start(f32[256,128]{1,0:T(8,128)S(1)} %get-tuple-element.66), channel_id=1, source_target_pairs={{0,132},{4,128},{8,140},{12,136},{16,148},{20,144},{24,156},{28,15... | collective-permute-start | bytes 393224 | tf_op jit(solution)/shard_map/ppermute | solution.py:432
  162.8 10.0 %collective-permute-start.26 = (f32[256,128]{1,0:T(8,128)S(1)}, f32[256,128]{1,0:T(8,128)S(1)}, u32[]{:S(2)}, u32[]{:S(2)}) collective-permute-start(f32[256,128]{1,0:T(8,128)S(1)} %get-tuple-element.67), channel_id=1, source_target_pairs={{0,192},{4,196},{8,200},{12,204},{16,208},{20,212},{24,216},{28,22... | collective-permute-start | bytes 393224 | tf_op jit(solution)/shard_map/ppermute | solution.py:432
  165.3 9.7 %collective-permute-start.27 = (f32[256,128]{1,0:T(8,128)S(1)}, f32[256,128]{1,0:T(8,128)S(1)}, u32[]{:S(2)}, u32[]{:S(2)}) collective-permute-start(f32[256,128]{1,0:T(8,128)S(1)} %get-tuple-element.68), channel_id=1, source_target_pairs={{0,196},{4,192},{8,204},{12,200},{16,212},{20,208},{24,220},{28,21... | collective-permute-start | bytes 393224 | tf_op jit(solution)/shard_map/ppermute | solution.py:432
  (9 other events, 48.6 us)

commit v5 on v4

--- a/solution.py
+++ b/solution.py
@@ -173,7 +173,7 @@
         fft_a_kernel,
         in_specs=[VMEM] * 3,
         out_specs=HBM,
-        out_shape=f32(PEERS, KEPT, LANES),
+        out_shape=pltpu.HBM((PEERS, KEPT, LANES), jnp.float32),
         scratch_shapes=FFT_SCRATCH
         + [pltpu.VMEM((PEERS, KEPT, LANES), jnp.float32), pltpu.SemaphoreType.DMA((PIECES,))],
         compiler_params=PARAMS,
@@ -353,7 +353,8 @@
 ]
 
 
-def store_p_kernel(pos_ref, *refs):
+def store_p_kernel(pos_ref, prior_ref, *refs):
+    del prior_ref
     q_refs, o_ref = refs[:8], refs[8]
     x_ref, buf_ref, sem = refs[9:]
     x, c = pos_ref[0], pos_ref[2]
@@ -366,21 +367,20 @@
     store_half(x_ref, buf_ref, o_ref, sem, 0)
 
 
-def store_p(pos, blocks):
+def store_p(pos, prior, blocks):
     return pl.pallas_call(
         store_p_kernel,
-        in_specs=[SMEM] + [VMEM] * 8,
+        in_specs=[SMEM, HBM] + [VMEM] * 8,
         out_specs=HBM,
         out_shape=f32(KEPT, FIELDS, 2 * LANES),
         scratch_shapes=STORE_SCRATCH,
+        input_output_aliases={1: 0},
         compiler_params=PARAMS,
         name="store_p",
-    )(pos, *blocks)
-
-
-def store_a_kernel(prior_ref, q_ref, o_ref, x_ref, buf_ref, sem):
-    del prior_ref
-
+    )(pos, prior, *blocks)
+
+
+def store_a_kernel(q_ref, o_ref, x_ref, buf_ref, sem):
     def field(f, carry):
         x_ref[pl.ds(pl.multiple_of(f * PAD_K, 8), KEPT), :] = q_ref[f]
         return carry
@@ -389,17 +389,16 @@
     store_half(x_ref, buf_ref, o_ref, sem, LANES)
 
 
-def store_a(prior, shares):
+def store_a(shares):
     return pl.pallas_call(
         store_a_kernel,
-        in_specs=[HBM, VMEM],
+        in_specs=[VMEM],
         out_specs=HBM,
         out_shape=f32(KEPT, FIELDS, 2 * LANES),
         scratch_shapes=STORE_SCRATCH,
-        input_output_aliases={0: 0},
         compiler_params=PARAMS,
         name="store_a",
-    )(prior, shares)
+    )(shares)
 
 
 def shifts(dx, dz, dc):
@@ -411,7 +410,7 @@
     ]
 
 
-Z_ORDER = (4, 3, 5, 2, 6, 1, 7)
+Z_ORDER = (1, 7, 4, 3, 5, 2, 6)
 
 
 def exchange_z(blocks):
@@ -437,9 +436,9 @@
     device = lax.axis_index("lon")
     pos = jnp.stack([device // (NZ * NC), (device // NC) % NZ, device % NC]).astype(jnp.int32)
     wh, wl = twiddle_matrices(1.0 / math.sqrt(NLON))
-    pieces = split_z(pos, state)
+    pieces = split_z(pos, pltpu.with_memory_space_constraint(state, pltpu.HBM))
     pieces = exchange_z(pieces)
-    sent = relayout_a(state)
+    sent = relayout_a(pltpu.with_memory_space_constraint(state, pltpu.HBM))
     gathered = lax.all_to_all(sent, "lon", split_axis=0, concat_axis=0, tiled=True)
     pieces = spread_x(pos, [b.reshape(LON * 8, LANES) for b in pieces])
     pieces = exchange_xc(pieces)
@@ -449,8 +448,8 @@
     shares = lax.all_to_all(spectrum, "lon", split_axis=0, concat_axis=0, tiled=True)
     pieces = spread_out(pos, pieces)
     pieces = exchange_xc(pieces)
-    out = store_p(pos, pieces)
-    out = store_a(out, shares)
+    out = store_a(shares)
+    out = store_p(pos, out, pieces)
     return out.reshape(2, RADIX, FIELDS, 2 * LANES)
 
 

time: 178 us -> 174 us (0.978)
  local copies, waits for them, and re-layouts: 4.16 us -> 0 us
  Pallas kernels: 10.8 us -> 13.6 us
  waiting for transfers between devices: 91.4 us -> 88.9 us
    unnamed x6 -> x0, local copies, waits for them, and re-layouts: 4.16 us -> none
    ppermute x14, waiting for transfers between devices: 16.6 us -> 13 us  [exchange_xc(): lax.ppermute(blocks[dx * NC + dc], 'lon', shifts(dx, 0, dc))]
where the time goes in v5:
time: 174 us; the launch traced here: 173 us
  waiting for transfers between devices  88.9 us (51%)
  starting transfers between devices  67.1 us (39%)
  Pallas kernels  13.6 us (8%)
  other arithmetic  3.31 us (2%)
    ppermute x14, waiting for transfers between devices, exchange_z(): out[dz] = lax.ppermute(blocks[dz], 'lon', shifts(0, dz, 0))  50.7 us
    ppermute x14, starting transfers between devices, exchange_z(): out[dz] = lax.ppermute(blocks[dz], 'lon', shifts(0, dz, 0))  27.7 us
    all_to_all x1, waiting for transfers between devices, local(): lax.all_to_all(sent, 'lon', split_axis=0, concat_axis=0, tiled=True)  25.2 us
    ppermute x14, starting transfers between devices, exchange_xc(): lax.ppermute(blocks[dx * NC + dc], 'lon', shifts(dx, 0, dc))  20.3 us
    all_to_all x1, starting transfers between devices, local(): lax.all_to_all(sent, 'lon', split_axis=0, concat_axis=0, tiled=True)  13 us
    ppermute x14, waiting for transfers between devices, exchange_xc(): lax.ppermute(blocks[dx * NC + dc], 'lon', shifts(dx, 0, dc))  13 us
    all_to_all x1, starting transfers between devices, local(): lax.all_to_all(spectrum, 'lon', split_axis=0, concat_axis=0, tiled=True)  6.21 us
  transfers between devices with their start and end apart: 30, of which 15 were waited for; matrix products, arithmetic and copies ran while one was open for 2% of the time, Pallas kernels for 4%

profile of v5, /device:TPU:1, one launch (start us, length us, event | category | flops | bytes accessed | tf_op | source)
XLA Modules:
  0.0 173.3 jit_solution(16264387594776403792)
XLA Ops:
  0.0 2.5 %relayout_a.1 = f32[64,32,128]{2,1,0:T(8,128)} custom-call(f32[32,64,256]{2,1,0:T(8,128)} %s_ref.3), custom_call_target="tpu_custom_call" | custom-call | tf_op jit(solution)/shard_map/relayout_a/pallas_call | solution.py:312
  2.5 13.0 %all-to-all-start = ((f32[64,32,128]{2,1,0:T(8,128)}), f32[64,32,128]{2,1,0:T(8,128)S(1)}, u32[]{:S(2)}, u32[]{:S(2)}) async-start(f32[64,32,128]{2,1,0:T(8,128)} %relayout_a.1), calls=%async_computation | async-start | bytes 2097152 | tf_op jit(solution)/shard_map/all_to_all | solution.py:442
  15.5 2.5 %select_select_fusion.1 = (f32[8,2,64,128]{3,2,1,0:T(8,128)S(1)}, f32[8,2,64,128]{3,2,1,0:T(8,128)S(1)}, f32[8,2,64,128]{3,2,1,0:T(8,128)S(1)}, f32[8,2,64,128]{3,2,1,0:T(8,128)S(1)}) fusion(pred[2]{0:T(512)(128)(4,1)S(1)} %iota_compare_fusion.1, pred[8]{0:T(512)(128)(4,1)S(1)} %iota_compare_fusion, s32[64]{0:T(128)S(1)} %iota_multiply_fusion, ...), kind=kLoop, calls=%fused_computation.9 | loop fusion | flops 4456448 | bytes 2097450 | tf_op jit(solution)/shard_map/jit(_where)/select_n | solution.py:56
  18.8 25.2 %all-to-all-done = f32[64,32,128]{2,1,0:T(8,128)S(1)} async-done(((f32[64,32,128]{2,1,0:T(8,128)}), f32[64,32,128]{2,1,0:T(8,128)S(1)}, u32[]{:S(2)}, u32[]{:S(2)}) %all-to-all-start) | async-done | bytes 1048608 | tf_op jit(solution)/shard_map/all_to_all | solution.py:442
  44.0 2.5 %fft_a.1 = f32[64,32,128]{2,1,0:T(8,128)} custom-call(f32[2048,128]{1,0:T(8,128)S(1)} %bitcast.22, bf16[8,256,256]{2,1,0:T(8,128)(2,1)S(1)} %get-tuple-element.70.wh_ref.refs_8_, bf16[8,256,256]{2,1,0:T(8,128)(2,1)S(1)} %get-tuple-element.69.wl_ref.refs_9_), custom_call_target="tpu_custom_call" | custom-call | tf_op jit(solution)/shard_map/fft_a/pallas_call | solution.py:172
  46.5 6.2 %all-to-all-start.1 = ((f32[64,32,128]{2,1,0:T(8,128)}), f32[64,32,128]{2,1,0:T(8,128)S(1)}, u32[]{:S(2)}, u32[]{:S(2)}) async-start(f32[64,32,128]{2,1,0:T(8,128)} %fft_a.1), calls=%async_computation.1 | async-start | bytes 2097152 | tf_op jit(solution)/shard_map/all_to_all | solution.py:448
  54.8 2.3 %collective-permute-start.1 = (f32[32,8,128]{2,1,0:T(8,128)S(1)}, f32[32,8,128]{2,1,0:T(8,128)S(1)}, u32[]{:S(2)}, u32[]{:S(2)}) collective-permute-start(f32[32,8,128]{2,1,0:T(8,128)S(1)} %get-tuple-element.39), channel_id=1, source_target_pairs={{0,16},{4,20},{8,24},{12,28},{16,32},{20,36},{24,40},{28,44},{32,4... | collective-permute-start | bytes 393224 | tf_op jit(solution)/shard_map/ppermute | solution.py:420
  57.1 3.3 %collective-permute-start.2 = (f32[32,8,128]{2,1,0:T(8,128)S(1)}, f32[32,8,128]{2,1,0:T(8,128)S(1)}, u32[]{:S(2)}, u32[]{:S(2)}) collective-permute-start(f32[32,8,128]{2,1,0:T(8,128)S(1)} %get-tuple-element.40), channel_id=1, source_target_pairs={{0,24},{4,28},{8,32},{12,36},{16,40},{20,44},{24,48},{28,52},{32,5... | collective-permute-start | bytes 393224 | tf_op jit(solution)/shard_map/ppermute | solution.py:420
  61.6 3.3 %collective-permute-start.4 = (f32[32,8,128]{2,1,0:T(8,128)S(1)}, f32[32,8,128]{2,1,0:T(8,128)S(1)}, u32[]{:S(2)}, u32[]{:S(2)}) collective-permute-start(f32[32,8,128]{2,1,0:T(8,128)S(1)} %get-tuple-element.42), channel_id=1, source_target_pairs={{0,40},{4,44},{8,48},{12,52},{16,56},{20,60},{24,0},{28,4},{32,8},... | collective-permute-start | bytes 393224 | tf_op jit(solution)/shard_map/ppermute | solution.py:420
  64.9 3.3 %collective-permute-start.5 = (f32[32,8,128]{2,1,0:T(8,128)S(1)}, f32[32,8,128]{2,1,0:T(8,128)S(1)}, u32[]{:S(2)}, u32[]{:S(2)}) collective-permute-start(f32[32,8,128]{2,1,0:T(8,128)S(1)} %get-tuple-element.43), channel_id=1, source_target_pairs={{0,48},{4,52},{8,56},{12,60},{16,0},{20,4},{24,8},{28,12},{32,16},... | collective-permute-start | bytes 393224 | tf_op jit(solution)/shard_map/ppermute | solution.py:420
  68.2 15.2 %collective-permute-done.1 = f32[32,8,128]{2,1,0:T(8,128)S(1)} collective-permute-done((f32[32,8,128]{2,1,0:T(8,128)S(1)}, f32[32,8,128]{2,1,0:T(8,128)S(1)}, u32[]{:S(2)}, u32[]{:S(2)}) %collective-permute-start.1) | collective-permute-done | bytes 131104 | tf_op jit(solution)/shard_map/ppermute | solution.py:420
  85.4 9.0 %collective-permute-done.2 = f32[32,8,128]{2,1,0:T(8,128)S(1)} collective-permute-done((f32[32,8,128]{2,1,0:T(8,128)S(1)}, f32[32,8,128]{2,1,0:T(8,128)S(1)}, u32[]{:S(2)}, u32[]{:S(2)}) %collective-permute-start.2) | collective-permute-done | bytes 131104 | tf_op jit(solution)/shard_map/ppermute | solution.py:420
  94.5 4.7 %collective-permute-done.3 = f32[32,8,128]{2,1,0:T(8,128)S(1)} collective-permute-done((f32[32,8,128]{2,1,0:T(8,128)S(1)}, f32[32,8,128]{2,1,0:T(8,128)S(1)}, u32[]{:S(2)}, u32[]{:S(2)}) %collective-permute-start.3) | collective-permute-done | bytes 131104 | tf_op jit(solution)/shard_map/ppermute | solution.py:420
  102.6 3.1 %collective-permute-start.10 = (f32[256,128]{1,0:T(8,128)S(1)}, f32[256,128]{1,0:T(8,128)S(1)}, u32[]{:S(2)}, u32[]{:S(2)}) collective-permute-start(f32[256,128]{1,0:T(8,128)S(1)} %get-tuple-element.49), channel_id=1, source_target_pairs={{0,128},{4,132},{8,136},{12,140},{16,144},{20,148},{24,152},{28,15... | collective-permute-start | bytes 393224 | tf_op jit(solution)/shard_map/ppermute | solution.py:431
  107.0 2.6 %collective-permute-start.12 = (f32[256,128]{1,0:T(8,128)S(1)}, f32[256,128]{1,0:T(8,128)S(1)}, u32[]{:S(2)}, u32[]{:S(2)}) collective-permute-start(f32[256,128]{1,0:T(8,128)S(1)} %get-tuple-element.51), channel_id=1, source_target_pairs={{0,192},{4,196},{8,200},{12,204},{16,208},{20,212},{24,216},{28,22... | collective-permute-start | bytes 393224 | tf_op jit(solution)/shard_map/ppermute | solution.py:431
  115.1 3.6 %collective-permute-done.13.refs_7_ = f32[256,128]{1,0:T(8,128)S(1)} collective-permute-done((f32[256,128]{1,0:T(8,128)S(1)}, f32[256,128]{1,0:T(8,128)S(1)}, u32[]{:S(2)}, u32[]{:S(2)}) %collective-permute-start.13) | collective-permute-done | bytes 131104 | tf_op jit(solution)/shard_map/ppermute | solution.py:431
  119.8 2.3 %fft_p.1 = (f32[256,128]{1,0:T(8,128)S(1)}, f32[256,128]{1,0:T(8,128)S(1)}, f32[256,128]{1,0:T(8,128)S(1)}, f32[256,128]{1,0:T(8,128)S(1)}, f32[256,128]{1,0:T(8...) custom-call(s32[3]{0:T(128)S(1)} %pad_add_fusion.pos_ref, ...), custom_call_target="tpu_custom_call" | custom-call | tf_op jit(solution)/shard_map/fft_p/pallas_call | solution.py:206
  122.3 2.9 %collective-permute-start.15 = (f32[256,128]{1,0:T(8,128)S(1)}, f32[256,128]{1,0:T(8,128)S(1)}, u32[]{:S(2)}, u32[]{:S(2)}) collective-permute-start(f32[256,128]{1,0:T(8,128)S(1)} %get-tuple-element.55), channel_id=1, source_target_pairs={{0,16},{4,20},{8,24},{12,28},{16,32},{20,36},{24,40},{28,44},{32,4... | collective-permute-start | bytes 393224 | tf_op jit(solution)/shard_map/ppermute | solution.py:420
  127.9 3.6 %collective-permute-start.18 = (f32[256,128]{1,0:T(8,128)S(1)}, f32[256,128]{1,0:T(8,128)S(1)}, u32[]{:S(2)}, u32[]{:S(2)}) collective-permute-start(f32[256,128]{1,0:T(8,128)S(1)} %get-tuple-element.58), channel_id=1, source_target_pairs={{0,40},{4,44},{8,48},{12,52},{16,56},{20,60},{24,0},{28,4},{32,8},... | collective-permute-start | bytes 393224 | tf_op jit(solution)/shard_map/ppermute | solution.py:420
  131.5 2.6 %collective-permute-start.19 = (f32[256,128]{1,0:T(8,128)S(1)}, f32[256,128]{1,0:T(8,128)S(1)}, u32[]{:S(2)}, u32[]{:S(2)}) collective-permute-start(f32[256,128]{1,0:T(8,128)S(1)} %get-tuple-element.59), channel_id=1, source_target_pairs={{0,48},{4,52},{8,56},{12,60},{16,0},{20,4},{24,8},{28,12},{32,16},... | collective-permute-start | bytes 393224 | tf_op jit(solution)/shard_map/ppermute | solution.py:420
  134.4 11.0 %collective-permute-done.16.refs_3_ = f32[256,128]{1,0:T(8,128)S(1)} collective-permute-done((f32[256,128]{1,0:T(8,128)S(1)}, f32[256,128]{1,0:T(8,128)S(1)}, u32[]{:S(2)}, u32[]{:S(2)}) %collective-permute-start.16) | collective-permute-done | bytes 131104 | tf_op jit(solution)/shard_map/ppermute | solution.py:420
  145.4 7.0 %collective-permute-done.19.refs_6_ = f32[256,128]{1,0:T(8,128)S(1)} collective-permute-done((f32[256,128]{1,0:T(8,128)S(1)}, f32[256,128]{1,0:T(8,128)S(1)}, u32[]{:S(2)}, u32[]{:S(2)}) %collective-permute-start.19) | collective-permute-done | bytes 131104 | tf_op jit(solution)/shard_map/ppermute | solution.py:420
  156.9 3.1 %collective-permute-start.24 = (f32[256,128]{1,0:T(8,128)S(1)}, f32[256,128]{1,0:T(8,128)S(1)}, u32[]{:S(2)}, u32[]{:S(2)}) collective-permute-start(f32[256,128]{1,0:T(8,128)S(1)} %get-tuple-element.65), channel_id=1, source_target_pairs={{0,128},{4,132},{8,136},{12,140},{16,144},{20,148},{24,152},{28,15... | collective-permute-start | bytes 393224 | tf_op jit(solution)/shard_map/ppermute | solution.py:431
  165.0 5.6 %collective-permute-done.23.refs_3_ = f32[256,128]{1,0:T(8,128)S(1)} collective-permute-done((f32[256,128]{1,0:T(8,128)S(1)}, f32[256,128]{1,0:T(8,128)S(1)}, u32[]{:S(2)}, u32[]{:S(2)}) %collective-permute-start.23) | collective-permute-done | bytes 131104 | tf_op jit(solution)/shard_map/ppermute | solution.py:431
  (53 shorter events, 32.5 us)
Async XLA Ops:
  2.5 41.5 %all-to-all-start = ((f32[64,32,128]{2,1,0:T(8,128)}), f32[64,32,128]{2,1,0:T(8,128)S(1)}, u32[]{:S(2)}, u32[]{:S(2)}) async-start(f32[64,32,128]{2,1,0:T(8,128)} %relayout_a.1), calls=%async_computation | async-start | bytes 2097152 | tf_op jit(solution)/shard_map/all_to_all | solution.py:442
  46.5 117.3 %all-to-all-start.1 = ((f32[64,32,128]{2,1,0:T(8,128)}), f32[64,32,128]{2,1,0:T(8,128)S(1)}, u32[]{:S(2)}, u32[]{:S(2)}) async-start(f32[64,32,128]{2,1,0:T(8,128)} %fft_a.1), calls=%async_computation.1 | async-start | bytes 2097152 | tf_op jit(solution)/shard_map/all_to_all | solution.py:448
  54.8 28.5 %collective-permute-start.1 = (f32[32,8,128]{2,1,0:T(8,128)S(1)}, f32[32,8,128]{2,1,0:T(8,128)S(1)}, u32[]{:S(2)}, u32[]{:S(2)}) collective-permute-start(f32[32,8,128]{2,1,0:T(8,128)S(1)} %get-tuple-element.39), channel_id=1, source_target_pairs={{0,16},{4,20},{8,24},{12,28},{16,32},{20,36},{24,40},{28,44},{32,4... | collective-permute-start | bytes 393224 | tf_op jit(solution)/shard_map/ppermute | solution.py:420
  57.1 37.3 %collective-permute-start.2 = (f32[32,8,128]{2,1,0:T(8,128)S(1)}, f32[32,8,128]{2,1,0:T(8,128)S(1)}, u32[]{:S(2)}, u32[]{:S(2)}) collective-permute-start(f32[32,8,128]{2,1,0:T(8,128)S(1)} %get-tuple-element.40), channel_id=1, source_target_pairs={{0,24},{4,28},{8,32},{12,36},{16,40},{20,44},{24,48},{28,52},{32,5... | collective-permute-start | bytes 393224 | tf_op jit(solution)/shard_map/ppermute | solution.py:420
  60.4 38.8 %collective-permute-start.3 = (f32[32,8,128]{2,1,0:T(8,128)S(1)}, f32[32,8,128]{2,1,0:T(8,128)S(1)}, u32[]{:S(2)}, u32[]{:S(2)}) collective-permute-start(f32[32,8,128]{2,1,0:T(8,128)S(1)} %get-tuple-element.41), channel_id=1, source_target_pairs={{0,32},{4,36},{8,40},{12,44},{16,48},{20,52},{24,56},{28,60},{32,0... | collective-permute-start | bytes 393224 | tf_op jit(solution)/shard_map/ppermute | solution.py:420
  61.6 37.6 %collective-permute-start.4 = (f32[32,8,128]{2,1,0:T(8,128)S(1)}, f32[32,8,128]{2,1,0:T(8,128)S(1)}, u32[]{:S(2)}, u32[]{:S(2)}) collective-permute-start(f32[32,8,128]{2,1,0:T(8,128)S(1)} %get-tuple-element.42), channel_id=1, source_target_pairs={{0,40},{4,44},{8,48},{12,52},{16,56},{20,60},{24,0},{28,4},{32,8},... | collective-permute-start | bytes 393224 | tf_op jit(solution)/shard_map/ppermute | solution.py:420
  64.9 34.3 %collective-permute-start.5 = (f32[32,8,128]{2,1,0:T(8,128)S(1)}, f32[32,8,128]{2,1,0:T(8,128)S(1)}, u32[]{:S(2)}, u32[]{:S(2)}) collective-permute-start(f32[32,8,128]{2,1,0:T(8,128)S(1)} %get-tuple-element.43), channel_id=1, source_target_pairs={{0,48},{4,52},{8,56},{12,60},{16,0},{20,4},{24,8},{28,12},{32,16},... | collective-permute-start | bytes 393224 | tf_op jit(solution)/shard_map/ppermute | solution.py:420
  83.4 16.2 %collective-permute-start.6 = (f32[32,8,128]{2,1,0:T(8,128)S(1)}, f32[32,8,128]{2,1,0:T(8,128)S(1)}, u32[]{:S(2)}, u32[]{:S(2)}) collective-permute-start(f32[32,8,128]{2,1,0:T(8,128)S(1)} %get-tuple-element.44), channel_id=1, source_target_pairs={{0,56},{4,60},{8,0},{12,4},{16,8},{20,12},{24,16},{28,20},{32,24},... | collective-permute-start | bytes 393224 | tf_op jit(solution)/shard_map/ppermute | solution.py:420
  107.0 8.0 %collective-permute-start.12 = (f32[256,128]{1,0:T(8,128)S(1)}, f32[256,128]{1,0:T(8,128)S(1)}, u32[]{:S(2)}, u32[]{:S(2)}) collective-permute-start(f32[256,128]{1,0:T(8,128)S(1)} %get-tuple-element.51), channel_id=1, source_target_pairs={{0,192},{4,196},{8,200},{12,204},{16,208},{20,212},{24,216},{28,22... | collective-permute-start | bytes 393224 | tf_op jit(solution)/shard_map/ppermute | solution.py:431
  109.6 9.0 %collective-permute-start.13 = (f32[256,128]{1,0:T(8,128)S(1)}, f32[256,128]{1,0:T(8,128)S(1)}, u32[]{:S(2)}, u32[]{:S(2)}) collective-permute-start(f32[256,128]{1,0:T(8,128)S(1)} %get-tuple-element.52), channel_id=1, source_target_pairs={{0,196},{4,192},{8,204},{12,200},{16,212},{20,208},{24,220},{28,21... | collective-permute-start | bytes 393224 | tf_op jit(solution)/shard_map/ppermute | solution.py:431
  109.6 9.0 %collective-permute-start.7 = (f32[256,128]{1,0:T(8,128)S(1)}, f32[256,128]{1,0:T(8,128)S(1)}, u32[]{:S(2)}, u32[]{:S(2)}) collective-permute-start(f32[256,128]{1,0:T(8,128)S(1)} %get-tuple-element.46), channel_id=1, source_target_pairs={{0,4},{4,0},{8,12},{12,8},{16,20},{20,16},{24,28},{28,24},{32,36},... | collective-permute-start | bytes 393224 | tf_op jit(solution)/shard_map/ppermute | solution.py:431
  110.5 8.1 %collective-permute-start.8 = (f32[256,128]{1,0:T(8,128)S(1)}, f32[256,128]{1,0:T(8,128)S(1)}, u32[]{:S(2)}, u32[]{:S(2)}) collective-permute-start(f32[256,128]{1,0:T(8,128)S(1)} %get-tuple-element.47), channel_id=1, source_target_pairs={{0,64},{4,68},{8,72},{12,76},{16,80},{20,84},{24,88},{28,92},{32,9... | collective-permute-start | bytes 393224 | tf_op jit(solution)/shard_map/ppermute | solution.py:431
  122.2 9.3 %collective-permute-start.14 = (f32[256,128]{1,0:T(8,128)S(1)}, f32[256,128]{1,0:T(8,128)S(1)}, u32[]{:S(2)}, u32[]{:S(2)}) collective-permute-start(f32[256,128]{1,0:T(8,128)S(1)} %get-tuple-element.54), channel_id=1, source_target_pairs={{0,8},{4,12},{8,16},{12,20},{16,24},{20,28},{24,32},{28,36},{32,40... | collective-permute-start | bytes 393224 | tf_op jit(solution)/shard_map/ppermute | solution.py:420
  122.3 11.8 %collective-permute-start.15 = (f32[256,128]{1,0:T(8,128)S(1)}, f32[256,128]{1,0:T(8,128)S(1)}, u32[]{:S(2)}, u32[]{:S(2)}) collective-permute-start(f32[256,128]{1,0:T(8,128)S(1)} %get-tuple-element.55), channel_id=1, source_target_pairs={{0,16},{4,20},{8,24},{12,28},{16,32},{20,36},{24,40},{28,44},{32,4... | collective-permute-start | bytes 393224 | tf_op jit(solution)/shard_map/ppermute | solution.py:420
  125.1 20.2 %collective-permute-start.16 = (f32[256,128]{1,0:T(8,128)S(1)}, f32[256,128]{1,0:T(8,128)S(1)}, u32[]{:S(2)}, u32[]{:S(2)}) collective-permute-start(f32[256,128]{1,0:T(8,128)S(1)} %get-tuple-element.56), channel_id=1, source_target_pairs={{0,24},{4,28},{8,32},{12,36},{16,40},{20,44},{24,48},{28,52},{32,5... | collective-permute-start | bytes 393224 | tf_op jit(solution)/shard_map/ppermute | solution.py:420
  127.2 18.2 %collective-permute-start.17 = (f32[256,128]{1,0:T(8,128)S(1)}, f32[256,128]{1,0:T(8,128)S(1)}, u32[]{:S(2)}, u32[]{:S(2)}) collective-permute-start(f32[256,128]{1,0:T(8,128)S(1)} %get-tuple-element.57), channel_id=1, source_target_pairs={{0,32},{4,36},{8,40},{12,44},{16,48},{20,52},{24,56},{28,60},{32,0... | collective-permute-start | bytes 393224 | tf_op jit(solution)/shard_map/ppermute | solution.py:420
  127.9 17.5 %collective-permute-start.18 = (f32[256,128]{1,0:T(8,128)S(1)}, f32[256,128]{1,0:T(8,128)S(1)}, u32[]{:S(2)}, u32[]{:S(2)}) collective-permute-start(f32[256,128]{1,0:T(8,128)S(1)} %get-tuple-element.58), channel_id=1, source_target_pairs={{0,40},{4,44},{8,48},{12,52},{16,56},{20,60},{24,0},{28,4},{32,8},... | collective-permute-start | bytes 393224 | tf_op jit(solution)/shard_map/ppermute | solution.py:420
  131.5 20.9 %collective-permute-start.19 = (f32[256,128]{1,0:T(8,128)S(1)}, f32[256,128]{1,0:T(8,128)S(1)}, u32[]{:S(2)}, u32[]{:S(2)}) collective-permute-start(f32[256,128]{1,0:T(8,128)S(1)} %get-tuple-element.59), channel_id=1, source_target_pairs={{0,48},{4,52},{8,56},{12,60},{16,0},{20,4},{24,8},{28,12},{32,16},... | collective-permute-start | bytes 393224 | tf_op jit(solution)/shard_map/ppermute | solution.py:420
  134.1 19.5 %collective-permute-start.20 = (f32[256,128]{1,0:T(8,128)S(1)}, f32[256,128]{1,0:T(8,128)S(1)}, u32[]{:S(2)}, u32[]{:S(2)}) collective-permute-start(f32[256,128]{1,0:T(8,128)S(1)} %get-tuple-element.60), channel_id=1, source_target_pairs={{0,56},{4,60},{8,0},{12,4},{16,8},{20,12},{24,16},{28,20},{32,24},... | collective-permute-start | bytes 393224 | tf_op jit(solution)/shard_map/ppermute | solution.py:420
  155.7 14.9 %collective-permute-start.23 = (f32[256,128]{1,0:T(8,128)S(1)}, f32[256,128]{1,0:T(8,128)S(1)}, u32[]{:S(2)}, u32[]{:S(2)}) collective-permute-start(f32[256,128]{1,0:T(8,128)S(1)} %get-tuple-element.64), channel_id=1, source_target_pairs={{0,68},{4,64},{8,76},{12,72},{16,84},{20,80},{24,92},{28,88},{32,1... | collective-permute-start | bytes 393224 | tf_op jit(solution)/shard_map/ppermute | solution.py:431
  156.9 13.7 %collective-permute-start.24 = (f32[256,128]{1,0:T(8,128)S(1)}, f32[256,128]{1,0:T(8,128)S(1)}, u32[]{:S(2)}, u32[]{:S(2)}) collective-permute-start(f32[256,128]{1,0:T(8,128)S(1)} %get-tuple-element.65), channel_id=1, source_target_pairs={{0,128},{4,132},{8,136},{12,140},{16,144},{20,148},{24,152},{28,15... | collective-permute-start | bytes 393224 | tf_op jit(solution)/shard_map/ppermute | solution.py:431
  160.1 10.5 %collective-permute-start.25 = (f32[256,128]{1,0:T(8,128)S(1)}, f32[256,128]{1,0:T(8,128)S(1)}, u32[]{:S(2)}, u32[]{:S(2)}) collective-permute-start(f32[256,128]{1,0:T(8,128)S(1)} %get-tuple-element.66), channel_id=1, source_target_pairs={{0,132},{4,128},{8,140},{12,136},{16,148},{20,144},{24,156},{28,15... | collective-permute-start | bytes 393224 | tf_op jit(solution)/shard_map/ppermute | solution.py:431
  160.1 10.5 %collective-permute-start.26 = (f32[256,128]{1,0:T(8,128)S(1)}, f32[256,128]{1,0:T(8,128)S(1)}, u32[]{:S(2)}, u32[]{:S(2)}) collective-permute-start(f32[256,128]{1,0:T(8,128)S(1)} %get-tuple-element.67), channel_id=1, source_target_pairs={{0,192},{4,196},{8,200},{12,204},{16,208},{20,212},{24,216},{28,22... | collective-permute-start | bytes 393224 | tf_op jit(solution)/shard_map/ppermute | solution.py:431
  162.1 9.3 %collective-permute-start.27 = (f32[256,128]{1,0:T(8,128)S(1)}, f32[256,128]{1,0:T(8,128)S(1)}, u32[]{:S(2)}, u32[]{:S(2)}) collective-permute-start(f32[256,128]{1,0:T(8,128)S(1)} %get-tuple-element.68), channel_id=1, source_target_pairs={{0,196},{4,192},{8,204},{12,200},{16,212},{20,208},{24,220},{28,21... | collective-permute-start | bytes 393224 | tf_op jit(solution)/shard_map/ppermute | solution.py:431
  (6 other events, 41.5 us)

commit v6 on v5

--- a/solution.py
+++ b/solution.py
@@ -108,10 +108,18 @@
 PAD_R = PEERS + 8
 
 
-def fft_core(x_ref, wh_ref, wl_ref, y_ref, r_ref):
+def natural_row(n2, base):
+    return n2 * INNER + base
+
+
+def grouped_row(n2, base):
+    return ((n2 % 4) * 4 + base // LON) * INNER + (n2 // 4) * LON + base % LON
+
+
+def fft_core(x_ref, wh_ref, wl_ref, y_ref, r_ref, row_of):
     def butterfly(i, carry):
         base = pl.multiple_of(i * 8, 8)
-        x = [x_ref[pl.ds(n2 * INNER + base, 8), :] for n2 in range(RADIX)]
+        x = [x_ref[pl.ds(pl.multiple_of(row_of(n2, base), 8), 8), :] for n2 in range(RADIX)]
         y = fft_real16(x)
         for k in range(HALF):
             parts = (y[0][0], y[HALF][0]) if k == 0 else y[k]
@@ -158,7 +166,7 @@
 
 
 def fft_a_kernel(x_ref, wh_ref, wl_ref, o_ref, y_ref, r_ref, buf_ref, sem):
-    fft_core(x_ref, wh_ref, wl_ref, y_ref, r_ref)
+    fft_core(x_ref, wh_ref, wl_ref, y_ref, r_ref, grouped_row)
 
     def peer(k1, carry):
         for eight in range(KEPT // 8):
@@ -191,7 +199,7 @@
             for zz in range(NZ):
                 row = pl.multiple_of(start + zz * NC * LON, LON)
                 x_ref[pl.ds(row, LON), :] = g_refs[dx * NC + dc][zz * LON : (zz + 1) * LON, :]
-    fft_core(x_ref, wh_ref, wl_ref, y_ref, r_ref)
+    fft_core(x_ref, wh_ref, wl_ref, y_ref, r_ref, natural_row)
     for dz in range(NZ):
         target = (z + dz) % NZ
         for xx in range(NX):
@@ -285,44 +293,62 @@
     )(pos, *blocks)
 
 
-PAD_F = FIELDS + 8
-
-
-def relayout_a_kernel(s_ref, o_ref, x_ref, buf_ref, sem, out_sem):
-    copies = [
-        pltpu.make_async_copy(
-            s_ref.at[n, :, pl.ds(LANES, LANES)], x_ref.at[pl.ds(n * PAD_F, FIELDS), :], sem.at[n]
+GROUP = NZ * NC
+
+
+def split_a_kernel(pos_ref, s_ref, *refs):
+    o_refs, sem = refs[:NX], refs[NX]
+    x = pos_ref[0]
+    copies = []
+    for dx in range(NX):
+        field = pl.multiple_of(((x + dx) % NX) * GROUP, GROUP)
+        copies.append(
+            pltpu.make_async_copy(s_ref.at[:, pl.ds(field, GROUP), pl.ds(LANES, LANES)], o_refs[dx], sem.at[dx])
         )
-        for n in range(LON)
-    ]
     for copy in copies:
         copy.start()
     for copy in copies:
         copy.wait()
 
+
+def split_a(pos, state):
+    return pl.pallas_call(
+        split_a_kernel,
+        in_specs=[SMEM, HBM],
+        out_specs=[VMEM] * NX,
+        out_shape=[f32(LON, GROUP, LANES)] * NX,
+        scratch_shapes=[pltpu.SemaphoreType.DMA((NX,))],
+        compiler_params=PARAMS,
+        name="split_a",
+    )(pos, state)
+
+
+def spread_a_kernel(pos_ref, *refs):
+    b_refs, o_ref, buf_ref, sem = refs[:NX], refs[NX], refs[NX + 1], refs[NX + 2]
+    x = pos_ref[0]
+
     def field(f, carry):
-        for eight in range(LON // 8):
-            buf_ref[f, eight * 8 : eight * 8 + 8, :] = x_ref[pl.ds(eight * 8 * PAD_F + f, 8, stride=PAD_F), :]
+        for dx in range(NX):
+            row = pl.multiple_of(((x + NX - dx) % NX) * LON, LON)
+            buf_ref[f, pl.ds(row, LON), :] = b_refs[dx][pl.ds(f, LON, stride=GROUP), :]
         return carry
 
-    send_pieces(field, FIELDS, buf_ref, o_ref, out_sem)
-
-
-def relayout_a(state):
-    return pl.pallas_call(
-        relayout_a_kernel,
-        in_specs=[HBM],
+    send_pieces(field, GROUP, buf_ref, o_ref, sem)
+
+
+def spread_a(pos, blocks):
+    return pl.pallas_call(
+        spread_a_kernel,
+        in_specs=[SMEM] + [VMEM] * NX,
         out_specs=HBM,
-        out_shape=f32(FIELDS, LON, LANES),
+        out_shape=pltpu.HBM((GROUP, NX * LON, LANES), jnp.float32),
         scratch_shapes=[
-            pltpu.VMEM((LON * PAD_F, LANES), jnp.float32),
-            pltpu.VMEM((FIELDS, LON, LANES), jnp.float32),
-            pltpu.SemaphoreType.DMA((LON,)),
+            pltpu.VMEM((GROUP, NX * LON, LANES), jnp.float32),
             pltpu.SemaphoreType.DMA((PIECES,)),
         ],
         compiler_params=PARAMS,
-        name="relayout_a",
-    )(state)
+        name="spread_a",
+    )(pos, *blocks)
 
 
 PAD_K = KEPT + 8
@@ -421,6 +447,18 @@
     return out
 
 
+AX_ORDER = (2, 1, 3)
+GROUPS = [[x * GROUP + g for g in range(GROUP)] for x in range(NX)]
+
+
+def exchange_x(blocks):
+    out = [None] * NX
+    out[0] = blocks[0]
+    for dx in AX_ORDER:
+        out[dx] = lax.ppermute(blocks[dx], "lon", shifts(dx, 0, 0))
+    return out
+
+
 X_ORDER = ((2, 0), (2, 1), (1, 0), (3, 0), (1, 1), (3, 1), (0, 1))
 
 
@@ -438,8 +476,12 @@
     wh, wl = twiddle_matrices(1.0 / math.sqrt(NLON))
     pieces = split_z(pos, pltpu.with_memory_space_constraint(state, pltpu.HBM))
     pieces = exchange_z(pieces)
-    sent = relayout_a(pltpu.with_memory_space_constraint(state, pltpu.HBM))
-    gathered = lax.all_to_all(sent, "lon", split_axis=0, concat_axis=0, tiled=True)
+    parts = split_a(pos, pltpu.with_memory_space_constraint(state, pltpu.HBM))
+    parts = exchange_x(parts)
+    sent = spread_a(pos, [b.reshape(LON * GROUP, LANES) for b in parts])
+    gathered = lax.all_to_all(
+        sent, "lon", split_axis=0, concat_axis=0, axis_index_groups=GROUPS, tiled=True
+    )
     pieces = spread_x(pos, [b.reshape(LON * 8, LANES) for b in pieces])
     pieces = exchange_xc(pieces)
     pieces = fft_p(pos, pieces, wh, wl)

time: 174 us -> 189 us (1.086)
  waiting for transfers between devices: 88.9 us -> 101 us
  starting transfers between devices: 67.1 us -> 70.3 us
    ppermute x0 -> x3, waiting for transfers between devices: none -> 10.2 us  [exchange_x(): out[dx] = lax.ppermute(blocks[dx], 'lon', shifts(dx, 0, 0))]
    ppermute x0 -> x3, starting transfers between devices: none -> 5.71 us  [exchange_x(): out[dx] = lax.ppermute(blocks[dx], 'lon', shifts(dx, 0, 0))]
    all_to_all x1, starting transfers between devices: 13 us -> 10 us  [local(): lax.all_to_all(sent, 'lon', split_axis=0, concat_axis=0, axis_index_group...]
    ppermute x14, waiting for transfers between devices: 13 us -> 15.4 us  [exchange_xc(): lax.ppermute(blocks[dx * NC + dc], 'lon', shifts(dx, 0, dc))]
  transfers between devices with their start and end apart: 30 -> 33, of which waited for: 15 -> 16; matrix products, arithmetic and copies ran while one was open for 2% -> 2% of each run, Pallas kernels for 4% -> 4%
where the time goes in v6:
time: 189 us
  waiting for transfers between devices  101 us (53%)
  starting transfers between devices  70.3 us (37%)
  Pallas kernels  14.7 us (8%)
  other arithmetic  3.31 us (2%)
    ppermute x14, waiting for transfers between devices, exchange_z(): out[dz] = lax.ppermute(blocks[dz], 'lon', shifts(0, dz, 0))  50.2 us
    ppermute x14, starting transfers between devices, exchange_z(): out[dz] = lax.ppermute(blocks[dz], 'lon', shifts(0, dz, 0))  28.5 us
    all_to_all x1, waiting for transfers between devices, local(): lax.all_to_all(sent, 'lon', split_axis=0, concat_axis=0, axis_index_group...  24.7 us
    ppermute x14, starting transfers between devices, exchange_xc(): lax.ppermute(blocks[dx * NC + dc], 'lon', shifts(dx, 0, dc))  20 us
    ppermute x14, waiting for transfers between devices, exchange_xc(): lax.ppermute(blocks[dx * NC + dc], 'lon', shifts(dx, 0, dc))  15.4 us
    ppermute x3, waiting for transfers between devices, exchange_x(): out[dx] = lax.ppermute(blocks[dx], 'lon', shifts(dx, 0, 0))  10.2 us
    all_to_all x1, starting transfers between devices, local(): lax.all_to_all(sent, 'lon', split_axis=0, concat_axis=0, axis_index_group...  10 us
    all_to_all x1, starting transfers between devices, local(): lax.all_to_all(spectrum, 'lon', split_axis=0, concat_axis=0, tiled=True)  6.08 us
  transfers between devices with their start and end apart: 33, of which 16 were waited for; matrix products, arithmetic and copies ran while one was open for 2% of the time, Pallas kernels for 4%

profile of v6, /device:TPU:1, one launch (start us, length us, event | category | flops | bytes accessed | tf_op | source)
XLA Modules:
  0.0 189.1 jit_solution(12526462356712223446)
XLA Ops:
  4.0 2.5 %collective-permute-start.1 = (f32[32,16,128]{2,1,0:T(8,128)S(1)}, f32[32,16,128]{2,1,0:T(8,128)S(1)}, u32[]{:S(2)}, u32[]{:S(2)}) collective-permute-start(f32[32,16,128]{2,1,0:T(8,128)S(1)} %get-tuple-element.43), channel_id=1, source_target_pairs={{0,128},{4,132},{8,136},{12,140},{16,144},{20,148},{24,152},{28,15... | collective-permute-start | bytes 786440 | tf_op jit(solution)/shard_map/ppermute | solution.py:458
  9.0 8.8 %collective-permute-done.1 = f32[32,16,128]{2,1,0:T(8,128)S(1)} collective-permute-done((f32[32,16,128]{2,1,0:T(8,128)S(1)}, f32[32,16,128]{2,1,0:T(8,128)S(1)}, u32[]{:S(2)}, u32[]{:S(2)}) %collective-permute-start.1) | collective-permute-done | bytes 262176 | tf_op jit(solution)/shard_map/ppermute | solution.py:458
  19.4 10.0 %all-to-all-start = ((f32[16,128,128]{2,1,0:T(8,128)}), f32[16,128,128]{2,1,0:T(8,128)S(1)}, u32[]{:S(2)}, u32[]{:S(2)}) async-start(f32[16,128,128]{2,1,0:T(8,128)} %spread_a.1), calls=%async_computation | async-start | bytes 2097152 | tf_op jit(solution)/shard_map/all_to_all | solution.py:482
  29.5 2.5 %select_select_fusion.1 = (f32[8,2,64,128]{3,2,1,0:T(8,128)S(1)}, f32[8,2,64,128]{3,2,1,0:T(8,128)S(1)}, f32[8,2,64,128]{3,2,1,0:T(8,128)S(1)}, f32[8,2,64,128]{3,2,1,0:T(8,128)S(1)}) fusion(pred[2]{0:T(512)(128)(4,1)S(1)} %iota_compare_fusion.1, pred[8]{0:T(512)(128)(4,1)S(1)} %iota_compare_fusion, s32[64]{0:T(128)S(1)} %iota_multiply_fusion, ...), kind=kLoop, calls=%fused_computation.9 | loop fusion | flops 4456448 | bytes 2097450 | tf_op jit(solution)/shard_map/jit(_where)/select_n | solution.py:56
  32.7 24.7 %all-to-all-done = f32[16,128,128]{2,1,0:T(8,128)S(1)} async-done(((f32[16,128,128]{2,1,0:T(8,128)}), f32[16,128,128]{2,1,0:T(8,128)S(1)}, u32[]{:S(2)}, u32[]{:S(2)}) %all-to-all-start) | async-done | bytes 1048608 | tf_op jit(solution)/shard_map/all_to_all | solution.py:482
  57.4 2.6 %fft_a.1 = f32[64,32,128]{2,1,0:T(8,128)} custom-call(f32[2048,128]{1,0:T(8,128)S(1)} %bitcast.26, bf16[8,256,256]{2,1,0:T(8,128)(2,1)S(1)} %get-tuple-element.78.wh_ref.refs_8_, bf16[8,256,256]{2,1,0:T(8,128)(2,1)S(1)} %get-tuple-element.77.wl_ref.refs_9_), custom_call_target="tpu_custom_call" | custom-call | tf_op jit(solution)/shard_map/fft_a/pallas_call | solution.py:180
  60.1 6.1 %all-to-all-start.1 = ((f32[64,32,128]{2,1,0:T(8,128)}), f32[64,32,128]{2,1,0:T(8,128)S(1)}, u32[]{:S(2)}, u32[]{:S(2)}) async-start(f32[64,32,128]{2,1,0:T(8,128)} %fft_a.1), calls=%async_computation.1 | async-start | bytes 2097152 | tf_op jit(solution)/shard_map/all_to_all | solution.py:490
  71.6 2.4 %collective-permute-start.5 = (f32[32,8,128]{2,1,0:T(8,128)S(1)}, f32[32,8,128]{2,1,0:T(8,128)S(1)}, u32[]{:S(2)}, u32[]{:S(2)}) collective-permute-start(f32[32,8,128]{2,1,0:T(8,128)S(1)} %get-tuple-element.48), channel_id=1, source_target_pairs={{0,24},{4,28},{8,32},{12,36},{16,40},{20,44},{24,48},{28,52},{32,5... | collective-permute-start | bytes 393224 | tf_op jit(solution)/shard_map/ppermute | solution.py:446
  76.1 2.4 %collective-permute-start.7 = (f32[32,8,128]{2,1,0:T(8,128)S(1)}, f32[32,8,128]{2,1,0:T(8,128)S(1)}, u32[]{:S(2)}, u32[]{:S(2)}) collective-permute-start(f32[32,8,128]{2,1,0:T(8,128)S(1)} %get-tuple-element.50), channel_id=1, source_target_pairs={{0,40},{4,44},{8,48},{12,52},{16,56},{20,60},{24,0},{28,4},{32,8},... | collective-permute-start | bytes 393224 | tf_op jit(solution)/shard_map/ppermute | solution.py:446
  78.5 15.9 %collective-permute-done.3 = f32[32,8,128]{2,1,0:T(8,128)S(1)} collective-permute-done((f32[32,8,128]{2,1,0:T(8,128)S(1)}, f32[32,8,128]{2,1,0:T(8,128)S(1)}, u32[]{:S(2)}, u32[]{:S(2)}) %collective-permute-start.3) | collective-permute-done | bytes 131104 | tf_op jit(solution)/shard_map/ppermute | solution.py:446
  96.6 2.8 %collective-permute-done.4 = f32[32,8,128]{2,1,0:T(8,128)S(1)} collective-permute-done((f32[32,8,128]{2,1,0:T(8,128)S(1)}, f32[32,8,128]{2,1,0:T(8,128)S(1)}, u32[]{:S(2)}, u32[]{:S(2)}) %collective-permute-start.4) | collective-permute-done | bytes 131104 | tf_op jit(solution)/shard_map/ppermute | solution.py:446
  101.8 8.8 %collective-permute-done.5 = f32[32,8,128]{2,1,0:T(8,128)S(1)} collective-permute-done((f32[32,8,128]{2,1,0:T(8,128)S(1)}, f32[32,8,128]{2,1,0:T(8,128)S(1)}, u32[]{:S(2)}, u32[]{:S(2)}) %collective-permute-start.5) | collective-permute-done | bytes 131104 | tf_op jit(solution)/shard_map/ppermute | solution.py:446
  110.6 4.9 %collective-permute-done.6 = f32[32,8,128]{2,1,0:T(8,128)S(1)} collective-permute-done((f32[32,8,128]{2,1,0:T(8,128)S(1)}, f32[32,8,128]{2,1,0:T(8,128)S(1)}, u32[]{:S(2)}, u32[]{:S(2)}) %collective-permute-start.6) | collective-permute-done | bytes 131104 | tf_op jit(solution)/shard_map/ppermute | solution.py:446
  116.4 2.5 %collective-permute-start.10 = (f32[256,128]{1,0:T(8,128)S(1)}, f32[256,128]{1,0:T(8,128)S(1)}, u32[]{:S(2)}, u32[]{:S(2)}) collective-permute-start(f32[256,128]{1,0:T(8,128)S(1)} %get-tuple-element.54), channel_id=1, source_target_pairs={{0,4},{4,0},{8,12},{12,8},{16,20},{20,16},{24,28},{28,24},{32,36},... | collective-permute-start | bytes 393224 | tf_op jit(solution)/shard_map/ppermute | solution.py:469
  119.8 3.2 %collective-permute-start.13 = (f32[256,128]{1,0:T(8,128)S(1)}, f32[256,128]{1,0:T(8,128)S(1)}, u32[]{:S(2)}, u32[]{:S(2)}) collective-permute-start(f32[256,128]{1,0:T(8,128)S(1)} %get-tuple-element.57), channel_id=1, source_target_pairs={{0,128},{4,132},{8,136},{12,140},{16,144},{20,148},{24,152},{28,15... | collective-permute-start | bytes 393224 | tf_op jit(solution)/shard_map/ppermute | solution.py:469
  126.8 6.9 %collective-permute-done.12.refs_3_ = f32[256,128]{1,0:T(8,128)S(1)} collective-permute-done((f32[256,128]{1,0:T(8,128)S(1)}, f32[256,128]{1,0:T(8,128)S(1)}, u32[]{:S(2)}, u32[]{:S(2)}) %collective-permute-start.12) | collective-permute-done | bytes 131104 | tf_op jit(solution)/shard_map/ppermute | solution.py:469
  140.9 3.3 %collective-permute-start.20 = (f32[256,128]{1,0:T(8,128)S(1)}, f32[256,128]{1,0:T(8,128)S(1)}, u32[]{:S(2)}, u32[]{:S(2)}) collective-permute-start(f32[256,128]{1,0:T(8,128)S(1)} %get-tuple-element.65), channel_id=1, source_target_pairs={{0,32},{4,36},{8,40},{12,44},{16,48},{20,52},{24,56},{28,60},{32,0... | collective-permute-start | bytes 393224 | tf_op jit(solution)/shard_map/ppermute | solution.py:446
  146.9 4.6 %collective-permute-start.23 = (f32[256,128]{1,0:T(8,128)S(1)}, f32[256,128]{1,0:T(8,128)S(1)}, u32[]{:S(2)}, u32[]{:S(2)}) collective-permute-start(f32[256,128]{1,0:T(8,128)S(1)} %get-tuple-element.68), channel_id=1, source_target_pairs={{0,56},{4,60},{8,0},{12,4},{16,8},{20,12},{24,16},{28,20},{32,24},... | collective-permute-start | bytes 393224 | tf_op jit(solution)/shard_map/ppermute | solution.py:446
  151.4 9.8 %collective-permute-done.19.refs_3_ = f32[256,128]{1,0:T(8,128)S(1)} collective-permute-done((f32[256,128]{1,0:T(8,128)S(1)}, f32[256,128]{1,0:T(8,128)S(1)}, u32[]{:S(2)}, u32[]{:S(2)}) %collective-permute-start.19) | collective-permute-done | bytes 131104 | tf_op jit(solution)/shard_map/ppermute | solution.py:446
  161.2 4.1 %collective-permute-done.22.refs_6_ = f32[256,128]{1,0:T(8,128)S(1)} collective-permute-done((f32[256,128]{1,0:T(8,128)S(1)}, f32[256,128]{1,0:T(8,128)S(1)}, u32[]{:S(2)}, u32[]{:S(2)}) %collective-permute-start.22) | collective-permute-done | bytes 131104 | tf_op jit(solution)/shard_map/ppermute | solution.py:446
  165.4 2.7 %collective-permute-done.23.refs_7_ = f32[256,128]{1,0:T(8,128)S(1)} collective-permute-done((f32[256,128]{1,0:T(8,128)S(1)}, f32[256,128]{1,0:T(8,128)S(1)}, u32[]{:S(2)}, u32[]{:S(2)}) %collective-permute-start.23) | collective-permute-done | bytes 131104 | tf_op jit(solution)/shard_map/ppermute | solution.py:446
  175.2 2.6 %collective-permute-start.29 = (f32[256,128]{1,0:T(8,128)S(1)}, f32[256,128]{1,0:T(8,128)S(1)}, u32[]{:S(2)}, u32[]{:S(2)}) collective-permute-start(f32[256,128]{1,0:T(8,128)S(1)} %get-tuple-element.75), channel_id=1, source_target_pairs={{0,192},{4,196},{8,200},{12,204},{16,208},{20,212},{24,216},{28,22... | collective-permute-start | bytes 393224 | tf_op jit(solution)/shard_map/ppermute | solution.py:469
  179.4 2.8 %collective-permute-done.27.refs_4_ = f32[256,128]{1,0:T(8,128)S(1)} collective-permute-done((f32[256,128]{1,0:T(8,128)S(1)}, f32[256,128]{1,0:T(8,128)S(1)}, u32[]{:S(2)}, u32[]{:S(2)}) %collective-permute-start.27) | collective-permute-done | bytes 131104 | tf_op jit(solution)/shard_map/ppermute | solution.py:469
  182.3 3.1 %collective-permute-done.28.refs_5_ = f32[256,128]{1,0:T(8,128)S(1)} collective-permute-done((f32[256,128]{1,0:T(8,128)S(1)}, f32[256,128]{1,0:T(8,128)S(1)}, u32[]{:S(2)}, u32[]{:S(2)}) %collective-permute-start.28) | collective-permute-done | bytes 131104 | tf_op jit(solution)/shard_map/ppermute | solution.py:469
  (60 shorter events, 48.9 us)
Async XLA Ops:
  4.0 13.8 %collective-permute-start.1 = (f32[32,16,128]{2,1,0:T(8,128)S(1)}, f32[32,16,128]{2,1,0:T(8,128)S(1)}, u32[]{:S(2)}, u32[]{:S(2)}) collective-permute-start(f32[32,16,128]{2,1,0:T(8,128)S(1)} %get-tuple-element.43), channel_id=1, source_target_pairs={{0,128},{4,132},{8,136},{12,140},{16,144},{20,148},{24,152},{28,15... | collective-permute-start | bytes 786440 | tf_op jit(solution)/shard_map/ppermute | solution.py:458
  6.4 11.3 %collective-permute-start.2 = (f32[32,16,128]{2,1,0:T(8,128)S(1)}, f32[32,16,128]{2,1,0:T(8,128)S(1)}, u32[]{:S(2)}, u32[]{:S(2)}) collective-permute-start(f32[32,16,128]{2,1,0:T(8,128)S(1)} %get-tuple-element.44), channel_id=1, source_target_pairs={{0,192},{4,196},{8,200},{12,204},{16,208},{20,212},{24,216},{28,22... | collective-permute-start | bytes 786440 | tf_op jit(solution)/shard_map/ppermute | solution.py:458
  19.4 38.0 %all-to-all-start = ((f32[16,128,128]{2,1,0:T(8,128)}), f32[16,128,128]{2,1,0:T(8,128)S(1)}, u32[]{:S(2)}, u32[]{:S(2)}) async-start(f32[16,128,128]{2,1,0:T(8,128)} %spread_a.1), calls=%async_computation | async-start | bytes 2097152 | tf_op jit(solution)/shard_map/all_to_all | solution.py:482
  60.1 118.2 %all-to-all-start.1 = ((f32[64,32,128]{2,1,0:T(8,128)}), f32[64,32,128]{2,1,0:T(8,128)S(1)}, u32[]{:S(2)}, u32[]{:S(2)}) async-start(f32[64,32,128]{2,1,0:T(8,128)} %fft_a.1), calls=%async_computation.1 | async-start | bytes 2097152 | tf_op jit(solution)/shard_map/all_to_all | solution.py:490
  68.1 26.3 %collective-permute-start.3 = (f32[32,8,128]{2,1,0:T(8,128)S(1)}, f32[32,8,128]{2,1,0:T(8,128)S(1)}, u32[]{:S(2)}, u32[]{:S(2)}) collective-permute-start(f32[32,8,128]{2,1,0:T(8,128)S(1)} %get-tuple-element.46), channel_id=1, source_target_pairs={{0,8},{4,12},{8,16},{12,20},{16,24},{20,28},{24,32},{28,36},{32,40... | collective-permute-start | bytes 393224 | tf_op jit(solution)/shard_map/ppermute | solution.py:446
  69.5 29.9 %collective-permute-start.4 = (f32[32,8,128]{2,1,0:T(8,128)S(1)}, f32[32,8,128]{2,1,0:T(8,128)S(1)}, u32[]{:S(2)}, u32[]{:S(2)}) collective-permute-start(f32[32,8,128]{2,1,0:T(8,128)S(1)} %get-tuple-element.47), channel_id=1, source_target_pairs={{0,16},{4,20},{8,24},{12,28},{16,32},{20,36},{24,40},{28,44},{32,4... | collective-permute-start | bytes 393224 | tf_op jit(solution)/shard_map/ppermute | solution.py:446
  71.6 39.0 %collective-permute-start.5 = (f32[32,8,128]{2,1,0:T(8,128)S(1)}, f32[32,8,128]{2,1,0:T(8,128)S(1)}, u32[]{:S(2)}, u32[]{:S(2)}) collective-permute-start(f32[32,8,128]{2,1,0:T(8,128)S(1)} %get-tuple-element.48), channel_id=1, source_target_pairs={{0,24},{4,28},{8,32},{12,36},{16,40},{20,44},{24,48},{28,52},{32,5... | collective-permute-start | bytes 393224 | tf_op jit(solution)/shard_map/ppermute | solution.py:446
  74.0 41.5 %collective-permute-start.6 = (f32[32,8,128]{2,1,0:T(8,128)S(1)}, f32[32,8,128]{2,1,0:T(8,128)S(1)}, u32[]{:S(2)}, u32[]{:S(2)}) collective-permute-start(f32[32,8,128]{2,1,0:T(8,128)S(1)} %get-tuple-element.49), channel_id=1, source_target_pairs={{0,32},{4,36},{8,40},{12,44},{16,48},{20,52},{24,56},{28,60},{32,0... | collective-permute-start | bytes 393224 | tf_op jit(solution)/shard_map/ppermute | solution.py:446
  76.1 39.4 %collective-permute-start.7 = (f32[32,8,128]{2,1,0:T(8,128)S(1)}, f32[32,8,128]{2,1,0:T(8,128)S(1)}, u32[]{:S(2)}, u32[]{:S(2)}) collective-permute-start(f32[32,8,128]{2,1,0:T(8,128)S(1)} %get-tuple-element.50), channel_id=1, source_target_pairs={{0,40},{4,44},{8,48},{12,52},{16,56},{20,60},{24,0},{28,4},{32,8},... | collective-permute-start | bytes 393224 | tf_op jit(solution)/shard_map/ppermute | solution.py:446
  94.4 21.1 %collective-permute-start.8 = (f32[32,8,128]{2,1,0:T(8,128)S(1)}, f32[32,8,128]{2,1,0:T(8,128)S(1)}, u32[]{:S(2)}, u32[]{:S(2)}) collective-permute-start(f32[32,8,128]{2,1,0:T(8,128)S(1)} %get-tuple-element.51), channel_id=1, source_target_pairs={{0,48},{4,52},{8,56},{12,60},{16,0},{20,4},{24,8},{28,12},{32,16},... | collective-permute-start | bytes 393224 | tf_op jit(solution)/shard_map/ppermute | solution.py:446
  99.4 16.0 %collective-permute-start.9 = (f32[32,8,128]{2,1,0:T(8,128)S(1)}, f32[32,8,128]{2,1,0:T(8,128)S(1)}, u32[]{:S(2)}, u32[]{:S(2)}) collective-permute-start(f32[32,8,128]{2,1,0:T(8,128)S(1)} %get-tuple-element.52), channel_id=1, source_target_pairs={{0,56},{4,60},{8,0},{12,4},{16,8},{20,12},{24,16},{28,20},{32,24},... | collective-permute-start | bytes 393224 | tf_op jit(solution)/shard_map/ppermute | solution.py:446
  118.9 14.9 %collective-permute-start.12 = (f32[256,128]{1,0:T(8,128)S(1)}, f32[256,128]{1,0:T(8,128)S(1)}, u32[]{:S(2)}, u32[]{:S(2)}) collective-permute-start(f32[256,128]{1,0:T(8,128)S(1)} %get-tuple-element.56), channel_id=1, source_target_pairs={{0,68},{4,64},{8,76},{12,72},{16,84},{20,80},{24,92},{28,88},{32,1... | collective-permute-start | bytes 393224 | tf_op jit(solution)/shard_map/ppermute | solution.py:469
  119.8 13.9 %collective-permute-start.13 = (f32[256,128]{1,0:T(8,128)S(1)}, f32[256,128]{1,0:T(8,128)S(1)}, u32[]{:S(2)}, u32[]{:S(2)}) collective-permute-start(f32[256,128]{1,0:T(8,128)S(1)} %get-tuple-element.57), channel_id=1, source_target_pairs={{0,128},{4,132},{8,136},{12,140},{16,144},{20,148},{24,152},{28,15... | collective-permute-start | bytes 393224 | tf_op jit(solution)/shard_map/ppermute | solution.py:469
  123.0 10.8 %collective-permute-start.14 = (f32[256,128]{1,0:T(8,128)S(1)}, f32[256,128]{1,0:T(8,128)S(1)}, u32[]{:S(2)}, u32[]{:S(2)}) collective-permute-start(f32[256,128]{1,0:T(8,128)S(1)} %get-tuple-element.58), channel_id=1, source_target_pairs={{0,132},{4,128},{8,140},{12,136},{16,148},{20,144},{24,156},{28,15... | collective-permute-start | bytes 393224 | tf_op jit(solution)/shard_map/ppermute | solution.py:469
  123.1 10.7 %collective-permute-start.15 = (f32[256,128]{1,0:T(8,128)S(1)}, f32[256,128]{1,0:T(8,128)S(1)}, u32[]{:S(2)}, u32[]{:S(2)}) collective-permute-start(f32[256,128]{1,0:T(8,128)S(1)} %get-tuple-element.59), channel_id=1, source_target_pairs={{0,192},{4,196},{8,200},{12,204},{16,208},{20,212},{24,216},{28,22... | collective-permute-start | bytes 393224 | tf_op jit(solution)/shard_map/ppermute | solution.py:469
  136.9 10.0 %collective-permute-start.18 = (f32[256,128]{1,0:T(8,128)S(1)}, f32[256,128]{1,0:T(8,128)S(1)}, u32[]{:S(2)}, u32[]{:S(2)}) collective-permute-start(f32[256,128]{1,0:T(8,128)S(1)} %get-tuple-element.63), channel_id=1, source_target_pairs={{0,16},{4,20},{8,24},{12,28},{16,32},{20,36},{24,40},{28,44},{32,4... | collective-permute-start | bytes 393224 | tf_op jit(solution)/shard_map/ppermute | solution.py:446
  138.8 22.5 %collective-permute-start.19 = (f32[256,128]{1,0:T(8,128)S(1)}, f32[256,128]{1,0:T(8,128)S(1)}, u32[]{:S(2)}, u32[]{:S(2)}) collective-permute-start(f32[256,128]{1,0:T(8,128)S(1)} %get-tuple-element.64), channel_id=1, source_target_pairs={{0,24},{4,28},{8,32},{12,36},{16,40},{20,44},{24,48},{28,52},{32,5... | collective-permute-start | bytes 393224 | tf_op jit(solution)/shard_map/ppermute | solution.py:446
  140.9 20.3 %collective-permute-start.20 = (f32[256,128]{1,0:T(8,128)S(1)}, f32[256,128]{1,0:T(8,128)S(1)}, u32[]{:S(2)}, u32[]{:S(2)}) collective-permute-start(f32[256,128]{1,0:T(8,128)S(1)} %get-tuple-element.65), channel_id=1, source_target_pairs={{0,32},{4,36},{8,40},{12,44},{16,48},{20,52},{24,56},{28,60},{32,0... | collective-permute-start | bytes 393224 | tf_op jit(solution)/shard_map/ppermute | solution.py:446
  144.2 17.0 %collective-permute-start.21 = (f32[256,128]{1,0:T(8,128)S(1)}, f32[256,128]{1,0:T(8,128)S(1)}, u32[]{:S(2)}, u32[]{:S(2)}) collective-permute-start(f32[256,128]{1,0:T(8,128)S(1)} %get-tuple-element.66), channel_id=1, source_target_pairs={{0,40},{4,44},{8,48},{12,52},{16,56},{20,60},{24,0},{28,4},{32,8},... | collective-permute-start | bytes 393224 | tf_op jit(solution)/shard_map/ppermute | solution.py:446
  146.4 19.0 %collective-permute-start.22 = (f32[256,128]{1,0:T(8,128)S(1)}, f32[256,128]{1,0:T(8,128)S(1)}, u32[]{:S(2)}, u32[]{:S(2)}) collective-permute-start(f32[256,128]{1,0:T(8,128)S(1)} %get-tuple-element.67), channel_id=1, source_target_pairs={{0,48},{4,52},{8,56},{12,60},{16,0},{20,4},{24,8},{28,12},{32,16},... | collective-permute-start | bytes 393224 | tf_op jit(solution)/shard_map/ppermute | solution.py:446
  146.9 21.2 %collective-permute-start.23 = (f32[256,128]{1,0:T(8,128)S(1)}, f32[256,128]{1,0:T(8,128)S(1)}, u32[]{:S(2)}, u32[]{:S(2)}) collective-permute-start(f32[256,128]{1,0:T(8,128)S(1)} %get-tuple-element.68), channel_id=1, source_target_pairs={{0,56},{4,60},{8,0},{12,4},{16,8},{20,12},{24,16},{28,20},{32,24},... | collective-permute-start | bytes 393224 | tf_op jit(solution)/shard_map/ppermute | solution.py:446
  171.9 10.3 %collective-permute-start.27 = (f32[256,128]{1,0:T(8,128)S(1)}, f32[256,128]{1,0:T(8,128)S(1)}, u32[]{:S(2)}, u32[]{:S(2)}) collective-permute-start(f32[256,128]{1,0:T(8,128)S(1)} %get-tuple-element.73), channel_id=1, source_target_pairs={{0,128},{4,132},{8,136},{12,140},{16,144},{20,148},{24,152},{28,15... | collective-permute-start | bytes 393224 | tf_op jit(solution)/shard_map/ppermute | solution.py:469
  173.5 11.8 %collective-permute-start.28 = (f32[256,128]{1,0:T(8,128)S(1)}, f32[256,128]{1,0:T(8,128)S(1)}, u32[]{:S(2)}, u32[]{:S(2)}) collective-permute-start(f32[256,128]{1,0:T(8,128)S(1)} %get-tuple-element.74), channel_id=1, source_target_pairs={{0,132},{4,128},{8,140},{12,136},{16,148},{20,144},{24,156},{28,15... | collective-permute-start | bytes 393224 | tf_op jit(solution)/shard_map/ppermute | solution.py:469
  175.2 10.1 %collective-permute-start.29 = (f32[256,128]{1,0:T(8,128)S(1)}, f32[256,128]{1,0:T(8,128)S(1)}, u32[]{:S(2)}, u32[]{:S(2)}) collective-permute-start(f32[256,128]{1,0:T(8,128)S(1)} %get-tuple-element.75), channel_id=1, source_target_pairs={{0,192},{4,196},{8,200},{12,204},{16,208},{20,212},{24,216},{28,22... | collective-permute-start | bytes 393224 | tf_op jit(solution)/shard_map/ppermute | solution.py:469
  (9 other events, 71.2 us)

commit v7 on v6

--- a/solution.py
+++ b/solution.py
@@ -26,6 +26,10 @@
 
 def f32(*shape):
     return jax.ShapeDtypeStruct(shape, jnp.float32)
+
+
+def vmem(*shape):
+    return pltpu.VMEM(shape, jnp.float32)
 
 
 def split_bf16(v):
@@ -62,7 +66,8 @@
     full = jnp.stack([re, im], axis=2)
     full = full.reshape(HALF, 4 * PEERS, 2 * INNER)
     high = lax.reduce_precision(full, 8, 7)
-    return high.astype(jnp.bfloat16), (full - high).astype(jnp.bfloat16)
+    high, low = high.astype(jnp.bfloat16), (full - high).astype(jnp.bfloat16)
+    return jnp.concatenate([high, low], axis=-1)
 
 
 def fft_real16(x):
@@ -116,7 +121,7 @@
     return ((n2 % 4) * 4 + base // LON) * INNER + (n2 // 4) * LON + base % LON
 
 
-def fft_core(x_ref, wh_ref, wl_ref, y_ref, r_ref, row_of):
+def fft_core(x_ref, w_ref, y_ref, r_ref, row_of, loads):
     def butterfly(i, carry):
         base = pl.multiple_of(i * 8, 8)
         x = [x_ref[pl.ds(pl.multiple_of(row_of(n2, base), 8), 8), :] for n2 in range(RADIX)]
@@ -130,10 +135,13 @@
     lax.fori_loop(0, INNER // 8, butterfly, 0)
     for k in range(HALF):
         yh, yl = split_bf16(y_ref[k])
-        wh = wh_ref[k]
-        r = jnp.dot(wh, yh, preferred_element_type=jnp.float32)
-        r = r + jnp.dot(wh, yl, preferred_element_type=jnp.float32)
-        r = r + jnp.dot(wl_ref[k], yh, preferred_element_type=jnp.float32)
+        loads[k].wait()
+        high, both = w_ref[k, :, : 2 * INNER], w_ref[k]
+        r = jnp.dot(
+            jnp.concatenate([high, both], axis=1),
+            jnp.concatenate([yl, yh, yh], axis=0),
+            preferred_element_type=jnp.float32,
+        )
         mirror = HALF if k == 0 else RADIX - k
         for q, row in enumerate((k, RADIX + k, mirror, RADIX + mirror)):
             r_ref[pl.ds(row * PAD_R, PEERS), :] = r[q * PEERS : (q + 1) * PEERS]
@@ -155,7 +163,16 @@
         copy.wait()
 
 
+def load_matrices(w_hbm, w_ref, sem):
+    loads = [pltpu.make_async_copy(w_hbm.at[k], w_ref.at[k], sem.at[k]) for k in range(HALF)]
+    for load in loads:
+        load.start()
+    return loads
+
+
 FFT_SCRATCH = [
+    pltpu.VMEM((HALF, 4 * PEERS, 4 * INNER), jnp.bfloat16),
+    pltpu.SemaphoreType.DMA((HALF,)),
     pltpu.VMEM((HALF, 2 * INNER, LANES), jnp.float32),
     pltpu.VMEM((KEPT * PAD_R, LANES), jnp.float32),
 ]
@@ -165,8 +182,9 @@
     return r_ref[pl.ds(eight * 8 * PAD_R + k1, 8, stride=PAD_R), :]
 
 
-def fft_a_kernel(x_ref, wh_ref, wl_ref, o_ref, y_ref, r_ref, buf_ref, sem):
-    fft_core(x_ref, wh_ref, wl_ref, y_ref, r_ref, grouped_row)
+def fft_a_kernel(x_ref, w_hbm, o_ref, w_ref, w_sem, y_ref, r_ref, buf_ref, sem):
+    loads = load_matrices(w_hbm, w_ref, w_sem)
+    fft_core(x_ref, w_ref, y_ref, r_ref, grouped_row, loads)
 
     def peer(k1, carry):
         for eight in range(KEPT // 8):
@@ -176,22 +194,23 @@
     send_pieces(peer, PEERS, buf_ref, o_ref, sem)
 
 
-def fft_a(gathered, wh, wl):
+def fft_a(gathered, w):
     return pl.pallas_call(
         fft_a_kernel,
-        in_specs=[VMEM] * 3,
+        in_specs=[VMEM, HBM],
         out_specs=HBM,
         out_shape=pltpu.HBM((PEERS, KEPT, LANES), jnp.float32),
         scratch_shapes=FFT_SCRATCH
         + [pltpu.VMEM((PEERS, KEPT, LANES), jnp.float32), pltpu.SemaphoreType.DMA((PIECES,))],
         compiler_params=PARAMS,
         name="fft_a",
-    )(gathered, wh, wl)
+    )(gathered, pltpu.with_memory_space_constraint(w, pltpu.HBM))
 
 
 def fft_p_kernel(pos_ref, *refs):
-    g_refs, (wh_ref, wl_ref), o_refs = refs[:8], refs[8:10], refs[10:18]
-    x_ref, y_ref, r_ref = refs[18:]
+    g_refs, w_hbm, o_refs = refs[:8], refs[8], refs[9:17]
+    x_ref, w_ref, w_sem, y_ref, r_ref = refs[17:]
+    loads = load_matrices(w_hbm, w_ref, w_sem)
     x, z, c = pos_ref[0], pos_ref[1], pos_ref[2]
     for dx in range(NX):
         for dc in range(NC):
@@ -199,7 +218,7 @@
             for zz in range(NZ):
                 row = pl.multiple_of(start + zz * NC * LON, LON)
                 x_ref[pl.ds(row, LON), :] = g_refs[dx * NC + dc][zz * LON : (zz + 1) * LON, :]
-    fft_core(x_ref, wh_ref, wl_ref, y_ref, r_ref, natural_row)
+    fft_core(x_ref, w_ref, y_ref, r_ref, natural_row, loads)
     for dz in range(NZ):
         target = (z + dz) % NZ
         for xx in range(NX):
@@ -210,43 +229,50 @@
                     o_refs[dz][row : row + 8, :] = mode_rows(r_ref, k1, eight)
 
 
-def fft_p(pos, blocks, wh, wl):
+def fft_p(pos, blocks, w):
     return pl.pallas_call(
         fft_p_kernel,
-        in_specs=[SMEM] + [VMEM] * 10,
+        in_specs=[SMEM] + [VMEM] * 8 + [HBM],
         out_specs=[VMEM] * NZ,
-        out_shape=[f32(NX * NC * KEPT, LANES)] * NZ,
+        out_shape=[vmem(NX * NC * KEPT, LANES)] * NZ,
         scratch_shapes=[pltpu.VMEM((NLON, LANES), jnp.float32)] + FFT_SCRATCH,
         compiler_params=PARAMS,
         name="fft_p",
-    )(pos, *blocks, wh, wl)
-
-
-def split_z_kernel(pos_ref, s_ref, *refs):
-    o_refs, sem = refs[:NZ], refs[NZ]
-    z = pos_ref[1]
+    )(pos, *blocks, pltpu.with_memory_space_constraint(w, pltpu.HBM))
+
+
+GROUP = NZ * NC
+
+
+def split_kernel(pos_ref, s_ref, *refs):
+    o_refs, sem = refs[: NZ + NX], refs[NZ + NX]
+    x, z = pos_ref[0], pos_ref[1]
     copies = []
     for dz in range(NZ):
         field = pl.multiple_of(((z + dz) % NZ) * 8, 8)
-        copies.append(
-            pltpu.make_async_copy(s_ref.at[:, pl.ds(field, 8), pl.ds(0, LANES)], o_refs[dz], sem.at[dz])
-        )
+        source = s_ref.at[:, pl.ds(field, 8), pl.ds(0, LANES)]
+        copies.append(pltpu.make_async_copy(source, o_refs[dz], sem.at[dz]))
+    for dx in range(NX):
+        field = pl.multiple_of(((x + dx) % NX) * GROUP, GROUP)
+        source = s_ref.at[:, pl.ds(field, GROUP), pl.ds(LANES, LANES)]
+        copies.append(pltpu.make_async_copy(source, o_refs[NZ + dx], sem.at[NZ + dx]))
     for copy in copies:
         copy.start()
     for copy in copies:
         copy.wait()
 
 
-def split_z(pos, state):
-    return pl.pallas_call(
-        split_z_kernel,
+def split(pos, state):
+    out = pl.pallas_call(
+        split_kernel,
         in_specs=[SMEM, HBM],
-        out_specs=[VMEM] * NZ,
-        out_shape=[f32(LON, 8, LANES)] * NZ,
-        scratch_shapes=[pltpu.SemaphoreType.DMA((NZ,))],
-        compiler_params=PARAMS,
-        name="split_z",
-    )(pos, state)
+        out_specs=[VMEM] * (NZ + NX),
+        out_shape=[vmem(LON, 8, LANES)] * NZ + [vmem(LON, GROUP, LANES)] * NX,
+        scratch_shapes=[pltpu.SemaphoreType.DMA((NZ + NX,))],
+        compiler_params=PARAMS,
+        name="split",
+    )(pos, pltpu.with_memory_space_constraint(state, pltpu.HBM))
+    return out[:NZ], out[NZ:]
 
 
 def spread_x_kernel(pos_ref, *refs):
@@ -265,7 +291,7 @@
         spread_x_kernel,
         in_specs=[SMEM] + [VMEM] * NZ,
         out_specs=[VMEM] * (NX * NC),
-        out_shape=[f32(NZ * LON, LANES)] * (NX * NC),
+        out_shape=[vmem(NZ * LON, LANES)] * (NX * NC),
         compiler_params=PARAMS,
         name="spread_x",
     )(pos, *blocks)
@@ -287,40 +313,10 @@
         spread_out_kernel,
         in_specs=[SMEM] + [VMEM] * NZ,
         out_specs=[VMEM] * (NX * NC),
-        out_shape=[f32(NZ * KEPT, LANES)] * (NX * NC),
+        out_shape=[vmem(NZ * KEPT, LANES)] * (NX * NC),
         compiler_params=PARAMS,
         name="spread_out",
     )(pos, *blocks)
-
-
-GROUP = NZ * NC
-
-
-def split_a_kernel(pos_ref, s_ref, *refs):
-    o_refs, sem = refs[:NX], refs[NX]
-    x = pos_ref[0]
-    copies = []
-    for dx in range(NX):
-        field = pl.multiple_of(((x + dx) % NX) * GROUP, GROUP)
-        copies.append(
-            pltpu.make_async_copy(s_ref.at[:, pl.ds(field, GROUP), pl.ds(LANES, LANES)], o_refs[dx], sem.at[dx])
-        )
-    for copy in copies:
-        copy.start()
-    for copy in copies:
-        copy.wait()
-
-
-def split_a(pos, state):
-    return pl.pallas_call(
-        split_a_kernel,
-        in_specs=[SMEM, HBM],
-        out_specs=[VMEM] * NX,
-        out_shape=[f32(LON, GROUP, LANES)] * NX,
-        scratch_shapes=[pltpu.SemaphoreType.DMA((NX,))],
-        compiler_params=PARAMS,
-        name="split_a",
-    )(pos, state)
 
 
 def spread_a_kernel(pos_ref, *refs):
@@ -473,10 +469,9 @@
 def local(state):
     device = lax.axis_index("lon")
     pos = jnp.stack([device // (NZ * NC), (device // NC) % NZ, device % NC]).astype(jnp.int32)
-    wh, wl = twiddle_matrices(1.0 / math.sqrt(NLON))
-    pieces = split_z(pos, pltpu.with_memory_space_constraint(state, pltpu.HBM))
+    w = twiddle_matrices(1.0 / math.sqrt(NLON))
+    pieces, parts = split(pos, state)
     pieces = exchange_z(pieces)
-    parts = split_a(pos, pltpu.with_memory_space_constraint(state, pltpu.HBM))
     parts = exchange_x(parts)
     sent = spread_a(pos, [b.reshape(LON * GROUP, LANES) for b in parts])
     gathered = lax.all_to_all(
@@ -484,9 +479,9 @@
     )
     pieces = spread_x(pos, [b.reshape(LON * 8, LANES) for b in pieces])
     pieces = exchange_xc(pieces)
-    pieces = fft_p(pos, pieces, wh, wl)
+    pieces = fft_p(pos, pieces, w)
     pieces = exchange_z(pieces)
-    spectrum = fft_a(gathered.reshape(NLON, LANES), wh, wl)
+    spectrum = fft_a(gathered.reshape(NLON, LANES), w)
     shares = lax.all_to_all(spectrum, "lon", split_axis=0, concat_axis=0, tiled=True)
     pieces = spread_out(pos, pieces)
     pieces = exchange_xc(pieces)

time: 189 us -> 194 us (1.026)
  Pallas kernels: 14.7 us -> 16.8 us
    pallas_call x4 -> x3, Pallas kernels: 8.69 us -> 10.8 us  [the longest x1 4.41 us: fft_a(): pl.pallas_call(fft_a_kernel, in_specs=[VMEM, HBM], out_specs=HBM, out_sha...]
  transfers between devices with their start and end apart: 33 -> 33, of which waited for: 16 -> 16; matrix products, arithmetic and copies ran while one was open for 2% -> 2% of each run, Pallas kernels for 4% -> 3%
where the time goes in v7:
time: 194 us; the launch traced here: 193 us
  waiting for transfers between devices  101 us (52%)
  starting transfers between devices  70.3 us (36%)
  Pallas kernels  16.8 us (9%)
  other arithmetic  4.81 us (2%)
    ppermute x14, waiting for transfers between devices, exchange_z(): out[dz] = lax.ppermute(blocks[dz], 'lon', shifts(0, dz, 0))  52.1 us
    ppermute x14, starting transfers between devices, exchange_z(): out[dz] = lax.ppermute(blocks[dz], 'lon', shifts(0, dz, 0))  28.5 us
    all_to_all x1, waiting for transfers between devices, local(): lax.all_to_all(sent, 'lon', split_axis=0, concat_axis=0, axis_index_group...  23.2 us
    ppermute x14, starting transfers between devices, exchange_xc(): lax.ppermute(blocks[dx * NC + dc], 'lon', shifts(dx, 0, dc))  20 us
    ppermute x14, waiting for transfers between devices, exchange_xc(): lax.ppermute(blocks[dx * NC + dc], 'lon', shifts(dx, 0, dc))  15.4 us
    ppermute x3, waiting for transfers between devices, exchange_x(): out[dx] = lax.ppermute(blocks[dx], 'lon', shifts(dx, 0, 0))  10.2 us
    all_to_all x1, starting transfers between devices, local(): lax.all_to_all(sent, 'lon', split_axis=0, concat_axis=0, axis_index_group...  10 us
    all_to_all x1, starting transfers between devices, local(): lax.all_to_all(spectrum, 'lon', split_axis=0, concat_axis=0, tiled=True)  6.08 us
  transfers between devices with their start and end apart: 33, of which 16 were waited for; matrix products, arithmetic and copies ran while one was open for 2% of the time, Pallas kernels for 3%

profile of v7, /device:TPU:1, one launch (start us, length us, event | category | flops | bytes accessed | tf_op | source)
XLA Modules:
  0.0 193.2 jit_solution(8907852200630126491)
XLA Ops:
  4.5 2.5 %collective-permute-start.1 = (f32[32,16,128]{2,1,0:T(8,128)S(1)}, f32[32,16,128]{2,1,0:T(8,128)S(1)}, u32[]{:S(2)}, u32[]{:S(2)}) collective-permute-start(f32[32,16,128]{2,1,0:T(8,128)S(1)} %get-tuple-element.43), channel_id=1, source_target_pairs={{0,128},{4,132},{8,136},{12,140},{16,144},{20,148},{24,152},{28,15... | collective-permute-start | bytes 786440 | tf_op jit(solution)/shard_map/ppermute | solution.py:454
  9.5 8.8 %collective-permute-done.1 = f32[32,16,128]{2,1,0:T(8,128)S(1)} collective-permute-done((f32[32,16,128]{2,1,0:T(8,128)S(1)}, f32[32,16,128]{2,1,0:T(8,128)S(1)}, u32[]{:S(2)}, u32[]{:S(2)}) %collective-permute-start.1) | collective-permute-done | bytes 262176 | tf_op jit(solution)/shard_map/ppermute | solution.py:454
  20.0 10.0 %all-to-all-start = ((f32[16,128,128]{2,1,0:T(8,128)}), f32[16,128,128]{2,1,0:T(8,128)S(1)}, u32[]{:S(2)}, u32[]{:S(2)}) async-start(f32[16,128,128]{2,1,0:T(8,128)} %spread_a.1), calls=%async_computation | async-start | bytes 2097152 | tf_op jit(solution)/shard_map/all_to_all | solution.py:477
  30.0 2.5 %select_select_fusion.1 = (f32[8,2,64,128]{3,2,1,0:T(8,128)S(1)}, f32[8,2,64,128]{3,2,1,0:T(8,128)S(1)}, f32[8,2,64,128]{3,2,1,0:T(8,128)S(1)}, f32[8,2,64,128]{3,2,1,0:T(8,128)S(1)}) fusion(pred[2]{0:T(512)(128)(4,1)S(1)} %iota_compare_fusion.1, pred[8]{0:T(512)(128)(4,1)S(1)} %iota_compare_fusion, s32[64]{0:T(128)S(1)} %iota_multiply_fusion, ...), kind=kLoop, calls=%fused_computation.10 | loop fusion | flops 4456448 | bytes 2097450 | tf_op jit(solution)/shard_map/jit(_where)/select_n | solution.py:60
  34.8 23.2 %all-to-all-done = f32[16,128,128]{2,1,0:T(8,128)S(1)} async-done(((f32[16,128,128]{2,1,0:T(8,128)}), f32[16,128,128]{2,1,0:T(8,128)S(1)}, u32[]{:S(2)}, u32[]{:S(2)}) %all-to-all-start) | async-done | bytes 1048608 | tf_op jit(solution)/shard_map/all_to_all | solution.py:477
  58.0 4.4 %fft_a.1 = f32[64,32,128]{2,1,0:T(8,128)} custom-call(f32[2048,128]{1,0:T(8,128)S(1)} %bitcast.26, bf16[8,256,512]{2,1,0:T(8,128)(2,1)} %pad_maximum_fusion.1.w_hbm.refs_8_), custom_call_target="tpu_custom_call" | custom-call | tf_op jit(solution)/shard_map/fft_a/pallas_call | solution.py:198
  62.4 6.1 %all-to-all-start.1 = ((f32[64,32,128]{2,1,0:T(8,128)}), f32[64,32,128]{2,1,0:T(8,128)S(1)}, u32[]{:S(2)}, u32[]{:S(2)}) async-start(f32[64,32,128]{2,1,0:T(8,128)} %fft_a.1), calls=%async_computation.1 | async-start | bytes 2097152 | tf_op jit(solution)/shard_map/all_to_all | solution.py:485
  76.5 2.4 %collective-permute-start.7 = (f32[32,8,128]{2,1,0:T(8,128)S(1)}, f32[32,8,128]{2,1,0:T(8,128)S(1)}, u32[]{:S(2)}, u32[]{:S(2)}) collective-permute-start(f32[32,8,128]{2,1,0:T(8,128)S(1)} %get-tuple-element.50), channel_id=1, source_target_pairs={{0,40},{4,44},{8,48},{12,52},{16,56},{20,60},{24,0},{28,4},{32,8},... | collective-permute-start | bytes 393224 | tf_op jit(solution)/shard_map/ppermute | solution.py:442
  78.9 17.8 %collective-permute-done.3 = f32[32,8,128]{2,1,0:T(8,128)S(1)} collective-permute-done((f32[32,8,128]{2,1,0:T(8,128)S(1)}, f32[32,8,128]{2,1,0:T(8,128)S(1)}, u32[]{:S(2)}, u32[]{:S(2)}) %collective-permute-start.3) | collective-permute-done | bytes 131104 | tf_op jit(solution)/shard_map/ppermute | solution.py:442
  98.9 2.8 %collective-permute-done.4 = f32[32,8,128]{2,1,0:T(8,128)S(1)} collective-permute-done((f32[32,8,128]{2,1,0:T(8,128)S(1)}, f32[32,8,128]{2,1,0:T(8,128)S(1)}, u32[]{:S(2)}, u32[]{:S(2)}) %collective-permute-start.4) | collective-permute-done | bytes 131104 | tf_op jit(solution)/shard_map/ppermute | solution.py:442
  104.1 8.8 %collective-permute-done.5 = f32[32,8,128]{2,1,0:T(8,128)S(1)} collective-permute-done((f32[32,8,128]{2,1,0:T(8,128)S(1)}, f32[32,8,128]{2,1,0:T(8,128)S(1)}, u32[]{:S(2)}, u32[]{:S(2)}) %collective-permute-start.5) | collective-permute-done | bytes 131104 | tf_op jit(solution)/shard_map/ppermute | solution.py:442
  112.9 4.9 %collective-permute-done.6 = f32[32,8,128]{2,1,0:T(8,128)S(1)} collective-permute-done((f32[32,8,128]{2,1,0:T(8,128)S(1)}, f32[32,8,128]{2,1,0:T(8,128)S(1)}, u32[]{:S(2)}, u32[]{:S(2)}) %collective-permute-start.6) | collective-permute-done | bytes 131104 | tf_op jit(solution)/shard_map/ppermute | solution.py:442
  118.7 2.5 %collective-permute-start.10 = (f32[256,128]{1,0:T(8,128)S(1)}, f32[256,128]{1,0:T(8,128)S(1)}, u32[]{:S(2)}, u32[]{:S(2)}) collective-permute-start(f32[256,128]{1,0:T(8,128)S(1)} %get-tuple-element.54), channel_id=1, source_target_pairs={{0,4},{4,0},{8,12},{12,8},{16,20},{20,16},{24,28},{28,24},{32,36},... | collective-permute-start | bytes 393224 | tf_op jit(solution)/shard_map/ppermute | solution.py:465
  122.1 3.2 %collective-permute-start.13 = (f32[256,128]{1,0:T(8,128)S(1)}, f32[256,128]{1,0:T(8,128)S(1)}, u32[]{:S(2)}, u32[]{:S(2)}) collective-permute-start(f32[256,128]{1,0:T(8,128)S(1)} %get-tuple-element.57), channel_id=1, source_target_pairs={{0,128},{4,132},{8,136},{12,140},{16,144},{20,148},{24,152},{28,15... | collective-permute-start | bytes 393224 | tf_op jit(solution)/shard_map/ppermute | solution.py:465
  129.2 6.9 %collective-permute-done.12.refs_3_ = f32[256,128]{1,0:T(8,128)S(1)} collective-permute-done((f32[256,128]{1,0:T(8,128)S(1)}, f32[256,128]{1,0:T(8,128)S(1)}, u32[]{:S(2)}, u32[]{:S(2)}) %collective-permute-start.12) | collective-permute-done | bytes 131104 | tf_op jit(solution)/shard_map/ppermute | solution.py:465
  136.7 4.1 %fft_p.1 = (f32[256,128]{1,0:T(8,128)S(1)}, f32[256,128]{1,0:T(8,128)S(1)}, f32[256,128]{1,0:T(8,128)S(1)}, f32[256,128]{1,0:T(8,128)S(1)}, f32[256,128]{1,0:T(8...) custom-call(s32[3]{0:T(128)S(1)} %pad_add_fusion.pos_ref, ...), custom_call_target="tpu_custom_call" | custom-call | tf_op jit(solution)/shard_map/fft_p/pallas_call | solution.py:233
  145.0 3.3 %collective-permute-start.20 = (f32[256,128]{1,0:T(8,128)S(1)}, f32[256,128]{1,0:T(8,128)S(1)}, u32[]{:S(2)}, u32[]{:S(2)}) collective-permute-start(f32[256,128]{1,0:T(8,128)S(1)} %get-tuple-element.65), channel_id=1, source_target_pairs={{0,32},{4,36},{8,40},{12,44},{16,48},{20,52},{24,56},{28,60},{32,0... | collective-permute-start | bytes 393224 | tf_op jit(solution)/shard_map/ppermute | solution.py:442
  150.9 4.6 %collective-permute-start.23 = (f32[256,128]{1,0:T(8,128)S(1)}, f32[256,128]{1,0:T(8,128)S(1)}, u32[]{:S(2)}, u32[]{:S(2)}) collective-permute-start(f32[256,128]{1,0:T(8,128)S(1)} %get-tuple-element.68), channel_id=1, source_target_pairs={{0,56},{4,60},{8,0},{12,4},{16,8},{20,12},{24,16},{28,20},{32,24},... | collective-permute-start | bytes 393224 | tf_op jit(solution)/shard_map/ppermute | solution.py:442
  155.5 9.8 %collective-permute-done.19.refs_3_ = f32[256,128]{1,0:T(8,128)S(1)} collective-permute-done((f32[256,128]{1,0:T(8,128)S(1)}, f32[256,128]{1,0:T(8,128)S(1)}, u32[]{:S(2)}, u32[]{:S(2)}) %collective-permute-start.19) | collective-permute-done | bytes 131104 | tf_op jit(solution)/shard_map/ppermute | solution.py:442
  165.3 4.1 %collective-permute-done.22.refs_6_ = f32[256,128]{1,0:T(8,128)S(1)} collective-permute-done((f32[256,128]{1,0:T(8,128)S(1)}, f32[256,128]{1,0:T(8,128)S(1)}, u32[]{:S(2)}, u32[]{:S(2)}) %collective-permute-start.22) | collective-permute-done | bytes 131104 | tf_op jit(solution)/shard_map/ppermute | solution.py:442
  169.4 2.7 %collective-permute-done.23.refs_7_ = f32[256,128]{1,0:T(8,128)S(1)} collective-permute-done((f32[256,128]{1,0:T(8,128)S(1)}, f32[256,128]{1,0:T(8,128)S(1)}, u32[]{:S(2)}, u32[]{:S(2)}) %collective-permute-start.23) | collective-permute-done | bytes 131104 | tf_op jit(solution)/shard_map/ppermute | solution.py:442
  179.2 2.6 %collective-permute-start.29 = (f32[256,128]{1,0:T(8,128)S(1)}, f32[256,128]{1,0:T(8,128)S(1)}, u32[]{:S(2)}, u32[]{:S(2)}) collective-permute-start(f32[256,128]{1,0:T(8,128)S(1)} %get-tuple-element.75), channel_id=1, source_target_pairs={{0,192},{4,196},{8,200},{12,204},{16,208},{20,212},{24,216},{28,22... | collective-permute-start | bytes 393224 | tf_op jit(solution)/shard_map/ppermute | solution.py:465
  183.5 2.8 %collective-permute-done.27.refs_4_ = f32[256,128]{1,0:T(8,128)S(1)} collective-permute-done((f32[256,128]{1,0:T(8,128)S(1)}, f32[256,128]{1,0:T(8,128)S(1)}, u32[]{:S(2)}, u32[]{:S(2)}) %collective-permute-start.27) | collective-permute-done | bytes 131104 | tf_op jit(solution)/shard_map/ppermute | solution.py:465
  186.3 3.1 %collective-permute-done.28.refs_5_ = f32[256,128]{1,0:T(8,128)S(1)} collective-permute-done((f32[256,128]{1,0:T(8,128)S(1)}, f32[256,128]{1,0:T(8,128)S(1)}, u32[]{:S(2)}, u32[]{:S(2)}) %collective-permute-start.28) | collective-permute-done | bytes 131104 | tf_op jit(solution)/shard_map/ppermute | solution.py:465
  (60 shorter events, 49.1 us)
Async XLA Ops:
  4.5 13.8 %collective-permute-start.1 = (f32[32,16,128]{2,1,0:T(8,128)S(1)}, f32[32,16,128]{2,1,0:T(8,128)S(1)}, u32[]{:S(2)}, u32[]{:S(2)}) collective-permute-start(f32[32,16,128]{2,1,0:T(8,128)S(1)} %get-tuple-element.43), channel_id=1, source_target_pairs={{0,128},{4,132},{8,136},{12,140},{16,144},{20,148},{24,152},{28,15... | collective-permute-start | bytes 786440 | tf_op jit(solution)/shard_map/ppermute | solution.py:454
  7.0 11.3 %collective-permute-start.2 = (f32[32,16,128]{2,1,0:T(8,128)S(1)}, f32[32,16,128]{2,1,0:T(8,128)S(1)}, u32[]{:S(2)}, u32[]{:S(2)}) collective-permute-start(f32[32,16,128]{2,1,0:T(8,128)S(1)} %get-tuple-element.44), channel_id=1, source_target_pairs={{0,192},{4,196},{8,200},{12,204},{16,208},{20,212},{24,216},{28,22... | collective-permute-start | bytes 786440 | tf_op jit(solution)/shard_map/ppermute | solution.py:454
  20.0 38.0 %all-to-all-start = ((f32[16,128,128]{2,1,0:T(8,128)}), f32[16,128,128]{2,1,0:T(8,128)S(1)}, u32[]{:S(2)}, u32[]{:S(2)}) async-start(f32[16,128,128]{2,1,0:T(8,128)} %spread_a.1), calls=%async_computation | async-start | bytes 2097152 | tf_op jit(solution)/shard_map/all_to_all | solution.py:477
  62.4 119.9 %all-to-all-start.1 = ((f32[64,32,128]{2,1,0:T(8,128)}), f32[64,32,128]{2,1,0:T(8,128)S(1)}, u32[]{:S(2)}, u32[]{:S(2)}) async-start(f32[64,32,128]{2,1,0:T(8,128)} %fft_a.1), calls=%async_computation.1 | async-start | bytes 2097152 | tf_op jit(solution)/shard_map/all_to_all | solution.py:485
  68.5 28.2 %collective-permute-start.3 = (f32[32,8,128]{2,1,0:T(8,128)S(1)}, f32[32,8,128]{2,1,0:T(8,128)S(1)}, u32[]{:S(2)}, u32[]{:S(2)}) collective-permute-start(f32[32,8,128]{2,1,0:T(8,128)S(1)} %get-tuple-element.46), channel_id=1, source_target_pairs={{0,8},{4,12},{8,16},{12,20},{16,24},{20,28},{24,32},{28,36},{32,40... | collective-permute-start | bytes 393224 | tf_op jit(solution)/shard_map/ppermute | solution.py:442
  69.9 31.8 %collective-permute-start.4 = (f32[32,8,128]{2,1,0:T(8,128)S(1)}, f32[32,8,128]{2,1,0:T(8,128)S(1)}, u32[]{:S(2)}, u32[]{:S(2)}) collective-permute-start(f32[32,8,128]{2,1,0:T(8,128)S(1)} %get-tuple-element.47), channel_id=1, source_target_pairs={{0,16},{4,20},{8,24},{12,28},{16,32},{20,36},{24,40},{28,44},{32,4... | collective-permute-start | bytes 393224 | tf_op jit(solution)/shard_map/ppermute | solution.py:442
  72.0 40.9 %collective-permute-start.5 = (f32[32,8,128]{2,1,0:T(8,128)S(1)}, f32[32,8,128]{2,1,0:T(8,128)S(1)}, u32[]{:S(2)}, u32[]{:S(2)}) collective-permute-start(f32[32,8,128]{2,1,0:T(8,128)S(1)} %get-tuple-element.48), channel_id=1, source_target_pairs={{0,24},{4,28},{8,32},{12,36},{16,40},{20,44},{24,48},{28,52},{32,5... | collective-permute-start | bytes 393224 | tf_op jit(solution)/shard_map/ppermute | solution.py:442
  74.4 43.4 %collective-permute-start.6 = (f32[32,8,128]{2,1,0:T(8,128)S(1)}, f32[32,8,128]{2,1,0:T(8,128)S(1)}, u32[]{:S(2)}, u32[]{:S(2)}) collective-permute-start(f32[32,8,128]{2,1,0:T(8,128)S(1)} %get-tuple-element.49), channel_id=1, source_target_pairs={{0,32},{4,36},{8,40},{12,44},{16,48},{20,52},{24,56},{28,60},{32,0... | collective-permute-start | bytes 393224 | tf_op jit(solution)/shard_map/ppermute | solution.py:442
  76.5 41.3 %collective-permute-start.7 = (f32[32,8,128]{2,1,0:T(8,128)S(1)}, f32[32,8,128]{2,1,0:T(8,128)S(1)}, u32[]{:S(2)}, u32[]{:S(2)}) collective-permute-start(f32[32,8,128]{2,1,0:T(8,128)S(1)} %get-tuple-element.50), channel_id=1, source_target_pairs={{0,40},{4,44},{8,48},{12,52},{16,56},{20,60},{24,0},{28,4},{32,8},... | collective-permute-start | bytes 393224 | tf_op jit(solution)/shard_map/ppermute | solution.py:442
  96.7 21.1 %collective-permute-start.8 = (f32[32,8,128]{2,1,0:T(8,128)S(1)}, f32[32,8,128]{2,1,0:T(8,128)S(1)}, u32[]{:S(2)}, u32[]{:S(2)}) collective-permute-start(f32[32,8,128]{2,1,0:T(8,128)S(1)} %get-tuple-element.51), channel_id=1, source_target_pairs={{0,48},{4,52},{8,56},{12,60},{16,0},{20,4},{24,8},{28,12},{32,16},... | collective-permute-start | bytes 393224 | tf_op jit(solution)/shard_map/ppermute | solution.py:442
  101.8 16.0 %collective-permute-start.9 = (f32[32,8,128]{2,1,0:T(8,128)S(1)}, f32[32,8,128]{2,1,0:T(8,128)S(1)}, u32[]{:S(2)}, u32[]{:S(2)}) collective-permute-start(f32[32,8,128]{2,1,0:T(8,128)S(1)} %get-tuple-element.52), channel_id=1, source_target_pairs={{0,56},{4,60},{8,0},{12,4},{16,8},{20,12},{24,16},{28,20},{32,24},... | collective-permute-start | bytes 393224 | tf_op jit(solution)/shard_map/ppermute | solution.py:442
  121.2 14.9 %collective-permute-start.12 = (f32[256,128]{1,0:T(8,128)S(1)}, f32[256,128]{1,0:T(8,128)S(1)}, u32[]{:S(2)}, u32[]{:S(2)}) collective-permute-start(f32[256,128]{1,0:T(8,128)S(1)} %get-tuple-element.56), channel_id=1, source_target_pairs={{0,68},{4,64},{8,76},{12,72},{16,84},{20,80},{24,92},{28,88},{32,1... | collective-permute-start | bytes 393224 | tf_op jit(solution)/shard_map/ppermute | solution.py:465
  122.1 13.9 %collective-permute-start.13 = (f32[256,128]{1,0:T(8,128)S(1)}, f32[256,128]{1,0:T(8,128)S(1)}, u32[]{:S(2)}, u32[]{:S(2)}) collective-permute-start(f32[256,128]{1,0:T(8,128)S(1)} %get-tuple-element.57), channel_id=1, source_target_pairs={{0,128},{4,132},{8,136},{12,140},{16,144},{20,148},{24,152},{28,15... | collective-permute-start | bytes 393224 | tf_op jit(solution)/shard_map/ppermute | solution.py:465
  125.3 10.8 %collective-permute-start.14 = (f32[256,128]{1,0:T(8,128)S(1)}, f32[256,128]{1,0:T(8,128)S(1)}, u32[]{:S(2)}, u32[]{:S(2)}) collective-permute-start(f32[256,128]{1,0:T(8,128)S(1)} %get-tuple-element.58), channel_id=1, source_target_pairs={{0,132},{4,128},{8,140},{12,136},{16,148},{20,144},{24,156},{28,15... | collective-permute-start | bytes 393224 | tf_op jit(solution)/shard_map/ppermute | solution.py:465
  125.4 10.7 %collective-permute-start.15 = (f32[256,128]{1,0:T(8,128)S(1)}, f32[256,128]{1,0:T(8,128)S(1)}, u32[]{:S(2)}, u32[]{:S(2)}) collective-permute-start(f32[256,128]{1,0:T(8,128)S(1)} %get-tuple-element.59), channel_id=1, source_target_pairs={{0,192},{4,196},{8,200},{12,204},{16,208},{20,212},{24,216},{28,22... | collective-permute-start | bytes 393224 | tf_op jit(solution)/shard_map/ppermute | solution.py:465
  140.9 10.0 %collective-permute-start.18 = (f32[256,128]{1,0:T(8,128)S(1)}, f32[256,128]{1,0:T(8,128)S(1)}, u32[]{:S(2)}, u32[]{:S(2)}) collective-permute-start(f32[256,128]{1,0:T(8,128)S(1)} %get-tuple-element.63), channel_id=1, source_target_pairs={{0,16},{4,20},{8,24},{12,28},{16,32},{20,36},{24,40},{28,44},{32,4... | collective-permute-start | bytes 393224 | tf_op jit(solution)/shard_map/ppermute | solution.py:442
  142.8 22.5 %collective-permute-start.19 = (f32[256,128]{1,0:T(8,128)S(1)}, f32[256,128]{1,0:T(8,128)S(1)}, u32[]{:S(2)}, u32[]{:S(2)}) collective-permute-start(f32[256,128]{1,0:T(8,128)S(1)} %get-tuple-element.64), channel_id=1, source_target_pairs={{0,24},{4,28},{8,32},{12,36},{16,40},{20,44},{24,48},{28,52},{32,5... | collective-permute-start | bytes 393224 | tf_op jit(solution)/shard_map/ppermute | solution.py:442
  145.0 20.3 %collective-permute-start.20 = (f32[256,128]{1,0:T(8,128)S(1)}, f32[256,128]{1,0:T(8,128)S(1)}, u32[]{:S(2)}, u32[]{:S(2)}) collective-permute-start(f32[256,128]{1,0:T(8,128)S(1)} %get-tuple-element.65), channel_id=1, source_target_pairs={{0,32},{4,36},{8,40},{12,44},{16,48},{20,52},{24,56},{28,60},{32,0... | collective-permute-start | bytes 393224 | tf_op jit(solution)/shard_map/ppermute | solution.py:442
  148.2 17.0 %collective-permute-start.21 = (f32[256,128]{1,0:T(8,128)S(1)}, f32[256,128]{1,0:T(8,128)S(1)}, u32[]{:S(2)}, u32[]{:S(2)}) collective-permute-start(f32[256,128]{1,0:T(8,128)S(1)} %get-tuple-element.66), channel_id=1, source_target_pairs={{0,40},{4,44},{8,48},{12,52},{16,56},{20,60},{24,0},{28,4},{32,8},... | collective-permute-start | bytes 393224 | tf_op jit(solution)/shard_map/ppermute | solution.py:442
  150.4 19.0 %collective-permute-start.22 = (f32[256,128]{1,0:T(8,128)S(1)}, f32[256,128]{1,0:T(8,128)S(1)}, u32[]{:S(2)}, u32[]{:S(2)}) collective-permute-start(f32[256,128]{1,0:T(8,128)S(1)} %get-tuple-element.67), channel_id=1, source_target_pairs={{0,48},{4,52},{8,56},{12,60},{16,0},{20,4},{24,8},{28,12},{32,16},... | collective-permute-start | bytes 393224 | tf_op jit(solution)/shard_map/ppermute | solution.py:442
  150.9 21.2 %collective-permute-start.23 = (f32[256,128]{1,0:T(8,128)S(1)}, f32[256,128]{1,0:T(8,128)S(1)}, u32[]{:S(2)}, u32[]{:S(2)}) collective-permute-start(f32[256,128]{1,0:T(8,128)S(1)} %get-tuple-element.68), channel_id=1, source_target_pairs={{0,56},{4,60},{8,0},{12,4},{16,8},{20,12},{24,16},{28,20},{32,24},... | collective-permute-start | bytes 393224 | tf_op jit(solution)/shard_map/ppermute | solution.py:442
  175.9 10.3 %collective-permute-start.27 = (f32[256,128]{1,0:T(8,128)S(1)}, f32[256,128]{1,0:T(8,128)S(1)}, u32[]{:S(2)}, u32[]{:S(2)}) collective-permute-start(f32[256,128]{1,0:T(8,128)S(1)} %get-tuple-element.73), channel_id=1, source_target_pairs={{0,128},{4,132},{8,136},{12,140},{16,144},{20,148},{24,152},{28,15... | collective-permute-start | bytes 393224 | tf_op jit(solution)/shard_map/ppermute | solution.py:465
  177.5 11.8 %collective-permute-start.28 = (f32[256,128]{1,0:T(8,128)S(1)}, f32[256,128]{1,0:T(8,128)S(1)}, u32[]{:S(2)}, u32[]{:S(2)}) collective-permute-start(f32[256,128]{1,0:T(8,128)S(1)} %get-tuple-element.74), channel_id=1, source_target_pairs={{0,132},{4,128},{8,140},{12,136},{16,148},{20,144},{24,156},{28,15... | collective-permute-start | bytes 393224 | tf_op jit(solution)/shard_map/ppermute | solution.py:465
  179.2 10.1 %collective-permute-start.29 = (f32[256,128]{1,0:T(8,128)S(1)}, f32[256,128]{1,0:T(8,128)S(1)}, u32[]{:S(2)}, u32[]{:S(2)}) collective-permute-start(f32[256,128]{1,0:T(8,128)S(1)} %get-tuple-element.75), channel_id=1, source_target_pairs={{0,192},{4,196},{8,200},{12,204},{16,208},{20,212},{24,216},{28,22... | collective-permute-start | bytes 393224 | tf_op jit(solution)/shard_map/ppermute | solution.py:465
  (9 other events, 71.3 us)

commit v8 on v7

--- a/solution.py
+++ b/solution.py
@@ -67,7 +67,7 @@
     full = full.reshape(HALF, 4 * PEERS, 2 * INNER)
     high = lax.reduce_precision(full, 8, 7)
     high, low = high.astype(jnp.bfloat16), (full - high).astype(jnp.bfloat16)
-    return jnp.concatenate([high, low], axis=-1)
+    return high, low
 
 
 def fft_real16(x):
@@ -121,7 +121,7 @@
     return ((n2 % 4) * 4 + base // LON) * INNER + (n2 // 4) * LON + base % LON
 
 
-def fft_core(x_ref, w_ref, y_ref, r_ref, row_of, loads):
+def fft_core(x_ref, wh_ref, wl_ref, y_ref, r_ref, row_of):
     def butterfly(i, carry):
         base = pl.multiple_of(i * 8, 8)
         x = [x_ref[pl.ds(pl.multiple_of(row_of(n2, base), 8), 8), :] for n2 in range(RADIX)]
@@ -132,16 +132,12 @@
                 y_ref[k, pl.ds(j * INNER + base, 8), :] = part
         return carry
 
-    lax.fori_loop(0, INNER // 8, butterfly, 0)
+    lax.fori_loop(0, INNER // 8, butterfly, 0, unroll=4)
     for k in range(HALF):
         yh, yl = split_bf16(y_ref[k])
-        loads[k].wait()
-        high, both = w_ref[k, :, : 2 * INNER], w_ref[k]
-        r = jnp.dot(
-            jnp.concatenate([high, both], axis=1),
-            jnp.concatenate([yl, yh, yh], axis=0),
-            preferred_element_type=jnp.float32,
-        )
+        two = jnp.dot(wh_ref[k], jnp.concatenate([yh, yl], axis=1), preferred_element_type=jnp.float32)
+        r = two[:, :LANES] + two[:, LANES:]
+        r = r + jnp.dot(wl_ref[k], yh, preferred_element_type=jnp.float32)
         mirror = HALF if k == 0 else RADIX - k
         for q, row in enumerate((k, RADIX + k, mirror, RADIX + mirror)):
             r_ref[pl.ds(row * PAD_R, PEERS), :] = r[q * PEERS : (q + 1) * PEERS]
@@ -163,16 +159,7 @@
         copy.wait()
 
 
-def load_matrices(w_hbm, w_ref, sem):
-    loads = [pltpu.make_async_copy(w_hbm.at[k], w_ref.at[k], sem.at[k]) for k in range(HALF)]
-    for load in loads:
-        load.start()
-    return loads
-
-
 FFT_SCRATCH = [
-    pltpu.VMEM((HALF, 4 * PEERS, 4 * INNER), jnp.bfloat16),
-    pltpu.SemaphoreType.DMA((HALF,)),
     pltpu.VMEM((HALF, 2 * INNER, LANES), jnp.float32),
     pltpu.VMEM((KEPT * PAD_R, LANES), jnp.float32),
 ]
@@ -182,9 +169,8 @@
     return r_ref[pl.ds(eight * 8 * PAD_R + k1, 8, stride=PAD_R), :]
 
 
-def fft_a_kernel(x_ref, w_hbm, o_ref, w_ref, w_sem, y_ref, r_ref, buf_ref, sem):
-    loads = load_matrices(w_hbm, w_ref, w_sem)
-    fft_core(x_ref, w_ref, y_ref, r_ref, grouped_row, loads)
+def fft_a_kernel(x_ref, wh_ref, wl_ref, o_ref, y_ref, r_ref, buf_ref, sem):
+    fft_core(x_ref, wh_ref, wl_ref, y_ref, r_ref, grouped_row)
 
     def peer(k1, carry):
         for eight in range(KEPT // 8):
@@ -194,68 +180,80 @@
     send_pieces(peer, PEERS, buf_ref, o_ref, sem)
 
 
-def fft_a(gathered, w):
+def fft_a(gathered, wh, wl):
     return pl.pallas_call(
         fft_a_kernel,
-        in_specs=[VMEM, HBM],
+        in_specs=[VMEM] * 3,
         out_specs=HBM,
         out_shape=pltpu.HBM((PEERS, KEPT, LANES), jnp.float32),
         scratch_shapes=FFT_SCRATCH
         + [pltpu.VMEM((PEERS, KEPT, LANES), jnp.float32), pltpu.SemaphoreType.DMA((PIECES,))],
         compiler_params=PARAMS,
         name="fft_a",
-    )(gathered, pltpu.with_memory_space_constraint(w, pltpu.HBM))
+    )(gathered, wh, wl)
 
 
 def fft_p_kernel(pos_ref, *refs):
-    g_refs, w_hbm, o_refs = refs[:8], refs[8], refs[9:17]
-    x_ref, w_ref, w_sem, y_ref, r_ref = refs[17:]
-    loads = load_matrices(w_hbm, w_ref, w_sem)
+    g_refs, (wh_ref, wl_ref) = refs[:8], refs[8:10]
+    stay_ref, far_ref, send_refs, swap_ref = refs[10], refs[11], refs[12:15], refs[15]
+    x_ref, y_ref, r_ref = refs[16:]
     x, z, c = pos_ref[0], pos_ref[1], pos_ref[2]
     for dx in range(NX):
         for dc in range(NC):
-            start = ((x + NX - dx) % NX) * (NLON // NX) + ((c + dc) % NC) * LON
-            for zz in range(NZ):
-                row = pl.multiple_of(start + zz * NC * LON, LON)
-                x_ref[pl.ds(row, LON), :] = g_refs[dx * NC + dc][zz * LON : (zz + 1) * LON, :]
-    fft_core(x_ref, w_ref, y_ref, r_ref, natural_row, loads)
-    for dz in range(NZ):
-        target = (z + dz) % NZ
+            xx, core = (x + NX - dx) % NX, (c + dc) % NC
+            for piece in range(NZ):
+                zz, cc = piece_source(z, core, piece)
+                row = pl.multiple_of(xx * (NLON // NX) + zz * (NC * LON) + cc * LON, LON)
+                x_ref[pl.ds(row, LON), :] = g_refs[dx * NC + dc][piece * LON : (piece + 1) * LON, :]
+    fft_core(x_ref, wh_ref, wl_ref, y_ref, r_ref, natural_row)
+    way = 1 - 2 * c
+    places = [(stay_ref, 0, z), (far_ref, 0, z + NZ // 2)]
+    places += [(swap_ref, i, z - way * k) for i, k in enumerate(STEPS)]
+    places += [(send_refs[i], 0, z + way * k) for i, k in enumerate(STEPS)]
+    for ref, slot, place in places:
+        target = (place + NZ) % NZ
         for xx in range(NX):
             for cc in range(NC):
-                k1 = xx * NZ * NC + target * NC + cc
                 for eight in range(KEPT // 8):
-                    row = (xx * NC + cc) * KEPT + eight * 8
-                    o_refs[dz][row : row + 8, :] = mode_rows(r_ref, k1, eight)
-
-
-def fft_p(pos, blocks, w):
+                    row = slot * BLOCK + (xx * NC + cc) * KEPT + eight * 8
+                    ref[row : row + 8, :] = mode_rows(r_ref, xx * NZ * NC + target * NC + cc, eight)
+
+
+def fft_p(pos, blocks, wh, wl):
     return pl.pallas_call(
         fft_p_kernel,
-        in_specs=[SMEM] + [VMEM] * 8 + [HBM],
-        out_specs=[VMEM] * NZ,
-        out_shape=[vmem(NX * NC * KEPT, LANES)] * NZ,
+        in_specs=[SMEM] + [VMEM] * 10,
+        out_specs=[VMEM] * 6,
+        out_shape=[vmem(BLOCK, LANES)] * 2 + [vmem(2 * BLOCK, LANES)] * 3 + [vmem(3 * BLOCK, LANES)],
         scratch_shapes=[pltpu.VMEM((NLON, LANES), jnp.float32)] + FFT_SCRATCH,
         compiler_params=PARAMS,
         name="fft_p",
-    )(pos, *blocks, pltpu.with_memory_space_constraint(w, pltpu.HBM))
+    )(pos, *blocks, wh, wl)
 
 
 GROUP = NZ * NC
 
 
+STEPS = (1, 2, 3)
+
+
 def split_kernel(pos_ref, s_ref, *refs):
-    o_refs, sem = refs[: NZ + NX], refs[NZ + NX]
-    x, z = pos_ref[0], pos_ref[1]
+    stay_ref, far_ref, send_refs, swap_ref = refs[0], refs[1], refs[2:5], refs[5]
+    part_refs, sem = refs[6 : 6 + NX], refs[6 + NX]
+    x, z, c = pos_ref[0], pos_ref[1], pos_ref[2]
+    way = 1 - 2 * c
+    places = [(stay_ref, 0, z), (far_ref, 0, z + NZ // 2)]
+    places += [(swap_ref, i, z - way * k) for i, k in enumerate(STEPS)]
+    places += [(send_refs[i], 0, z + way * k) for i, k in enumerate(STEPS)]
     copies = []
-    for dz in range(NZ):
-        field = pl.multiple_of(((z + dz) % NZ) * 8, 8)
+    for ref, slot, target in places:
+        field = pl.multiple_of(((target + NZ) % NZ) * 8, 8)
         source = s_ref.at[:, pl.ds(field, 8), pl.ds(0, LANES)]
-        copies.append(pltpu.make_async_copy(source, o_refs[dz], sem.at[dz]))
+        copies.append(pltpu.make_async_copy(source, ref.at[pl.ds(slot * LON, LON)], sem.at[len(copies)]))
     for dx in range(NX):
         field = pl.multiple_of(((x + dx) % NX) * GROUP, GROUP)
         source = s_ref.at[:, pl.ds(field, GROUP), pl.ds(LANES, LANES)]
-        copies.append(pltpu.make_async_copy(source, o_refs[NZ + dx], sem.at[NZ + dx]))
+        copies.append(pltpu.make_async_copy(source, part_refs[dx], sem.at[len(copies)]))
     for copy in copies:
         copy.start()
     for copy in copies:
@@ -266,30 +264,77 @@
     out = pl.pallas_call(
         split_kernel,
         in_specs=[SMEM, HBM],
-        out_specs=[VMEM] * (NZ + NX),
-        out_shape=[vmem(LON, 8, LANES)] * NZ + [vmem(LON, GROUP, LANES)] * NX,
+        out_specs=[VMEM] * (6 + NX),
+        out_shape=[vmem(LON, 8, LANES)] * 2
+        + [vmem(2 * LON, 8, LANES)] * 3
+        + [vmem(3 * LON, 8, LANES)]
+        + [vmem(LON, GROUP, LANES)] * NX,
         scratch_shapes=[pltpu.SemaphoreType.DMA((NZ + NX,))],
         compiler_params=PARAMS,
         name="split",
     )(pos, pltpu.with_memory_space_constraint(state, pltpu.HBM))
-    return out[:NZ], out[NZ:]
+    return [v.reshape(-1, LANES) for v in out[:6]], out[6:]
+
+
+BLOCK = 256
+
+
+def merge_kernel(swap_ref, *refs):
+    o_refs, sem = refs[3:6], refs[6]
+    copies = [
+        pltpu.make_async_copy(swap_ref.at[pl.ds(i * BLOCK, BLOCK)], o_refs[i].at[pl.ds(BLOCK, BLOCK)], sem.at[i])
+        for i in range(3)
+    ]
+    for copy in copies:
+        copy.start()
+    for copy in copies:
+        copy.wait()
+
+
+def merge(swap, sends):
+    anywhere = pl.BlockSpec(memory_space=pl.ANY)
+    return pl.pallas_call(
+        merge_kernel,
+        in_specs=[anywhere] * 4,
+        out_specs=[anywhere] * 3,
+        out_shape=[f32(2 * BLOCK, LANES)] * 3,
+        scratch_shapes=[pltpu.SemaphoreType.DMA((3,))],
+        input_output_aliases={1: 0, 2: 1, 3: 2},
+        compiler_params=PARAMS,
+        name="merge",
+    )(swap, *sends)
+
+
+def piece_of(refs, piece):
+    if piece < 2:
+        return refs[piece], 0
+    return refs[1 + piece // 2], (piece % 2) * BLOCK
+
+
+def piece_source(z, core, piece):
+    if piece == 0:
+        return z, core
+    if piece == 1:
+        return (z + NZ // 2) % NZ, core
+    way = 1 - 2 * core
+    return (z - way * (piece // 2) + NZ) % NZ, core if piece % 2 == 0 else 1 - core
 
 
 def spread_x_kernel(pos_ref, *refs):
-    b_refs, o_refs = refs[:NZ], refs[NZ:]
-    x, z, c = pos_ref[0], pos_ref[1], pos_ref[2]
+    b_refs, o_refs = refs[:5], refs[5:]
+    x, c = pos_ref[0], pos_ref[2]
     for dx in range(NX):
         for dc in range(NC):
             field = ((x + dx) % NX) * NC + (c + dc) % NC
-            for dz in range(NZ):
-                row = pl.multiple_of(((z + NZ - dz) % NZ) * LON, LON)
-                o_refs[dx * NC + dc][pl.ds(row, LON), :] = b_refs[dz][pl.ds(field, LON, stride=8), :]
+            for piece in range(NZ):
+                ref, row = piece_of(b_refs, piece)
+                o_refs[dx * NC + dc][piece * LON : (piece + 1) * LON, :] = ref[pl.ds(row + field, LON, stride=8), :]
 
 
 def spread_x(pos, blocks):
     return pl.pallas_call(
         spread_x_kernel,
-        in_specs=[SMEM] + [VMEM] * NZ,
+        in_specs=[SMEM] + [VMEM] * 5,
         out_specs=[VMEM] * (NX * NC),
         out_shape=[vmem(NZ * LON, LANES)] * (NX * NC),
         compiler_params=PARAMS,
@@ -298,20 +343,21 @@
 
 
 def spread_out_kernel(pos_ref, *refs):
-    h_refs, o_refs = refs[:NZ], refs[NZ:]
-    x, z, c = pos_ref[0], pos_ref[1], pos_ref[2]
+    h_refs, o_refs = refs[:5], refs[5:]
+    x, c = pos_ref[0], pos_ref[2]
     for dx in range(NX):
         for dc in range(NC):
-            source = pl.multiple_of((((x + dx) % NX) * NC + (c + dc) % NC) * KEPT, KEPT)
-            for dz in range(NZ):
-                row = pl.multiple_of(((z + NZ - dz) % NZ) * KEPT, KEPT)
-                o_refs[dx * NC + dc][pl.ds(row, KEPT), :] = h_refs[dz][pl.ds(source, KEPT), :]
+            source = (((x + dx) % NX) * NC + (c + dc) % NC) * KEPT
+            for piece in range(NZ):
+                ref, row = piece_of(h_refs, piece)
+                start = pl.multiple_of(source + row, KEPT)
+                o_refs[dx * NC + dc][piece * KEPT : (piece + 1) * KEPT, :] = ref[pl.ds(start, KEPT), :]
 
 
 def spread_out(pos, blocks):
     return pl.pallas_call(
         spread_out_kernel,
-        in_specs=[SMEM] + [VMEM] * NZ,
+        in_specs=[SMEM] + [VMEM] * 5,
         out_specs=[VMEM] * (NX * NC),
         out_shape=[vmem(NZ * KEPT, LANES)] * (NX * NC),
         compiler_params=PARAMS,
@@ -379,13 +425,14 @@
     del prior_ref
     q_refs, o_ref = refs[:8], refs[8]
     x_ref, buf_ref, sem = refs[9:]
-    x, c = pos_ref[0], pos_ref[2]
+    x, z, c = pos_ref[0], pos_ref[1], pos_ref[2]
     for dx in range(NX):
         for dc in range(NC):
-            base = ((x + NX - dx) % NX) * NC + (c + dc) % NC
-            for zz in range(NZ):
-                row = pl.multiple_of((base + zz * NX * NC) * PAD_K, 8)
-                x_ref[pl.ds(row, KEPT), :] = q_refs[dx * NC + dc][zz * KEPT : (zz + 1) * KEPT, :]
+            xx, core = (x + NX - dx) % NX, (c + dc) % NC
+            for piece in range(NZ):
+                zz, cc = piece_source(z, core, piece)
+                row = pl.multiple_of((zz * NX * NC + xx * NC + cc) * PAD_K, 8)
+                x_ref[pl.ds(row, KEPT), :] = q_refs[dx * NC + dc][piece * KEPT : (piece + 1) * KEPT, :]
     store_half(x_ref, buf_ref, o_ref, sem, 0)
 
 
@@ -432,15 +479,27 @@
     ]
 
 
-Z_ORDER = (1, 7, 4, 3, 5, 2, 6)
+def two_ways(k):
+    return [
+        pair
+        for c in range(NC)
+        for pair in shifts(0, k if c == 0 else NZ - k, 0)
+        if pair[0] % NC == c
+    ]
+
+
+Z_ORDER = (1, 3, 2)
 
 
 def exchange_z(blocks):
-    out = [None] * NZ
-    out[0] = blocks[0]
-    for dz in Z_ORDER:
-        out[dz] = lax.ppermute(blocks[dz], "lon", shifts(0, dz, 0))
-    return out
+    stay, far, sends, swap = blocks[0], blocks[1], blocks[2:5], blocks[5]
+    swap = lax.ppermute(swap, "lon", shifts(0, 0, 1))
+    far = lax.ppermute(far, "lon", shifts(0, NZ // 2, 0))
+    sends = merge(swap, sends)
+    got = [None] * 3
+    for k in Z_ORDER:
+        got[k - 1] = lax.ppermute(sends[k - 1], "lon", two_ways(k))
+    return [stay, far, *got]
 
 
 AX_ORDER = (2, 1, 3)
@@ -469,7 +528,7 @@
 def local(state):
     device = lax.axis_index("lon")
     pos = jnp.stack([device // (NZ * NC), (device // NC) % NZ, device % NC]).astype(jnp.int32)
-    w = twiddle_matrices(1.0 / math.sqrt(NLON))
+    wh, wl = twiddle_matrices(1.0 / math.sqrt(NLON))
     pieces, parts = split(pos, state)
     pieces = exchange_z(pieces)
     parts = exchange_x(parts)
@@ -477,11 +536,11 @@
     gathered = lax.all_to_all(
         sent, "lon", split_axis=0, concat_axis=0, axis_index_groups=GROUPS, tiled=True
     )
-    pieces = spread_x(pos, [b.reshape(LON * 8, LANES) for b in pieces])
+    pieces = spread_x(pos, pieces)
     pieces = exchange_xc(pieces)
-    pieces = fft_p(pos, pieces, w)
+    pieces = fft_p(pos, pieces, wh, wl)
     pieces = exchange_z(pieces)
-    spectrum = fft_a(gathered.reshape(NLON, LANES), w)
+    spectrum = fft_a(gathered.reshape(NLON, LANES), wh, wl)
     shares = lax.all_to_all(spectrum, "lon", split_axis=0, concat_axis=0, tiled=True)
     pieces = spread_out(pos, pieces)
     pieces = exchange_xc(pieces)

time: 194 us -> 189 us (0.974)
  waiting for transfers between devices: 101 us -> 91.8 us
  starting transfers between devices: 70.3 us -> 75.6 us
  local copies, waits for them, and re-layouts: 0 us -> 4.67 us
  Pallas kernels: 16.8 us -> 13.3 us
    ppermute x14, starting transfers between devices: 20 us -> 36.7 us  [exchange_xc(): lax.ppermute(blocks[dx * NC + dc], 'lon', shifts(dx, 0, dc))]
    ppermute x14 -> x10, starting transfers between devices: 28.5 us -> 17.2 us  [the longest x6 10.3 us: exchange_z(): got[k - 1] = lax.ppermute(sends[k - 1], 'lon', two_ways(k))]
    ppermute x14 -> x10, waiting for transfers between devices: 52.1 us -> 41.4 us  [the longest x2 28.1 us: exchange_z(): far = lax.ppermute(far, 'lon', shifts(0, NZ // 2, 0))]
    unnamed x0 -> x12, local copies, waits for them, and re-layouts: none -> 4.67 us
    pallas_call x5 -> x7, Pallas kernels: 12.3 us -> 8.83 us  [the longest x1 2.31 us: split(): pl.pallas_call(split_kernel, in_specs=[SMEM, HBM], out_specs=[VMEM] * (6...]
  transfers between devices with their start and end apart: 33 -> 29, of which waited for: 16 -> 16; matrix products, arithmetic and copies ran while one was open for 2% -> 2% of each run, Pallas kernels for 3% -> 3%
where the time goes in v8:
time: 189 us
  waiting for transfers between devices  91.8 us (49%)
  starting transfers between devices  75.6 us (40%)
  Pallas kernels  13.3 us (7%)
  local copies, waits for them, and re-layouts  4.67 us (2%)
  other arithmetic  3.31 us (2%)
    ppermute x14, starting transfers between devices, exchange_xc(): lax.ppermute(blocks[dx * NC + dc], 'lon', shifts(dx, 0, dc))  36.7 us
    ppermute x2, waiting for transfers between devices, exchange_z(): far = lax.ppermute(far, 'lon', shifts(0, NZ // 2, 0))  28.1 us
    all_to_all x1, waiting for transfers between devices, local(): lax.all_to_all(sent, 'lon', split_axis=0, concat_axis=0, axis_index_group...  24.7 us
    ppermute x14, waiting for transfers between devices, exchange_xc(): lax.ppermute(blocks[dx * NC + dc], 'lon', shifts(dx, 0, dc))  15.5 us
    ppermute x6, starting transfers between devices, exchange_z(): got[k - 1] = lax.ppermute(sends[k - 1], 'lon', two_ways(k))  10.3 us
    ppermute x3, waiting for transfers between devices, exchange_x(): out[dx] = lax.ppermute(blocks[dx], 'lon', shifts(dx, 0, 0))  10.2 us
    all_to_all x1, starting transfers between devices, local(): lax.all_to_all(sent, 'lon', split_axis=0, concat_axis=0, axis_index_group...  10 us
    ppermute x6, waiting for transfers between devices, exchange_z(): got[k - 1] = lax.ppermute(sends[k - 1], 'lon', two_ways(k))  10 us
  transfers between devices with their start and end apart: 29, of which 16 were waited for; matrix products, arithmetic and copies ran while one was open for 2% of the time, Pallas kernels for 3%

profile of v8, /device:TPU:1, one launch (start us, length us, event | category | flops | bytes accessed | tf_op | source)
XLA Modules:
  0.0 189.0 jit_solution(8193265922857682654)
XLA Ops:
  0.1 2.3 %split.1 = (f32[32,8,128]{2,1,0:T(8,128)S(1)}, f32[32,8,128]{2,1,0:T(8,128)S(1)}, f32[64,8,128]{2,1,0:T(8,128)S(1)}, f32[64,8,128]{2,1,0:T(8,128)S(1)}, f32[64,8...) custom-call(s32[3]{0:T(128)S(1)} %pad_add_fusion.pos_ref, ...), custom_call_target="tpu_custom_call" | custom-call | tf_op jit(solution)/shard_map/split/pallas_call | solution.py:264
  7.2 2.5 %collective-permute-start.1 = (f32[32,16,128]{2,1,0:T(8,128)S(1)}, f32[32,16,128]{2,1,0:T(8,128)S(1)}, u32[]{:S(2)}, u32[]{:S(2)}) collective-permute-start(f32[32,16,128]{2,1,0:T(8,128)S(1)} %get-tuple-element.45), channel_id=1, source_target_pairs={{0,128},{4,132},{8,136},{12,140},{16,144},{20,148},{24,152},{28,15... | collective-permute-start | bytes 786440 | tf_op jit(solution)/shard_map/ppermute | solution.py:513
  12.2 8.8 %collective-permute-done.1 = f32[32,16,128]{2,1,0:T(8,128)S(1)} collective-permute-done((f32[32,16,128]{2,1,0:T(8,128)S(1)}, f32[32,16,128]{2,1,0:T(8,128)S(1)}, u32[]{:S(2)}, u32[]{:S(2)}) %collective-permute-start.1) | collective-permute-done | bytes 262176 | tf_op jit(solution)/shard_map/ppermute | solution.py:513
  22.6 10.0 %all-to-all-start = ((f32[16,128,128]{2,1,0:T(8,128)}), f32[16,128,128]{2,1,0:T(8,128)S(1)}, u32[]{:S(2)}, u32[]{:S(2)}) async-start(f32[16,128,128]{2,1,0:T(8,128)} %spread_a.1), calls=%async_computation | async-start | bytes 2097152 | tf_op jit(solution)/shard_map/all_to_all | solution.py:536
  32.7 2.5 %select_select_fusion.1 = (f32[8,2,64,128]{3,2,1,0:T(8,128)S(1)}, f32[8,2,64,128]{3,2,1,0:T(8,128)S(1)}, f32[8,2,64,128]{3,2,1,0:T(8,128)S(1)}, f32[8,2,64,128]{3,2,1,0:T(8,128)S(1)}) fusion(pred[2]{0:T(512)(128)(4,1)S(1)} %iota_compare_fusion.1, pred[8]{0:T(512)(128)(4,1)S(1)} %iota_compare_fusion, s32[64]{0:T(128)S(1)} %iota_multiply_fusion, ...), kind=kLoop, calls=%fused_computation.9 | loop fusion | flops 4456448 | bytes 2097450 | tf_op jit(solution)/shard_map/jit(_where)/select_n | solution.py:60
  36.0 24.7 %all-to-all-done = f32[16,128,128]{2,1,0:T(8,128)S(1)} async-done(((f32[16,128,128]{2,1,0:T(8,128)}), f32[16,128,128]{2,1,0:T(8,128)S(1)}, u32[]{:S(2)}, u32[]{:S(2)}) %all-to-all-start) | async-done | bytes 1048608 | tf_op jit(solution)/shard_map/all_to_all | solution.py:536
  60.7 2.1 %fft_a.1 = f32[64,32,128]{2,1,0:T(8,128)} custom-call(f32[2048,128]{1,0:T(8,128)S(1)} %bitcast.24, bf16[8,256,256]{2,1,0:T(8,128)(2,1)S(1)} %get-tuple-element.82.wh_ref.refs_8_, bf16[8,256,256]{2,1,0:T(8,128)(2,1)S(1)} %get-tuple-element.81.wl_ref.refs_9_), custom_call_target="tpu_custom_call" | custom-call | tf_op jit(solution)/shard_map/fft_a/pallas_call | solution.py:184
  62.8 6.1 %all-to-all-start.1 = ((f32[64,32,128]{2,1,0:T(8,128)}), f32[64,32,128]{2,1,0:T(8,128)S(1)}, u32[]{:S(2)}, u32[]{:S(2)}) async-start(f32[64,32,128]{2,1,0:T(8,128)} %fft_a.1), calls=%async_computation.1 | async-start | bytes 2097152 | tf_op jit(solution)/shard_map/all_to_all | solution.py:544
  73.4 2.6 %collective-permute-start.5 = (f32[512,128]{1,0:T(8,128)S(1)}, f32[512,128]{1,0:T(8,128)S(1)}, u32[]{:S(2)}, u32[]{:S(2)}) collective-permute-start(f32[512,128]{1,0:T(8,128)S(1)} %get-tuple-element.53), channel_id=1, source_target_pairs={{0,8},{8,16},{16,24},{24,32},{32,40},{40,48},{48,56},{56,0},{64,72... | collective-permute-start | bytes 786440 | tf_op jit(solution)/shard_map/ppermute | solution.py:501
  79.3 3.3 %collective-permute-start.3 = (f32[256,128]{1,0:T(8,128)}, f32[256,128]{1,0:T(8,128)S(1)}, u32[]{:S(2)}, u32[]{:S(2)}) collective-permute-start(f32[256,128]{1,0:T(8,128)} %bitcast.34), channel_id=1, source_target_pairs={{0,32},{4,36},{8,40},{12,44},{16,48},{20,52},{24,56},{28,60},{32,0... | collective-permute-start | bytes 393224 | tf_op jit(solution)/shard_map/ppermute | solution.py:497
  82.6 18.9 %collective-permute-done.3.refs_1_ = f32[256,128]{1,0:T(8,128)S(1)} collective-permute-done((f32[256,128]{1,0:T(8,128)}, f32[256,128]{1,0:T(8,128)S(1)}, u32[]{:S(2)}, u32[]{:S(2)}) %collective-permute-start.3) | collective-permute-done | bytes 131104 | tf_op jit(solution)/shard_map/ppermute | solution.py:497
  101.4 3.9 %collective-permute-done.6.refs_3_ = f32[512,128]{1,0:T(8,128)S(1)} collective-permute-done((f32[512,128]{1,0:T(8,128)S(1)}, f32[512,128]{1,0:T(8,128)S(1)}, u32[]{:S(2)}, u32[]{:S(2)}) %collective-permute-start.6) | collective-permute-done | bytes 262176 | tf_op jit(solution)/shard_map/ppermute | solution.py:501
  105.3 5.6 %collective-permute-done.7.refs_4_ = f32[512,128]{1,0:T(8,128)S(1)} collective-permute-done((f32[512,128]{1,0:T(8,128)S(1)}, f32[512,128]{1,0:T(8,128)S(1)}, u32[]{:S(2)}, u32[]{:S(2)}) %collective-permute-start.7) | collective-permute-done | bytes 262176 | tf_op jit(solution)/shard_map/ppermute | solution.py:501
  111.8 10.0 %collective-permute-start.8 = (f32[256,128]{1,0:T(8,128)S(1)}, f32[256,128]{1,0:T(8,128)S(1)}, u32[]{:S(2)}, u32[]{:S(2)}) collective-permute-start(f32[256,128]{1,0:T(8,128)S(1)} %get-tuple-element.57), channel_id=1, source_target_pairs={{0,4},{4,0},{8,12},{12,8},{16,20},{20,16},{24,28},{28,24},{32,36},... | collective-permute-start | bytes 393224 | tf_op jit(solution)/shard_map/ppermute | solution.py:524
  122.9 3.0 %collective-permute-start.11 = (f32[256,128]{1,0:T(8,128)S(1)}, f32[256,128]{1,0:T(8,128)S(1)}, u32[]{:S(2)}, u32[]{:S(2)}) collective-permute-start(f32[256,128]{1,0:T(8,128)S(1)} %get-tuple-element.60), channel_id=1, source_target_pairs={{0,128},{4,132},{8,136},{12,140},{16,144},{20,148},{24,152},{28,15... | collective-permute-start | bytes 393224 | tf_op jit(solution)/shard_map/ppermute | solution.py:524
  129.7 6.9 %collective-permute-done.10.refs_3_ = f32[256,128]{1,0:T(8,128)S(1)} collective-permute-done((f32[256,128]{1,0:T(8,128)S(1)}, f32[256,128]{1,0:T(8,128)S(1)}, u32[]{:S(2)}, u32[]{:S(2)}) %collective-permute-start.10) | collective-permute-done | bytes 131104 | tf_op jit(solution)/shard_map/ppermute | solution.py:524
  143.4 2.6 %collective-permute-start.19 = (f32[512,128]{1,0:T(8,128)S(1)}, f32[512,128]{1,0:T(8,128)S(1)}, u32[]{:S(2)}, u32[]{:S(2)}) collective-permute-start(f32[512,128]{1,0:T(8,128)S(1)} %get-tuple-element.72), channel_id=1, source_target_pairs={{0,24},{8,32},{16,40},{24,48},{32,56},{40,0},{48,8},{56,16},{64,88... | collective-permute-start | bytes 786440 | tf_op jit(solution)/shard_map/ppermute | solution.py:501
  146.1 2.9 %collective-permute-start.15 = (f32[256,128]{1,0:T(8,128)S(1)}, f32[256,128]{1,0:T(8,128)S(1)}, u32[]{:S(2)}, u32[]{:S(2)}) collective-permute-start(f32[256,128]{1,0:T(8,128)S(1)} %get-tuple-element.65), channel_id=1, source_target_pairs={{0,32},{4,36},{8,40},{12,44},{16,48},{20,52},{24,56},{28,60},{32,0... | collective-permute-start | bytes 393224 | tf_op jit(solution)/shard_map/ppermute | solution.py:497
  149.0 9.3 %collective-permute-done.15.refs_1_ = f32[256,128]{1,0:T(8,128)S(1)} collective-permute-done((f32[256,128]{1,0:T(8,128)S(1)}, f32[256,128]{1,0:T(8,128)S(1)}, u32[]{:S(2)}, u32[]{:S(2)}) %collective-permute-start.15) | collective-permute-done | bytes 131104 | tf_op jit(solution)/shard_map/ppermute | solution.py:497
  159.3 9.4 %collective-permute-start.20 = (f32[256,128]{1,0:T(8,128)S(1)}, f32[256,128]{1,0:T(8,128)S(1)}, u32[]{:S(2)}, u32[]{:S(2)}) collective-permute-start(f32[256,128]{1,0:T(8,128)S(1)} %get-tuple-element.74), channel_id=1, source_target_pairs={{0,4},{4,0},{8,12},{12,8},{16,20},{20,16},{24,28},{28,24},{32,36},... | collective-permute-start | bytes 393224 | tf_op jit(solution)/shard_map/ppermute | solution.py:524
  168.8 2.6 %collective-permute-start.21 = (f32[256,128]{1,0:T(8,128)S(1)}, f32[256,128]{1,0:T(8,128)S(1)}, u32[]{:S(2)}, u32[]{:S(2)}) collective-permute-start(f32[256,128]{1,0:T(8,128)S(1)} %get-tuple-element.75), channel_id=1, source_target_pairs={{0,64},{4,68},{8,72},{12,76},{16,80},{20,84},{24,88},{28,92},{32,9... | collective-permute-start | bytes 393224 | tf_op jit(solution)/shard_map/ppermute | solution.py:524
  174.9 2.7 %collective-permute-start.25 = (f32[256,128]{1,0:T(8,128)S(1)}, f32[256,128]{1,0:T(8,128)S(1)}, u32[]{:S(2)}, u32[]{:S(2)}) collective-permute-start(f32[256,128]{1,0:T(8,128)S(1)} %get-tuple-element.79), channel_id=1, source_target_pairs={{0,192},{4,196},{8,200},{12,204},{16,208},{20,212},{24,216},{28,22... | collective-permute-start | bytes 393224 | tf_op jit(solution)/shard_map/ppermute | solution.py:524
  179.3 2.8 %collective-permute-done.23.refs_4_ = f32[256,128]{1,0:T(8,128)S(1)} collective-permute-done((f32[256,128]{1,0:T(8,128)S(1)}, f32[256,128]{1,0:T(8,128)S(1)}, u32[]{:S(2)}, u32[]{:S(2)}) %collective-permute-start.23) | collective-permute-done | bytes 131104 | tf_op jit(solution)/shard_map/ppermute | solution.py:524
  182.1 3.1 %collective-permute-done.24.refs_5_ = f32[256,128]{1,0:T(8,128)S(1)} collective-permute-done((f32[256,128]{1,0:T(8,128)S(1)}, f32[256,128]{1,0:T(8,128)S(1)}, u32[]{:S(2)}, u32[]{:S(2)}) %collective-permute-start.24) | collective-permute-done | bytes 131104 | tf_op jit(solution)/shard_map/ppermute | solution.py:524
  (65 shorter events, 40.0 us)
Async XLA Ops:
  7.2 13.8 %collective-permute-start.1 = (f32[32,16,128]{2,1,0:T(8,128)S(1)}, f32[32,16,128]{2,1,0:T(8,128)S(1)}, u32[]{:S(2)}, u32[]{:S(2)}) collective-permute-start(f32[32,16,128]{2,1,0:T(8,128)S(1)} %get-tuple-element.45), channel_id=1, source_target_pairs={{0,128},{4,132},{8,136},{12,140},{16,144},{20,148},{24,152},{28,15... | collective-permute-start | bytes 786440 | tf_op jit(solution)/shard_map/ppermute | solution.py:513
  9.7 11.3 %collective-permute-start.2 = (f32[32,16,128]{2,1,0:T(8,128)S(1)}, f32[32,16,128]{2,1,0:T(8,128)S(1)}, u32[]{:S(2)}, u32[]{:S(2)}) collective-permute-start(f32[32,16,128]{2,1,0:T(8,128)S(1)} %get-tuple-element.46), channel_id=1, source_target_pairs={{0,192},{4,196},{8,200},{12,204},{16,208},{20,212},{24,216},{28,22... | collective-permute-start | bytes 786440 | tf_op jit(solution)/shard_map/ppermute | solution.py:513
  22.6 38.0 %all-to-all-start = ((f32[16,128,128]{2,1,0:T(8,128)}), f32[16,128,128]{2,1,0:T(8,128)S(1)}, u32[]{:S(2)}, u32[]{:S(2)}) async-start(f32[16,128,128]{2,1,0:T(8,128)} %spread_a.1), calls=%async_computation | async-start | bytes 2097152 | tf_op jit(solution)/shard_map/all_to_all | solution.py:536
  62.8 115.3 %all-to-all-start.1 = ((f32[64,32,128]{2,1,0:T(8,128)}), f32[64,32,128]{2,1,0:T(8,128)S(1)}, u32[]{:S(2)}, u32[]{:S(2)}) async-start(f32[64,32,128]{2,1,0:T(8,128)} %fft_a.1), calls=%async_computation.1 | async-start | bytes 2097152 | tf_op jit(solution)/shard_map/all_to_all | solution.py:544
  73.4 28.0 %collective-permute-start.5 = (f32[512,128]{1,0:T(8,128)S(1)}, f32[512,128]{1,0:T(8,128)S(1)}, u32[]{:S(2)}, u32[]{:S(2)}) collective-permute-start(f32[512,128]{1,0:T(8,128)S(1)} %get-tuple-element.53), channel_id=1, source_target_pairs={{0,8},{8,16},{16,24},{24,32},{32,40},{40,48},{48,56},{56,0},{64,72... | collective-permute-start | bytes 786440 | tf_op jit(solution)/shard_map/ppermute | solution.py:501
  76.0 29.4 %collective-permute-start.6 = (f32[512,128]{1,0:T(8,128)S(1)}, f32[512,128]{1,0:T(8,128)S(1)}, u32[]{:S(2)}, u32[]{:S(2)}) collective-permute-start(f32[512,128]{1,0:T(8,128)S(1)} %get-tuple-element.54), channel_id=1, source_target_pairs={{0,16},{8,24},{16,32},{24,40},{32,48},{40,56},{48,0},{56,8},{64,80... | collective-permute-start | bytes 786440 | tf_op jit(solution)/shard_map/ppermute | solution.py:501
  78.1 32.9 %collective-permute-start.7 = (f32[512,128]{1,0:T(8,128)S(1)}, f32[512,128]{1,0:T(8,128)S(1)}, u32[]{:S(2)}, u32[]{:S(2)}) collective-permute-start(f32[512,128]{1,0:T(8,128)S(1)} %get-tuple-element.55), channel_id=1, source_target_pairs={{0,24},{8,32},{16,40},{24,48},{32,56},{40,0},{48,8},{56,16},{64,88... | collective-permute-start | bytes 786440 | tf_op jit(solution)/shard_map/ppermute | solution.py:501
  79.3 22.2 %collective-permute-start.3 = (f32[256,128]{1,0:T(8,128)}, f32[256,128]{1,0:T(8,128)S(1)}, u32[]{:S(2)}, u32[]{:S(2)}) collective-permute-start(f32[256,128]{1,0:T(8,128)} %bitcast.34), channel_id=1, source_target_pairs={{0,32},{4,36},{8,40},{12,44},{16,48},{20,52},{24,56},{28,60},{32,0... | collective-permute-start | bytes 393224 | tf_op jit(solution)/shard_map/ppermute | solution.py:497
  111.8 14.4 %collective-permute-start.8 = (f32[256,128]{1,0:T(8,128)S(1)}, f32[256,128]{1,0:T(8,128)S(1)}, u32[]{:S(2)}, u32[]{:S(2)}) collective-permute-start(f32[256,128]{1,0:T(8,128)S(1)} %get-tuple-element.57), channel_id=1, source_target_pairs={{0,4},{4,0},{8,12},{12,8},{16,20},{20,16},{24,28},{28,24},{32,36},... | collective-permute-start | bytes 393224 | tf_op jit(solution)/shard_map/ppermute | solution.py:524
  121.8 14.9 %collective-permute-start.10 = (f32[256,128]{1,0:T(8,128)S(1)}, f32[256,128]{1,0:T(8,128)S(1)}, u32[]{:S(2)}, u32[]{:S(2)}) collective-permute-start(f32[256,128]{1,0:T(8,128)S(1)} %get-tuple-element.59), channel_id=1, source_target_pairs={{0,68},{4,64},{8,76},{12,72},{16,84},{20,80},{24,92},{28,88},{32,1... | collective-permute-start | bytes 393224 | tf_op jit(solution)/shard_map/ppermute | solution.py:524
  122.9 13.8 %collective-permute-start.11 = (f32[256,128]{1,0:T(8,128)S(1)}, f32[256,128]{1,0:T(8,128)S(1)}, u32[]{:S(2)}, u32[]{:S(2)}) collective-permute-start(f32[256,128]{1,0:T(8,128)S(1)} %get-tuple-element.60), channel_id=1, source_target_pairs={{0,128},{4,132},{8,136},{12,140},{16,144},{20,148},{24,152},{28,15... | collective-permute-start | bytes 393224 | tf_op jit(solution)/shard_map/ppermute | solution.py:524
  125.9 10.8 %collective-permute-start.12 = (f32[256,128]{1,0:T(8,128)S(1)}, f32[256,128]{1,0:T(8,128)S(1)}, u32[]{:S(2)}, u32[]{:S(2)}) collective-permute-start(f32[256,128]{1,0:T(8,128)S(1)} %get-tuple-element.61), channel_id=1, source_target_pairs={{0,132},{4,128},{8,140},{12,136},{16,148},{20,144},{24,156},{28,15... | collective-permute-start | bytes 393224 | tf_op jit(solution)/shard_map/ppermute | solution.py:524
  126.2 10.5 %collective-permute-start.13 = (f32[256,128]{1,0:T(8,128)S(1)}, f32[256,128]{1,0:T(8,128)S(1)}, u32[]{:S(2)}, u32[]{:S(2)}) collective-permute-start(f32[256,128]{1,0:T(8,128)S(1)} %get-tuple-element.62), channel_id=1, source_target_pairs={{0,192},{4,196},{8,200},{12,204},{16,208},{20,212},{24,216},{28,22... | collective-permute-start | bytes 393224 | tf_op jit(solution)/shard_map/ppermute | solution.py:524
  128.0 9.3 %collective-permute-start.14 = (f32[256,128]{1,0:T(8,128)S(1)}, f32[256,128]{1,0:T(8,128)S(1)}, u32[]{:S(2)}, u32[]{:S(2)}) collective-permute-start(f32[256,128]{1,0:T(8,128)S(1)} %get-tuple-element.63), channel_id=1, source_target_pairs={{0,196},{4,192},{8,204},{12,200},{16,212},{20,208},{24,220},{28,21... | collective-permute-start | bytes 393224 | tf_op jit(solution)/shard_map/ppermute | solution.py:524
  141.6 16.7 %collective-permute-start.17 = (f32[512,128]{1,0:T(8,128)S(1)}, f32[512,128]{1,0:T(8,128)S(1)}, u32[]{:S(2)}, u32[]{:S(2)}) collective-permute-start(f32[512,128]{1,0:T(8,128)S(1)} %get-tuple-element.70), channel_id=1, source_target_pairs={{0,8},{8,16},{16,24},{24,32},{32,40},{40,48},{48,56},{56,0},{64,72... | collective-permute-start | bytes 786440 | tf_op jit(solution)/shard_map/ppermute | solution.py:501
  141.8 16.5 %collective-permute-start.18 = (f32[512,128]{1,0:T(8,128)S(1)}, f32[512,128]{1,0:T(8,128)S(1)}, u32[]{:S(2)}, u32[]{:S(2)}) collective-permute-start(f32[512,128]{1,0:T(8,128)S(1)} %get-tuple-element.71), channel_id=1, source_target_pairs={{0,16},{8,24},{16,32},{24,40},{32,48},{40,56},{48,0},{56,8},{64,80... | collective-permute-start | bytes 786440 | tf_op jit(solution)/shard_map/ppermute | solution.py:501
  143.4 15.3 %collective-permute-start.19 = (f32[512,128]{1,0:T(8,128)S(1)}, f32[512,128]{1,0:T(8,128)S(1)}, u32[]{:S(2)}, u32[]{:S(2)}) collective-permute-start(f32[512,128]{1,0:T(8,128)S(1)} %get-tuple-element.72), channel_id=1, source_target_pairs={{0,24},{8,32},{16,40},{24,48},{32,56},{40,0},{48,8},{56,16},{64,88... | collective-permute-start | bytes 786440 | tf_op jit(solution)/shard_map/ppermute | solution.py:501
  146.1 12.2 %collective-permute-start.15 = (f32[256,128]{1,0:T(8,128)S(1)}, f32[256,128]{1,0:T(8,128)S(1)}, u32[]{:S(2)}, u32[]{:S(2)}) collective-permute-start(f32[256,128]{1,0:T(8,128)S(1)} %get-tuple-element.65), channel_id=1, source_target_pairs={{0,32},{4,36},{8,40},{12,44},{16,48},{20,52},{24,56},{28,60},{32,0... | collective-permute-start | bytes 393224 | tf_op jit(solution)/shard_map/ppermute | solution.py:497
  159.3 15.6 %collective-permute-start.20 = (f32[256,128]{1,0:T(8,128)S(1)}, f32[256,128]{1,0:T(8,128)S(1)}, u32[]{:S(2)}, u32[]{:S(2)}) collective-permute-start(f32[256,128]{1,0:T(8,128)S(1)} %get-tuple-element.74), channel_id=1, source_target_pairs={{0,4},{4,0},{8,12},{12,8},{16,20},{20,16},{24,28},{28,24},{32,36},... | collective-permute-start | bytes 393224 | tf_op jit(solution)/shard_map/ppermute | solution.py:524
  168.8 8.9 %collective-permute-start.21 = (f32[256,128]{1,0:T(8,128)S(1)}, f32[256,128]{1,0:T(8,128)S(1)}, u32[]{:S(2)}, u32[]{:S(2)}) collective-permute-start(f32[256,128]{1,0:T(8,128)S(1)} %get-tuple-element.75), channel_id=1, source_target_pairs={{0,64},{4,68},{8,72},{12,76},{16,80},{20,84},{24,88},{28,92},{32,9... | collective-permute-start | bytes 393224 | tf_op jit(solution)/shard_map/ppermute | solution.py:524
  171.5 10.6 %collective-permute-start.23 = (f32[256,128]{1,0:T(8,128)S(1)}, f32[256,128]{1,0:T(8,128)S(1)}, u32[]{:S(2)}, u32[]{:S(2)}) collective-permute-start(f32[256,128]{1,0:T(8,128)S(1)} %get-tuple-element.77), channel_id=1, source_target_pairs={{0,128},{4,132},{8,136},{12,140},{16,144},{20,148},{24,152},{28,15... | collective-permute-start | bytes 393224 | tf_op jit(solution)/shard_map/ppermute | solution.py:524
  173.0 12.1 %collective-permute-start.24 = (f32[256,128]{1,0:T(8,128)S(1)}, f32[256,128]{1,0:T(8,128)S(1)}, u32[]{:S(2)}, u32[]{:S(2)}) collective-permute-start(f32[256,128]{1,0:T(8,128)S(1)} %get-tuple-element.78), channel_id=1, source_target_pairs={{0,132},{4,128},{8,140},{12,136},{16,148},{20,144},{24,156},{28,15... | collective-permute-start | bytes 393224 | tf_op jit(solution)/shard_map/ppermute | solution.py:524
  174.9 10.2 %collective-permute-start.25 = (f32[256,128]{1,0:T(8,128)S(1)}, f32[256,128]{1,0:T(8,128)S(1)}, u32[]{:S(2)}, u32[]{:S(2)}) collective-permute-start(f32[256,128]{1,0:T(8,128)S(1)} %get-tuple-element.79), channel_id=1, source_target_pairs={{0,192},{4,196},{8,200},{12,204},{16,208},{20,212},{24,216},{28,22... | collective-permute-start | bytes 393224 | tf_op jit(solution)/shard_map/ppermute | solution.py:524
  177.6 9.5 %collective-permute-start.26 = (f32[256,128]{1,0:T(8,128)S(1)}, f32[256,128]{1,0:T(8,128)S(1)}, u32[]{:S(2)}, u32[]{:S(2)}) collective-permute-start(f32[256,128]{1,0:T(8,128)S(1)} %get-tuple-element.80), channel_id=1, source_target_pairs={{0,196},{4,192},{8,204},{12,200},{16,212},{20,208},{24,220},{28,21... | collective-permute-start | bytes 393224 | tf_op jit(solution)/shard_map/ppermute | solution.py:524
  (11 other events, 29.7 us)

commit v9 on v8

--- a/solution.py
+++ b/solution.py
@@ -488,18 +488,19 @@
     ]
 
 
-Z_ORDER = (1, 3, 2)
-
-
-def exchange_z(blocks):
+Z_IN = (1, 3, 4, 2)
+Z_OUT = (4, 3, 1, 2)
+
+
+def exchange_z(blocks, order):
     stay, far, sends, swap = blocks[0], blocks[1], blocks[2:5], blocks[5]
     swap = lax.ppermute(swap, "lon", shifts(0, 0, 1))
-    far = lax.ppermute(far, "lon", shifts(0, NZ // 2, 0))
     sends = merge(swap, sends)
-    got = [None] * 3
-    for k in Z_ORDER:
-        got[k - 1] = lax.ppermute(sends[k - 1], "lon", two_ways(k))
-    return [stay, far, *got]
+    got = {}
+    for k in order:
+        block = far if k == NZ // 2 else sends[k - 1]
+        got[k] = lax.ppermute(block, "lon", two_ways(k))
+    return [stay, got[NZ // 2], *(got[k] for k in STEPS)]
 
 
 AX_ORDER = (2, 1, 3)
@@ -530,7 +531,7 @@
     pos = jnp.stack([device // (NZ * NC), (device // NC) % NZ, device % NC]).astype(jnp.int32)
     wh, wl = twiddle_matrices(1.0 / math.sqrt(NLON))
     pieces, parts = split(pos, state)
-    pieces = exchange_z(pieces)
+    pieces = exchange_z(pieces, Z_IN)
     parts = exchange_x(parts)
     sent = spread_a(pos, [b.reshape(LON * GROUP, LANES) for b in parts])
     gathered = lax.all_to_all(
@@ -539,7 +540,7 @@
     pieces = spread_x(pos, pieces)
     pieces = exchange_xc(pieces)
     pieces = fft_p(pos, pieces, wh, wl)
-    pieces = exchange_z(pieces)
+    pieces = exchange_z(pieces, Z_OUT)
     spectrum = fft_a(gathered.reshape(NLON, LANES), wh, wl)
     shares = lax.all_to_all(spectrum, "lon", split_axis=0, concat_axis=0, tiled=True)
     pieces = spread_out(pos, pieces)

time: 189 us -> 189 us (level)
  no operation moved by 1% of the time
where the time goes in v9:
time: 189 us
  waiting for transfers between devices  91.8 us (49%)
  starting transfers between devices  75.6 us (40%)
  Pallas kernels  13.3 us (7%)
  local copies, waits for them, and re-layouts  4.67 us (2%)
  other arithmetic  3.31 us (2%)
    ppermute x8, waiting for transfers between devices, exchange_z(): got[k] = lax.ppermute(block, 'lon', two_ways(k))  38.1 us
    ppermute x14, starting transfers between devices, exchange_xc(): lax.ppermute(blocks[dx * NC + dc], 'lon', shifts(dx, 0, dc))  36.7 us
    all_to_all x1, waiting for transfers between devices, local(): lax.all_to_all(sent, 'lon', split_axis=0, concat_axis=0, axis_index_group...  24.7 us
    ppermute x8, starting transfers between devices, exchange_z(): got[k] = lax.ppermute(block, 'lon', two_ways(k))  16.6 us
    ppermute x14, waiting for transfers between devices, exchange_xc(): lax.ppermute(blocks[dx * NC + dc], 'lon', shifts(dx, 0, dc))  15.5 us
    ppermute x3, waiting for transfers between devices, exchange_x(): out[dx] = lax.ppermute(blocks[dx], 'lon', shifts(dx, 0, 0))  10.2 us
    all_to_all x1, starting transfers between devices, local(): lax.all_to_all(sent, 'lon', split_axis=0, concat_axis=0, axis_index_group...  10 us
    all_to_all x1, starting transfers between devices, local(): lax.all_to_all(spectrum, 'lon', split_axis=0, concat_axis=0, tiled=True)  6.08 us
  transfers between devices with their start and end apart: 29, of which 16 were waited for; matrix products, arithmetic and copies ran while one was open for 2% of the time, Pallas kernels for 3%

profile of v9, /device:TPU:1, one launch (start us, length us, event | category | flops | bytes accessed | tf_op | source)
XLA Modules:
  0.0 189.0 jit_solution(8193265922857682654)
XLA Ops:
  0.1 2.3 %split.1 = (f32[32,8,128]{2,1,0:T(8,128)S(1)}, f32[32,8,128]{2,1,0:T(8,128)S(1)}, f32[64,8,128]{2,1,0:T(8,128)S(1)}, f32[64,8,128]{2,1,0:T(8,128)S(1)}, f32[64,8...) custom-call(s32[3]{0:T(128)S(1)} %pad_add_fusion.pos_ref, ...), custom_call_target="tpu_custom_call" | custom-call | tf_op jit(solution)/shard_map/split/pallas_call | solution.py:264
  7.2 2.5 %collective-permute-start.1 = (f32[32,16,128]{2,1,0:T(8,128)S(1)}, f32[32,16,128]{2,1,0:T(8,128)S(1)}, u32[]{:S(2)}, u32[]{:S(2)}) collective-permute-start(f32[32,16,128]{2,1,0:T(8,128)S(1)} %get-tuple-element.45), channel_id=1, source_target_pairs={{0,128},{4,132},{8,136},{12,140},{16,144},{20,148},{24,152},{28,15... | collective-permute-start | bytes 786440 | tf_op jit(solution)/shard_map/ppermute | solution.py:514
  12.2 8.8 %collective-permute-done.1 = f32[32,16,128]{2,1,0:T(8,128)S(1)} collective-permute-done((f32[32,16,128]{2,1,0:T(8,128)S(1)}, f32[32,16,128]{2,1,0:T(8,128)S(1)}, u32[]{:S(2)}, u32[]{:S(2)}) %collective-permute-start.1) | collective-permute-done | bytes 262176 | tf_op jit(solution)/shard_map/ppermute | solution.py:514
  22.6 10.0 %all-to-all-start = ((f32[16,128,128]{2,1,0:T(8,128)}), f32[16,128,128]{2,1,0:T(8,128)S(1)}, u32[]{:S(2)}, u32[]{:S(2)}) async-start(f32[16,128,128]{2,1,0:T(8,128)} %spread_a.1), calls=%async_computation | async-start | bytes 2097152 | tf_op jit(solution)/shard_map/all_to_all | solution.py:537
  32.7 2.5 %select_select_fusion.1 = (f32[8,2,64,128]{3,2,1,0:T(8,128)S(1)}, f32[8,2,64,128]{3,2,1,0:T(8,128)S(1)}, f32[8,2,64,128]{3,2,1,0:T(8,128)S(1)}, f32[8,2,64,128]{3,2,1,0:T(8,128)S(1)}) fusion(pred[2]{0:T(512)(128)(4,1)S(1)} %iota_compare_fusion.1, pred[8]{0:T(512)(128)(4,1)S(1)} %iota_compare_fusion, s32[64]{0:T(128)S(1)} %iota_multiply_fusion, ...), kind=kLoop, calls=%fused_computation.9 | loop fusion | flops 4456448 | bytes 2097450 | tf_op jit(solution)/shard_map/jit(_where)/select_n | solution.py:60
  36.0 24.7 %all-to-all-done = f32[16,128,128]{2,1,0:T(8,128)S(1)} async-done(((f32[16,128,128]{2,1,0:T(8,128)}), f32[16,128,128]{2,1,0:T(8,128)S(1)}, u32[]{:S(2)}, u32[]{:S(2)}) %all-to-all-start) | async-done | bytes 1048608 | tf_op jit(solution)/shard_map/all_to_all | solution.py:537
  60.7 2.1 %fft_a.1 = f32[64,32,128]{2,1,0:T(8,128)} custom-call(f32[2048,128]{1,0:T(8,128)S(1)} %bitcast.24, bf16[8,256,256]{2,1,0:T(8,128)(2,1)S(1)} %get-tuple-element.82.wh_ref.refs_8_, bf16[8,256,256]{2,1,0:T(8,128)(2,1)S(1)} %get-tuple-element.81.wl_ref.refs_9_), custom_call_target="tpu_custom_call" | custom-call | tf_op jit(solution)/shard_map/fft_a/pallas_call | solution.py:184
  62.8 6.1 %all-to-all-start.1 = ((f32[64,32,128]{2,1,0:T(8,128)}), f32[64,32,128]{2,1,0:T(8,128)S(1)}, u32[]{:S(2)}, u32[]{:S(2)}) async-start(f32[64,32,128]{2,1,0:T(8,128)} %fft_a.1), calls=%async_computation.1 | async-start | bytes 2097152 | tf_op jit(solution)/shard_map/all_to_all | solution.py:545
  73.4 2.6 %collective-permute-start.5 = (f32[512,128]{1,0:T(8,128)S(1)}, f32[512,128]{1,0:T(8,128)S(1)}, u32[]{:S(2)}, u32[]{:S(2)}) collective-permute-start(f32[512,128]{1,0:T(8,128)S(1)} %get-tuple-element.53), channel_id=1, source_target_pairs={{0,8},{8,16},{16,24},{24,32},{32,40},{40,48},{48,56},{56,0},{64,72... | collective-permute-start | bytes 786440 | tf_op jit(solution)/shard_map/ppermute | solution.py:502
  79.3 3.3 %collective-permute-start.3 = (f32[256,128]{1,0:T(8,128)}, f32[256,128]{1,0:T(8,128)S(1)}, u32[]{:S(2)}, u32[]{:S(2)}) collective-permute-start(f32[256,128]{1,0:T(8,128)} %bitcast.34), channel_id=1, source_target_pairs={{0,32},{8,40},{16,48},{24,56},{32,0},{40,8},{48,16},{56,24},{64,96... | collective-permute-start | bytes 393224 | tf_op jit(solution)/shard_map/ppermute | solution.py:502
  82.6 18.9 %collective-permute-done.3.refs_1_ = f32[256,128]{1,0:T(8,128)S(1)} collective-permute-done((f32[256,128]{1,0:T(8,128)}, f32[256,128]{1,0:T(8,128)S(1)}, u32[]{:S(2)}, u32[]{:S(2)}) %collective-permute-start.3) | collective-permute-done | bytes 131104 | tf_op jit(solution)/shard_map/ppermute | solution.py:502
  101.4 3.9 %collective-permute-done.6.refs_3_ = f32[512,128]{1,0:T(8,128)S(1)} collective-permute-done((f32[512,128]{1,0:T(8,128)S(1)}, f32[512,128]{1,0:T(8,128)S(1)}, u32[]{:S(2)}, u32[]{:S(2)}) %collective-permute-start.6) | collective-permute-done | bytes 262176 | tf_op jit(solution)/shard_map/ppermute | solution.py:502
  105.3 5.6 %collective-permute-done.7.refs_4_ = f32[512,128]{1,0:T(8,128)S(1)} collective-permute-done((f32[512,128]{1,0:T(8,128)S(1)}, f32[512,128]{1,0:T(8,128)S(1)}, u32[]{:S(2)}, u32[]{:S(2)}) %collective-permute-start.7) | collective-permute-done | bytes 262176 | tf_op jit(solution)/shard_map/ppermute | solution.py:502
  111.8 10.0 %collective-permute-start.8 = (f32[256,128]{1,0:T(8,128)S(1)}, f32[256,128]{1,0:T(8,128)S(1)}, u32[]{:S(2)}, u32[]{:S(2)}) collective-permute-start(f32[256,128]{1,0:T(8,128)S(1)} %get-tuple-element.57), channel_id=1, source_target_pairs={{0,4},{4,0},{8,12},{12,8},{16,20},{20,16},{24,28},{28,24},{32,36},... | collective-permute-start | bytes 393224 | tf_op jit(solution)/shard_map/ppermute | solution.py:525
  122.9 3.0 %collective-permute-start.11 = (f32[256,128]{1,0:T(8,128)S(1)}, f32[256,128]{1,0:T(8,128)S(1)}, u32[]{:S(2)}, u32[]{:S(2)}) collective-permute-start(f32[256,128]{1,0:T(8,128)S(1)} %get-tuple-element.60), channel_id=1, source_target_pairs={{0,128},{4,132},{8,136},{12,140},{16,144},{20,148},{24,152},{28,15... | collective-permute-start | bytes 393224 | tf_op jit(solution)/shard_map/ppermute | solution.py:525
  129.7 6.9 %collective-permute-done.10.refs_3_ = f32[256,128]{1,0:T(8,128)S(1)} collective-permute-done((f32[256,128]{1,0:T(8,128)S(1)}, f32[256,128]{1,0:T(8,128)S(1)}, u32[]{:S(2)}, u32[]{:S(2)}) %collective-permute-start.10) | collective-permute-done | bytes 131104 | tf_op jit(solution)/shard_map/ppermute | solution.py:525
  143.4 2.6 %collective-permute-start.19 = (f32[512,128]{1,0:T(8,128)S(1)}, f32[512,128]{1,0:T(8,128)S(1)}, u32[]{:S(2)}, u32[]{:S(2)}) collective-permute-start(f32[512,128]{1,0:T(8,128)S(1)} %get-tuple-element.72), channel_id=1, source_target_pairs={{0,24},{8,32},{16,40},{24,48},{32,56},{40,0},{48,8},{56,16},{64,88... | collective-permute-start | bytes 786440 | tf_op jit(solution)/shard_map/ppermute | solution.py:502
  146.1 2.9 %collective-permute-start.15 = (f32[256,128]{1,0:T(8,128)S(1)}, f32[256,128]{1,0:T(8,128)S(1)}, u32[]{:S(2)}, u32[]{:S(2)}) collective-permute-start(f32[256,128]{1,0:T(8,128)S(1)} %get-tuple-element.65), channel_id=1, source_target_pairs={{0,32},{8,40},{16,48},{24,56},{32,0},{40,8},{48,16},{56,24},{64,96... | collective-permute-start | bytes 393224 | tf_op jit(solution)/shard_map/ppermute | solution.py:502
  149.0 9.3 %collective-permute-done.15.refs_1_ = f32[256,128]{1,0:T(8,128)S(1)} collective-permute-done((f32[256,128]{1,0:T(8,128)S(1)}, f32[256,128]{1,0:T(8,128)S(1)}, u32[]{:S(2)}, u32[]{:S(2)}) %collective-permute-start.15) | collective-permute-done | bytes 131104 | tf_op jit(solution)/shard_map/ppermute | solution.py:502
  159.3 9.4 %collective-permute-start.20 = (f32[256,128]{1,0:T(8,128)S(1)}, f32[256,128]{1,0:T(8,128)S(1)}, u32[]{:S(2)}, u32[]{:S(2)}) collective-permute-start(f32[256,128]{1,0:T(8,128)S(1)} %get-tuple-element.74), channel_id=1, source_target_pairs={{0,4},{4,0},{8,12},{12,8},{16,20},{20,16},{24,28},{28,24},{32,36},... | collective-permute-start | bytes 393224 | tf_op jit(solution)/shard_map/ppermute | solution.py:525
  168.8 2.6 %collective-permute-start.21 = (f32[256,128]{1,0:T(8,128)S(1)}, f32[256,128]{1,0:T(8,128)S(1)}, u32[]{:S(2)}, u32[]{:S(2)}) collective-permute-start(f32[256,128]{1,0:T(8,128)S(1)} %get-tuple-element.75), channel_id=1, source_target_pairs={{0,64},{4,68},{8,72},{12,76},{16,80},{20,84},{24,88},{28,92},{32,9... | collective-permute-start | bytes 393224 | tf_op jit(solution)/shard_map/ppermute | solution.py:525
  174.9 2.7 %collective-permute-start.25 = (f32[256,128]{1,0:T(8,128)S(1)}, f32[256,128]{1,0:T(8,128)S(1)}, u32[]{:S(2)}, u32[]{:S(2)}) collective-permute-start(f32[256,128]{1,0:T(8,128)S(1)} %get-tuple-element.79), channel_id=1, source_target_pairs={{0,192},{4,196},{8,200},{12,204},{16,208},{20,212},{24,216},{28,22... | collective-permute-start | bytes 393224 | tf_op jit(solution)/shard_map/ppermute | solution.py:525
  179.3 2.8 %collective-permute-done.23.refs_4_ = f32[256,128]{1,0:T(8,128)S(1)} collective-permute-done((f32[256,128]{1,0:T(8,128)S(1)}, f32[256,128]{1,0:T(8,128)S(1)}, u32[]{:S(2)}, u32[]{:S(2)}) %collective-permute-start.23) | collective-permute-done | bytes 131104 | tf_op jit(solution)/shard_map/ppermute | solution.py:525
  182.1 3.1 %collective-permute-done.24.refs_5_ = f32[256,128]{1,0:T(8,128)S(1)} collective-permute-done((f32[256,128]{1,0:T(8,128)S(1)}, f32[256,128]{1,0:T(8,128)S(1)}, u32[]{:S(2)}, u32[]{:S(2)}) %collective-permute-start.24) | collective-permute-done | bytes 131104 | tf_op jit(solution)/shard_map/ppermute | solution.py:525
  (65 shorter events, 40.0 us)
Async XLA Ops:
  7.2 13.8 %collective-permute-start.1 = (f32[32,16,128]{2,1,0:T(8,128)S(1)}, f32[32,16,128]{2,1,0:T(8,128)S(1)}, u32[]{:S(2)}, u32[]{:S(2)}) collective-permute-start(f32[32,16,128]{2,1,0:T(8,128)S(1)} %get-tuple-element.45), channel_id=1, source_target_pairs={{0,128},{4,132},{8,136},{12,140},{16,144},{20,148},{24,152},{28,15... | collective-permute-start | bytes 786440 | tf_op jit(solution)/shard_map/ppermute | solution.py:514
  9.7 11.3 %collective-permute-start.2 = (f32[32,16,128]{2,1,0:T(8,128)S(1)}, f32[32,16,128]{2,1,0:T(8,128)S(1)}, u32[]{:S(2)}, u32[]{:S(2)}) collective-permute-start(f32[32,16,128]{2,1,0:T(8,128)S(1)} %get-tuple-element.46), channel_id=1, source_target_pairs={{0,192},{4,196},{8,200},{12,204},{16,208},{20,212},{24,216},{28,22... | collective-permute-start | bytes 786440 | tf_op jit(solution)/shard_map/ppermute | solution.py:514
  22.6 38.0 %all-to-all-start = ((f32[16,128,128]{2,1,0:T(8,128)}), f32[16,128,128]{2,1,0:T(8,128)S(1)}, u32[]{:S(2)}, u32[]{:S(2)}) async-start(f32[16,128,128]{2,1,0:T(8,128)} %spread_a.1), calls=%async_computation | async-start | bytes 2097152 | tf_op jit(solution)/shard_map/all_to_all | solution.py:537
  62.8 115.3 %all-to-all-start.1 = ((f32[64,32,128]{2,1,0:T(8,128)}), f32[64,32,128]{2,1,0:T(8,128)S(1)}, u32[]{:S(2)}, u32[]{:S(2)}) async-start(f32[64,32,128]{2,1,0:T(8,128)} %fft_a.1), calls=%async_computation.1 | async-start | bytes 2097152 | tf_op jit(solution)/shard_map/all_to_all | solution.py:545
  73.4 28.0 %collective-permute-start.5 = (f32[512,128]{1,0:T(8,128)S(1)}, f32[512,128]{1,0:T(8,128)S(1)}, u32[]{:S(2)}, u32[]{:S(2)}) collective-permute-start(f32[512,128]{1,0:T(8,128)S(1)} %get-tuple-element.53), channel_id=1, source_target_pairs={{0,8},{8,16},{16,24},{24,32},{32,40},{40,48},{48,56},{56,0},{64,72... | collective-permute-start | bytes 786440 | tf_op jit(solution)/shard_map/ppermute | solution.py:502
  76.0 29.4 %collective-permute-start.6 = (f32[512,128]{1,0:T(8,128)S(1)}, f32[512,128]{1,0:T(8,128)S(1)}, u32[]{:S(2)}, u32[]{:S(2)}) collective-permute-start(f32[512,128]{1,0:T(8,128)S(1)} %get-tuple-element.54), channel_id=1, source_target_pairs={{0,16},{8,24},{16,32},{24,40},{32,48},{40,56},{48,0},{56,8},{64,80... | collective-permute-start | bytes 786440 | tf_op jit(solution)/shard_map/ppermute | solution.py:502
  78.1 32.9 %collective-permute-start.7 = (f32[512,128]{1,0:T(8,128)S(1)}, f32[512,128]{1,0:T(8,128)S(1)}, u32[]{:S(2)}, u32[]{:S(2)}) collective-permute-start(f32[512,128]{1,0:T(8,128)S(1)} %get-tuple-element.55), channel_id=1, source_target_pairs={{0,24},{8,32},{16,40},{24,48},{32,56},{40,0},{48,8},{56,16},{64,88... | collective-permute-start | bytes 786440 | tf_op jit(solution)/shard_map/ppermute | solution.py:502
  79.3 22.2 %collective-permute-start.3 = (f32[256,128]{1,0:T(8,128)}, f32[256,128]{1,0:T(8,128)S(1)}, u32[]{:S(2)}, u32[]{:S(2)}) collective-permute-start(f32[256,128]{1,0:T(8,128)} %bitcast.34), channel_id=1, source_target_pairs={{0,32},{8,40},{16,48},{24,56},{32,0},{40,8},{48,16},{56,24},{64,96... | collective-permute-start | bytes 393224 | tf_op jit(solution)/shard_map/ppermute | solution.py:502
  111.8 14.4 %collective-permute-start.8 = (f32[256,128]{1,0:T(8,128)S(1)}, f32[256,128]{1,0:T(8,128)S(1)}, u32[]{:S(2)}, u32[]{:S(2)}) collective-permute-start(f32[256,128]{1,0:T(8,128)S(1)} %get-tuple-element.57), channel_id=1, source_target_pairs={{0,4},{4,0},{8,12},{12,8},{16,20},{20,16},{24,28},{28,24},{32,36},... | collective-permute-start | bytes 393224 | tf_op jit(solution)/shard_map/ppermute | solution.py:525
  121.8 14.9 %collective-permute-start.10 = (f32[256,128]{1,0:T(8,128)S(1)}, f32[256,128]{1,0:T(8,128)S(1)}, u32[]{:S(2)}, u32[]{:S(2)}) collective-permute-start(f32[256,128]{1,0:T(8,128)S(1)} %get-tuple-element.59), channel_id=1, source_target_pairs={{0,68},{4,64},{8,76},{12,72},{16,84},{20,80},{24,92},{28,88},{32,1... | collective-permute-start | bytes 393224 | tf_op jit(solution)/shard_map/ppermute | solution.py:525
  122.9 13.8 %collective-permute-start.11 = (f32[256,128]{1,0:T(8,128)S(1)}, f32[256,128]{1,0:T(8,128)S(1)}, u32[]{:S(2)}, u32[]{:S(2)}) collective-permute-start(f32[256,128]{1,0:T(8,128)S(1)} %get-tuple-element.60), channel_id=1, source_target_pairs={{0,128},{4,132},{8,136},{12,140},{16,144},{20,148},{24,152},{28,15... | collective-permute-start | bytes 393224 | tf_op jit(solution)/shard_map/ppermute | solution.py:525
  125.9 10.8 %collective-permute-start.12 = (f32[256,128]{1,0:T(8,128)S(1)}, f32[256,128]{1,0:T(8,128)S(1)}, u32[]{:S(2)}, u32[]{:S(2)}) collective-permute-start(f32[256,128]{1,0:T(8,128)S(1)} %get-tuple-element.61), channel_id=1, source_target_pairs={{0,132},{4,128},{8,140},{12,136},{16,148},{20,144},{24,156},{28,15... | collective-permute-start | bytes 393224 | tf_op jit(solution)/shard_map/ppermute | solution.py:525
  126.2 10.5 %collective-permute-start.13 = (f32[256,128]{1,0:T(8,128)S(1)}, f32[256,128]{1,0:T(8,128)S(1)}, u32[]{:S(2)}, u32[]{:S(2)}) collective-permute-start(f32[256,128]{1,0:T(8,128)S(1)} %get-tuple-element.62), channel_id=1, source_target_pairs={{0,192},{4,196},{8,200},{12,204},{16,208},{20,212},{24,216},{28,22... | collective-permute-start | bytes 393224 | tf_op jit(solution)/shard_map/ppermute | solution.py:525
  128.0 9.3 %collective-permute-start.14 = (f32[256,128]{1,0:T(8,128)S(1)}, f32[256,128]{1,0:T(8,128)S(1)}, u32[]{:S(2)}, u32[]{:S(2)}) collective-permute-start(f32[256,128]{1,0:T(8,128)S(1)} %get-tuple-element.63), channel_id=1, source_target_pairs={{0,196},{4,192},{8,204},{12,200},{16,212},{20,208},{24,220},{28,21... | collective-permute-start | bytes 393224 | tf_op jit(solution)/shard_map/ppermute | solution.py:525
  141.6 16.7 %collective-permute-start.17 = (f32[512,128]{1,0:T(8,128)S(1)}, f32[512,128]{1,0:T(8,128)S(1)}, u32[]{:S(2)}, u32[]{:S(2)}) collective-permute-start(f32[512,128]{1,0:T(8,128)S(1)} %get-tuple-element.70), channel_id=1, source_target_pairs={{0,8},{8,16},{16,24},{24,32},{32,40},{40,48},{48,56},{56,0},{64,72... | collective-permute-start | bytes 786440 | tf_op jit(solution)/shard_map/ppermute | solution.py:502
  141.8 16.5 %collective-permute-start.18 = (f32[512,128]{1,0:T(8,128)S(1)}, f32[512,128]{1,0:T(8,128)S(1)}, u32[]{:S(2)}, u32[]{:S(2)}) collective-permute-start(f32[512,128]{1,0:T(8,128)S(1)} %get-tuple-element.71), channel_id=1, source_target_pairs={{0,16},{8,24},{16,32},{24,40},{32,48},{40,56},{48,0},{56,8},{64,80... | collective-permute-start | bytes 786440 | tf_op jit(solution)/shard_map/ppermute | solution.py:502
  143.4 15.3 %collective-permute-start.19 = (f32[512,128]{1,0:T(8,128)S(1)}, f32[512,128]{1,0:T(8,128)S(1)}, u32[]{:S(2)}, u32[]{:S(2)}) collective-permute-start(f32[512,128]{1,0:T(8,128)S(1)} %get-tuple-element.72), channel_id=1, source_target_pairs={{0,24},{8,32},{16,40},{24,48},{32,56},{40,0},{48,8},{56,16},{64,88... | collective-permute-start | bytes 786440 | tf_op jit(solution)/shard_map/ppermute | solution.py:502
  146.1 12.2 %collective-permute-start.15 = (f32[256,128]{1,0:T(8,128)S(1)}, f32[256,128]{1,0:T(8,128)S(1)}, u32[]{:S(2)}, u32[]{:S(2)}) collective-permute-start(f32[256,128]{1,0:T(8,128)S(1)} %get-tuple-element.65), channel_id=1, source_target_pairs={{0,32},{8,40},{16,48},{24,56},{32,0},{40,8},{48,16},{56,24},{64,96... | collective-permute-start | bytes 393224 | tf_op jit(solution)/shard_map/ppermute | solution.py:502
  159.3 15.6 %collective-permute-start.20 = (f32[256,128]{1,0:T(8,128)S(1)}, f32[256,128]{1,0:T(8,128)S(1)}, u32[]{:S(2)}, u32[]{:S(2)}) collective-permute-start(f32[256,128]{1,0:T(8,128)S(1)} %get-tuple-element.74), channel_id=1, source_target_pairs={{0,4},{4,0},{8,12},{12,8},{16,20},{20,16},{24,28},{28,24},{32,36},... | collective-permute-start | bytes 393224 | tf_op jit(solution)/shard_map/ppermute | solution.py:525
  168.8 8.9 %collective-permute-start.21 = (f32[256,128]{1,0:T(8,128)S(1)}, f32[256,128]{1,0:T(8,128)S(1)}, u32[]{:S(2)}, u32[]{:S(2)}) collective-permute-start(f32[256,128]{1,0:T(8,128)S(1)} %get-tuple-element.75), channel_id=1, source_target_pairs={{0,64},{4,68},{8,72},{12,76},{16,80},{20,84},{24,88},{28,92},{32,9... | collective-permute-start | bytes 393224 | tf_op jit(solution)/shard_map/ppermute | solution.py:525
  171.5 10.6 %collective-permute-start.23 = (f32[256,128]{1,0:T(8,128)S(1)}, f32[256,128]{1,0:T(8,128)S(1)}, u32[]{:S(2)}, u32[]{:S(2)}) collective-permute-start(f32[256,128]{1,0:T(8,128)S(1)} %get-tuple-element.77), channel_id=1, source_target_pairs={{0,128},{4,132},{8,136},{12,140},{16,144},{20,148},{24,152},{28,15... | collective-permute-start | bytes 393224 | tf_op jit(solution)/shard_map/ppermute | solution.py:525
  173.0 12.1 %collective-permute-start.24 = (f32[256,128]{1,0:T(8,128)S(1)}, f32[256,128]{1,0:T(8,128)S(1)}, u32[]{:S(2)}, u32[]{:S(2)}) collective-permute-start(f32[256,128]{1,0:T(8,128)S(1)} %get-tuple-element.78), channel_id=1, source_target_pairs={{0,132},{4,128},{8,140},{12,136},{16,148},{20,144},{24,156},{28,15... | collective-permute-start | bytes 393224 | tf_op jit(solution)/shard_map/ppermute | solution.py:525
  174.9 10.2 %collective-permute-start.25 = (f32[256,128]{1,0:T(8,128)S(1)}, f32[256,128]{1,0:T(8,128)S(1)}, u32[]{:S(2)}, u32[]{:S(2)}) collective-permute-start(f32[256,128]{1,0:T(8,128)S(1)} %get-tuple-element.79), channel_id=1, source_target_pairs={{0,192},{4,196},{8,200},{12,204},{16,208},{20,212},{24,216},{28,22... | collective-permute-start | bytes 393224 | tf_op jit(solution)/shard_map/ppermute | solution.py:525
  177.6 9.5 %collective-permute-start.26 = (f32[256,128]{1,0:T(8,128)S(1)}, f32[256,128]{1,0:T(8,128)S(1)}, u32[]{:S(2)}, u32[]{:S(2)}) collective-permute-start(f32[256,128]{1,0:T(8,128)S(1)} %get-tuple-element.80), channel_id=1, source_target_pairs={{0,196},{4,192},{8,204},{12,200},{16,212},{20,208},{24,220},{28,21... | collective-permute-start | bytes 393224 | tf_op jit(solution)/shard_map/ppermute | solution.py:525
  (11 other events, 29.7 us)

commit v10 on v7

--- a/solution.py
+++ b/solution.py
@@ -67,7 +67,7 @@
     full = full.reshape(HALF, 4 * PEERS, 2 * INNER)
     high = lax.reduce_precision(full, 8, 7)
     high, low = high.astype(jnp.bfloat16), (full - high).astype(jnp.bfloat16)
-    return jnp.concatenate([high, low], axis=-1)
+    return high, low
 
 
 def fft_real16(x):
@@ -121,7 +121,7 @@
     return ((n2 % 4) * 4 + base // LON) * INNER + (n2 // 4) * LON + base % LON
 
 
-def fft_core(x_ref, w_ref, y_ref, r_ref, row_of, loads):
+def fft_core(x_ref, wh_ref, wl_ref, y_ref, r_ref, row_of):
     def butterfly(i, carry):
         base = pl.multiple_of(i * 8, 8)
         x = [x_ref[pl.ds(pl.multiple_of(row_of(n2, base), 8), 8), :] for n2 in range(RADIX)]
@@ -132,16 +132,12 @@
                 y_ref[k, pl.ds(j * INNER + base, 8), :] = part
         return carry
 
-    lax.fori_loop(0, INNER // 8, butterfly, 0)
+    lax.fori_loop(0, INNER // 8, butterfly, 0, unroll=4)
     for k in range(HALF):
         yh, yl = split_bf16(y_ref[k])
-        loads[k].wait()
-        high, both = w_ref[k, :, : 2 * INNER], w_ref[k]
-        r = jnp.dot(
-            jnp.concatenate([high, both], axis=1),
-            jnp.concatenate([yl, yh, yh], axis=0),
-            preferred_element_type=jnp.float32,
-        )
+        two = jnp.dot(wh_ref[k], jnp.concatenate([yh, yl], axis=1), preferred_element_type=jnp.float32)
+        r = two[:, :LANES] + two[:, LANES:]
+        r = r + jnp.dot(wl_ref[k], yh, preferred_element_type=jnp.float32)
         mirror = HALF if k == 0 else RADIX - k
         for q, row in enumerate((k, RADIX + k, mirror, RADIX + mirror)):
             r_ref[pl.ds(row * PAD_R, PEERS), :] = r[q * PEERS : (q + 1) * PEERS]
@@ -163,16 +159,7 @@
         copy.wait()
 
 
-def load_matrices(w_hbm, w_ref, sem):
-    loads = [pltpu.make_async_copy(w_hbm.at[k], w_ref.at[k], sem.at[k]) for k in range(HALF)]
-    for load in loads:
-        load.start()
-    return loads
-
-
 FFT_SCRATCH = [
-    pltpu.VMEM((HALF, 4 * PEERS, 4 * INNER), jnp.bfloat16),
-    pltpu.SemaphoreType.DMA((HALF,)),
     pltpu.VMEM((HALF, 2 * INNER, LANES), jnp.float32),
     pltpu.VMEM((KEPT * PAD_R, LANES), jnp.float32),
 ]
@@ -182,9 +169,8 @@
     return r_ref[pl.ds(eight * 8 * PAD_R + k1, 8, stride=PAD_R), :]
 
 
-def fft_a_kernel(x_ref, w_hbm, o_ref, w_ref, w_sem, y_ref, r_ref, buf_ref, sem):
-    loads = load_matrices(w_hbm, w_ref, w_sem)
-    fft_core(x_ref, w_ref, y_ref, r_ref, grouped_row, loads)
+def fft_a_kernel(x_ref, wh_ref, wl_ref, o_ref, y_ref, r_ref, buf_ref, sem):
+    fft_core(x_ref, wh_ref, wl_ref, y_ref, r_ref, grouped_row)
 
     def peer(k1, carry):
         for eight in range(KEPT // 8):
@@ -194,23 +180,22 @@
     send_pieces(peer, PEERS, buf_ref, o_ref, sem)
 
 
-def fft_a(gathered, w):
+def fft_a(gathered, wh, wl):
     return pl.pallas_call(
         fft_a_kernel,
-        in_specs=[VMEM, HBM],
+        in_specs=[VMEM] * 3,
         out_specs=HBM,
         out_shape=pltpu.HBM((PEERS, KEPT, LANES), jnp.float32),
         scratch_shapes=FFT_SCRATCH
         + [pltpu.VMEM((PEERS, KEPT, LANES), jnp.float32), pltpu.SemaphoreType.DMA((PIECES,))],
         compiler_params=PARAMS,
         name="fft_a",
-    )(gathered, pltpu.with_memory_space_constraint(w, pltpu.HBM))
+    )(gathered, wh, wl)
 
 
 def fft_p_kernel(pos_ref, *refs):
-    g_refs, w_hbm, o_refs = refs[:8], refs[8], refs[9:17]
-    x_ref, w_ref, w_sem, y_ref, r_ref = refs[17:]
-    loads = load_matrices(w_hbm, w_ref, w_sem)
+    g_refs, (wh_ref, wl_ref), o_refs = refs[:8], refs[8:10], refs[10:18]
+    x_ref, y_ref, r_ref = refs[18:]
     x, z, c = pos_ref[0], pos_ref[1], pos_ref[2]
     for dx in range(NX):
         for dc in range(NC):
@@ -218,7 +203,7 @@
             for zz in range(NZ):
                 row = pl.multiple_of(start + zz * NC * LON, LON)
                 x_ref[pl.ds(row, LON), :] = g_refs[dx * NC + dc][zz * LON : (zz + 1) * LON, :]
-    fft_core(x_ref, w_ref, y_ref, r_ref, natural_row, loads)
+    fft_core(x_ref, wh_ref, wl_ref, y_ref, r_ref, natural_row)
     for dz in range(NZ):
         target = (z + dz) % NZ
         for xx in range(NX):
@@ -229,16 +214,16 @@
                     o_refs[dz][row : row + 8, :] = mode_rows(r_ref, k1, eight)
 
 
-def fft_p(pos, blocks, w):
+def fft_p(pos, blocks, wh, wl):
     return pl.pallas_call(
         fft_p_kernel,
-        in_specs=[SMEM] + [VMEM] * 8 + [HBM],
+        in_specs=[SMEM] + [VMEM] * 10,
         out_specs=[VMEM] * NZ,
         out_shape=[vmem(NX * NC * KEPT, LANES)] * NZ,
         scratch_shapes=[pltpu.VMEM((NLON, LANES), jnp.float32)] + FFT_SCRATCH,
         compiler_params=PARAMS,
         name="fft_p",
-    )(pos, *blocks, pltpu.with_memory_space_constraint(w, pltpu.HBM))
+    )(pos, *blocks, wh, wl)
 
 
 GROUP = NZ * NC
@@ -443,7 +428,7 @@
     return out
 
 
-AX_ORDER = (2, 1, 3)
+AX_ORDER = (1, 3, 2)
 GROUPS = [[x * GROUP + g for g in range(GROUP)] for x in range(NX)]
 
 
@@ -455,7 +440,7 @@
     return out
 
 
-X_ORDER = ((2, 0), (2, 1), (1, 0), (3, 0), (1, 1), (3, 1), (0, 1))
+X_ORDER = ((1, 0), (3, 0), (2, 0), (2, 1), (1, 1), (3, 1), (0, 1))
 
 
 def exchange_xc(blocks):
@@ -469,7 +454,7 @@
 def local(state):
     device = lax.axis_index("lon")
     pos = jnp.stack([device // (NZ * NC), (device // NC) % NZ, device % NC]).astype(jnp.int32)
-    w = twiddle_matrices(1.0 / math.sqrt(NLON))
+    wh, wl = twiddle_matrices(1.0 / math.sqrt(NLON))
     pieces, parts = split(pos, state)
     pieces = exchange_z(pieces)
     parts = exchange_x(parts)
@@ -479,9 +464,9 @@
     )
     pieces = spread_x(pos, [b.reshape(LON * 8, LANES) for b in pieces])
     pieces = exchange_xc(pieces)
-    pieces = fft_p(pos, pieces, w)
+    pieces = fft_p(pos, pieces, wh, wl)
     pieces = exchange_z(pieces)
-    spectrum = fft_a(gathered.reshape(NLON, LANES), w)
+    spectrum = fft_a(gathered.reshape(NLON, LANES), wh, wl)
     shares = lax.all_to_all(spectrum, "lon", split_axis=0, concat_axis=0, tiled=True)
     pieces = spread_out(pos, pieces)
     pieces = exchange_xc(pieces)

time: 194 us -> 192 us (0.990)
  Pallas kernels: 16.8 us -> 12.3 us
  local copies, waits for them, and re-layouts: 0 us -> 2.6 us
    pallas_call x2, Pallas kernels: 8.47 us -> 4.03 us  [the longest x1 2.14 us: fft_a(): pl.pallas_call(fft_a_kernel, in_specs=[VMEM] * 3, out_specs=HBM, out_shap...]
    unnamed x0 -> x10, local copies, waits for them, and re-layouts: none -> 2.6 us
  transfers between devices with their start and end apart: 33 -> 33, of which waited for: 16 -> 16; matrix products, arithmetic and copies ran while one was open for 2% -> 2% of each run, Pallas kernels for 3% -> 2%
where the time goes in v10:
time: 192 us; the launch traced here: 191 us
  waiting for transfers between devices  102 us (53%)
  starting transfers between devices  70.4 us (37%)
  Pallas kernels  12.3 us (6%)
  other arithmetic  3.34 us (2%)
  local copies, waits for them, and re-layouts  2.6 us (1%)
    ppermute x14, waiting for transfers between devices, exchange_z(): out[dz] = lax.ppermute(blocks[dz], 'lon', shifts(0, dz, 0))  52.1 us
    ppermute x14, starting transfers between devices, exchange_z(): out[dz] = lax.ppermute(blocks[dz], 'lon', shifts(0, dz, 0))  28.5 us
    all_to_all x1, waiting for transfers between devices, local(): lax.all_to_all(sent, 'lon', split_axis=0, concat_axis=0, axis_index_group...  24.7 us
    ppermute x14, starting transfers between devices, exchange_xc(): lax.ppermute(blocks[dx * NC + dc], 'lon', shifts(dx, 0, dc))  20.2 us
    ppermute x14, waiting for transfers between devices, exchange_xc(): lax.ppermute(blocks[dx * NC + dc], 'lon', shifts(dx, 0, dc))  15.4 us
    ppermute x3, waiting for transfers between devices, exchange_x(): out[dx] = lax.ppermute(blocks[dx], 'lon', shifts(dx, 0, 0))  10.2 us
    all_to_all x1, starting transfers between devices, local(): lax.all_to_all(sent, 'lon', split_axis=0, concat_axis=0, axis_index_group...  10 us
    all_to_all x1, starting transfers between devices, local(): lax.all_to_all(spectrum, 'lon', split_axis=0, concat_axis=0, tiled=True)  6.08 us
  transfers between devices with their start and end apart: 33, of which 16 were waited for; matrix products, arithmetic and copies ran while one was open for 2% of the time, Pallas kernels for 2%

profile of v10, /device:TPU:1, one launch (start us, length us, event | category | flops | bytes accessed | tf_op | source)
XLA Modules:
  0.0 191.5 jit_solution(12004514534498852743)
XLA Ops:
  7.0 2.5 %collective-permute-start.1 = (f32[32,16,128]{2,1,0:T(8,128)S(1)}, f32[32,16,128]{2,1,0:T(8,128)S(1)}, u32[]{:S(2)}, u32[]{:S(2)}) collective-permute-start(f32[32,16,128]{2,1,0:T(8,128)S(1)} %get-tuple-element.43), channel_id=1, source_target_pairs={{0,128},{4,132},{8,136},{12,140},{16,144},{20,148},{24,152},{28,15... | collective-permute-start | bytes 786440 | tf_op jit(solution)/shard_map/ppermute | solution.py:439
  12.1 8.8 %collective-permute-done.1 = f32[32,16,128]{2,1,0:T(8,128)S(1)} collective-permute-done((f32[32,16,128]{2,1,0:T(8,128)S(1)}, f32[32,16,128]{2,1,0:T(8,128)S(1)}, u32[]{:S(2)}, u32[]{:S(2)}) %collective-permute-start.1) | collective-permute-done | bytes 262176 | tf_op jit(solution)/shard_map/ppermute | solution.py:439
  22.5 10.0 %all-to-all-start = ((f32[16,128,128]{2,1,0:T(8,128)}), f32[16,128,128]{2,1,0:T(8,128)S(1)}, u32[]{:S(2)}, u32[]{:S(2)}) async-start(f32[16,128,128]{2,1,0:T(8,128)} %spread_a.1), calls=%async_computation | async-start | bytes 2097152 | tf_op jit(solution)/shard_map/all_to_all | solution.py:462
  32.5 2.5 %select_select_fusion.1 = (f32[8,2,64,128]{3,2,1,0:T(8,128)S(1)}, f32[8,2,64,128]{3,2,1,0:T(8,128)S(1)}, f32[8,2,64,128]{3,2,1,0:T(8,128)S(1)}, f32[8,2,64,128]{3,2,1,0:T(8,128)S(1)}) fusion(pred[2]{0:T(512)(128)(4,1)S(1)} %iota_compare_fusion.1, pred[8]{0:T(512)(128)(4,1)S(1)} %iota_compare_fusion, s32[64]{0:T(128)S(1)} %iota_multiply_fusion, ...), kind=kLoop, calls=%fused_computation.9 | loop fusion | flops 4456448 | bytes 2097450 | tf_op jit(solution)/shard_map/jit(_where)/select_n | solution.py:60
  35.8 24.7 %all-to-all-done = f32[16,128,128]{2,1,0:T(8,128)S(1)} async-done(((f32[16,128,128]{2,1,0:T(8,128)}), f32[16,128,128]{2,1,0:T(8,128)S(1)}, u32[]{:S(2)}, u32[]{:S(2)}) %all-to-all-start) | async-done | bytes 1048608 | tf_op jit(solution)/shard_map/all_to_all | solution.py:462
  62.6 6.1 %all-to-all-start.1 = ((f32[64,32,128]{2,1,0:T(8,128)}), f32[64,32,128]{2,1,0:T(8,128)S(1)}, u32[]{:S(2)}, u32[]{:S(2)}) async-start(f32[64,32,128]{2,1,0:T(8,128)} %fft_a.1), calls=%async_computation.1 | async-start | bytes 2097152 | tf_op jit(solution)/shard_map/all_to_all | solution.py:470
  72.2 2.4 %collective-permute-start.5 = (f32[32,8,128]{2,1,0:T(8,128)}, f32[32,8,128]{2,1,0:T(8,128)S(1)}, u32[]{:S(2)}, u32[]{:S(2)}) collective-permute-start(f32[32,8,128]{2,1,0:T(8,128)} %copy-done.2), channel_id=1, source_target_pairs={{0,24},{4,28},{8,32},{12,36},{16,40},{20,44},{24,48},{28,52},{32,5... | collective-permute-start | bytes 393224 | tf_op jit(solution)/shard_map/ppermute | solution.py:427
  76.7 2.4 %collective-permute-start.7 = (f32[32,8,128]{2,1,0:T(8,128)}, f32[32,8,128]{2,1,0:T(8,128)S(1)}, u32[]{:S(2)}, u32[]{:S(2)}) collective-permute-start(f32[32,8,128]{2,1,0:T(8,128)} %copy-done), channel_id=1, source_target_pairs={{0,40},{4,44},{8,48},{12,52},{16,56},{20,60},{24,0},{28,4},{32,8},... | collective-permute-start | bytes 393224 | tf_op jit(solution)/shard_map/ppermute | solution.py:427
  79.1 17.8 %collective-permute-done.3 = f32[32,8,128]{2,1,0:T(8,128)S(1)} collective-permute-done((f32[32,8,128]{2,1,0:T(8,128)}, f32[32,8,128]{2,1,0:T(8,128)S(1)}, u32[]{:S(2)}, u32[]{:S(2)}) %collective-permute-start.3) | collective-permute-done | bytes 131104 | tf_op jit(solution)/shard_map/ppermute | solution.py:427
  99.2 2.8 %collective-permute-done.4 = f32[32,8,128]{2,1,0:T(8,128)S(1)} collective-permute-done((f32[32,8,128]{2,1,0:T(8,128)}, f32[32,8,128]{2,1,0:T(8,128)S(1)}, u32[]{:S(2)}, u32[]{:S(2)}) %collective-permute-start.4) | collective-permute-done | bytes 131104 | tf_op jit(solution)/shard_map/ppermute | solution.py:427
  102.0 2.3 %collective-permute-start.9 = (f32[32,8,128]{2,1,0:T(8,128)S(1)}, f32[32,8,128]{2,1,0:T(8,128)S(1)}, u32[]{:S(2)}, u32[]{:S(2)}) collective-permute-start(f32[32,8,128]{2,1,0:T(8,128)S(1)} %get-tuple-element.52), channel_id=1, source_target_pairs={{0,56},{4,60},{8,0},{12,4},{16,8},{20,12},{24,16},{28,20},{32,24},... | collective-permute-start | bytes 393224 | tf_op jit(solution)/shard_map/ppermute | solution.py:427
  104.3 8.8 %collective-permute-done.5 = f32[32,8,128]{2,1,0:T(8,128)S(1)} collective-permute-done((f32[32,8,128]{2,1,0:T(8,128)}, f32[32,8,128]{2,1,0:T(8,128)S(1)}, u32[]{:S(2)}, u32[]{:S(2)}) %collective-permute-start.5) | collective-permute-done | bytes 131104 | tf_op jit(solution)/shard_map/ppermute | solution.py:427
  113.1 4.9 %collective-permute-done.6 = f32[32,8,128]{2,1,0:T(8,128)S(1)} collective-permute-done((f32[32,8,128]{2,1,0:T(8,128)}, f32[32,8,128]{2,1,0:T(8,128)S(1)}, u32[]{:S(2)}, u32[]{:S(2)}) %collective-permute-start.6) | collective-permute-done | bytes 131104 | tf_op jit(solution)/shard_map/ppermute | solution.py:427
  118.9 2.5 %collective-permute-start.10 = (f32[256,128]{1,0:T(8,128)S(1)}, f32[256,128]{1,0:T(8,128)S(1)}, u32[]{:S(2)}, u32[]{:S(2)}) collective-permute-start(f32[256,128]{1,0:T(8,128)S(1)} %get-tuple-element.54), channel_id=1, source_target_pairs={{0,4},{4,0},{8,12},{12,8},{16,20},{20,16},{24,28},{28,24},{32,36},... | collective-permute-start | bytes 393224 | tf_op jit(solution)/shard_map/ppermute | solution.py:450
  122.4 3.2 %collective-permute-start.13 = (f32[256,128]{1,0:T(8,128)S(1)}, f32[256,128]{1,0:T(8,128)S(1)}, u32[]{:S(2)}, u32[]{:S(2)}) collective-permute-start(f32[256,128]{1,0:T(8,128)S(1)} %get-tuple-element.57), channel_id=1, source_target_pairs={{0,128},{4,132},{8,136},{12,140},{16,144},{20,148},{24,152},{28,15... | collective-permute-start | bytes 393224 | tf_op jit(solution)/shard_map/ppermute | solution.py:450
  129.4 6.9 %collective-permute-done.12.refs_3_ = f32[256,128]{1,0:T(8,128)S(1)} collective-permute-done((f32[256,128]{1,0:T(8,128)S(1)}, f32[256,128]{1,0:T(8,128)S(1)}, u32[]{:S(2)}, u32[]{:S(2)}) %collective-permute-start.12) | collective-permute-done | bytes 131104 | tf_op jit(solution)/shard_map/ppermute | solution.py:450
  143.0 3.3 %collective-permute-start.20 = (f32[256,128]{1,0:T(8,128)S(1)}, f32[256,128]{1,0:T(8,128)S(1)}, u32[]{:S(2)}, u32[]{:S(2)}) collective-permute-start(f32[256,128]{1,0:T(8,128)S(1)} %get-tuple-element.65), channel_id=1, source_target_pairs={{0,32},{4,36},{8,40},{12,44},{16,48},{20,52},{24,56},{28,60},{32,0... | collective-permute-start | bytes 393224 | tf_op jit(solution)/shard_map/ppermute | solution.py:427
  149.0 4.6 %collective-permute-start.23 = (f32[256,128]{1,0:T(8,128)S(1)}, f32[256,128]{1,0:T(8,128)S(1)}, u32[]{:S(2)}, u32[]{:S(2)}) collective-permute-start(f32[256,128]{1,0:T(8,128)S(1)} %get-tuple-element.68), channel_id=1, source_target_pairs={{0,56},{4,60},{8,0},{12,4},{16,8},{20,12},{24,16},{28,20},{32,24},... | collective-permute-start | bytes 393224 | tf_op jit(solution)/shard_map/ppermute | solution.py:427
  153.5 9.8 %collective-permute-done.19.refs_3_ = f32[256,128]{1,0:T(8,128)S(1)} collective-permute-done((f32[256,128]{1,0:T(8,128)S(1)}, f32[256,128]{1,0:T(8,128)S(1)}, u32[]{:S(2)}, u32[]{:S(2)}) %collective-permute-start.19) | collective-permute-done | bytes 131104 | tf_op jit(solution)/shard_map/ppermute | solution.py:427
  163.3 4.1 %collective-permute-done.22.refs_6_ = f32[256,128]{1,0:T(8,128)S(1)} collective-permute-done((f32[256,128]{1,0:T(8,128)S(1)}, f32[256,128]{1,0:T(8,128)S(1)}, u32[]{:S(2)}, u32[]{:S(2)}) %collective-permute-start.22) | collective-permute-done | bytes 131104 | tf_op jit(solution)/shard_map/ppermute | solution.py:427
  167.5 2.7 %collective-permute-done.23.refs_7_ = f32[256,128]{1,0:T(8,128)S(1)} collective-permute-done((f32[256,128]{1,0:T(8,128)S(1)}, f32[256,128]{1,0:T(8,128)S(1)}, u32[]{:S(2)}, u32[]{:S(2)}) %collective-permute-start.23) | collective-permute-done | bytes 131104 | tf_op jit(solution)/shard_map/ppermute | solution.py:427
  177.5 2.6 %collective-permute-start.29 = (f32[256,128]{1,0:T(8,128)S(1)}, f32[256,128]{1,0:T(8,128)S(1)}, u32[]{:S(2)}, u32[]{:S(2)}) collective-permute-start(f32[256,128]{1,0:T(8,128)S(1)} %get-tuple-element.75), channel_id=1, source_target_pairs={{0,192},{4,196},{8,200},{12,204},{16,208},{20,212},{24,216},{28,22... | collective-permute-start | bytes 393224 | tf_op jit(solution)/shard_map/ppermute | solution.py:450
  181.8 2.8 %collective-permute-done.27.refs_4_ = f32[256,128]{1,0:T(8,128)S(1)} collective-permute-done((f32[256,128]{1,0:T(8,128)S(1)}, f32[256,128]{1,0:T(8,128)S(1)}, u32[]{:S(2)}, u32[]{:S(2)}) %collective-permute-start.27) | collective-permute-done | bytes 131104 | tf_op jit(solution)/shard_map/ppermute | solution.py:450
  184.6 3.1 %collective-permute-done.28.refs_5_ = f32[256,128]{1,0:T(8,128)S(1)} collective-permute-done((f32[256,128]{1,0:T(8,128)S(1)}, f32[256,128]{1,0:T(8,128)S(1)}, u32[]{:S(2)}, u32[]{:S(2)}) %collective-permute-start.28) | collective-permute-done | bytes 131104 | tf_op jit(solution)/shard_map/ppermute | solution.py:450
  (69 shorter events, 49.6 us)
Async XLA Ops:
  7.0 13.8 %collective-permute-start.1 = (f32[32,16,128]{2,1,0:T(8,128)S(1)}, f32[32,16,128]{2,1,0:T(8,128)S(1)}, u32[]{:S(2)}, u32[]{:S(2)}) collective-permute-start(f32[32,16,128]{2,1,0:T(8,128)S(1)} %get-tuple-element.43), channel_id=1, source_target_pairs={{0,128},{4,132},{8,136},{12,140},{16,144},{20,148},{24,152},{28,15... | collective-permute-start | bytes 786440 | tf_op jit(solution)/shard_map/ppermute | solution.py:439
  9.5 11.3 %collective-permute-start.2 = (f32[32,16,128]{2,1,0:T(8,128)S(1)}, f32[32,16,128]{2,1,0:T(8,128)S(1)}, u32[]{:S(2)}, u32[]{:S(2)}) collective-permute-start(f32[32,16,128]{2,1,0:T(8,128)S(1)} %get-tuple-element.44), channel_id=1, source_target_pairs={{0,192},{4,196},{8,200},{12,204},{16,208},{20,212},{24,216},{28,22... | collective-permute-start | bytes 786440 | tf_op jit(solution)/shard_map/ppermute | solution.py:439
  22.5 38.0 %all-to-all-start = ((f32[16,128,128]{2,1,0:T(8,128)}), f32[16,128,128]{2,1,0:T(8,128)S(1)}, u32[]{:S(2)}, u32[]{:S(2)}) async-start(f32[16,128,128]{2,1,0:T(8,128)} %spread_a.1), calls=%async_computation | async-start | bytes 2097152 | tf_op jit(solution)/shard_map/all_to_all | solution.py:462
  62.6 118.0 %all-to-all-start.1 = ((f32[64,32,128]{2,1,0:T(8,128)}), f32[64,32,128]{2,1,0:T(8,128)S(1)}, u32[]{:S(2)}, u32[]{:S(2)}) async-start(f32[64,32,128]{2,1,0:T(8,128)} %fft_a.1), calls=%async_computation.1 | async-start | bytes 2097152 | tf_op jit(solution)/shard_map/all_to_all | solution.py:470
  68.7 28.2 %collective-permute-start.3 = (f32[32,8,128]{2,1,0:T(8,128)}, f32[32,8,128]{2,1,0:T(8,128)S(1)}, u32[]{:S(2)}, u32[]{:S(2)}) collective-permute-start(f32[32,8,128]{2,1,0:T(8,128)} %copy-done.4), channel_id=1, source_target_pairs={{0,8},{4,12},{8,16},{12,20},{16,24},{20,28},{24,32},{28,36},{32,40... | collective-permute-start | bytes 393224 | tf_op jit(solution)/shard_map/ppermute | solution.py:427
  70.2 31.8 %collective-permute-start.4 = (f32[32,8,128]{2,1,0:T(8,128)}, f32[32,8,128]{2,1,0:T(8,128)S(1)}, u32[]{:S(2)}, u32[]{:S(2)}) collective-permute-start(f32[32,8,128]{2,1,0:T(8,128)} %copy-done.3), channel_id=1, source_target_pairs={{0,16},{4,20},{8,24},{12,28},{16,32},{20,36},{24,40},{28,44},{32,4... | collective-permute-start | bytes 393224 | tf_op jit(solution)/shard_map/ppermute | solution.py:427
  72.2 40.9 %collective-permute-start.5 = (f32[32,8,128]{2,1,0:T(8,128)}, f32[32,8,128]{2,1,0:T(8,128)S(1)}, u32[]{:S(2)}, u32[]{:S(2)}) collective-permute-start(f32[32,8,128]{2,1,0:T(8,128)} %copy-done.2), channel_id=1, source_target_pairs={{0,24},{4,28},{8,32},{12,36},{16,40},{20,44},{24,48},{28,52},{32,5... | collective-permute-start | bytes 393224 | tf_op jit(solution)/shard_map/ppermute | solution.py:427
  74.6 43.4 %collective-permute-start.6 = (f32[32,8,128]{2,1,0:T(8,128)}, f32[32,8,128]{2,1,0:T(8,128)S(1)}, u32[]{:S(2)}, u32[]{:S(2)}) collective-permute-start(f32[32,8,128]{2,1,0:T(8,128)} %copy-done.1), channel_id=1, source_target_pairs={{0,32},{4,36},{8,40},{12,44},{16,48},{20,52},{24,56},{28,60},{32,0... | collective-permute-start | bytes 393224 | tf_op jit(solution)/shard_map/ppermute | solution.py:427
  76.7 41.3 %collective-permute-start.7 = (f32[32,8,128]{2,1,0:T(8,128)}, f32[32,8,128]{2,1,0:T(8,128)S(1)}, u32[]{:S(2)}, u32[]{:S(2)}) collective-permute-start(f32[32,8,128]{2,1,0:T(8,128)} %copy-done), channel_id=1, source_target_pairs={{0,40},{4,44},{8,48},{12,52},{16,56},{20,60},{24,0},{28,4},{32,8},... | collective-permute-start | bytes 393224 | tf_op jit(solution)/shard_map/ppermute | solution.py:427
  96.9 21.1 %collective-permute-start.8 = (f32[32,8,128]{2,1,0:T(8,128)S(1)}, f32[32,8,128]{2,1,0:T(8,128)S(1)}, u32[]{:S(2)}, u32[]{:S(2)}) collective-permute-start(f32[32,8,128]{2,1,0:T(8,128)S(1)} %get-tuple-element.51), channel_id=1, source_target_pairs={{0,48},{4,52},{8,56},{12,60},{16,0},{20,4},{24,8},{28,12},{32,16},... | collective-permute-start | bytes 393224 | tf_op jit(solution)/shard_map/ppermute | solution.py:427
  102.0 16.0 %collective-permute-start.9 = (f32[32,8,128]{2,1,0:T(8,128)S(1)}, f32[32,8,128]{2,1,0:T(8,128)S(1)}, u32[]{:S(2)}, u32[]{:S(2)}) collective-permute-start(f32[32,8,128]{2,1,0:T(8,128)S(1)} %get-tuple-element.52), channel_id=1, source_target_pairs={{0,56},{4,60},{8,0},{12,4},{16,8},{20,12},{24,16},{28,20},{32,24},... | collective-permute-start | bytes 393224 | tf_op jit(solution)/shard_map/ppermute | solution.py:427
  121.5 14.9 %collective-permute-start.12 = (f32[256,128]{1,0:T(8,128)S(1)}, f32[256,128]{1,0:T(8,128)S(1)}, u32[]{:S(2)}, u32[]{:S(2)}) collective-permute-start(f32[256,128]{1,0:T(8,128)S(1)} %get-tuple-element.56), channel_id=1, source_target_pairs={{0,68},{4,64},{8,76},{12,72},{16,84},{20,80},{24,92},{28,88},{32,1... | collective-permute-start | bytes 393224 | tf_op jit(solution)/shard_map/ppermute | solution.py:450
  122.4 13.9 %collective-permute-start.13 = (f32[256,128]{1,0:T(8,128)S(1)}, f32[256,128]{1,0:T(8,128)S(1)}, u32[]{:S(2)}, u32[]{:S(2)}) collective-permute-start(f32[256,128]{1,0:T(8,128)S(1)} %get-tuple-element.57), channel_id=1, source_target_pairs={{0,128},{4,132},{8,136},{12,140},{16,144},{20,148},{24,152},{28,15... | collective-permute-start | bytes 393224 | tf_op jit(solution)/shard_map/ppermute | solution.py:450
  125.6 10.8 %collective-permute-start.14 = (f32[256,128]{1,0:T(8,128)S(1)}, f32[256,128]{1,0:T(8,128)S(1)}, u32[]{:S(2)}, u32[]{:S(2)}) collective-permute-start(f32[256,128]{1,0:T(8,128)S(1)} %get-tuple-element.58), channel_id=1, source_target_pairs={{0,132},{4,128},{8,140},{12,136},{16,148},{20,144},{24,156},{28,15... | collective-permute-start | bytes 393224 | tf_op jit(solution)/shard_map/ppermute | solution.py:450
  125.6 10.7 %collective-permute-start.15 = (f32[256,128]{1,0:T(8,128)S(1)}, f32[256,128]{1,0:T(8,128)S(1)}, u32[]{:S(2)}, u32[]{:S(2)}) collective-permute-start(f32[256,128]{1,0:T(8,128)S(1)} %get-tuple-element.59), channel_id=1, source_target_pairs={{0,192},{4,196},{8,200},{12,204},{16,208},{20,212},{24,216},{28,22... | collective-permute-start | bytes 393224 | tf_op jit(solution)/shard_map/ppermute | solution.py:450
  139.0 10.0 %collective-permute-start.18 = (f32[256,128]{1,0:T(8,128)S(1)}, f32[256,128]{1,0:T(8,128)S(1)}, u32[]{:S(2)}, u32[]{:S(2)}) collective-permute-start(f32[256,128]{1,0:T(8,128)S(1)} %get-tuple-element.63), channel_id=1, source_target_pairs={{0,16},{4,20},{8,24},{12,28},{16,32},{20,36},{24,40},{28,44},{32,4... | collective-permute-start | bytes 393224 | tf_op jit(solution)/shard_map/ppermute | solution.py:427
  140.9 22.5 %collective-permute-start.19 = (f32[256,128]{1,0:T(8,128)S(1)}, f32[256,128]{1,0:T(8,128)S(1)}, u32[]{:S(2)}, u32[]{:S(2)}) collective-permute-start(f32[256,128]{1,0:T(8,128)S(1)} %get-tuple-element.64), channel_id=1, source_target_pairs={{0,24},{4,28},{8,32},{12,36},{16,40},{20,44},{24,48},{28,52},{32,5... | collective-permute-start | bytes 393224 | tf_op jit(solution)/shard_map/ppermute | solution.py:427
  143.0 20.3 %collective-permute-start.20 = (f32[256,128]{1,0:T(8,128)S(1)}, f32[256,128]{1,0:T(8,128)S(1)}, u32[]{:S(2)}, u32[]{:S(2)}) collective-permute-start(f32[256,128]{1,0:T(8,128)S(1)} %get-tuple-element.65), channel_id=1, source_target_pairs={{0,32},{4,36},{8,40},{12,44},{16,48},{20,52},{24,56},{28,60},{32,0... | collective-permute-start | bytes 393224 | tf_op jit(solution)/shard_map/ppermute | solution.py:427
  146.3 17.0 %collective-permute-start.21 = (f32[256,128]{1,0:T(8,128)S(1)}, f32[256,128]{1,0:T(8,128)S(1)}, u32[]{:S(2)}, u32[]{:S(2)}) collective-permute-start(f32[256,128]{1,0:T(8,128)S(1)} %get-tuple-element.66), channel_id=1, source_target_pairs={{0,40},{4,44},{8,48},{12,52},{16,56},{20,60},{24,0},{28,4},{32,8},... | collective-permute-start | bytes 393224 | tf_op jit(solution)/shard_map/ppermute | solution.py:427
  148.5 19.0 %collective-permute-start.22 = (f32[256,128]{1,0:T(8,128)S(1)}, f32[256,128]{1,0:T(8,128)S(1)}, u32[]{:S(2)}, u32[]{:S(2)}) collective-permute-start(f32[256,128]{1,0:T(8,128)S(1)} %get-tuple-element.67), channel_id=1, source_target_pairs={{0,48},{4,52},{8,56},{12,60},{16,0},{20,4},{24,8},{28,12},{32,16},... | collective-permute-start | bytes 393224 | tf_op jit(solution)/shard_map/ppermute | solution.py:427
  149.0 21.2 %collective-permute-start.23 = (f32[256,128]{1,0:T(8,128)S(1)}, f32[256,128]{1,0:T(8,128)S(1)}, u32[]{:S(2)}, u32[]{:S(2)}) collective-permute-start(f32[256,128]{1,0:T(8,128)S(1)} %get-tuple-element.68), channel_id=1, source_target_pairs={{0,56},{4,60},{8,0},{12,4},{16,8},{20,12},{24,16},{28,20},{32,24},... | collective-permute-start | bytes 393224 | tf_op jit(solution)/shard_map/ppermute | solution.py:427
  174.2 10.3 %collective-permute-start.27 = (f32[256,128]{1,0:T(8,128)S(1)}, f32[256,128]{1,0:T(8,128)S(1)}, u32[]{:S(2)}, u32[]{:S(2)}) collective-permute-start(f32[256,128]{1,0:T(8,128)S(1)} %get-tuple-element.73), channel_id=1, source_target_pairs={{0,128},{4,132},{8,136},{12,140},{16,144},{20,148},{24,152},{28,15... | collective-permute-start | bytes 393224 | tf_op jit(solution)/shard_map/ppermute | solution.py:450
  175.8 11.8 %collective-permute-start.28 = (f32[256,128]{1,0:T(8,128)S(1)}, f32[256,128]{1,0:T(8,128)S(1)}, u32[]{:S(2)}, u32[]{:S(2)}) collective-permute-start(f32[256,128]{1,0:T(8,128)S(1)} %get-tuple-element.74), channel_id=1, source_target_pairs={{0,132},{4,128},{8,140},{12,136},{16,148},{20,144},{24,156},{28,15... | collective-permute-start | bytes 393224 | tf_op jit(solution)/shard_map/ppermute | solution.py:450
  177.5 10.1 %collective-permute-start.29 = (f32[256,128]{1,0:T(8,128)S(1)}, f32[256,128]{1,0:T(8,128)S(1)}, u32[]{:S(2)}, u32[]{:S(2)}) collective-permute-start(f32[256,128]{1,0:T(8,128)S(1)} %get-tuple-element.75), channel_id=1, source_target_pairs={{0,192},{4,196},{8,200},{12,204},{16,208},{20,212},{24,216},{28,22... | collective-permute-start | bytes 393224 | tf_op jit(solution)/shard_map/ppermute | solution.py:450
  (14 other events, 91.5 us)

commit v11 on v10

--- a/solution.py
+++ b/solution.py
@@ -229,35 +229,39 @@
 GROUP = NZ * NC
 
 
-def split_kernel(pos_ref, s_ref, *refs):
-    o_refs, sem = refs[: NZ + NX], refs[NZ + NX]
-    x, z = pos_ref[0], pos_ref[1]
-    copies = []
-    for dz in range(NZ):
-        field = pl.multiple_of(((z + dz) % NZ) * 8, 8)
-        source = s_ref.at[:, pl.ds(field, 8), pl.ds(0, LANES)]
-        copies.append(pltpu.make_async_copy(source, o_refs[dz], sem.at[dz]))
-    for dx in range(NX):
-        field = pl.multiple_of(((x + dx) % NX) * GROUP, GROUP)
-        source = s_ref.at[:, pl.ds(field, GROUP), pl.ds(LANES, LANES)]
-        copies.append(pltpu.make_async_copy(source, o_refs[NZ + dx], sem.at[NZ + dx]))
+def start_and_wait(pairs, sem):
+    copies = [pltpu.make_async_copy(source, target, sem.at[i]) for i, (source, target) in enumerate(pairs)]
     for copy in copies:
         copy.start()
     for copy in copies:
         copy.wait()
 
 
-def split(pos, state):
-    out = pl.pallas_call(
-        split_kernel,
+def split_z_kernel(pos_ref, s_ref, *refs):
+    pairs = []
+    for dz in range(NZ):
+        field = pl.multiple_of(((pos_ref[1] + dz) % NZ) * 8, 8)
+        pairs.append((s_ref.at[:, pl.ds(field, 8), pl.ds(0, LANES)], refs[dz]))
+    start_and_wait(pairs, refs[NZ])
+
+
+def split_x_kernel(pos_ref, s_ref, *refs):
+    pairs = []
+    for dx in range(NX):
+        field = pl.multiple_of(((pos_ref[0] + dx) % NX) * GROUP, GROUP)
+        pairs.append((s_ref.at[:, pl.ds(field, GROUP), pl.ds(LANES, LANES)], refs[dx]))
+    start_and_wait(pairs, refs[NX])
+
+
+def split(pos, state, kernel, count, fields):
+    return pl.pallas_call(
+        kernel,
         in_specs=[SMEM, HBM],
-        out_specs=[VMEM] * (NZ + NX),
-        out_shape=[vmem(LON, 8, LANES)] * NZ + [vmem(LON, GROUP, LANES)] * NX,
-        scratch_shapes=[pltpu.SemaphoreType.DMA((NZ + NX,))],
-        compiler_params=PARAMS,
-        name="split",
+        out_specs=[VMEM] * count,
+        out_shape=[vmem(LON, fields, LANES)] * count,
+        scratch_shapes=[pltpu.SemaphoreType.DMA((count,))],
+        compiler_params=PARAMS,
     )(pos, pltpu.with_memory_space_constraint(state, pltpu.HBM))
-    return out[:NZ], out[NZ:]
 
 
 def spread_x_kernel(pos_ref, *refs):
@@ -360,8 +364,7 @@
 ]
 
 
-def store_p_kernel(pos_ref, prior_ref, *refs):
-    del prior_ref
+def store_p_kernel(pos_ref, *refs):
     q_refs, o_ref = refs[:8], refs[8]
     x_ref, buf_ref, sem = refs[9:]
     x, c = pos_ref[0], pos_ref[2]
@@ -374,20 +377,21 @@
     store_half(x_ref, buf_ref, o_ref, sem, 0)
 
 
-def store_p(pos, prior, blocks):
+def store_p(pos, blocks):
     return pl.pallas_call(
         store_p_kernel,
-        in_specs=[SMEM, HBM] + [VMEM] * 8,
+        in_specs=[SMEM] + [VMEM] * 8,
         out_specs=HBM,
         out_shape=f32(KEPT, FIELDS, 2 * LANES),
         scratch_shapes=STORE_SCRATCH,
-        input_output_aliases={1: 0},
         compiler_params=PARAMS,
         name="store_p",
-    )(pos, prior, *blocks)
-
-
-def store_a_kernel(q_ref, o_ref, x_ref, buf_ref, sem):
+    )(pos, *blocks)
+
+
+def store_a_kernel(prior_ref, q_ref, o_ref, x_ref, buf_ref, sem):
+    del prior_ref
+
     def field(f, carry):
         x_ref[pl.ds(pl.multiple_of(f * PAD_K, 8), KEPT), :] = q_ref[f]
         return carry
@@ -396,16 +400,17 @@
     store_half(x_ref, buf_ref, o_ref, sem, LANES)
 
 
-def store_a(shares):
+def store_a(prior, shares):
     return pl.pallas_call(
         store_a_kernel,
-        in_specs=[VMEM],
+        in_specs=[HBM, VMEM],
         out_specs=HBM,
         out_shape=f32(KEPT, FIELDS, 2 * LANES),
         scratch_shapes=STORE_SCRATCH,
+        input_output_aliases={0: 0},
         compiler_params=PARAMS,
         name="store_a",
-    )(shares)
+    )(prior, shares)
 
 
 def shifts(dx, dz, dc):
@@ -455,8 +460,9 @@
     device = lax.axis_index("lon")
     pos = jnp.stack([device // (NZ * NC), (device // NC) % NZ, device % NC]).astype(jnp.int32)
     wh, wl = twiddle_matrices(1.0 / math.sqrt(NLON))
-    pieces, parts = split(pos, state)
+    pieces = split(pos, state, split_z_kernel, NZ, 8)
     pieces = exchange_z(pieces)
+    parts = split(pos, state, split_x_kernel, NX, GROUP)
     parts = exchange_x(parts)
     sent = spread_a(pos, [b.reshape(LON * GROUP, LANES) for b in parts])
     gathered = lax.all_to_all(
@@ -470,8 +476,8 @@
     shares = lax.all_to_all(spectrum, "lon", split_axis=0, concat_axis=0, tiled=True)
     pieces = spread_out(pos, pieces)
     pieces = exchange_xc(pieces)
-    out = store_a(shares)
-    out = store_p(pos, out, pieces)
+    out = store_p(pos, pieces)
+    out = store_a(out, shares)
     return out.reshape(2, RADIX, FIELDS, 2 * LANES)
 
 

time: 192 us -> 187 us (0.974)
  local copies, waits for them, and re-layouts: 2.6 us -> 0 us
  starting transfers between devices: 70.4 us -> 68.3 us
    ppermute x14, waiting for transfers between devices: 52.1 us -> 48.8 us  [exchange_z(): out[dz] = lax.ppermute(blocks[dz], 'lon', shifts(0, dz, 0))]
    ppermute x14, starting transfers between devices: 20.2 us -> 17 us  [exchange_xc(): lax.ppermute(blocks[dx * NC + dc], 'lon', shifts(dx, 0, dc))]
    unnamed x10 -> x0, local copies, waits for them, and re-layouts: 2.6 us -> none
    pallas_call x3 -> x4, Pallas kernels: 5.09 us -> 6.51 us  [the longest x2 3.72 us: split(): pl.pallas_call(kernel, in_specs=[SMEM, HBM], out_specs=[VMEM] * count, ou...]
  transfers between devices with their start and end apart: 33 -> 33, of which waited for: 16 -> 16; matrix products, arithmetic and copies ran while one was open for 2% -> 2% of each run, Pallas kernels for 2% -> 4%
where the time goes in v11:
time: 187 us
  waiting for transfers between devices  101 us (54%)
  starting transfers between devices  68.3 us (37%)
  Pallas kernels  13.8 us (7%)
  other arithmetic  3.31 us (2%)
    ppermute x14, waiting for transfers between devices, exchange_z(): out[dz] = lax.ppermute(blocks[dz], 'lon', shifts(0, dz, 0))  48.8 us
    ppermute x14, starting transfers between devices, exchange_z(): out[dz] = lax.ppermute(blocks[dz], 'lon', shifts(0, dz, 0))  29.5 us
    all_to_all x1, waiting for transfers between devices, local(): lax.all_to_all(sent, 'lon', split_axis=0, concat_axis=0, axis_index_group...  24.7 us
    ppermute x14, waiting for transfers between devices, exchange_xc(): lax.ppermute(blocks[dx * NC + dc], 'lon', shifts(dx, 0, dc))  17.3 us
    ppermute x14, starting transfers between devices, exchange_xc(): lax.ppermute(blocks[dx * NC + dc], 'lon', shifts(dx, 0, dc))  17 us
    ppermute x3, waiting for transfers between devices, exchange_x(): out[dx] = lax.ppermute(blocks[dx], 'lon', shifts(dx, 0, 0))  10.2 us
    all_to_all x1, starting transfers between devices, local(): lax.all_to_all(sent, 'lon', split_axis=0, concat_axis=0, axis_index_group...  10 us
    all_to_all x1, starting transfers between devices, local(): lax.all_to_all(spectrum, 'lon', split_axis=0, concat_axis=0, tiled=True)  6.08 us
  transfers between devices with their start and end apart: 33, of which 16 were waited for; matrix products, arithmetic and copies ran while one was open for 2% of the time, Pallas kernels for 4%

profile of v11, /device:TPU:1, one launch (start us, length us, event | category | flops | bytes accessed | tf_op | source)
XLA Modules:
  0.0 186.7 jit_solution(4181430920365203060)
XLA Ops:
  4.0 2.5 %collective-permute-start.29 = (f32[32,16,128]{2,1,0:T(8,128)S(1)}, f32[32,16,128]{2,1,0:T(8,128)S(1)}, u32[]{:S(2)}, u32[]{:S(2)}) collective-permute-start(f32[32,16,128]{2,1,0:T(8,128)S(1)} %get-tuple-element.75), channel_id=1, source_target_pairs={{0,128},{4,132},{8,136},{12,140},{16,144},{20,148},{24,152},{28,15... | collective-permute-start | bytes 786440 | tf_op jit(solution)/shard_map/ppermute | solution.py:444
  9.0 8.8 %collective-permute-done.29 = f32[32,16,128]{2,1,0:T(8,128)S(1)} collective-permute-done((f32[32,16,128]{2,1,0:T(8,128)S(1)}, f32[32,16,128]{2,1,0:T(8,128)S(1)}, u32[]{:S(2)}, u32[]{:S(2)}) %collective-permute-start.29) | collective-permute-done | bytes 262176 | tf_op jit(solution)/shard_map/ppermute | solution.py:444
  19.4 10.0 %all-to-all-start = ((f32[16,128,128]{2,1,0:T(8,128)}), f32[16,128,128]{2,1,0:T(8,128)S(1)}, u32[]{:S(2)}, u32[]{:S(2)}) async-start(f32[16,128,128]{2,1,0:T(8,128)} %spread_a.1), calls=%async_computation | async-start | bytes 2097152 | tf_op jit(solution)/shard_map/all_to_all | solution.py:468
  29.5 2.5 %select_select_fusion.1 = (f32[8,2,64,128]{3,2,1,0:T(8,128)S(1)}, f32[8,2,64,128]{3,2,1,0:T(8,128)S(1)}, f32[8,2,64,128]{3,2,1,0:T(8,128)S(1)}, f32[8,2,64,128]{3,2,1,0:T(8,128)S(1)}) fusion(pred[2]{0:T(512)(128)(4,1)S(1)} %iota_compare_fusion.1, pred[8]{0:T(512)(128)(4,1)S(1)} %iota_compare_fusion, s32[64]{0:T(128)S(1)} %iota_multiply_fusion, ...), kind=kLoop, calls=%fused_computation.9 | loop fusion | flops 4456448 | bytes 2097450 | tf_op jit(solution)/shard_map/jit(_where)/select_n | solution.py:60
  32.7 24.7 %all-to-all-done = f32[16,128,128]{2,1,0:T(8,128)S(1)} async-done(((f32[16,128,128]{2,1,0:T(8,128)}), f32[16,128,128]{2,1,0:T(8,128)S(1)}, u32[]{:S(2)}, u32[]{:S(2)}) %all-to-all-start) | async-done | bytes 1048608 | tf_op jit(solution)/shard_map/all_to_all | solution.py:468
  59.6 6.1 %all-to-all-start.1 = ((f32[64,32,128]{2,1,0:T(8,128)}), f32[64,32,128]{2,1,0:T(8,128)S(1)}, u32[]{:S(2)}, u32[]{:S(2)}) async-start(f32[64,32,128]{2,1,0:T(8,128)} %fft_a.1), calls=%async_computation.1 | async-start | bytes 2097152 | tf_op jit(solution)/shard_map/all_to_all | solution.py:476
  67.6 2.6 %collective-permute-start.6 = (f32[32,8,128]{2,1,0:T(8,128)S(1)}, f32[32,8,128]{2,1,0:T(8,128)S(1)}, u32[]{:S(2)}, u32[]{:S(2)}) collective-permute-start(f32[32,8,128]{2,1,0:T(8,128)S(1)} %get-tuple-element.48), channel_id=1, source_target_pairs={{0,56},{4,60},{8,0},{12,4},{16,8},{20,12},{24,16},{28,20},{32,24},... | collective-permute-start | bytes 393224 | tf_op jit(solution)/shard_map/ppermute | solution.py:432
  71.4 3.3 %collective-permute-start.2 = (f32[32,8,128]{2,1,0:T(8,128)S(1)}, f32[32,8,128]{2,1,0:T(8,128)S(1)}, u32[]{:S(2)}, u32[]{:S(2)}) collective-permute-start(f32[32,8,128]{2,1,0:T(8,128)S(1)} %get-tuple-element.44), channel_id=1, source_target_pairs={{0,24},{4,28},{8,32},{12,36},{16,40},{20,44},{24,48},{28,52},{32,5... | collective-permute-start | bytes 393224 | tf_op jit(solution)/shard_map/ppermute | solution.py:432
  75.9 16.9 %collective-permute-done.6 = f32[32,8,128]{2,1,0:T(8,128)S(1)} collective-permute-done((f32[32,8,128]{2,1,0:T(8,128)S(1)}, f32[32,8,128]{2,1,0:T(8,128)S(1)}, u32[]{:S(2)}, u32[]{:S(2)}) %collective-permute-start.6) | collective-permute-done | bytes 131104 | tf_op jit(solution)/shard_map/ppermute | solution.py:432
  92.9 3.6 %collective-permute-start.4 = (f32[32,8,128]{2,1,0:T(8,128)S(1)}, f32[32,8,128]{2,1,0:T(8,128)S(1)}, u32[]{:S(2)}, u32[]{:S(2)}) collective-permute-start(f32[32,8,128]{2,1,0:T(8,128)S(1)} %get-tuple-element.46), channel_id=1, source_target_pairs={{0,40},{4,44},{8,48},{12,52},{16,56},{20,60},{24,0},{28,4},{32,8},... | collective-permute-start | bytes 393224 | tf_op jit(solution)/shard_map/ppermute | solution.py:432
  96.5 3.4 %collective-permute-start.5 = (f32[32,8,128]{2,1,0:T(8,128)S(1)}, f32[32,8,128]{2,1,0:T(8,128)S(1)}, u32[]{:S(2)}, u32[]{:S(2)}) collective-permute-start(f32[32,8,128]{2,1,0:T(8,128)S(1)} %get-tuple-element.47), channel_id=1, source_target_pairs={{0,48},{4,52},{8,56},{12,60},{16,0},{20,4},{24,8},{28,12},{32,16},... | collective-permute-start | bytes 393224 | tf_op jit(solution)/shard_map/ppermute | solution.py:432
  99.9 10.2 %collective-permute-done.2 = f32[32,8,128]{2,1,0:T(8,128)S(1)} collective-permute-done((f32[32,8,128]{2,1,0:T(8,128)S(1)}, f32[32,8,128]{2,1,0:T(8,128)S(1)}, u32[]{:S(2)}, u32[]{:S(2)}) %collective-permute-start.2) | collective-permute-done | bytes 131104 | tf_op jit(solution)/shard_map/ppermute | solution.py:432
  110.1 4.9 %collective-permute-done.3 = f32[32,8,128]{2,1,0:T(8,128)S(1)} collective-permute-done((f32[32,8,128]{2,1,0:T(8,128)S(1)}, f32[32,8,128]{2,1,0:T(8,128)S(1)}, u32[]{:S(2)}, u32[]{:S(2)}) %collective-permute-start.3) | collective-permute-done | bytes 131104 | tf_op jit(solution)/shard_map/ppermute | solution.py:432
  115.9 2.9 %collective-permute-start.10 = (f32[256,128]{1,0:T(8,128)S(1)}, f32[256,128]{1,0:T(8,128)S(1)}, u32[]{:S(2)}, u32[]{:S(2)}) collective-permute-start(f32[256,128]{1,0:T(8,128)S(1)} %get-tuple-element.53), channel_id=1, source_target_pairs={{0,128},{4,132},{8,136},{12,140},{16,144},{20,148},{24,152},{28,15... | collective-permute-start | bytes 393224 | tf_op jit(solution)/shard_map/ppermute | solution.py:455
  118.7 2.8 %collective-permute-start.11 = (f32[256,128]{1,0:T(8,128)S(1)}, f32[256,128]{1,0:T(8,128)S(1)}, u32[]{:S(2)}, u32[]{:S(2)}) collective-permute-start(f32[256,128]{1,0:T(8,128)S(1)} %get-tuple-element.54), channel_id=1, source_target_pairs={{0,132},{4,128},{8,140},{12,136},{16,148},{20,144},{24,156},{28,15... | collective-permute-start | bytes 393224 | tf_op jit(solution)/shard_map/ppermute | solution.py:455
  124.2 3.2 %collective-permute-done.11.refs_5_ = f32[256,128]{1,0:T(8,128)S(1)} collective-permute-done((f32[256,128]{1,0:T(8,128)S(1)}, f32[256,128]{1,0:T(8,128)S(1)}, u32[]{:S(2)}, u32[]{:S(2)}) %collective-permute-start.11) | collective-permute-done | bytes 131104 | tf_op jit(solution)/shard_map/ppermute | solution.py:455
  127.8 3.8 %collective-permute-done.13.refs_7_ = f32[256,128]{1,0:T(8,128)S(1)} collective-permute-done((f32[256,128]{1,0:T(8,128)S(1)}, f32[256,128]{1,0:T(8,128)S(1)}, u32[]{:S(2)}, u32[]{:S(2)}) %collective-permute-start.13) | collective-permute-done | bytes 131104 | tf_op jit(solution)/shard_map/ppermute | solution.py:455
  139.8 3.3 %collective-permute-start.17 = (f32[256,128]{1,0:T(8,128)S(1)}, f32[256,128]{1,0:T(8,128)S(1)}, u32[]{:S(2)}, u32[]{:S(2)}) collective-permute-start(f32[256,128]{1,0:T(8,128)S(1)} %get-tuple-element.61), channel_id=1, source_target_pairs={{0,32},{4,36},{8,40},{12,44},{16,48},{20,52},{24,56},{28,60},{32,0... | collective-permute-start | bytes 393224 | tf_op jit(solution)/shard_map/ppermute | solution.py:432
  145.5 5.7 %collective-permute-start.20 = (f32[256,128]{1,0:T(8,128)S(1)}, f32[256,128]{1,0:T(8,128)S(1)}, u32[]{:S(2)}, u32[]{:S(2)}) collective-permute-start(f32[256,128]{1,0:T(8,128)S(1)} %get-tuple-element.64), channel_id=1, source_target_pairs={{0,56},{4,60},{8,0},{12,4},{16,8},{20,12},{24,16},{28,20},{32,24},... | collective-permute-start | bytes 393224 | tf_op jit(solution)/shard_map/ppermute | solution.py:432
  151.2 8.1 %collective-permute-done.16.refs_3_ = f32[256,128]{1,0:T(8,128)S(1)} collective-permute-done((f32[256,128]{1,0:T(8,128)S(1)}, f32[256,128]{1,0:T(8,128)S(1)}, u32[]{:S(2)}, u32[]{:S(2)}) %collective-permute-start.16) | collective-permute-done | bytes 131104 | tf_op jit(solution)/shard_map/ppermute | solution.py:432
  159.3 4.6 %collective-permute-done.19.refs_6_ = f32[256,128]{1,0:T(8,128)S(1)} collective-permute-done((f32[256,128]{1,0:T(8,128)S(1)}, f32[256,128]{1,0:T(8,128)S(1)}, u32[]{:S(2)}, u32[]{:S(2)}) %collective-permute-start.19) | collective-permute-done | bytes 131104 | tf_op jit(solution)/shard_map/ppermute | solution.py:432
  163.9 2.8 %collective-permute-done.20.refs_7_ = f32[256,128]{1,0:T(8,128)S(1)} collective-permute-done((f32[256,128]{1,0:T(8,128)S(1)}, f32[256,128]{1,0:T(8,128)S(1)}, u32[]{:S(2)}, u32[]{:S(2)}) %collective-permute-start.20) | collective-permute-done | bytes 131104 | tf_op jit(solution)/shard_map/ppermute | solution.py:432
  169.2 3.1 %collective-permute-start.24 = (f32[256,128]{1,0:T(8,128)S(1)}, f32[256,128]{1,0:T(8,128)S(1)}, u32[]{:S(2)}, u32[]{:S(2)}) collective-permute-start(f32[256,128]{1,0:T(8,128)S(1)} %get-tuple-element.69), channel_id=1, source_target_pairs={{0,128},{4,132},{8,136},{12,140},{16,144},{20,148},{24,152},{28,15... | collective-permute-start | bytes 393224 | tf_op jit(solution)/shard_map/ppermute | solution.py:455
  176.1 6.9 %collective-permute-done.23.refs_3_ = f32[256,128]{1,0:T(8,128)S(1)} collective-permute-done((f32[256,128]{1,0:T(8,128)S(1)}, f32[256,128]{1,0:T(8,128)S(1)}, u32[]{:S(2)}, u32[]{:S(2)}) %collective-permute-start.23) | collective-permute-done | bytes 131104 | tf_op jit(solution)/shard_map/ppermute | solution.py:455
  (60 shorter events, 39.6 us)
Async XLA Ops:
  4.0 13.8 %collective-permute-start.29 = (f32[32,16,128]{2,1,0:T(8,128)S(1)}, f32[32,16,128]{2,1,0:T(8,128)S(1)}, u32[]{:S(2)}, u32[]{:S(2)}) collective-permute-start(f32[32,16,128]{2,1,0:T(8,128)S(1)} %get-tuple-element.75), channel_id=1, source_target_pairs={{0,128},{4,132},{8,136},{12,140},{16,144},{20,148},{24,152},{28,15... | collective-permute-start | bytes 786440 | tf_op jit(solution)/shard_map/ppermute | solution.py:444
  6.4 11.3 %collective-permute-start.30 = (f32[32,16,128]{2,1,0:T(8,128)S(1)}, f32[32,16,128]{2,1,0:T(8,128)S(1)}, u32[]{:S(2)}, u32[]{:S(2)}) collective-permute-start(f32[32,16,128]{2,1,0:T(8,128)S(1)} %get-tuple-element.76), channel_id=1, source_target_pairs={{0,192},{4,196},{8,200},{12,204},{16,208},{20,212},{24,216},{28,22... | collective-permute-start | bytes 786440 | tf_op jit(solution)/shard_map/ppermute | solution.py:444
  19.4 38.0 %all-to-all-start = ((f32[16,128,128]{2,1,0:T(8,128)}), f32[16,128,128]{2,1,0:T(8,128)S(1)}, u32[]{:S(2)}, u32[]{:S(2)}) async-start(f32[16,128,128]{2,1,0:T(8,128)} %spread_a.1), calls=%async_computation | async-start | bytes 2097152 | tf_op jit(solution)/shard_map/all_to_all | solution.py:468
  59.6 125.8 %all-to-all-start.1 = ((f32[64,32,128]{2,1,0:T(8,128)}), f32[64,32,128]{2,1,0:T(8,128)S(1)}, u32[]{:S(2)}, u32[]{:S(2)}) async-start(f32[64,32,128]{2,1,0:T(8,128)} %fft_a.1), calls=%async_computation.1 | async-start | bytes 2097152 | tf_op jit(solution)/shard_map/all_to_all | solution.py:476
  67.6 25.2 %collective-permute-start.6 = (f32[32,8,128]{2,1,0:T(8,128)S(1)}, f32[32,8,128]{2,1,0:T(8,128)S(1)}, u32[]{:S(2)}, u32[]{:S(2)}) collective-permute-start(f32[32,8,128]{2,1,0:T(8,128)S(1)} %get-tuple-element.48), channel_id=1, source_target_pairs={{0,56},{4,60},{8,0},{12,4},{16,8},{20,12},{24,16},{28,20},{32,24},... | collective-permute-start | bytes 393224 | tf_op jit(solution)/shard_map/ppermute | solution.py:432
  70.3 26.2 %collective-permute-start = (f32[32,8,128]{2,1,0:T(8,128)S(1)}, f32[32,8,128]{2,1,0:T(8,128)S(1)}, u32[]{:S(2)}, u32[]{:S(2)}) collective-permute-start(f32[32,8,128]{2,1,0:T(8,128)S(1)} %get-tuple-element.42), channel_id=1, source_target_pairs={{0,8},{4,12},{8,16},{12,20},{16,24},{20,28},{24,32},{28,36},{32,40... | collective-permute-start | bytes 393224 | tf_op jit(solution)/shard_map/ppermute | solution.py:432
  70.3 29.7 %collective-permute-start.1 = (f32[32,8,128]{2,1,0:T(8,128)S(1)}, f32[32,8,128]{2,1,0:T(8,128)S(1)}, u32[]{:S(2)}, u32[]{:S(2)}) collective-permute-start(f32[32,8,128]{2,1,0:T(8,128)S(1)} %get-tuple-element.43), channel_id=1, source_target_pairs={{0,16},{4,20},{8,24},{12,28},{16,32},{20,36},{24,40},{28,44},{32,4... | collective-permute-start | bytes 393224 | tf_op jit(solution)/shard_map/ppermute | solution.py:432
  71.4 38.7 %collective-permute-start.2 = (f32[32,8,128]{2,1,0:T(8,128)S(1)}, f32[32,8,128]{2,1,0:T(8,128)S(1)}, u32[]{:S(2)}, u32[]{:S(2)}) collective-permute-start(f32[32,8,128]{2,1,0:T(8,128)S(1)} %get-tuple-element.44), channel_id=1, source_target_pairs={{0,24},{4,28},{8,32},{12,36},{16,40},{20,44},{24,48},{28,52},{32,5... | collective-permute-start | bytes 393224 | tf_op jit(solution)/shard_map/ppermute | solution.py:432
  74.7 40.3 %collective-permute-start.3 = (f32[32,8,128]{2,1,0:T(8,128)S(1)}, f32[32,8,128]{2,1,0:T(8,128)S(1)}, u32[]{:S(2)}, u32[]{:S(2)}) collective-permute-start(f32[32,8,128]{2,1,0:T(8,128)S(1)} %get-tuple-element.45), channel_id=1, source_target_pairs={{0,32},{4,36},{8,40},{12,44},{16,48},{20,52},{24,56},{28,60},{32,0... | collective-permute-start | bytes 393224 | tf_op jit(solution)/shard_map/ppermute | solution.py:432
  92.9 22.2 %collective-permute-start.4 = (f32[32,8,128]{2,1,0:T(8,128)S(1)}, f32[32,8,128]{2,1,0:T(8,128)S(1)}, u32[]{:S(2)}, u32[]{:S(2)}) collective-permute-start(f32[32,8,128]{2,1,0:T(8,128)S(1)} %get-tuple-element.46), channel_id=1, source_target_pairs={{0,40},{4,44},{8,48},{12,52},{16,56},{20,60},{24,0},{28,4},{32,8},... | collective-permute-start | bytes 393224 | tf_op jit(solution)/shard_map/ppermute | solution.py:432
  96.5 18.5 %collective-permute-start.5 = (f32[32,8,128]{2,1,0:T(8,128)S(1)}, f32[32,8,128]{2,1,0:T(8,128)S(1)}, u32[]{:S(2)}, u32[]{:S(2)}) collective-permute-start(f32[32,8,128]{2,1,0:T(8,128)S(1)} %get-tuple-element.47), channel_id=1, source_target_pairs={{0,48},{4,52},{8,56},{12,60},{16,0},{20,4},{24,8},{28,12},{32,16},... | collective-permute-start | bytes 393224 | tf_op jit(solution)/shard_map/ppermute | solution.py:432
  122.3 9.3 %collective-permute-start.13 = (f32[256,128]{1,0:T(8,128)S(1)}, f32[256,128]{1,0:T(8,128)S(1)}, u32[]{:S(2)}, u32[]{:S(2)}) collective-permute-start(f32[256,128]{1,0:T(8,128)S(1)} %get-tuple-element.56), channel_id=1, source_target_pairs={{0,196},{4,192},{8,204},{12,200},{16,212},{20,208},{24,220},{28,21... | collective-permute-start | bytes 393224 | tf_op jit(solution)/shard_map/ppermute | solution.py:455
  135.8 9.6 %collective-permute-start.14 = (f32[256,128]{1,0:T(8,128)S(1)}, f32[256,128]{1,0:T(8,128)S(1)}, u32[]{:S(2)}, u32[]{:S(2)}) collective-permute-start(f32[256,128]{1,0:T(8,128)S(1)} %get-tuple-element.58), channel_id=1, source_target_pairs={{0,8},{4,12},{8,16},{12,20},{16,24},{20,28},{24,32},{28,36},{32,40... | collective-permute-start | bytes 393224 | tf_op jit(solution)/shard_map/ppermute | solution.py:432
  135.9 9.6 %collective-permute-start.15 = (f32[256,128]{1,0:T(8,128)S(1)}, f32[256,128]{1,0:T(8,128)S(1)}, u32[]{:S(2)}, u32[]{:S(2)}) collective-permute-start(f32[256,128]{1,0:T(8,128)S(1)} %get-tuple-element.59), channel_id=1, source_target_pairs={{0,16},{4,20},{8,24},{12,28},{16,32},{20,36},{24,40},{28,44},{32,4... | collective-permute-start | bytes 393224 | tf_op jit(solution)/shard_map/ppermute | solution.py:432
  137.5 21.8 %collective-permute-start.16 = (f32[256,128]{1,0:T(8,128)S(1)}, f32[256,128]{1,0:T(8,128)S(1)}, u32[]{:S(2)}, u32[]{:S(2)}) collective-permute-start(f32[256,128]{1,0:T(8,128)S(1)} %get-tuple-element.60), channel_id=1, source_target_pairs={{0,24},{4,28},{8,32},{12,36},{16,40},{20,44},{24,48},{28,52},{32,5... | collective-permute-start | bytes 393224 | tf_op jit(solution)/shard_map/ppermute | solution.py:432
  139.8 19.6 %collective-permute-start.17 = (f32[256,128]{1,0:T(8,128)S(1)}, f32[256,128]{1,0:T(8,128)S(1)}, u32[]{:S(2)}, u32[]{:S(2)}) collective-permute-start(f32[256,128]{1,0:T(8,128)S(1)} %get-tuple-element.61), channel_id=1, source_target_pairs={{0,32},{4,36},{8,40},{12,44},{16,48},{20,52},{24,56},{28,60},{32,0... | collective-permute-start | bytes 393224 | tf_op jit(solution)/shard_map/ppermute | solution.py:432
  143.1 16.3 %collective-permute-start.18 = (f32[256,128]{1,0:T(8,128)S(1)}, f32[256,128]{1,0:T(8,128)S(1)}, u32[]{:S(2)}, u32[]{:S(2)}) collective-permute-start(f32[256,128]{1,0:T(8,128)S(1)} %get-tuple-element.62), channel_id=1, source_target_pairs={{0,40},{4,44},{8,48},{12,52},{16,56},{20,60},{24,0},{28,4},{32,8},... | collective-permute-start | bytes 393224 | tf_op jit(solution)/shard_map/ppermute | solution.py:432
  145.3 18.5 %collective-permute-start.19 = (f32[256,128]{1,0:T(8,128)S(1)}, f32[256,128]{1,0:T(8,128)S(1)}, u32[]{:S(2)}, u32[]{:S(2)}) collective-permute-start(f32[256,128]{1,0:T(8,128)S(1)} %get-tuple-element.63), channel_id=1, source_target_pairs={{0,48},{4,52},{8,56},{12,60},{16,0},{20,4},{24,8},{28,12},{32,16},... | collective-permute-start | bytes 393224 | tf_op jit(solution)/shard_map/ppermute | solution.py:432
  145.5 21.3 %collective-permute-start.20 = (f32[256,128]{1,0:T(8,128)S(1)}, f32[256,128]{1,0:T(8,128)S(1)}, u32[]{:S(2)}, u32[]{:S(2)}) collective-permute-start(f32[256,128]{1,0:T(8,128)S(1)} %get-tuple-element.64), channel_id=1, source_target_pairs={{0,56},{4,60},{8,0},{12,4},{16,8},{20,12},{24,16},{28,20},{32,24},... | collective-permute-start | bytes 393224 | tf_op jit(solution)/shard_map/ppermute | solution.py:432
  168.2 14.9 %collective-permute-start.23 = (f32[256,128]{1,0:T(8,128)S(1)}, f32[256,128]{1,0:T(8,128)S(1)}, u32[]{:S(2)}, u32[]{:S(2)}) collective-permute-start(f32[256,128]{1,0:T(8,128)S(1)} %get-tuple-element.68), channel_id=1, source_target_pairs={{0,68},{4,64},{8,76},{12,72},{16,84},{20,80},{24,92},{28,88},{32,1... | collective-permute-start | bytes 393224 | tf_op jit(solution)/shard_map/ppermute | solution.py:455
  169.2 13.8 %collective-permute-start.24 = (f32[256,128]{1,0:T(8,128)S(1)}, f32[256,128]{1,0:T(8,128)S(1)}, u32[]{:S(2)}, u32[]{:S(2)}) collective-permute-start(f32[256,128]{1,0:T(8,128)S(1)} %get-tuple-element.69), channel_id=1, source_target_pairs={{0,128},{4,132},{8,136},{12,140},{16,144},{20,148},{24,152},{28,15... | collective-permute-start | bytes 393224 | tf_op jit(solution)/shard_map/ppermute | solution.py:455
  172.3 10.8 %collective-permute-start.25 = (f32[256,128]{1,0:T(8,128)S(1)}, f32[256,128]{1,0:T(8,128)S(1)}, u32[]{:S(2)}, u32[]{:S(2)}) collective-permute-start(f32[256,128]{1,0:T(8,128)S(1)} %get-tuple-element.70), channel_id=1, source_target_pairs={{0,132},{4,128},{8,140},{12,136},{16,148},{20,144},{24,156},{28,15... | collective-permute-start | bytes 393224 | tf_op jit(solution)/shard_map/ppermute | solution.py:455
  172.5 10.6 %collective-permute-start.26 = (f32[256,128]{1,0:T(8,128)S(1)}, f32[256,128]{1,0:T(8,128)S(1)}, u32[]{:S(2)}, u32[]{:S(2)}) collective-permute-start(f32[256,128]{1,0:T(8,128)S(1)} %get-tuple-element.71), channel_id=1, source_target_pairs={{0,192},{4,196},{8,200},{12,204},{16,208},{20,212},{24,216},{28,22... | collective-permute-start | bytes 393224 | tf_op jit(solution)/shard_map/ppermute | solution.py:455
  174.4 9.3 %collective-permute-start.27 = (f32[256,128]{1,0:T(8,128)S(1)}, f32[256,128]{1,0:T(8,128)S(1)}, u32[]{:S(2)}, u32[]{:S(2)}) collective-permute-start(f32[256,128]{1,0:T(8,128)S(1)} %get-tuple-element.72), channel_id=1, source_target_pairs={{0,196},{4,192},{8,204},{12,200},{16,212},{20,208},{24,220},{28,21... | collective-permute-start | bytes 393224 | tf_op jit(solution)/shard_map/ppermute | solution.py:455
  (9 other events, 64.6 us)

commit v12 on v10

--- a/solution.py
+++ b/solution.py
@@ -417,13 +417,14 @@
     ]
 
 
-Z_ORDER = (1, 7, 4, 3, 5, 2, 6)
-
-
-def exchange_z(blocks):
+Z_IN = (1, 7, 4, 3, 5, 2, 6)
+Z_OUT = (1, 7, 2, 6, 3, 5, 4)
+
+
+def exchange_z(blocks, order):
     out = [None] * NZ
     out[0] = blocks[0]
-    for dz in Z_ORDER:
+    for dz in order:
         out[dz] = lax.ppermute(blocks[dz], "lon", shifts(0, dz, 0))
     return out
 
@@ -456,7 +457,7 @@
     pos = jnp.stack([device // (NZ * NC), (device // NC) % NZ, device % NC]).astype(jnp.int32)
     wh, wl = twiddle_matrices(1.0 / math.sqrt(NLON))
     pieces, parts = split(pos, state)
-    pieces = exchange_z(pieces)
+    pieces = exchange_z(pieces, Z_IN)
     parts = exchange_x(parts)
     sent = spread_a(pos, [b.reshape(LON * GROUP, LANES) for b in parts])
     gathered = lax.all_to_all(
@@ -465,7 +466,7 @@
     pieces = spread_x(pos, [b.reshape(LON * 8, LANES) for b in pieces])
     pieces = exchange_xc(pieces)
     pieces = fft_p(pos, pieces, wh, wl)
-    pieces = exchange_z(pieces)
+    pieces = exchange_z(pieces, Z_OUT)
     spectrum = fft_a(gathered.reshape(NLON, LANES), wh, wl)
     shares = lax.all_to_all(spectrum, "lon", split_axis=0, concat_axis=0, tiled=True)
     pieces = spread_out(pos, pieces)

time: 192 us -> 192 us (level)
  no operation moved by 1% of the time
where the time goes in v12:
time: 192 us; the launch traced here: 191 us
  waiting for transfers between devices  102 us (53%)
  starting transfers between devices  70.4 us (37%)
  Pallas kernels  12.3 us (6%)
  other arithmetic  3.34 us (2%)
  local copies, waits for them, and re-layouts  2.6 us (1%)
    ppermute x14, waiting for transfers between devices, exchange_z(): out[dz] = lax.ppermute(blocks[dz], 'lon', shifts(0, dz, 0))  52.1 us
    ppermute x14, starting transfers between devices, exchange_z(): out[dz] = lax.ppermute(blocks[dz], 'lon', shifts(0, dz, 0))  28.5 us
    all_to_all x1, waiting for transfers between devices, local(): lax.all_to_all(sent, 'lon', split_axis=0, concat_axis=0, axis_index_group...  24.7 us
    ppermute x14, starting transfers between devices, exchange_xc(): lax.ppermute(blocks[dx * NC + dc], 'lon', shifts(dx, 0, dc))  20.2 us
    ppermute x14, waiting for transfers between devices, exchange_xc(): lax.ppermute(blocks[dx * NC + dc], 'lon', shifts(dx, 0, dc))  15.4 us
    ppermute x3, waiting for transfers between devices, exchange_x(): out[dx] = lax.ppermute(blocks[dx], 'lon', shifts(dx, 0, 0))  10.2 us
    all_to_all x1, starting transfers between devices, local(): lax.all_to_all(sent, 'lon', split_axis=0, concat_axis=0, axis_index_group...  10 us
    all_to_all x1, starting transfers between devices, local(): lax.all_to_all(spectrum, 'lon', split_axis=0, concat_axis=0, tiled=True)  6.08 us
  transfers between devices with their start and end apart: 33, of which 16 were waited for; matrix products, arithmetic and copies ran while one was open for 2% of the time, Pallas kernels for 2%

profile of v12, /device:TPU:1, one launch (start us, length us, event | category | flops | bytes accessed | tf_op | source)
XLA Modules:
  0.0 191.5 jit_solution(12004514534498852743)
XLA Ops:
  7.0 2.5 %collective-permute-start.1 = (f32[32,16,128]{2,1,0:T(8,128)S(1)}, f32[32,16,128]{2,1,0:T(8,128)S(1)}, u32[]{:S(2)}, u32[]{:S(2)}) collective-permute-start(f32[32,16,128]{2,1,0:T(8,128)S(1)} %get-tuple-element.43), channel_id=1, source_target_pairs={{0,128},{4,132},{8,136},{12,140},{16,144},{20,148},{24,152},{28,15... | collective-permute-start | bytes 786440 | tf_op jit(solution)/shard_map/ppermute | solution.py:440
  12.1 8.8 %collective-permute-done.1 = f32[32,16,128]{2,1,0:T(8,128)S(1)} collective-permute-done((f32[32,16,128]{2,1,0:T(8,128)S(1)}, f32[32,16,128]{2,1,0:T(8,128)S(1)}, u32[]{:S(2)}, u32[]{:S(2)}) %collective-permute-start.1) | collective-permute-done | bytes 262176 | tf_op jit(solution)/shard_map/ppermute | solution.py:440
  22.5 10.0 %all-to-all-start = ((f32[16,128,128]{2,1,0:T(8,128)}), f32[16,128,128]{2,1,0:T(8,128)S(1)}, u32[]{:S(2)}, u32[]{:S(2)}) async-start(f32[16,128,128]{2,1,0:T(8,128)} %spread_a.1), calls=%async_computation | async-start | bytes 2097152 | tf_op jit(solution)/shard_map/all_to_all | solution.py:463
  32.5 2.5 %select_select_fusion.1 = (f32[8,2,64,128]{3,2,1,0:T(8,128)S(1)}, f32[8,2,64,128]{3,2,1,0:T(8,128)S(1)}, f32[8,2,64,128]{3,2,1,0:T(8,128)S(1)}, f32[8,2,64,128]{3,2,1,0:T(8,128)S(1)}) fusion(pred[2]{0:T(512)(128)(4,1)S(1)} %iota_compare_fusion.1, pred[8]{0:T(512)(128)(4,1)S(1)} %iota_compare_fusion, s32[64]{0:T(128)S(1)} %iota_multiply_fusion, ...), kind=kLoop, calls=%fused_computation.9 | loop fusion | flops 4456448 | bytes 2097450 | tf_op jit(solution)/shard_map/jit(_where)/select_n | solution.py:60
  35.8 24.7 %all-to-all-done = f32[16,128,128]{2,1,0:T(8,128)S(1)} async-done(((f32[16,128,128]{2,1,0:T(8,128)}), f32[16,128,128]{2,1,0:T(8,128)S(1)}, u32[]{:S(2)}, u32[]{:S(2)}) %all-to-all-start) | async-done | bytes 1048608 | tf_op jit(solution)/shard_map/all_to_all | solution.py:463
  62.6 6.1 %all-to-all-start.1 = ((f32[64,32,128]{2,1,0:T(8,128)}), f32[64,32,128]{2,1,0:T(8,128)S(1)}, u32[]{:S(2)}, u32[]{:S(2)}) async-start(f32[64,32,128]{2,1,0:T(8,128)} %fft_a.1), calls=%async_computation.1 | async-start | bytes 2097152 | tf_op jit(solution)/shard_map/all_to_all | solution.py:471
  72.2 2.4 %collective-permute-start.5 = (f32[32,8,128]{2,1,0:T(8,128)}, f32[32,8,128]{2,1,0:T(8,128)S(1)}, u32[]{:S(2)}, u32[]{:S(2)}) collective-permute-start(f32[32,8,128]{2,1,0:T(8,128)} %copy-done.2), channel_id=1, source_target_pairs={{0,24},{4,28},{8,32},{12,36},{16,40},{20,44},{24,48},{28,52},{32,5... | collective-permute-start | bytes 393224 | tf_op jit(solution)/shard_map/ppermute | solution.py:428
  76.7 2.4 %collective-permute-start.7 = (f32[32,8,128]{2,1,0:T(8,128)}, f32[32,8,128]{2,1,0:T(8,128)S(1)}, u32[]{:S(2)}, u32[]{:S(2)}) collective-permute-start(f32[32,8,128]{2,1,0:T(8,128)} %copy-done), channel_id=1, source_target_pairs={{0,40},{4,44},{8,48},{12,52},{16,56},{20,60},{24,0},{28,4},{32,8},... | collective-permute-start | bytes 393224 | tf_op jit(solution)/shard_map/ppermute | solution.py:428
  79.1 17.8 %collective-permute-done.3 = f32[32,8,128]{2,1,0:T(8,128)S(1)} collective-permute-done((f32[32,8,128]{2,1,0:T(8,128)}, f32[32,8,128]{2,1,0:T(8,128)S(1)}, u32[]{:S(2)}, u32[]{:S(2)}) %collective-permute-start.3) | collective-permute-done | bytes 131104 | tf_op jit(solution)/shard_map/ppermute | solution.py:428
  99.2 2.8 %collective-permute-done.4 = f32[32,8,128]{2,1,0:T(8,128)S(1)} collective-permute-done((f32[32,8,128]{2,1,0:T(8,128)}, f32[32,8,128]{2,1,0:T(8,128)S(1)}, u32[]{:S(2)}, u32[]{:S(2)}) %collective-permute-start.4) | collective-permute-done | bytes 131104 | tf_op jit(solution)/shard_map/ppermute | solution.py:428
  102.0 2.3 %collective-permute-start.9 = (f32[32,8,128]{2,1,0:T(8,128)S(1)}, f32[32,8,128]{2,1,0:T(8,128)S(1)}, u32[]{:S(2)}, u32[]{:S(2)}) collective-permute-start(f32[32,8,128]{2,1,0:T(8,128)S(1)} %get-tuple-element.52), channel_id=1, source_target_pairs={{0,56},{4,60},{8,0},{12,4},{16,8},{20,12},{24,16},{28,20},{32,24},... | collective-permute-start | bytes 393224 | tf_op jit(solution)/shard_map/ppermute | solution.py:428
  104.3 8.8 %collective-permute-done.5 = f32[32,8,128]{2,1,0:T(8,128)S(1)} collective-permute-done((f32[32,8,128]{2,1,0:T(8,128)}, f32[32,8,128]{2,1,0:T(8,128)S(1)}, u32[]{:S(2)}, u32[]{:S(2)}) %collective-permute-start.5) | collective-permute-done | bytes 131104 | tf_op jit(solution)/shard_map/ppermute | solution.py:428
  113.1 4.9 %collective-permute-done.6 = f32[32,8,128]{2,1,0:T(8,128)S(1)} collective-permute-done((f32[32,8,128]{2,1,0:T(8,128)}, f32[32,8,128]{2,1,0:T(8,128)S(1)}, u32[]{:S(2)}, u32[]{:S(2)}) %collective-permute-start.6) | collective-permute-done | bytes 131104 | tf_op jit(solution)/shard_map/ppermute | solution.py:428
  118.9 2.5 %collective-permute-start.10 = (f32[256,128]{1,0:T(8,128)S(1)}, f32[256,128]{1,0:T(8,128)S(1)}, u32[]{:S(2)}, u32[]{:S(2)}) collective-permute-start(f32[256,128]{1,0:T(8,128)S(1)} %get-tuple-element.54), channel_id=1, source_target_pairs={{0,4},{4,0},{8,12},{12,8},{16,20},{20,16},{24,28},{28,24},{32,36},... | collective-permute-start | bytes 393224 | tf_op jit(solution)/shard_map/ppermute | solution.py:451
  122.4 3.2 %collective-permute-start.13 = (f32[256,128]{1,0:T(8,128)S(1)}, f32[256,128]{1,0:T(8,128)S(1)}, u32[]{:S(2)}, u32[]{:S(2)}) collective-permute-start(f32[256,128]{1,0:T(8,128)S(1)} %get-tuple-element.57), channel_id=1, source_target_pairs={{0,128},{4,132},{8,136},{12,140},{16,144},{20,148},{24,152},{28,15... | collective-permute-start | bytes 393224 | tf_op jit(solution)/shard_map/ppermute | solution.py:451
  129.4 6.9 %collective-permute-done.12.refs_3_ = f32[256,128]{1,0:T(8,128)S(1)} collective-permute-done((f32[256,128]{1,0:T(8,128)S(1)}, f32[256,128]{1,0:T(8,128)S(1)}, u32[]{:S(2)}, u32[]{:S(2)}) %collective-permute-start.12) | collective-permute-done | bytes 131104 | tf_op jit(solution)/shard_map/ppermute | solution.py:451
  143.0 3.3 %collective-permute-start.20 = (f32[256,128]{1,0:T(8,128)S(1)}, f32[256,128]{1,0:T(8,128)S(1)}, u32[]{:S(2)}, u32[]{:S(2)}) collective-permute-start(f32[256,128]{1,0:T(8,128)S(1)} %get-tuple-element.65), channel_id=1, source_target_pairs={{0,32},{4,36},{8,40},{12,44},{16,48},{20,52},{24,56},{28,60},{32,0... | collective-permute-start | bytes 393224 | tf_op jit(solution)/shard_map/ppermute | solution.py:428
  149.0 4.6 %collective-permute-start.23 = (f32[256,128]{1,0:T(8,128)S(1)}, f32[256,128]{1,0:T(8,128)S(1)}, u32[]{:S(2)}, u32[]{:S(2)}) collective-permute-start(f32[256,128]{1,0:T(8,128)S(1)} %get-tuple-element.68), channel_id=1, source_target_pairs={{0,56},{4,60},{8,0},{12,4},{16,8},{20,12},{24,16},{28,20},{32,24},... | collective-permute-start | bytes 393224 | tf_op jit(solution)/shard_map/ppermute | solution.py:428
  153.5 9.8 %collective-permute-done.19.refs_3_ = f32[256,128]{1,0:T(8,128)S(1)} collective-permute-done((f32[256,128]{1,0:T(8,128)S(1)}, f32[256,128]{1,0:T(8,128)S(1)}, u32[]{:S(2)}, u32[]{:S(2)}) %collective-permute-start.19) | collective-permute-done | bytes 131104 | tf_op jit(solution)/shard_map/ppermute | solution.py:428
  163.3 4.1 %collective-permute-done.22.refs_6_ = f32[256,128]{1,0:T(8,128)S(1)} collective-permute-done((f32[256,128]{1,0:T(8,128)S(1)}, f32[256,128]{1,0:T(8,128)S(1)}, u32[]{:S(2)}, u32[]{:S(2)}) %collective-permute-start.22) | collective-permute-done | bytes 131104 | tf_op jit(solution)/shard_map/ppermute | solution.py:428
  167.5 2.7 %collective-permute-done.23.refs_7_ = f32[256,128]{1,0:T(8,128)S(1)} collective-permute-done((f32[256,128]{1,0:T(8,128)S(1)}, f32[256,128]{1,0:T(8,128)S(1)}, u32[]{:S(2)}, u32[]{:S(2)}) %collective-permute-start.23) | collective-permute-done | bytes 131104 | tf_op jit(solution)/shard_map/ppermute | solution.py:428
  177.5 2.6 %collective-permute-start.29 = (f32[256,128]{1,0:T(8,128)S(1)}, f32[256,128]{1,0:T(8,128)S(1)}, u32[]{:S(2)}, u32[]{:S(2)}) collective-permute-start(f32[256,128]{1,0:T(8,128)S(1)} %get-tuple-element.75), channel_id=1, source_target_pairs={{0,192},{4,196},{8,200},{12,204},{16,208},{20,212},{24,216},{28,22... | collective-permute-start | bytes 393224 | tf_op jit(solution)/shard_map/ppermute | solution.py:451
  181.8 2.8 %collective-permute-done.27.refs_4_ = f32[256,128]{1,0:T(8,128)S(1)} collective-permute-done((f32[256,128]{1,0:T(8,128)S(1)}, f32[256,128]{1,0:T(8,128)S(1)}, u32[]{:S(2)}, u32[]{:S(2)}) %collective-permute-start.27) | collective-permute-done | bytes 131104 | tf_op jit(solution)/shard_map/ppermute | solution.py:451
  184.6 3.1 %collective-permute-done.28.refs_5_ = f32[256,128]{1,0:T(8,128)S(1)} collective-permute-done((f32[256,128]{1,0:T(8,128)S(1)}, f32[256,128]{1,0:T(8,128)S(1)}, u32[]{:S(2)}, u32[]{:S(2)}) %collective-permute-start.28) | collective-permute-done | bytes 131104 | tf_op jit(solution)/shard_map/ppermute | solution.py:451
  (69 shorter events, 49.6 us)
Async XLA Ops:
  7.0 13.8 %collective-permute-start.1 = (f32[32,16,128]{2,1,0:T(8,128)S(1)}, f32[32,16,128]{2,1,0:T(8,128)S(1)}, u32[]{:S(2)}, u32[]{:S(2)}) collective-permute-start(f32[32,16,128]{2,1,0:T(8,128)S(1)} %get-tuple-element.43), channel_id=1, source_target_pairs={{0,128},{4,132},{8,136},{12,140},{16,144},{20,148},{24,152},{28,15... | collective-permute-start | bytes 786440 | tf_op jit(solution)/shard_map/ppermute | solution.py:440
  9.5 11.3 %collective-permute-start.2 = (f32[32,16,128]{2,1,0:T(8,128)S(1)}, f32[32,16,128]{2,1,0:T(8,128)S(1)}, u32[]{:S(2)}, u32[]{:S(2)}) collective-permute-start(f32[32,16,128]{2,1,0:T(8,128)S(1)} %get-tuple-element.44), channel_id=1, source_target_pairs={{0,192},{4,196},{8,200},{12,204},{16,208},{20,212},{24,216},{28,22... | collective-permute-start | bytes 786440 | tf_op jit(solution)/shard_map/ppermute | solution.py:440
  22.5 38.0 %all-to-all-start = ((f32[16,128,128]{2,1,0:T(8,128)}), f32[16,128,128]{2,1,0:T(8,128)S(1)}, u32[]{:S(2)}, u32[]{:S(2)}) async-start(f32[16,128,128]{2,1,0:T(8,128)} %spread_a.1), calls=%async_computation | async-start | bytes 2097152 | tf_op jit(solution)/shard_map/all_to_all | solution.py:463
  62.6 118.0 %all-to-all-start.1 = ((f32[64,32,128]{2,1,0:T(8,128)}), f32[64,32,128]{2,1,0:T(8,128)S(1)}, u32[]{:S(2)}, u32[]{:S(2)}) async-start(f32[64,32,128]{2,1,0:T(8,128)} %fft_a.1), calls=%async_computation.1 | async-start | bytes 2097152 | tf_op jit(solution)/shard_map/all_to_all | solution.py:471
  68.7 28.2 %collective-permute-start.3 = (f32[32,8,128]{2,1,0:T(8,128)}, f32[32,8,128]{2,1,0:T(8,128)S(1)}, u32[]{:S(2)}, u32[]{:S(2)}) collective-permute-start(f32[32,8,128]{2,1,0:T(8,128)} %copy-done.4), channel_id=1, source_target_pairs={{0,8},{4,12},{8,16},{12,20},{16,24},{20,28},{24,32},{28,36},{32,40... | collective-permute-start | bytes 393224 | tf_op jit(solution)/shard_map/ppermute | solution.py:428
  70.2 31.8 %collective-permute-start.4 = (f32[32,8,128]{2,1,0:T(8,128)}, f32[32,8,128]{2,1,0:T(8,128)S(1)}, u32[]{:S(2)}, u32[]{:S(2)}) collective-permute-start(f32[32,8,128]{2,1,0:T(8,128)} %copy-done.3), channel_id=1, source_target_pairs={{0,16},{4,20},{8,24},{12,28},{16,32},{20,36},{24,40},{28,44},{32,4... | collective-permute-start | bytes 393224 | tf_op jit(solution)/shard_map/ppermute | solution.py:428
  72.2 40.9 %collective-permute-start.5 = (f32[32,8,128]{2,1,0:T(8,128)}, f32[32,8,128]{2,1,0:T(8,128)S(1)}, u32[]{:S(2)}, u32[]{:S(2)}) collective-permute-start(f32[32,8,128]{2,1,0:T(8,128)} %copy-done.2), channel_id=1, source_target_pairs={{0,24},{4,28},{8,32},{12,36},{16,40},{20,44},{24,48},{28,52},{32,5... | collective-permute-start | bytes 393224 | tf_op jit(solution)/shard_map/ppermute | solution.py:428
  74.6 43.4 %collective-permute-start.6 = (f32[32,8,128]{2,1,0:T(8,128)}, f32[32,8,128]{2,1,0:T(8,128)S(1)}, u32[]{:S(2)}, u32[]{:S(2)}) collective-permute-start(f32[32,8,128]{2,1,0:T(8,128)} %copy-done.1), channel_id=1, source_target_pairs={{0,32},{4,36},{8,40},{12,44},{16,48},{20,52},{24,56},{28,60},{32,0... | collective-permute-start | bytes 393224 | tf_op jit(solution)/shard_map/ppermute | solution.py:428
  76.7 41.3 %collective-permute-start.7 = (f32[32,8,128]{2,1,0:T(8,128)}, f32[32,8,128]{2,1,0:T(8,128)S(1)}, u32[]{:S(2)}, u32[]{:S(2)}) collective-permute-start(f32[32,8,128]{2,1,0:T(8,128)} %copy-done), channel_id=1, source_target_pairs={{0,40},{4,44},{8,48},{12,52},{16,56},{20,60},{24,0},{28,4},{32,8},... | collective-permute-start | bytes 393224 | tf_op jit(solution)/shard_map/ppermute | solution.py:428
  96.9 21.1 %collective-permute-start.8 = (f32[32,8,128]{2,1,0:T(8,128)S(1)}, f32[32,8,128]{2,1,0:T(8,128)S(1)}, u32[]{:S(2)}, u32[]{:S(2)}) collective-permute-start(f32[32,8,128]{2,1,0:T(8,128)S(1)} %get-tuple-element.51), channel_id=1, source_target_pairs={{0,48},{4,52},{8,56},{12,60},{16,0},{20,4},{24,8},{28,12},{32,16},... | collective-permute-start | bytes 393224 | tf_op jit(solution)/shard_map/ppermute | solution.py:428
  102.0 16.0 %collective-permute-start.9 = (f32[32,8,128]{2,1,0:T(8,128)S(1)}, f32[32,8,128]{2,1,0:T(8,128)S(1)}, u32[]{:S(2)}, u32[]{:S(2)}) collective-permute-start(f32[32,8,128]{2,1,0:T(8,128)S(1)} %get-tuple-element.52), channel_id=1, source_target_pairs={{0,56},{4,60},{8,0},{12,4},{16,8},{20,12},{24,16},{28,20},{32,24},... | collective-permute-start | bytes 393224 | tf_op jit(solution)/shard_map/ppermute | solution.py:428
  121.5 14.9 %collective-permute-start.12 = (f32[256,128]{1,0:T(8,128)S(1)}, f32[256,128]{1,0:T(8,128)S(1)}, u32[]{:S(2)}, u32[]{:S(2)}) collective-permute-start(f32[256,128]{1,0:T(8,128)S(1)} %get-tuple-element.56), channel_id=1, source_target_pairs={{0,68},{4,64},{8,76},{12,72},{16,84},{20,80},{24,92},{28,88},{32,1... | collective-permute-start | bytes 393224 | tf_op jit(solution)/shard_map/ppermute | solution.py:451
  122.4 13.9 %collective-permute-start.13 = (f32[256,128]{1,0:T(8,128)S(1)}, f32[256,128]{1,0:T(8,128)S(1)}, u32[]{:S(2)}, u32[]{:S(2)}) collective-permute-start(f32[256,128]{1,0:T(8,128)S(1)} %get-tuple-element.57), channel_id=1, source_target_pairs={{0,128},{4,132},{8,136},{12,140},{16,144},{20,148},{24,152},{28,15... | collective-permute-start | bytes 393224 | tf_op jit(solution)/shard_map/ppermute | solution.py:451
  125.6 10.8 %collective-permute-start.14 = (f32[256,128]{1,0:T(8,128)S(1)}, f32[256,128]{1,0:T(8,128)S(1)}, u32[]{:S(2)}, u32[]{:S(2)}) collective-permute-start(f32[256,128]{1,0:T(8,128)S(1)} %get-tuple-element.58), channel_id=1, source_target_pairs={{0,132},{4,128},{8,140},{12,136},{16,148},{20,144},{24,156},{28,15... | collective-permute-start | bytes 393224 | tf_op jit(solution)/shard_map/ppermute | solution.py:451
  125.6 10.7 %collective-permute-start.15 = (f32[256,128]{1,0:T(8,128)S(1)}, f32[256,128]{1,0:T(8,128)S(1)}, u32[]{:S(2)}, u32[]{:S(2)}) collective-permute-start(f32[256,128]{1,0:T(8,128)S(1)} %get-tuple-element.59), channel_id=1, source_target_pairs={{0,192},{4,196},{8,200},{12,204},{16,208},{20,212},{24,216},{28,22... | collective-permute-start | bytes 393224 | tf_op jit(solution)/shard_map/ppermute | solution.py:451
  139.0 10.0 %collective-permute-start.18 = (f32[256,128]{1,0:T(8,128)S(1)}, f32[256,128]{1,0:T(8,128)S(1)}, u32[]{:S(2)}, u32[]{:S(2)}) collective-permute-start(f32[256,128]{1,0:T(8,128)S(1)} %get-tuple-element.63), channel_id=1, source_target_pairs={{0,16},{4,20},{8,24},{12,28},{16,32},{20,36},{24,40},{28,44},{32,4... | collective-permute-start | bytes 393224 | tf_op jit(solution)/shard_map/ppermute | solution.py:428
  140.9 22.5 %collective-permute-start.19 = (f32[256,128]{1,0:T(8,128)S(1)}, f32[256,128]{1,0:T(8,128)S(1)}, u32[]{:S(2)}, u32[]{:S(2)}) collective-permute-start(f32[256,128]{1,0:T(8,128)S(1)} %get-tuple-element.64), channel_id=1, source_target_pairs={{0,24},{4,28},{8,32},{12,36},{16,40},{20,44},{24,48},{28,52},{32,5... | collective-permute-start | bytes 393224 | tf_op jit(solution)/shard_map/ppermute | solution.py:428
  143.0 20.3 %collective-permute-start.20 = (f32[256,128]{1,0:T(8,128)S(1)}, f32[256,128]{1,0:T(8,128)S(1)}, u32[]{:S(2)}, u32[]{:S(2)}) collective-permute-start(f32[256,128]{1,0:T(8,128)S(1)} %get-tuple-element.65), channel_id=1, source_target_pairs={{0,32},{4,36},{8,40},{12,44},{16,48},{20,52},{24,56},{28,60},{32,0... | collective-permute-start | bytes 393224 | tf_op jit(solution)/shard_map/ppermute | solution.py:428
  146.3 17.0 %collective-permute-start.21 = (f32[256,128]{1,0:T(8,128)S(1)}, f32[256,128]{1,0:T(8,128)S(1)}, u32[]{:S(2)}, u32[]{:S(2)}) collective-permute-start(f32[256,128]{1,0:T(8,128)S(1)} %get-tuple-element.66), channel_id=1, source_target_pairs={{0,40},{4,44},{8,48},{12,52},{16,56},{20,60},{24,0},{28,4},{32,8},... | collective-permute-start | bytes 393224 | tf_op jit(solution)/shard_map/ppermute | solution.py:428
  148.5 19.0 %collective-permute-start.22 = (f32[256,128]{1,0:T(8,128)S(1)}, f32[256,128]{1,0:T(8,128)S(1)}, u32[]{:S(2)}, u32[]{:S(2)}) collective-permute-start(f32[256,128]{1,0:T(8,128)S(1)} %get-tuple-element.67), channel_id=1, source_target_pairs={{0,48},{4,52},{8,56},{12,60},{16,0},{20,4},{24,8},{28,12},{32,16},... | collective-permute-start | bytes 393224 | tf_op jit(solution)/shard_map/ppermute | solution.py:428
  149.0 21.2 %collective-permute-start.23 = (f32[256,128]{1,0:T(8,128)S(1)}, f32[256,128]{1,0:T(8,128)S(1)}, u32[]{:S(2)}, u32[]{:S(2)}) collective-permute-start(f32[256,128]{1,0:T(8,128)S(1)} %get-tuple-element.68), channel_id=1, source_target_pairs={{0,56},{4,60},{8,0},{12,4},{16,8},{20,12},{24,16},{28,20},{32,24},... | collective-permute-start | bytes 393224 | tf_op jit(solution)/shard_map/ppermute | solution.py:428
  174.2 10.3 %collective-permute-start.27 = (f32[256,128]{1,0:T(8,128)S(1)}, f32[256,128]{1,0:T(8,128)S(1)}, u32[]{:S(2)}, u32[]{:S(2)}) collective-permute-start(f32[256,128]{1,0:T(8,128)S(1)} %get-tuple-element.73), channel_id=1, source_target_pairs={{0,128},{4,132},{8,136},{12,140},{16,144},{20,148},{24,152},{28,15... | collective-permute-start | bytes 393224 | tf_op jit(solution)/shard_map/ppermute | solution.py:451
  175.8 11.8 %collective-permute-start.28 = (f32[256,128]{1,0:T(8,128)S(1)}, f32[256,128]{1,0:T(8,128)S(1)}, u32[]{:S(2)}, u32[]{:S(2)}) collective-permute-start(f32[256,128]{1,0:T(8,128)S(1)} %get-tuple-element.74), channel_id=1, source_target_pairs={{0,132},{4,128},{8,140},{12,136},{16,148},{20,144},{24,156},{28,15... | collective-permute-start | bytes 393224 | tf_op jit(solution)/shard_map/ppermute | solution.py:451
  177.5 10.1 %collective-permute-start.29 = (f32[256,128]{1,0:T(8,128)S(1)}, f32[256,128]{1,0:T(8,128)S(1)}, u32[]{:S(2)}, u32[]{:S(2)}) collective-permute-start(f32[256,128]{1,0:T(8,128)S(1)} %get-tuple-element.75), channel_id=1, source_target_pairs={{0,192},{4,196},{8,200},{12,204},{16,208},{20,212},{24,216},{28,22... | collective-permute-start | bytes 393224 | tf_op jit(solution)/shard_map/ppermute | solution.py:451
  (14 other events, 91.5 us)

commit v13 on v10

--- a/solution.py
+++ b/solution.py
@@ -335,28 +335,22 @@
 PAD_K = KEPT + 8
 
 
-def store_half(x_ref, buf_ref, o_ref, sem, lane):
-    copies = []
-    step = KEPT // PIECES
-    for piece in range(PIECES):
-        for kept in range(piece * step, (piece + 1) * step):
-            for eight in range(FIELDS // 8):
-                buf_ref[kept, eight * 8 : eight * 8 + 8, :] = x_ref[pl.ds(eight * 8 * PAD_K + kept, 8, stride=PAD_K), :]
-        copy = pltpu.make_async_copy(
-            buf_ref.at[pl.ds(piece * step, step)],
-            o_ref.at[pl.ds(piece * step, step), :, pl.ds(lane, LANES)],
-            sem.at[piece],
-        )
-        copy.start()
-        copies.append(copy)
-    for copy in copies:
-        copy.wait()
+def store_block(block, x_ref, buf_ref, o_ref, sem, lane):
+    for kept in range(KEPT):
+        buf_ref[block, kept] = x_ref[pl.ds(block * 8 * PAD_K + kept, 8, stride=PAD_K), :]
+    copy = pltpu.make_async_copy(
+        buf_ref.at[block],
+        o_ref.at[:, pl.ds(block * 8, 8), pl.ds(lane, LANES)],
+        sem.at[block],
+    )
+    copy.start()
+    return copy
 
 
 STORE_SCRATCH = [
     pltpu.VMEM((FIELDS * PAD_K, LANES), jnp.float32),
-    pltpu.VMEM((KEPT, FIELDS, LANES), jnp.float32),
-    pltpu.SemaphoreType.DMA((PIECES,)),
+    pltpu.VMEM((FIELDS // 8, KEPT, 8, LANES), jnp.float32),
+    pltpu.SemaphoreType.DMA((FIELDS // 8,)),
 ]
 
 
@@ -365,13 +359,16 @@
     q_refs, o_ref = refs[:8], refs[8]
     x_ref, buf_ref, sem = refs[9:]
     x, c = pos_ref[0], pos_ref[2]
-    for dx in range(NX):
-        for dc in range(NC):
-            base = ((x + NX - dx) % NX) * NC + (c + dc) % NC
-            for zz in range(NZ):
-                row = pl.multiple_of((base + zz * NX * NC) * PAD_K, 8)
+    copies = []
+    for zz in range(NZ):
+        for dx in range(NX):
+            for dc in range(NC):
+                field = zz * 8 + ((x + NX - dx) % NX) * NC + (c + dc) % NC
+                row = pl.multiple_of(field * PAD_K, 8)
                 x_ref[pl.ds(row, KEPT), :] = q_refs[dx * NC + dc][zz * KEPT : (zz + 1) * KEPT, :]
-    store_half(x_ref, buf_ref, o_ref, sem, 0)
+        copies.append(store_block(zz, x_ref, buf_ref, o_ref, sem, 0))
+    for copy in copies:
+        copy.wait()
 
 
 def store_p(pos, prior, blocks):
@@ -388,12 +385,13 @@
 
 
 def store_a_kernel(q_ref, o_ref, x_ref, buf_ref, sem):
-    def field(f, carry):
-        x_ref[pl.ds(pl.multiple_of(f * PAD_K, 8), KEPT), :] = q_ref[f]
-        return carry
-
-    lax.fori_loop(0, FIELDS, field, 0, unroll=8)
-    store_half(x_ref, buf_ref, o_ref, sem, LANES)
+    copies = []
+    for block in range(FIELDS // 8):
+        for f in range(block * 8, block * 8 + 8):
+            x_ref[pl.ds(f * PAD_K, KEPT), :] = q_ref[f]
+        copies.append(store_block(block, x_ref, buf_ref, o_ref, sem, LANES))
+    for copy in copies:
+        copy.wait()
 
 
 def store_a(shares):

time: 192 us -> 192 us (level)
  no operation moved by 1% of the time
where the time goes in v13:
time: 192 us; the launch traced here: 191 us
  waiting for transfers between devices  103 us (54%)
  starting transfers between devices  70.4 us (37%)
  Pallas kernels  12.2 us (6%)
  other arithmetic  3.34 us (2%)
  local copies, waits for them, and re-layouts  2.6 us (1%)
    ppermute x14, waiting for transfers between devices, exchange_z(): out[dz] = lax.ppermute(blocks[dz], 'lon', shifts(0, dz, 0))  52.1 us
    ppermute x14, starting transfers between devices, exchange_z(): out[dz] = lax.ppermute(blocks[dz], 'lon', shifts(0, dz, 0))  28.5 us
    all_to_all x1, waiting for transfers between devices, local(): lax.all_to_all(sent, 'lon', split_axis=0, concat_axis=0, axis_index_group...  24.7 us
    ppermute x14, starting transfers between devices, exchange_xc(): lax.ppermute(blocks[dx * NC + dc], 'lon', shifts(dx, 0, dc))  20.2 us
    ppermute x14, waiting for transfers between devices, exchange_xc(): lax.ppermute(blocks[dx * NC + dc], 'lon', shifts(dx, 0, dc))  15.5 us
    ppermute x3, waiting for transfers between devices, exchange_x(): out[dx] = lax.ppermute(blocks[dx], 'lon', shifts(dx, 0, 0))  10.2 us
    all_to_all x1, starting transfers between devices, local(): lax.all_to_all(sent, 'lon', split_axis=0, concat_axis=0, axis_index_group...  10 us
    all_to_all x1, starting transfers between devices, local(): lax.all_to_all(spectrum, 'lon', split_axis=0, concat_axis=0, tiled=True)  6.08 us
  transfers between devices with their start and end apart: 33, of which 16 were waited for; matrix products, arithmetic and copies ran while one was open for 2% of the time, Pallas kernels for 2%

profile of v13, /device:TPU:1, one launch (start us, length us, event | category | flops | bytes accessed | tf_op | source)
XLA Modules:
  0.0 191.4 jit_solution(8010308844559883195)
XLA Ops:
  7.0 2.5 %collective-permute-start.1 = (f32[32,16,128]{2,1,0:T(8,128)S(1)}, f32[32,16,128]{2,1,0:T(8,128)S(1)}, u32[]{:S(2)}, u32[]{:S(2)}) collective-permute-start(f32[32,16,128]{2,1,0:T(8,128)S(1)} %get-tuple-element.43), channel_id=1, source_target_pairs={{0,128},{4,132},{8,136},{12,140},{16,144},{20,148},{24,152},{28,15... | collective-permute-start | bytes 786440 | tf_op jit(solution)/shard_map/ppermute | solution.py:437
  12.1 8.8 %collective-permute-done.1 = f32[32,16,128]{2,1,0:T(8,128)S(1)} collective-permute-done((f32[32,16,128]{2,1,0:T(8,128)S(1)}, f32[32,16,128]{2,1,0:T(8,128)S(1)}, u32[]{:S(2)}, u32[]{:S(2)}) %collective-permute-start.1) | collective-permute-done | bytes 262176 | tf_op jit(solution)/shard_map/ppermute | solution.py:437
  22.5 10.0 %all-to-all-start = ((f32[16,128,128]{2,1,0:T(8,128)}), f32[16,128,128]{2,1,0:T(8,128)S(1)}, u32[]{:S(2)}, u32[]{:S(2)}) async-start(f32[16,128,128]{2,1,0:T(8,128)} %spread_a.1), calls=%async_computation | async-start | bytes 2097152 | tf_op jit(solution)/shard_map/all_to_all | solution.py:460
  32.5 2.5 %select_select_fusion.1 = (f32[8,2,64,128]{3,2,1,0:T(8,128)S(1)}, f32[8,2,64,128]{3,2,1,0:T(8,128)S(1)}, f32[8,2,64,128]{3,2,1,0:T(8,128)S(1)}, f32[8,2,64,128]{3,2,1,0:T(8,128)S(1)}) fusion(pred[2]{0:T(512)(128)(4,1)S(1)} %iota_compare_fusion.1, pred[8]{0:T(512)(128)(4,1)S(1)} %iota_compare_fusion, s32[64]{0:T(128)S(1)} %iota_multiply_fusion, ...), kind=kLoop, calls=%fused_computation.9 | loop fusion | flops 4456448 | bytes 2097450 | tf_op jit(solution)/shard_map/jit(_where)/select_n | solution.py:60
  35.8 24.7 %all-to-all-done = f32[16,128,128]{2,1,0:T(8,128)S(1)} async-done(((f32[16,128,128]{2,1,0:T(8,128)}), f32[16,128,128]{2,1,0:T(8,128)S(1)}, u32[]{:S(2)}, u32[]{:S(2)}) %all-to-all-start) | async-done | bytes 1048608 | tf_op jit(solution)/shard_map/all_to_all | solution.py:460
  62.6 6.1 %all-to-all-start.1 = ((f32[64,32,128]{2,1,0:T(8,128)}), f32[64,32,128]{2,1,0:T(8,128)S(1)}, u32[]{:S(2)}, u32[]{:S(2)}) async-start(f32[64,32,128]{2,1,0:T(8,128)} %fft_a.1), calls=%async_computation.1 | async-start | bytes 2097152 | tf_op jit(solution)/shard_map/all_to_all | solution.py:468
  72.2 2.4 %collective-permute-start.5 = (f32[32,8,128]{2,1,0:T(8,128)}, f32[32,8,128]{2,1,0:T(8,128)S(1)}, u32[]{:S(2)}, u32[]{:S(2)}) collective-permute-start(f32[32,8,128]{2,1,0:T(8,128)} %copy-done.2), channel_id=1, source_target_pairs={{0,24},{4,28},{8,32},{12,36},{16,40},{20,44},{24,48},{28,52},{32,5... | collective-permute-start | bytes 393224 | tf_op jit(solution)/shard_map/ppermute | solution.py:425
  76.7 2.4 %collective-permute-start.7 = (f32[32,8,128]{2,1,0:T(8,128)}, f32[32,8,128]{2,1,0:T(8,128)S(1)}, u32[]{:S(2)}, u32[]{:S(2)}) collective-permute-start(f32[32,8,128]{2,1,0:T(8,128)} %copy-done), channel_id=1, source_target_pairs={{0,40},{4,44},{8,48},{12,52},{16,56},{20,60},{24,0},{28,4},{32,8},... | collective-permute-start | bytes 393224 | tf_op jit(solution)/shard_map/ppermute | solution.py:425
  79.1 17.8 %collective-permute-done.3 = f32[32,8,128]{2,1,0:T(8,128)S(1)} collective-permute-done((f32[32,8,128]{2,1,0:T(8,128)}, f32[32,8,128]{2,1,0:T(8,128)S(1)}, u32[]{:S(2)}, u32[]{:S(2)}) %collective-permute-start.3) | collective-permute-done | bytes 131104 | tf_op jit(solution)/shard_map/ppermute | solution.py:425
  99.2 2.8 %collective-permute-done.4 = f32[32,8,128]{2,1,0:T(8,128)S(1)} collective-permute-done((f32[32,8,128]{2,1,0:T(8,128)}, f32[32,8,128]{2,1,0:T(8,128)S(1)}, u32[]{:S(2)}, u32[]{:S(2)}) %collective-permute-start.4) | collective-permute-done | bytes 131104 | tf_op jit(solution)/shard_map/ppermute | solution.py:425
  102.0 2.3 %collective-permute-start.9 = (f32[32,8,128]{2,1,0:T(8,128)S(1)}, f32[32,8,128]{2,1,0:T(8,128)S(1)}, u32[]{:S(2)}, u32[]{:S(2)}) collective-permute-start(f32[32,8,128]{2,1,0:T(8,128)S(1)} %get-tuple-element.52), channel_id=1, source_target_pairs={{0,56},{4,60},{8,0},{12,4},{16,8},{20,12},{24,16},{28,20},{32,24},... | collective-permute-start | bytes 393224 | tf_op jit(solution)/shard_map/ppermute | solution.py:425
  104.3 8.8 %collective-permute-done.5 = f32[32,8,128]{2,1,0:T(8,128)S(1)} collective-permute-done((f32[32,8,128]{2,1,0:T(8,128)}, f32[32,8,128]{2,1,0:T(8,128)S(1)}, u32[]{:S(2)}, u32[]{:S(2)}) %collective-permute-start.5) | collective-permute-done | bytes 131104 | tf_op jit(solution)/shard_map/ppermute | solution.py:425
  113.1 4.9 %collective-permute-done.6 = f32[32,8,128]{2,1,0:T(8,128)S(1)} collective-permute-done((f32[32,8,128]{2,1,0:T(8,128)}, f32[32,8,128]{2,1,0:T(8,128)S(1)}, u32[]{:S(2)}, u32[]{:S(2)}) %collective-permute-start.6) | collective-permute-done | bytes 131104 | tf_op jit(solution)/shard_map/ppermute | solution.py:425
  118.9 2.5 %collective-permute-start.10 = (f32[256,128]{1,0:T(8,128)S(1)}, f32[256,128]{1,0:T(8,128)S(1)}, u32[]{:S(2)}, u32[]{:S(2)}) collective-permute-start(f32[256,128]{1,0:T(8,128)S(1)} %get-tuple-element.54), channel_id=1, source_target_pairs={{0,4},{4,0},{8,12},{12,8},{16,20},{20,16},{24,28},{28,24},{32,36},... | collective-permute-start | bytes 393224 | tf_op jit(solution)/shard_map/ppermute | solution.py:448
  122.4 3.2 %collective-permute-start.13 = (f32[256,128]{1,0:T(8,128)S(1)}, f32[256,128]{1,0:T(8,128)S(1)}, u32[]{:S(2)}, u32[]{:S(2)}) collective-permute-start(f32[256,128]{1,0:T(8,128)S(1)} %get-tuple-element.57), channel_id=1, source_target_pairs={{0,128},{4,132},{8,136},{12,140},{16,144},{20,148},{24,152},{28,15... | collective-permute-start | bytes 393224 | tf_op jit(solution)/shard_map/ppermute | solution.py:448
  129.4 6.9 %collective-permute-done.12.refs_3_ = f32[256,128]{1,0:T(8,128)S(1)} collective-permute-done((f32[256,128]{1,0:T(8,128)S(1)}, f32[256,128]{1,0:T(8,128)S(1)}, u32[]{:S(2)}, u32[]{:S(2)}) %collective-permute-start.12) | collective-permute-done | bytes 131104 | tf_op jit(solution)/shard_map/ppermute | solution.py:448
  143.0 3.3 %collective-permute-start.20 = (f32[256,128]{1,0:T(8,128)S(1)}, f32[256,128]{1,0:T(8,128)S(1)}, u32[]{:S(2)}, u32[]{:S(2)}) collective-permute-start(f32[256,128]{1,0:T(8,128)S(1)} %get-tuple-element.65), channel_id=1, source_target_pairs={{0,32},{4,36},{8,40},{12,44},{16,48},{20,52},{24,56},{28,60},{32,0... | collective-permute-start | bytes 393224 | tf_op jit(solution)/shard_map/ppermute | solution.py:425
  149.0 4.6 %collective-permute-start.23 = (f32[256,128]{1,0:T(8,128)S(1)}, f32[256,128]{1,0:T(8,128)S(1)}, u32[]{:S(2)}, u32[]{:S(2)}) collective-permute-start(f32[256,128]{1,0:T(8,128)S(1)} %get-tuple-element.68), channel_id=1, source_target_pairs={{0,56},{4,60},{8,0},{12,4},{16,8},{20,12},{24,16},{28,20},{32,24},... | collective-permute-start | bytes 393224 | tf_op jit(solution)/shard_map/ppermute | solution.py:425
  153.5 9.8 %collective-permute-done.19.refs_3_ = f32[256,128]{1,0:T(8,128)S(1)} collective-permute-done((f32[256,128]{1,0:T(8,128)S(1)}, f32[256,128]{1,0:T(8,128)S(1)}, u32[]{:S(2)}, u32[]{:S(2)}) %collective-permute-start.19) | collective-permute-done | bytes 131104 | tf_op jit(solution)/shard_map/ppermute | solution.py:425
  163.3 4.1 %collective-permute-done.22.refs_6_ = f32[256,128]{1,0:T(8,128)S(1)} collective-permute-done((f32[256,128]{1,0:T(8,128)S(1)}, f32[256,128]{1,0:T(8,128)S(1)}, u32[]{:S(2)}, u32[]{:S(2)}) %collective-permute-start.22) | collective-permute-done | bytes 131104 | tf_op jit(solution)/shard_map/ppermute | solution.py:425
  167.5 2.7 %collective-permute-done.23.refs_7_ = f32[256,128]{1,0:T(8,128)S(1)} collective-permute-done((f32[256,128]{1,0:T(8,128)S(1)}, f32[256,128]{1,0:T(8,128)S(1)}, u32[]{:S(2)}, u32[]{:S(2)}) %collective-permute-start.23) | collective-permute-done | bytes 131104 | tf_op jit(solution)/shard_map/ppermute | solution.py:425
  177.5 2.6 %collective-permute-start.29 = (f32[256,128]{1,0:T(8,128)S(1)}, f32[256,128]{1,0:T(8,128)S(1)}, u32[]{:S(2)}, u32[]{:S(2)}) collective-permute-start(f32[256,128]{1,0:T(8,128)S(1)} %get-tuple-element.75), channel_id=1, source_target_pairs={{0,192},{4,196},{8,200},{12,204},{16,208},{20,212},{24,216},{28,22... | collective-permute-start | bytes 393224 | tf_op jit(solution)/shard_map/ppermute | solution.py:448
  181.7 2.9 %collective-permute-done.27.refs_4_ = f32[256,128]{1,0:T(8,128)S(1)} collective-permute-done((f32[256,128]{1,0:T(8,128)S(1)}, f32[256,128]{1,0:T(8,128)S(1)}, u32[]{:S(2)}, u32[]{:S(2)}) %collective-permute-start.27) | collective-permute-done | bytes 131104 | tf_op jit(solution)/shard_map/ppermute | solution.py:448
  184.6 3.1 %collective-permute-done.28.refs_5_ = f32[256,128]{1,0:T(8,128)S(1)} collective-permute-done((f32[256,128]{1,0:T(8,128)S(1)}, f32[256,128]{1,0:T(8,128)S(1)}, u32[]{:S(2)}, u32[]{:S(2)}) %collective-permute-start.28) | collective-permute-done | bytes 131104 | tf_op jit(solution)/shard_map/ppermute | solution.py:448
  (69 shorter events, 49.5 us)
Async XLA Ops:
  7.0 13.8 %collective-permute-start.1 = (f32[32,16,128]{2,1,0:T(8,128)S(1)}, f32[32,16,128]{2,1,0:T(8,128)S(1)}, u32[]{:S(2)}, u32[]{:S(2)}) collective-permute-start(f32[32,16,128]{2,1,0:T(8,128)S(1)} %get-tuple-element.43), channel_id=1, source_target_pairs={{0,128},{4,132},{8,136},{12,140},{16,144},{20,148},{24,152},{28,15... | collective-permute-start | bytes 786440 | tf_op jit(solution)/shard_map/ppermute | solution.py:437
  9.5 11.3 %collective-permute-start.2 = (f32[32,16,128]{2,1,0:T(8,128)S(1)}, f32[32,16,128]{2,1,0:T(8,128)S(1)}, u32[]{:S(2)}, u32[]{:S(2)}) collective-permute-start(f32[32,16,128]{2,1,0:T(8,128)S(1)} %get-tuple-element.44), channel_id=1, source_target_pairs={{0,192},{4,196},{8,200},{12,204},{16,208},{20,212},{24,216},{28,22... | collective-permute-start | bytes 786440 | tf_op jit(solution)/shard_map/ppermute | solution.py:437
  22.5 38.0 %all-to-all-start = ((f32[16,128,128]{2,1,0:T(8,128)}), f32[16,128,128]{2,1,0:T(8,128)S(1)}, u32[]{:S(2)}, u32[]{:S(2)}) async-start(f32[16,128,128]{2,1,0:T(8,128)} %spread_a.1), calls=%async_computation | async-start | bytes 2097152 | tf_op jit(solution)/shard_map/all_to_all | solution.py:460
  62.6 118.0 %all-to-all-start.1 = ((f32[64,32,128]{2,1,0:T(8,128)}), f32[64,32,128]{2,1,0:T(8,128)S(1)}, u32[]{:S(2)}, u32[]{:S(2)}) async-start(f32[64,32,128]{2,1,0:T(8,128)} %fft_a.1), calls=%async_computation.1 | async-start | bytes 2097152 | tf_op jit(solution)/shard_map/all_to_all | solution.py:468
  68.7 28.2 %collective-permute-start.3 = (f32[32,8,128]{2,1,0:T(8,128)}, f32[32,8,128]{2,1,0:T(8,128)S(1)}, u32[]{:S(2)}, u32[]{:S(2)}) collective-permute-start(f32[32,8,128]{2,1,0:T(8,128)} %copy-done.4), channel_id=1, source_target_pairs={{0,8},{4,12},{8,16},{12,20},{16,24},{20,28},{24,32},{28,36},{32,40... | collective-permute-start | bytes 393224 | tf_op jit(solution)/shard_map/ppermute | solution.py:425
  70.2 31.8 %collective-permute-start.4 = (f32[32,8,128]{2,1,0:T(8,128)}, f32[32,8,128]{2,1,0:T(8,128)S(1)}, u32[]{:S(2)}, u32[]{:S(2)}) collective-permute-start(f32[32,8,128]{2,1,0:T(8,128)} %copy-done.3), channel_id=1, source_target_pairs={{0,16},{4,20},{8,24},{12,28},{16,32},{20,36},{24,40},{28,44},{32,4... | collective-permute-start | bytes 393224 | tf_op jit(solution)/shard_map/ppermute | solution.py:425
  72.2 40.9 %collective-permute-start.5 = (f32[32,8,128]{2,1,0:T(8,128)}, f32[32,8,128]{2,1,0:T(8,128)S(1)}, u32[]{:S(2)}, u32[]{:S(2)}) collective-permute-start(f32[32,8,128]{2,1,0:T(8,128)} %copy-done.2), channel_id=1, source_target_pairs={{0,24},{4,28},{8,32},{12,36},{16,40},{20,44},{24,48},{28,52},{32,5... | collective-permute-start | bytes 393224 | tf_op jit(solution)/shard_map/ppermute | solution.py:425
  74.6 43.4 %collective-permute-start.6 = (f32[32,8,128]{2,1,0:T(8,128)}, f32[32,8,128]{2,1,0:T(8,128)S(1)}, u32[]{:S(2)}, u32[]{:S(2)}) collective-permute-start(f32[32,8,128]{2,1,0:T(8,128)} %copy-done.1), channel_id=1, source_target_pairs={{0,32},{4,36},{8,40},{12,44},{16,48},{20,52},{24,56},{28,60},{32,0... | collective-permute-start | bytes 393224 | tf_op jit(solution)/shard_map/ppermute | solution.py:425
  76.7 41.3 %collective-permute-start.7 = (f32[32,8,128]{2,1,0:T(8,128)}, f32[32,8,128]{2,1,0:T(8,128)S(1)}, u32[]{:S(2)}, u32[]{:S(2)}) collective-permute-start(f32[32,8,128]{2,1,0:T(8,128)} %copy-done), channel_id=1, source_target_pairs={{0,40},{4,44},{8,48},{12,52},{16,56},{20,60},{24,0},{28,4},{32,8},... | collective-permute-start | bytes 393224 | tf_op jit(solution)/shard_map/ppermute | solution.py:425
  96.9 21.1 %collective-permute-start.8 = (f32[32,8,128]{2,1,0:T(8,128)S(1)}, f32[32,8,128]{2,1,0:T(8,128)S(1)}, u32[]{:S(2)}, u32[]{:S(2)}) collective-permute-start(f32[32,8,128]{2,1,0:T(8,128)S(1)} %get-tuple-element.51), channel_id=1, source_target_pairs={{0,48},{4,52},{8,56},{12,60},{16,0},{20,4},{24,8},{28,12},{32,16},... | collective-permute-start | bytes 393224 | tf_op jit(solution)/shard_map/ppermute | solution.py:425
  102.0 16.0 %collective-permute-start.9 = (f32[32,8,128]{2,1,0:T(8,128)S(1)}, f32[32,8,128]{2,1,0:T(8,128)S(1)}, u32[]{:S(2)}, u32[]{:S(2)}) collective-permute-start(f32[32,8,128]{2,1,0:T(8,128)S(1)} %get-tuple-element.52), channel_id=1, source_target_pairs={{0,56},{4,60},{8,0},{12,4},{16,8},{20,12},{24,16},{28,20},{32,24},... | collective-permute-start | bytes 393224 | tf_op jit(solution)/shard_map/ppermute | solution.py:425
  121.5 14.9 %collective-permute-start.12 = (f32[256,128]{1,0:T(8,128)S(1)}, f32[256,128]{1,0:T(8,128)S(1)}, u32[]{:S(2)}, u32[]{:S(2)}) collective-permute-start(f32[256,128]{1,0:T(8,128)S(1)} %get-tuple-element.56), channel_id=1, source_target_pairs={{0,68},{4,64},{8,76},{12,72},{16,84},{20,80},{24,92},{28,88},{32,1... | collective-permute-start | bytes 393224 | tf_op jit(solution)/shard_map/ppermute | solution.py:448
  122.4 13.9 %collective-permute-start.13 = (f32[256,128]{1,0:T(8,128)S(1)}, f32[256,128]{1,0:T(8,128)S(1)}, u32[]{:S(2)}, u32[]{:S(2)}) collective-permute-start(f32[256,128]{1,0:T(8,128)S(1)} %get-tuple-element.57), channel_id=1, source_target_pairs={{0,128},{4,132},{8,136},{12,140},{16,144},{20,148},{24,152},{28,15... | collective-permute-start | bytes 393224 | tf_op jit(solution)/shard_map/ppermute | solution.py:448
  125.6 10.8 %collective-permute-start.14 = (f32[256,128]{1,0:T(8,128)S(1)}, f32[256,128]{1,0:T(8,128)S(1)}, u32[]{:S(2)}, u32[]{:S(2)}) collective-permute-start(f32[256,128]{1,0:T(8,128)S(1)} %get-tuple-element.58), channel_id=1, source_target_pairs={{0,132},{4,128},{8,140},{12,136},{16,148},{20,144},{24,156},{28,15... | collective-permute-start | bytes 393224 | tf_op jit(solution)/shard_map/ppermute | solution.py:448
  125.6 10.7 %collective-permute-start.15 = (f32[256,128]{1,0:T(8,128)S(1)}, f32[256,128]{1,0:T(8,128)S(1)}, u32[]{:S(2)}, u32[]{:S(2)}) collective-permute-start(f32[256,128]{1,0:T(8,128)S(1)} %get-tuple-element.59), channel_id=1, source_target_pairs={{0,192},{4,196},{8,200},{12,204},{16,208},{20,212},{24,216},{28,22... | collective-permute-start | bytes 393224 | tf_op jit(solution)/shard_map/ppermute | solution.py:448
  139.0 10.0 %collective-permute-start.18 = (f32[256,128]{1,0:T(8,128)S(1)}, f32[256,128]{1,0:T(8,128)S(1)}, u32[]{:S(2)}, u32[]{:S(2)}) collective-permute-start(f32[256,128]{1,0:T(8,128)S(1)} %get-tuple-element.63), channel_id=1, source_target_pairs={{0,16},{4,20},{8,24},{12,28},{16,32},{20,36},{24,40},{28,44},{32,4... | collective-permute-start | bytes 393224 | tf_op jit(solution)/shard_map/ppermute | solution.py:425
  140.9 22.5 %collective-permute-start.19 = (f32[256,128]{1,0:T(8,128)S(1)}, f32[256,128]{1,0:T(8,128)S(1)}, u32[]{:S(2)}, u32[]{:S(2)}) collective-permute-start(f32[256,128]{1,0:T(8,128)S(1)} %get-tuple-element.64), channel_id=1, source_target_pairs={{0,24},{4,28},{8,32},{12,36},{16,40},{20,44},{24,48},{28,52},{32,5... | collective-permute-start | bytes 393224 | tf_op jit(solution)/shard_map/ppermute | solution.py:425
  143.0 20.3 %collective-permute-start.20 = (f32[256,128]{1,0:T(8,128)S(1)}, f32[256,128]{1,0:T(8,128)S(1)}, u32[]{:S(2)}, u32[]{:S(2)}) collective-permute-start(f32[256,128]{1,0:T(8,128)S(1)} %get-tuple-element.65), channel_id=1, source_target_pairs={{0,32},{4,36},{8,40},{12,44},{16,48},{20,52},{24,56},{28,60},{32,0... | collective-permute-start | bytes 393224 | tf_op jit(solution)/shard_map/ppermute | solution.py:425
  146.3 17.0 %collective-permute-start.21 = (f32[256,128]{1,0:T(8,128)S(1)}, f32[256,128]{1,0:T(8,128)S(1)}, u32[]{:S(2)}, u32[]{:S(2)}) collective-permute-start(f32[256,128]{1,0:T(8,128)S(1)} %get-tuple-element.66), channel_id=1, source_target_pairs={{0,40},{4,44},{8,48},{12,52},{16,56},{20,60},{24,0},{28,4},{32,8},... | collective-permute-start | bytes 393224 | tf_op jit(solution)/shard_map/ppermute | solution.py:425
  148.5 19.0 %collective-permute-start.22 = (f32[256,128]{1,0:T(8,128)S(1)}, f32[256,128]{1,0:T(8,128)S(1)}, u32[]{:S(2)}, u32[]{:S(2)}) collective-permute-start(f32[256,128]{1,0:T(8,128)S(1)} %get-tuple-element.67), channel_id=1, source_target_pairs={{0,48},{4,52},{8,56},{12,60},{16,0},{20,4},{24,8},{28,12},{32,16},... | collective-permute-start | bytes 393224 | tf_op jit(solution)/shard_map/ppermute | solution.py:425
  149.0 21.2 %collective-permute-start.23 = (f32[256,128]{1,0:T(8,128)S(1)}, f32[256,128]{1,0:T(8,128)S(1)}, u32[]{:S(2)}, u32[]{:S(2)}) collective-permute-start(f32[256,128]{1,0:T(8,128)S(1)} %get-tuple-element.68), channel_id=1, source_target_pairs={{0,56},{4,60},{8,0},{12,4},{16,8},{20,12},{24,16},{28,20},{32,24},... | collective-permute-start | bytes 393224 | tf_op jit(solution)/shard_map/ppermute | solution.py:425
  174.2 10.3 %collective-permute-start.27 = (f32[256,128]{1,0:T(8,128)S(1)}, f32[256,128]{1,0:T(8,128)S(1)}, u32[]{:S(2)}, u32[]{:S(2)}) collective-permute-start(f32[256,128]{1,0:T(8,128)S(1)} %get-tuple-element.73), channel_id=1, source_target_pairs={{0,128},{4,132},{8,136},{12,140},{16,144},{20,148},{24,152},{28,15... | collective-permute-start | bytes 393224 | tf_op jit(solution)/shard_map/ppermute | solution.py:448
  175.8 11.8 %collective-permute-start.28 = (f32[256,128]{1,0:T(8,128)S(1)}, f32[256,128]{1,0:T(8,128)S(1)}, u32[]{:S(2)}, u32[]{:S(2)}) collective-permute-start(f32[256,128]{1,0:T(8,128)S(1)} %get-tuple-element.74), channel_id=1, source_target_pairs={{0,132},{4,128},{8,140},{12,136},{16,148},{20,144},{24,156},{28,15... | collective-permute-start | bytes 393224 | tf_op jit(solution)/shard_map/ppermute | solution.py:448
  177.5 10.1 %collective-permute-start.29 = (f32[256,128]{1,0:T(8,128)S(1)}, f32[256,128]{1,0:T(8,128)S(1)}, u32[]{:S(2)}, u32[]{:S(2)}) collective-permute-start(f32[256,128]{1,0:T(8,128)S(1)} %get-tuple-element.75), channel_id=1, source_target_pairs={{0,192},{4,196},{8,200},{12,204},{16,208},{20,212},{24,216},{28,22... | collective-permute-start | bytes 393224 | tf_op jit(solution)/shard_map/ppermute | solution.py:448
  (14 other events, 91.4 us)

commit v14 on v13

--- a/solution.py
+++ b/solution.py
@@ -45,29 +45,17 @@
 
 
 def twiddle_matrices(scale):
-    shape = (HALF, 2, PEERS, INNER)
+    shape = (HALF, 4, PEERS, INNER)
     pair = lax.broadcasted_iota(jnp.int32, shape, 0)
-    mirror = lax.broadcasted_iota(jnp.int32, shape, 1)
+    kind = lax.broadcasted_iota(jnp.int32, shape, 1)
     outer = lax.broadcasted_iota(jnp.int32, shape, 2)
     inner = lax.broadcasted_iota(jnp.int32, shape, 3)
-    first = jnp.where(mirror == 0, pair, jnp.where(pair == 0, HALF, RADIX - pair))
+    first = jnp.where(kind < 2, pair, jnp.where(pair == 0, HALF, RADIX - pair))
     angle = phase(inner, first + RADIX * outer)
-    c = jnp.cos(angle) * scale
-    s = jnp.sin(angle) * scale
-    real_only = pair == 0
-    zero = jnp.zeros_like(c)
-    plain = mirror == 0
-    re_a = jnp.where(real_only, jnp.where(plain, c, zero), c)
-    im_a = jnp.where(real_only, jnp.where(plain, -s, zero), -s)
-    re_b = jnp.where(real_only, jnp.where(plain, zero, c), jnp.where(plain, s, -s))
-    im_b = jnp.where(real_only, jnp.where(plain, zero, -s), jnp.where(plain, c, -c))
-    re = jnp.concatenate([re_a, re_b], axis=-1)
-    im = jnp.concatenate([im_a, im_b], axis=-1)
-    full = jnp.stack([re, im], axis=2)
-    full = full.reshape(HALF, 4 * PEERS, 2 * INNER)
+    full = jnp.where(kind % 2 == 0, jnp.cos(angle), jnp.sin(angle)) * scale
+    full = full.reshape(HALF, 4 * PEERS, INNER)
     high = lax.reduce_precision(full, 8, 7)
-    high, low = high.astype(jnp.bfloat16), (full - high).astype(jnp.bfloat16)
-    return high, low
+    return high.astype(jnp.bfloat16), (full - high).astype(jnp.bfloat16)
 
 
 def fft_real16(x):
@@ -135,12 +123,20 @@
     lax.fori_loop(0, INNER // 8, butterfly, 0, unroll=4)
     for k in range(HALF):
         yh, yl = split_bf16(y_ref[k])
-        two = jnp.dot(wh_ref[k], jnp.concatenate([yh, yl], axis=1), preferred_element_type=jnp.float32)
-        r = two[:, :LANES] + two[:, LANES:]
-        r = r + jnp.dot(wl_ref[k], yh, preferred_element_type=jnp.float32)
+        sides = jnp.concatenate([yh[:INNER], yh[INNER:], yl[:INNER], yl[INNER:]], axis=1)
+        r = jnp.dot(wh_ref[k], sides, preferred_element_type=jnp.float32)
+        r = r[:, : 2 * LANES] + r[:, 2 * LANES :]
+        r = r + jnp.dot(wl_ref[k], sides[:, : 2 * LANES], preferred_element_type=jnp.float32)
+        (c1, s1, c2, s2), (d1, t1, d2, t2) = (
+            [r[q * PEERS : (q + 1) * PEERS, p * LANES : (p + 1) * LANES] for q in range(4)] for p in range(2)
+        )
+        if k == 0:
+            parts = (c1, -s1, d2, -t2)
+        else:
+            parts = (c1 + t1, d1 - s1, c2 - t2, -d2 - s2)
         mirror = HALF if k == 0 else RADIX - k
-        for q, row in enumerate((k, RADIX + k, mirror, RADIX + mirror)):
-            r_ref[pl.ds(row * PAD_R, PEERS), :] = r[q * PEERS : (q + 1) * PEERS]
+        for row, part in zip((k, RADIX + k, mirror, RADIX + mirror), parts):
+            r_ref[pl.ds(row * PAD_R, PEERS), :] = part
 
 
 PIECES = 4

time: 192 us -> 189 us (0.984)
  waiting for transfers between devices: 103 us -> 101 us
    convert_element_type x1, other arithmetic: 0.39 us -> 4.53 us  [twiddle_matrices(): return (high.astype(jnp.bfloat16), (full - high).astype(jnp.bfloat16))]
    unnamed x10 -> x0, local copies, waits for them, and re-layouts: 2.6 us -> none
    select_n x1 -> x0, other arithmetic: 2.49 us -> none  [twiddle_matrices(): re_a = jnp.where(real_only, jnp.where(plain, c, zero), c)]
    all_to_all x1, waiting for transfers between devices: 24.7 us -> 22.7 us  [local(): lax.all_to_all(sent, 'lon', split_axis=0, concat_axis=0, axis_index_group...]
  transfers between devices with their start and end apart: 33 -> 33, of which waited for: 16 -> 16; matrix products, arithmetic and copies ran while one was open for 2% -> 3% of each run, Pallas kernels for 2% -> 3%
where the time goes in v14:
time: 189 us
  waiting for transfers between devices  101 us (53%)
  starting transfers between devices  70.3 us (37%)
  Pallas kernels  12.7 us (7%)
  other arithmetic  4.64 us (2%)
    ppermute x14, waiting for transfers between devices, exchange_z(): out[dz] = lax.ppermute(blocks[dz], 'lon', shifts(0, dz, 0))  52.1 us
    ppermute x14, starting transfers between devices, exchange_z(): out[dz] = lax.ppermute(blocks[dz], 'lon', shifts(0, dz, 0))  28.5 us
    all_to_all x1, waiting for transfers between devices, local(): lax.all_to_all(sent, 'lon', split_axis=0, concat_axis=0, axis_index_group...  22.7 us
    ppermute x14, starting transfers between devices, exchange_xc(): lax.ppermute(blocks[dx * NC + dc], 'lon', shifts(dx, 0, dc))  20 us
    ppermute x14, waiting for transfers between devices, exchange_xc(): lax.ppermute(blocks[dx * NC + dc], 'lon', shifts(dx, 0, dc))  15.5 us
    ppermute x3, waiting for transfers between devices, exchange_x(): out[dx] = lax.ppermute(blocks[dx], 'lon', shifts(dx, 0, 0))  10.2 us
    all_to_all x1, starting transfers between devices, local(): lax.all_to_all(sent, 'lon', split_axis=0, concat_axis=0, axis_index_group...  10 us
    all_to_all x1, starting transfers between devices, local(): lax.all_to_all(spectrum, 'lon', split_axis=0, concat_axis=0, tiled=True)  6.08 us
  transfers between devices with their start and end apart: 33, of which 16 were waited for; matrix products, arithmetic and copies ran while one was open for 3% of the time, Pallas kernels for 3%

profile of v14, /device:TPU:1, one launch (start us, length us, event | category | flops | bytes accessed | tf_op | source)
XLA Modules:
  0.0 189.2 jit_solution(17331072050220159035)
XLA Ops:
  4.5 2.5 %collective-permute-start.1 = (f32[32,16,128]{2,1,0:T(8,128)S(1)}, f32[32,16,128]{2,1,0:T(8,128)S(1)}, u32[]{:S(2)}, u32[]{:S(2)}) collective-permute-start(f32[32,16,128]{2,1,0:T(8,128)S(1)} %get-tuple-element.43), channel_id=1, source_target_pairs={{0,128},{4,132},{8,136},{12,140},{16,144},{20,148},{24,152},{28,15... | collective-permute-start | bytes 786440 | tf_op jit(solution)/shard_map/ppermute | solution.py:433
  9.5 8.8 %collective-permute-done.1 = f32[32,16,128]{2,1,0:T(8,128)S(1)} collective-permute-done((f32[32,16,128]{2,1,0:T(8,128)S(1)}, f32[32,16,128]{2,1,0:T(8,128)S(1)}, u32[]{:S(2)}, u32[]{:S(2)}) %collective-permute-start.1) | collective-permute-done | bytes 262176 | tf_op jit(solution)/shard_map/ppermute | solution.py:433
  19.9 10.0 %all-to-all-start = ((f32[16,128,128]{2,1,0:T(8,128)}), f32[16,128,128]{2,1,0:T(8,128)S(1)}, u32[]{:S(2)}, u32[]{:S(2)}) async-start(f32[16,128,128]{2,1,0:T(8,128)} %spread_a.1), calls=%async_computation | async-start | bytes 2097152 | tf_op jit(solution)/shard_map/all_to_all | solution.py:456
  30.7 4.5 %fusion = (bf16[8,256,128]{2,1,0:T(8,128)(2,1)S(1)}, bf16[8,256,128]{2,1,0:T(8,128)(2,1)S(1)}) fusion(s32[256]{0:T(256)S(1)} %iota.198, s32[8]{0:T(128)S(1)} %iota_subtract_fusion, pred[8]{0:T(512)(128)(4,1)S(1)} %iota_compare_fusion, pred[256]{0:T(512)(128)(4,1)S(1)} %iota.190, s32[256]{0:T(256)S(1)} %iota.186, s32[256]{0:T(256)S(1)} %iota.183, ...), kind=kLoop, calls=%fused_computation.6 | loop fusion | flops 7340032 | bytes 1052200 | tf_op jit(solution)/shard_map/convert_element_type | solution.py:58
  35.3 22.7 %all-to-all-done = f32[16,128,128]{2,1,0:T(8,128)S(1)} async-done(((f32[16,128,128]{2,1,0:T(8,128)}), f32[16,128,128]{2,1,0:T(8,128)S(1)}, u32[]{:S(2)}, u32[]{:S(2)}) %all-to-all-start) | async-done | bytes 1048608 | tf_op jit(solution)/shard_map/all_to_all | solution.py:456
  57.9 2.4 %fft_a.1 = f32[64,32,128]{2,1,0:T(8,128)} custom-call(f32[2048,128]{1,0:T(8,128)S(1)} %bitcast.17, bf16[8,256,128]{2,1,0:T(8,128)(2,1)S(1)} %get-tuple-element.78.wh_ref.refs_8_, bf16[8,256,128]{2,1,0:T(8,128)(2,1)S(1)} %get-tuple-element.77.wl_ref.refs_9_), custom_call_target="tpu_custom_call" | custom-call | tf_op jit(solution)/shard_map/fft_a/pallas_call | solution.py:180
  60.4 6.1 %all-to-all-start.1 = ((f32[64,32,128]{2,1,0:T(8,128)}), f32[64,32,128]{2,1,0:T(8,128)S(1)}, u32[]{:S(2)}, u32[]{:S(2)}) async-start(f32[64,32,128]{2,1,0:T(8,128)} %fft_a.1), calls=%async_computation.1 | async-start | bytes 2097152 | tf_op jit(solution)/shard_map/all_to_all | solution.py:464
  70.0 2.4 %collective-permute-start.5 = (f32[32,8,128]{2,1,0:T(8,128)S(1)}, f32[32,8,128]{2,1,0:T(8,128)S(1)}, u32[]{:S(2)}, u32[]{:S(2)}) collective-permute-start(f32[32,8,128]{2,1,0:T(8,128)S(1)} %get-tuple-element.48), channel_id=1, source_target_pairs={{0,24},{4,28},{8,32},{12,36},{16,40},{20,44},{24,48},{28,52},{32,5... | collective-permute-start | bytes 393224 | tf_op jit(solution)/shard_map/ppermute | solution.py:421
  74.4 2.4 %collective-permute-start.7 = (f32[32,8,128]{2,1,0:T(8,128)S(1)}, f32[32,8,128]{2,1,0:T(8,128)S(1)}, u32[]{:S(2)}, u32[]{:S(2)}) collective-permute-start(f32[32,8,128]{2,1,0:T(8,128)S(1)} %get-tuple-element.50), channel_id=1, source_target_pairs={{0,40},{4,44},{8,48},{12,52},{16,56},{20,60},{24,0},{28,4},{32,8},... | collective-permute-start | bytes 393224 | tf_op jit(solution)/shard_map/ppermute | solution.py:421
  76.8 17.8 %collective-permute-done.3 = f32[32,8,128]{2,1,0:T(8,128)S(1)} collective-permute-done((f32[32,8,128]{2,1,0:T(8,128)S(1)}, f32[32,8,128]{2,1,0:T(8,128)S(1)}, u32[]{:S(2)}, u32[]{:S(2)}) %collective-permute-start.3) | collective-permute-done | bytes 131104 | tf_op jit(solution)/shard_map/ppermute | solution.py:421
  96.9 2.8 %collective-permute-done.4 = f32[32,8,128]{2,1,0:T(8,128)S(1)} collective-permute-done((f32[32,8,128]{2,1,0:T(8,128)S(1)}, f32[32,8,128]{2,1,0:T(8,128)S(1)}, u32[]{:S(2)}, u32[]{:S(2)}) %collective-permute-start.4) | collective-permute-done | bytes 131104 | tf_op jit(solution)/shard_map/ppermute | solution.py:421
  102.0 8.8 %collective-permute-done.5 = f32[32,8,128]{2,1,0:T(8,128)S(1)} collective-permute-done((f32[32,8,128]{2,1,0:T(8,128)S(1)}, f32[32,8,128]{2,1,0:T(8,128)S(1)}, u32[]{:S(2)}, u32[]{:S(2)}) %collective-permute-start.5) | collective-permute-done | bytes 131104 | tf_op jit(solution)/shard_map/ppermute | solution.py:421
  110.9 4.9 %collective-permute-done.6 = f32[32,8,128]{2,1,0:T(8,128)S(1)} collective-permute-done((f32[32,8,128]{2,1,0:T(8,128)S(1)}, f32[32,8,128]{2,1,0:T(8,128)S(1)}, u32[]{:S(2)}, u32[]{:S(2)}) %collective-permute-start.6) | collective-permute-done | bytes 131104 | tf_op jit(solution)/shard_map/ppermute | solution.py:421
  116.7 2.5 %collective-permute-start.10 = (f32[256,128]{1,0:T(8,128)S(1)}, f32[256,128]{1,0:T(8,128)S(1)}, u32[]{:S(2)}, u32[]{:S(2)}) collective-permute-start(f32[256,128]{1,0:T(8,128)S(1)} %get-tuple-element.54), channel_id=1, source_target_pairs={{0,4},{4,0},{8,12},{12,8},{16,20},{20,16},{24,28},{28,24},{32,36},... | collective-permute-start | bytes 393224 | tf_op jit(solution)/shard_map/ppermute | solution.py:444
  120.1 3.2 %collective-permute-start.13 = (f32[256,128]{1,0:T(8,128)S(1)}, f32[256,128]{1,0:T(8,128)S(1)}, u32[]{:S(2)}, u32[]{:S(2)}) collective-permute-start(f32[256,128]{1,0:T(8,128)S(1)} %get-tuple-element.57), channel_id=1, source_target_pairs={{0,128},{4,132},{8,136},{12,140},{16,144},{20,148},{24,152},{28,15... | collective-permute-start | bytes 393224 | tf_op jit(solution)/shard_map/ppermute | solution.py:444
  127.1 6.9 %collective-permute-done.12.refs_3_ = f32[256,128]{1,0:T(8,128)S(1)} collective-permute-done((f32[256,128]{1,0:T(8,128)S(1)}, f32[256,128]{1,0:T(8,128)S(1)}, u32[]{:S(2)}, u32[]{:S(2)}) %collective-permute-start.12) | collective-permute-done | bytes 131104 | tf_op jit(solution)/shard_map/ppermute | solution.py:444
  141.0 3.3 %collective-permute-start.20 = (f32[256,128]{1,0:T(8,128)S(1)}, f32[256,128]{1,0:T(8,128)S(1)}, u32[]{:S(2)}, u32[]{:S(2)}) collective-permute-start(f32[256,128]{1,0:T(8,128)S(1)} %get-tuple-element.65), channel_id=1, source_target_pairs={{0,32},{4,36},{8,40},{12,44},{16,48},{20,52},{24,56},{28,60},{32,0... | collective-permute-start | bytes 393224 | tf_op jit(solution)/shard_map/ppermute | solution.py:421
  147.0 4.6 %collective-permute-start.23 = (f32[256,128]{1,0:T(8,128)S(1)}, f32[256,128]{1,0:T(8,128)S(1)}, u32[]{:S(2)}, u32[]{:S(2)}) collective-permute-start(f32[256,128]{1,0:T(8,128)S(1)} %get-tuple-element.68), channel_id=1, source_target_pairs={{0,56},{4,60},{8,0},{12,4},{16,8},{20,12},{24,16},{28,20},{32,24},... | collective-permute-start | bytes 393224 | tf_op jit(solution)/shard_map/ppermute | solution.py:421
  151.5 9.8 %collective-permute-done.19.refs_3_ = f32[256,128]{1,0:T(8,128)S(1)} collective-permute-done((f32[256,128]{1,0:T(8,128)S(1)}, f32[256,128]{1,0:T(8,128)S(1)}, u32[]{:S(2)}, u32[]{:S(2)}) %collective-permute-start.19) | collective-permute-done | bytes 131104 | tf_op jit(solution)/shard_map/ppermute | solution.py:421
  161.3 4.1 %collective-permute-done.22.refs_6_ = f32[256,128]{1,0:T(8,128)S(1)} collective-permute-done((f32[256,128]{1,0:T(8,128)S(1)}, f32[256,128]{1,0:T(8,128)S(1)}, u32[]{:S(2)}, u32[]{:S(2)}) %collective-permute-start.22) | collective-permute-done | bytes 131104 | tf_op jit(solution)/shard_map/ppermute | solution.py:421
  165.5 2.7 %collective-permute-done.23.refs_7_ = f32[256,128]{1,0:T(8,128)S(1)} collective-permute-done((f32[256,128]{1,0:T(8,128)S(1)}, f32[256,128]{1,0:T(8,128)S(1)}, u32[]{:S(2)}, u32[]{:S(2)}) %collective-permute-start.23) | collective-permute-done | bytes 131104 | tf_op jit(solution)/shard_map/ppermute | solution.py:421
  175.3 2.6 %collective-permute-start.29 = (f32[256,128]{1,0:T(8,128)S(1)}, f32[256,128]{1,0:T(8,128)S(1)}, u32[]{:S(2)}, u32[]{:S(2)}) collective-permute-start(f32[256,128]{1,0:T(8,128)S(1)} %get-tuple-element.75), channel_id=1, source_target_pairs={{0,192},{4,196},{8,200},{12,204},{16,208},{20,212},{24,216},{28,22... | collective-permute-start | bytes 393224 | tf_op jit(solution)/shard_map/ppermute | solution.py:444
  179.5 2.9 %collective-permute-done.27.refs_4_ = f32[256,128]{1,0:T(8,128)S(1)} collective-permute-done((f32[256,128]{1,0:T(8,128)S(1)}, f32[256,128]{1,0:T(8,128)S(1)}, u32[]{:S(2)}, u32[]{:S(2)}) %collective-permute-start.27) | collective-permute-done | bytes 131104 | tf_op jit(solution)/shard_map/ppermute | solution.py:444
  182.3 3.1 %collective-permute-done.28.refs_5_ = f32[256,128]{1,0:T(8,128)S(1)} collective-permute-done((f32[256,128]{1,0:T(8,128)S(1)}, f32[256,128]{1,0:T(8,128)S(1)}, u32[]{:S(2)}, u32[]{:S(2)}) %collective-permute-start.28) | collective-permute-done | bytes 131104 | tf_op jit(solution)/shard_map/ppermute | solution.py:444
  (69 shorter events, 47.2 us)
Async XLA Ops:
  4.5 13.8 %collective-permute-start.1 = (f32[32,16,128]{2,1,0:T(8,128)S(1)}, f32[32,16,128]{2,1,0:T(8,128)S(1)}, u32[]{:S(2)}, u32[]{:S(2)}) collective-permute-start(f32[32,16,128]{2,1,0:T(8,128)S(1)} %get-tuple-element.43), channel_id=1, source_target_pairs={{0,128},{4,132},{8,136},{12,140},{16,144},{20,148},{24,152},{28,15... | collective-permute-start | bytes 786440 | tf_op jit(solution)/shard_map/ppermute | solution.py:433
  7.0 11.3 %collective-permute-start.2 = (f32[32,16,128]{2,1,0:T(8,128)S(1)}, f32[32,16,128]{2,1,0:T(8,128)S(1)}, u32[]{:S(2)}, u32[]{:S(2)}) collective-permute-start(f32[32,16,128]{2,1,0:T(8,128)S(1)} %get-tuple-element.44), channel_id=1, source_target_pairs={{0,192},{4,196},{8,200},{12,204},{16,208},{20,212},{24,216},{28,22... | collective-permute-start | bytes 786440 | tf_op jit(solution)/shard_map/ppermute | solution.py:433
  19.9 38.0 %all-to-all-start = ((f32[16,128,128]{2,1,0:T(8,128)}), f32[16,128,128]{2,1,0:T(8,128)S(1)}, u32[]{:S(2)}, u32[]{:S(2)}) async-start(f32[16,128,128]{2,1,0:T(8,128)} %spread_a.1), calls=%async_computation | async-start | bytes 2097152 | tf_op jit(solution)/shard_map/all_to_all | solution.py:456
  60.4 118.0 %all-to-all-start.1 = ((f32[64,32,128]{2,1,0:T(8,128)}), f32[64,32,128]{2,1,0:T(8,128)S(1)}, u32[]{:S(2)}, u32[]{:S(2)}) async-start(f32[64,32,128]{2,1,0:T(8,128)} %fft_a.1), calls=%async_computation.1 | async-start | bytes 2097152 | tf_op jit(solution)/shard_map/all_to_all | solution.py:464
  66.5 28.2 %collective-permute-start.3 = (f32[32,8,128]{2,1,0:T(8,128)S(1)}, f32[32,8,128]{2,1,0:T(8,128)S(1)}, u32[]{:S(2)}, u32[]{:S(2)}) collective-permute-start(f32[32,8,128]{2,1,0:T(8,128)S(1)} %get-tuple-element.46), channel_id=1, source_target_pairs={{0,8},{4,12},{8,16},{12,20},{16,24},{20,28},{24,32},{28,36},{32,40... | collective-permute-start | bytes 393224 | tf_op jit(solution)/shard_map/ppermute | solution.py:421
  67.9 31.8 %collective-permute-start.4 = (f32[32,8,128]{2,1,0:T(8,128)S(1)}, f32[32,8,128]{2,1,0:T(8,128)S(1)}, u32[]{:S(2)}, u32[]{:S(2)}) collective-permute-start(f32[32,8,128]{2,1,0:T(8,128)S(1)} %get-tuple-element.47), channel_id=1, source_target_pairs={{0,16},{4,20},{8,24},{12,28},{16,32},{20,36},{24,40},{28,44},{32,4... | collective-permute-start | bytes 393224 | tf_op jit(solution)/shard_map/ppermute | solution.py:421
  70.0 40.9 %collective-permute-start.5 = (f32[32,8,128]{2,1,0:T(8,128)S(1)}, f32[32,8,128]{2,1,0:T(8,128)S(1)}, u32[]{:S(2)}, u32[]{:S(2)}) collective-permute-start(f32[32,8,128]{2,1,0:T(8,128)S(1)} %get-tuple-element.48), channel_id=1, source_target_pairs={{0,24},{4,28},{8,32},{12,36},{16,40},{20,44},{24,48},{28,52},{32,5... | collective-permute-start | bytes 393224 | tf_op jit(solution)/shard_map/ppermute | solution.py:421
  72.4 43.4 %collective-permute-start.6 = (f32[32,8,128]{2,1,0:T(8,128)S(1)}, f32[32,8,128]{2,1,0:T(8,128)S(1)}, u32[]{:S(2)}, u32[]{:S(2)}) collective-permute-start(f32[32,8,128]{2,1,0:T(8,128)S(1)} %get-tuple-element.49), channel_id=1, source_target_pairs={{0,32},{4,36},{8,40},{12,44},{16,48},{20,52},{24,56},{28,60},{32,0... | collective-permute-start | bytes 393224 | tf_op jit(solution)/shard_map/ppermute | solution.py:421
  74.4 41.3 %collective-permute-start.7 = (f32[32,8,128]{2,1,0:T(8,128)S(1)}, f32[32,8,128]{2,1,0:T(8,128)S(1)}, u32[]{:S(2)}, u32[]{:S(2)}) collective-permute-start(f32[32,8,128]{2,1,0:T(8,128)S(1)} %get-tuple-element.50), channel_id=1, source_target_pairs={{0,40},{4,44},{8,48},{12,52},{16,56},{20,60},{24,0},{28,4},{32,8},... | collective-permute-start | bytes 393224 | tf_op jit(solution)/shard_map/ppermute | solution.py:421
  94.6 21.1 %collective-permute-start.8 = (f32[32,8,128]{2,1,0:T(8,128)S(1)}, f32[32,8,128]{2,1,0:T(8,128)S(1)}, u32[]{:S(2)}, u32[]{:S(2)}) collective-permute-start(f32[32,8,128]{2,1,0:T(8,128)S(1)} %get-tuple-element.51), channel_id=1, source_target_pairs={{0,48},{4,52},{8,56},{12,60},{16,0},{20,4},{24,8},{28,12},{32,16},... | collective-permute-start | bytes 393224 | tf_op jit(solution)/shard_map/ppermute | solution.py:421
  99.7 16.0 %collective-permute-start.9 = (f32[32,8,128]{2,1,0:T(8,128)S(1)}, f32[32,8,128]{2,1,0:T(8,128)S(1)}, u32[]{:S(2)}, u32[]{:S(2)}) collective-permute-start(f32[32,8,128]{2,1,0:T(8,128)S(1)} %get-tuple-element.52), channel_id=1, source_target_pairs={{0,56},{4,60},{8,0},{12,4},{16,8},{20,12},{24,16},{28,20},{32,24},... | collective-permute-start | bytes 393224 | tf_op jit(solution)/shard_map/ppermute | solution.py:421
  119.2 14.9 %collective-permute-start.12 = (f32[256,128]{1,0:T(8,128)S(1)}, f32[256,128]{1,0:T(8,128)S(1)}, u32[]{:S(2)}, u32[]{:S(2)}) collective-permute-start(f32[256,128]{1,0:T(8,128)S(1)} %get-tuple-element.56), channel_id=1, source_target_pairs={{0,68},{4,64},{8,76},{12,72},{16,84},{20,80},{24,92},{28,88},{32,1... | collective-permute-start | bytes 393224 | tf_op jit(solution)/shard_map/ppermute | solution.py:444
  120.1 13.9 %collective-permute-start.13 = (f32[256,128]{1,0:T(8,128)S(1)}, f32[256,128]{1,0:T(8,128)S(1)}, u32[]{:S(2)}, u32[]{:S(2)}) collective-permute-start(f32[256,128]{1,0:T(8,128)S(1)} %get-tuple-element.57), channel_id=1, source_target_pairs={{0,128},{4,132},{8,136},{12,140},{16,144},{20,148},{24,152},{28,15... | collective-permute-start | bytes 393224 | tf_op jit(solution)/shard_map/ppermute | solution.py:444
  123.3 10.8 %collective-permute-start.14 = (f32[256,128]{1,0:T(8,128)S(1)}, f32[256,128]{1,0:T(8,128)S(1)}, u32[]{:S(2)}, u32[]{:S(2)}) collective-permute-start(f32[256,128]{1,0:T(8,128)S(1)} %get-tuple-element.58), channel_id=1, source_target_pairs={{0,132},{4,128},{8,140},{12,136},{16,148},{20,144},{24,156},{28,15... | collective-permute-start | bytes 393224 | tf_op jit(solution)/shard_map/ppermute | solution.py:444
  123.4 10.7 %collective-permute-start.15 = (f32[256,128]{1,0:T(8,128)S(1)}, f32[256,128]{1,0:T(8,128)S(1)}, u32[]{:S(2)}, u32[]{:S(2)}) collective-permute-start(f32[256,128]{1,0:T(8,128)S(1)} %get-tuple-element.59), channel_id=1, source_target_pairs={{0,192},{4,196},{8,200},{12,204},{16,208},{20,212},{24,216},{28,22... | collective-permute-start | bytes 393224 | tf_op jit(solution)/shard_map/ppermute | solution.py:444
  136.9 10.0 %collective-permute-start.18 = (f32[256,128]{1,0:T(8,128)S(1)}, f32[256,128]{1,0:T(8,128)S(1)}, u32[]{:S(2)}, u32[]{:S(2)}) collective-permute-start(f32[256,128]{1,0:T(8,128)S(1)} %get-tuple-element.63), channel_id=1, source_target_pairs={{0,16},{4,20},{8,24},{12,28},{16,32},{20,36},{24,40},{28,44},{32,4... | collective-permute-start | bytes 393224 | tf_op jit(solution)/shard_map/ppermute | solution.py:421
  138.9 22.5 %collective-permute-start.19 = (f32[256,128]{1,0:T(8,128)S(1)}, f32[256,128]{1,0:T(8,128)S(1)}, u32[]{:S(2)}, u32[]{:S(2)}) collective-permute-start(f32[256,128]{1,0:T(8,128)S(1)} %get-tuple-element.64), channel_id=1, source_target_pairs={{0,24},{4,28},{8,32},{12,36},{16,40},{20,44},{24,48},{28,52},{32,5... | collective-permute-start | bytes 393224 | tf_op jit(solution)/shard_map/ppermute | solution.py:421
  141.0 20.3 %collective-permute-start.20 = (f32[256,128]{1,0:T(8,128)S(1)}, f32[256,128]{1,0:T(8,128)S(1)}, u32[]{:S(2)}, u32[]{:S(2)}) collective-permute-start(f32[256,128]{1,0:T(8,128)S(1)} %get-tuple-element.65), channel_id=1, source_target_pairs={{0,32},{4,36},{8,40},{12,44},{16,48},{20,52},{24,56},{28,60},{32,0... | collective-permute-start | bytes 393224 | tf_op jit(solution)/shard_map/ppermute | solution.py:421
  144.3 17.0 %collective-permute-start.21 = (f32[256,128]{1,0:T(8,128)S(1)}, f32[256,128]{1,0:T(8,128)S(1)}, u32[]{:S(2)}, u32[]{:S(2)}) collective-permute-start(f32[256,128]{1,0:T(8,128)S(1)} %get-tuple-element.66), channel_id=1, source_target_pairs={{0,40},{4,44},{8,48},{12,52},{16,56},{20,60},{24,0},{28,4},{32,8},... | collective-permute-start | bytes 393224 | tf_op jit(solution)/shard_map/ppermute | solution.py:421
  146.5 19.0 %collective-permute-start.22 = (f32[256,128]{1,0:T(8,128)S(1)}, f32[256,128]{1,0:T(8,128)S(1)}, u32[]{:S(2)}, u32[]{:S(2)}) collective-permute-start(f32[256,128]{1,0:T(8,128)S(1)} %get-tuple-element.67), channel_id=1, source_target_pairs={{0,48},{4,52},{8,56},{12,60},{16,0},{20,4},{24,8},{28,12},{32,16},... | collective-permute-start | bytes 393224 | tf_op jit(solution)/shard_map/ppermute | solution.py:421
  147.0 21.2 %collective-permute-start.23 = (f32[256,128]{1,0:T(8,128)S(1)}, f32[256,128]{1,0:T(8,128)S(1)}, u32[]{:S(2)}, u32[]{:S(2)}) collective-permute-start(f32[256,128]{1,0:T(8,128)S(1)} %get-tuple-element.68), channel_id=1, source_target_pairs={{0,56},{4,60},{8,0},{12,4},{16,8},{20,12},{24,16},{28,20},{32,24},... | collective-permute-start | bytes 393224 | tf_op jit(solution)/shard_map/ppermute | solution.py:421
  172.0 10.3 %collective-permute-start.27 = (f32[256,128]{1,0:T(8,128)S(1)}, f32[256,128]{1,0:T(8,128)S(1)}, u32[]{:S(2)}, u32[]{:S(2)}) collective-permute-start(f32[256,128]{1,0:T(8,128)S(1)} %get-tuple-element.73), channel_id=1, source_target_pairs={{0,128},{4,132},{8,136},{12,140},{16,144},{20,148},{24,152},{28,15... | collective-permute-start | bytes 393224 | tf_op jit(solution)/shard_map/ppermute | solution.py:444
  173.6 11.8 %collective-permute-start.28 = (f32[256,128]{1,0:T(8,128)S(1)}, f32[256,128]{1,0:T(8,128)S(1)}, u32[]{:S(2)}, u32[]{:S(2)}) collective-permute-start(f32[256,128]{1,0:T(8,128)S(1)} %get-tuple-element.74), channel_id=1, source_target_pairs={{0,132},{4,128},{8,140},{12,136},{16,148},{20,144},{24,156},{28,15... | collective-permute-start | bytes 393224 | tf_op jit(solution)/shard_map/ppermute | solution.py:444
  175.3 10.1 %collective-permute-start.29 = (f32[256,128]{1,0:T(8,128)S(1)}, f32[256,128]{1,0:T(8,128)S(1)}, u32[]{:S(2)}, u32[]{:S(2)}) collective-permute-start(f32[256,128]{1,0:T(8,128)S(1)} %get-tuple-element.75), channel_id=1, source_target_pairs={{0,192},{4,196},{8,200},{12,204},{16,208},{20,212},{24,216},{28,22... | collective-permute-start | bytes 393224 | tf_op jit(solution)/shard_map/ppermute | solution.py:444
  (9 other events, 71.2 us)

commit v15 on v14

--- a/solution.py
+++ b/solution.py
@@ -45,14 +45,14 @@
 
 
 def twiddle_matrices(scale):
-    shape = (HALF, 4, PEERS, INNER)
+    shape = (HALF, 2, PEERS, INNER)
     pair = lax.broadcasted_iota(jnp.int32, shape, 0)
-    kind = lax.broadcasted_iota(jnp.int32, shape, 1)
+    mirror = lax.broadcasted_iota(jnp.int32, shape, 1)
     outer = lax.broadcasted_iota(jnp.int32, shape, 2)
     inner = lax.broadcasted_iota(jnp.int32, shape, 3)
-    first = jnp.where(kind < 2, pair, jnp.where(pair == 0, HALF, RADIX - pair))
+    first = jnp.where(mirror == 0, pair, jnp.where(pair == 0, HALF, RADIX - pair))
     angle = phase(inner, first + RADIX * outer)
-    full = jnp.where(kind % 2 == 0, jnp.cos(angle), jnp.sin(angle)) * scale
+    full = jnp.stack([jnp.cos(angle) * scale, jnp.sin(angle) * scale], axis=2)
     full = full.reshape(HALF, 4 * PEERS, INNER)
     high = lax.reduce_precision(full, 8, 7)
     return high.astype(jnp.bfloat16), (full - high).astype(jnp.bfloat16)

time: 189 us -> 190 us (level)
  waiting for transfers between devices: 101 us -> 103 us
  other arithmetic: 4.64 us -> 2.64 us
    convert_element_type x1, other arithmetic: 4.53 us -> 0.22 us  [twiddle_matrices(): return (high.astype(jnp.bfloat16), (full - high).astype(jnp.bfloat16))]
    all_to_all x1, waiting for transfers between devices: 22.7 us -> 25.4 us  [local(): lax.all_to_all(sent, 'lon', split_axis=0, concat_axis=0, axis_index_group...]
    mul x0 -> x1, other arithmetic: none -> 2.23 us  [twiddle_matrices(): full = jnp.stack([jnp.cos(angle) * scale, jnp.sin(angle) * scale], axis=2)]
  transfers between devices with their start and end apart: 33 -> 33, of which waited for: 16 -> 16; matrix products, arithmetic and copies ran while one was open for 3% -> 1% of each run, Pallas kernels for 3% -> 3%
where the time goes in v15:
time: 190 us; the launch traced here: 189 us
  waiting for transfers between devices  103 us (54%)
  starting transfers between devices  70.5 us (37%)
  Pallas kernels  12.8 us (7%)
  other arithmetic  2.64 us (1%)
    ppermute x14, waiting for transfers between devices, exchange_z(): out[dz] = lax.ppermute(blocks[dz], 'lon', shifts(0, dz, 0))  52.1 us
    ppermute x14, starting transfers between devices, exchange_z(): out[dz] = lax.ppermute(blocks[dz], 'lon', shifts(0, dz, 0))  28.5 us
    all_to_all x1, waiting for transfers between devices, local(): lax.all_to_all(sent, 'lon', split_axis=0, concat_axis=0, axis_index_group...  25.4 us
    ppermute x14, starting transfers between devices, exchange_xc(): lax.ppermute(blocks[dx * NC + dc], 'lon', shifts(dx, 0, dc))  20.2 us
    ppermute x14, waiting for transfers between devices, exchange_xc(): lax.ppermute(blocks[dx * NC + dc], 'lon', shifts(dx, 0, dc))  15.5 us
    ppermute x3, waiting for transfers between devices, exchange_x(): out[dx] = lax.ppermute(blocks[dx], 'lon', shifts(dx, 0, 0))  10.2 us
    all_to_all x1, starting transfers between devices, local(): lax.all_to_all(sent, 'lon', split_axis=0, concat_axis=0, axis_index_group...  10 us
    all_to_all x1, starting transfers between devices, local(): lax.all_to_all(spectrum, 'lon', split_axis=0, concat_axis=0, tiled=True)  6.08 us
  transfers between devices with their start and end apart: 33, of which 16 were waited for; matrix products, arithmetic and copies ran while one was open for 1% of the time, Pallas kernels for 3%

profile of v15, /device:TPU:1, one launch (start us, length us, event | category | flops | bytes accessed | tf_op | source)
XLA Modules:
  0.0 189.5 jit_solution(8182691387424050695)
XLA Ops:
  4.5 2.5 %collective-permute-start.1 = (f32[32,16,128]{2,1,0:T(8,128)S(1)}, f32[32,16,128]{2,1,0:T(8,128)S(1)}, u32[]{:S(2)}, u32[]{:S(2)}) collective-permute-start(f32[32,16,128]{2,1,0:T(8,128)S(1)} %get-tuple-element.43), channel_id=1, source_target_pairs={{0,128},{4,132},{8,136},{12,140},{16,144},{20,148},{24,152},{28,15... | collective-permute-start | bytes 786440 | tf_op jit(solution)/shard_map/ppermute | solution.py:433
  9.5 8.8 %collective-permute-done.1 = f32[32,16,128]{2,1,0:T(8,128)S(1)} collective-permute-done((f32[32,16,128]{2,1,0:T(8,128)S(1)}, f32[32,16,128]{2,1,0:T(8,128)S(1)}, u32[]{:S(2)}, u32[]{:S(2)}) %collective-permute-start.1) | collective-permute-done | bytes 262176 | tf_op jit(solution)/shard_map/ppermute | solution.py:433
  19.9 10.0 %all-to-all-start = ((f32[16,128,128]{2,1,0:T(8,128)}), f32[16,128,128]{2,1,0:T(8,128)S(1)}, u32[]{:S(2)}, u32[]{:S(2)}) async-start(f32[16,128,128]{2,1,0:T(8,128)} %spread_a.1), calls=%async_computation | async-start | bytes 2097152 | tf_op jit(solution)/shard_map/all_to_all | solution.py:456
  32.6 25.4 %all-to-all-done = f32[16,128,128]{2,1,0:T(8,128)S(1)} async-done(((f32[16,128,128]{2,1,0:T(8,128)}), f32[16,128,128]{2,1,0:T(8,128)S(1)}, u32[]{:S(2)}, u32[]{:S(2)}) %all-to-all-start) | async-done | bytes 1048608 | tf_op jit(solution)/shard_map/all_to_all | solution.py:456
  57.9 2.4 %fft_a.1 = f32[64,32,128]{2,1,0:T(8,128)} custom-call(f32[2048,128]{1,0:T(8,128)S(1)} %bitcast.20, bf16[8,256,128]{2,1,0:T(8,128)(2,1)S(1)} %get-tuple-element.78.wh_ref.refs_8_, bf16[8,256,128]{2,1,0:T(8,128)(2,1)S(1)} %get-tuple-element.77.wl_ref.refs_9_), custom_call_target="tpu_custom_call" | custom-call | tf_op jit(solution)/shard_map/fft_a/pallas_call | solution.py:180
  60.4 6.1 %all-to-all-start.1 = ((f32[64,32,128]{2,1,0:T(8,128)}), f32[64,32,128]{2,1,0:T(8,128)S(1)}, u32[]{:S(2)}, u32[]{:S(2)}) async-start(f32[64,32,128]{2,1,0:T(8,128)} %fft_a.1), calls=%async_computation.1 | async-start | bytes 2097152 | tf_op jit(solution)/shard_map/all_to_all | solution.py:464
  70.0 2.4 %collective-permute-start.5 = (f32[32,8,128]{2,1,0:T(8,128)S(1)}, f32[32,8,128]{2,1,0:T(8,128)S(1)}, u32[]{:S(2)}, u32[]{:S(2)}) collective-permute-start(f32[32,8,128]{2,1,0:T(8,128)S(1)} %get-tuple-element.48), channel_id=1, source_target_pairs={{0,24},{4,28},{8,32},{12,36},{16,40},{20,44},{24,48},{28,52},{32,5... | collective-permute-start | bytes 393224 | tf_op jit(solution)/shard_map/ppermute | solution.py:421
  74.5 2.4 %collective-permute-start.7 = (f32[32,8,128]{2,1,0:T(8,128)S(1)}, f32[32,8,128]{2,1,0:T(8,128)S(1)}, u32[]{:S(2)}, u32[]{:S(2)}) collective-permute-start(f32[32,8,128]{2,1,0:T(8,128)S(1)} %get-tuple-element.50), channel_id=1, source_target_pairs={{0,40},{4,44},{8,48},{12,52},{16,56},{20,60},{24,0},{28,4},{32,8},... | collective-permute-start | bytes 393224 | tf_op jit(solution)/shard_map/ppermute | solution.py:421
  76.9 17.8 %collective-permute-done.3 = f32[32,8,128]{2,1,0:T(8,128)S(1)} collective-permute-done((f32[32,8,128]{2,1,0:T(8,128)S(1)}, f32[32,8,128]{2,1,0:T(8,128)S(1)}, u32[]{:S(2)}, u32[]{:S(2)}) %collective-permute-start.3) | collective-permute-done | bytes 131104 | tf_op jit(solution)/shard_map/ppermute | solution.py:421
  96.9 2.8 %collective-permute-done.4 = f32[32,8,128]{2,1,0:T(8,128)S(1)} collective-permute-done((f32[32,8,128]{2,1,0:T(8,128)S(1)}, f32[32,8,128]{2,1,0:T(8,128)S(1)}, u32[]{:S(2)}, u32[]{:S(2)}) %collective-permute-start.4) | collective-permute-done | bytes 131104 | tf_op jit(solution)/shard_map/ppermute | solution.py:421
  99.7 2.3 %collective-permute-start.9 = (f32[32,8,128]{2,1,0:T(8,128)S(1)}, f32[32,8,128]{2,1,0:T(8,128)S(1)}, u32[]{:S(2)}, u32[]{:S(2)}) collective-permute-start(f32[32,8,128]{2,1,0:T(8,128)S(1)} %get-tuple-element.52), channel_id=1, source_target_pairs={{0,56},{4,60},{8,0},{12,4},{16,8},{20,12},{24,16},{28,20},{32,24},... | collective-permute-start | bytes 393224 | tf_op jit(solution)/shard_map/ppermute | solution.py:421
  102.1 8.8 %collective-permute-done.5 = f32[32,8,128]{2,1,0:T(8,128)S(1)} collective-permute-done((f32[32,8,128]{2,1,0:T(8,128)S(1)}, f32[32,8,128]{2,1,0:T(8,128)S(1)}, u32[]{:S(2)}, u32[]{:S(2)}) %collective-permute-start.5) | collective-permute-done | bytes 131104 | tf_op jit(solution)/shard_map/ppermute | solution.py:421
  110.9 4.9 %collective-permute-done.6 = f32[32,8,128]{2,1,0:T(8,128)S(1)} collective-permute-done((f32[32,8,128]{2,1,0:T(8,128)S(1)}, f32[32,8,128]{2,1,0:T(8,128)S(1)}, u32[]{:S(2)}, u32[]{:S(2)}) %collective-permute-start.6) | collective-permute-done | bytes 131104 | tf_op jit(solution)/shard_map/ppermute | solution.py:421
  116.7 2.5 %collective-permute-start.10 = (f32[256,128]{1,0:T(8,128)S(1)}, f32[256,128]{1,0:T(8,128)S(1)}, u32[]{:S(2)}, u32[]{:S(2)}) collective-permute-start(f32[256,128]{1,0:T(8,128)S(1)} %get-tuple-element.54), channel_id=1, source_target_pairs={{0,4},{4,0},{8,12},{12,8},{16,20},{20,16},{24,28},{28,24},{32,36},... | collective-permute-start | bytes 393224 | tf_op jit(solution)/shard_map/ppermute | solution.py:444
  120.1 3.2 %collective-permute-start.13 = (f32[256,128]{1,0:T(8,128)S(1)}, f32[256,128]{1,0:T(8,128)S(1)}, u32[]{:S(2)}, u32[]{:S(2)}) collective-permute-start(f32[256,128]{1,0:T(8,128)S(1)} %get-tuple-element.57), channel_id=1, source_target_pairs={{0,128},{4,132},{8,136},{12,140},{16,144},{20,148},{24,152},{28,15... | collective-permute-start | bytes 393224 | tf_op jit(solution)/shard_map/ppermute | solution.py:444
  127.1 6.9 %collective-permute-done.12.refs_3_ = f32[256,128]{1,0:T(8,128)S(1)} collective-permute-done((f32[256,128]{1,0:T(8,128)S(1)}, f32[256,128]{1,0:T(8,128)S(1)}, u32[]{:S(2)}, u32[]{:S(2)}) %collective-permute-start.12) | collective-permute-done | bytes 131104 | tf_op jit(solution)/shard_map/ppermute | solution.py:444
  141.1 3.3 %collective-permute-start.20 = (f32[256,128]{1,0:T(8,128)S(1)}, f32[256,128]{1,0:T(8,128)S(1)}, u32[]{:S(2)}, u32[]{:S(2)}) collective-permute-start(f32[256,128]{1,0:T(8,128)S(1)} %get-tuple-element.65), channel_id=1, source_target_pairs={{0,32},{4,36},{8,40},{12,44},{16,48},{20,52},{24,56},{28,60},{32,0... | collective-permute-start | bytes 393224 | tf_op jit(solution)/shard_map/ppermute | solution.py:421
  147.0 4.6 %collective-permute-start.23 = (f32[256,128]{1,0:T(8,128)S(1)}, f32[256,128]{1,0:T(8,128)S(1)}, u32[]{:S(2)}, u32[]{:S(2)}) collective-permute-start(f32[256,128]{1,0:T(8,128)S(1)} %get-tuple-element.68), channel_id=1, source_target_pairs={{0,56},{4,60},{8,0},{12,4},{16,8},{20,12},{24,16},{28,20},{32,24},... | collective-permute-start | bytes 393224 | tf_op jit(solution)/shard_map/ppermute | solution.py:421
  151.6 9.8 %collective-permute-done.19.refs_3_ = f32[256,128]{1,0:T(8,128)S(1)} collective-permute-done((f32[256,128]{1,0:T(8,128)S(1)}, f32[256,128]{1,0:T(8,128)S(1)}, u32[]{:S(2)}, u32[]{:S(2)}) %collective-permute-start.19) | collective-permute-done | bytes 131104 | tf_op jit(solution)/shard_map/ppermute | solution.py:421
  161.4 4.1 %collective-permute-done.22.refs_6_ = f32[256,128]{1,0:T(8,128)S(1)} collective-permute-done((f32[256,128]{1,0:T(8,128)S(1)}, f32[256,128]{1,0:T(8,128)S(1)}, u32[]{:S(2)}, u32[]{:S(2)}) %collective-permute-start.22) | collective-permute-done | bytes 131104 | tf_op jit(solution)/shard_map/ppermute | solution.py:421
  165.5 2.7 %collective-permute-done.23.refs_7_ = f32[256,128]{1,0:T(8,128)S(1)} collective-permute-done((f32[256,128]{1,0:T(8,128)S(1)}, f32[256,128]{1,0:T(8,128)S(1)}, u32[]{:S(2)}, u32[]{:S(2)}) %collective-permute-start.23) | collective-permute-done | bytes 131104 | tf_op jit(solution)/shard_map/ppermute | solution.py:421
  175.4 2.5 %collective-permute-start.29 = (f32[256,128]{1,0:T(8,128)S(1)}, f32[256,128]{1,0:T(8,128)S(1)}, u32[]{:S(2)}, u32[]{:S(2)}) collective-permute-start(f32[256,128]{1,0:T(8,128)S(1)} %get-tuple-element.75), channel_id=1, source_target_pairs={{0,192},{4,196},{8,200},{12,204},{16,208},{20,212},{24,216},{28,22... | collective-permute-start | bytes 393224 | tf_op jit(solution)/shard_map/ppermute | solution.py:444
  179.7 2.4 %collective-permute-done.27.refs_4_ = f32[256,128]{1,0:T(8,128)S(1)} collective-permute-done((f32[256,128]{1,0:T(8,128)S(1)}, f32[256,128]{1,0:T(8,128)S(1)}, u32[]{:S(2)}, u32[]{:S(2)}) %collective-permute-start.27) | collective-permute-done | bytes 131104 | tf_op jit(solution)/shard_map/ppermute | solution.py:444
  182.2 3.3 %collective-permute-done.28.refs_5_ = f32[256,128]{1,0:T(8,128)S(1)} collective-permute-done((f32[256,128]{1,0:T(8,128)S(1)}, f32[256,128]{1,0:T(8,128)S(1)}, u32[]{:S(2)}, u32[]{:S(2)}) %collective-permute-start.28) | collective-permute-done | bytes 131104 | tf_op jit(solution)/shard_map/ppermute | solution.py:444
  (58 shorter events, 47.3 us)
Async XLA Ops:
  4.5 13.8 %collective-permute-start.1 = (f32[32,16,128]{2,1,0:T(8,128)S(1)}, f32[32,16,128]{2,1,0:T(8,128)S(1)}, u32[]{:S(2)}, u32[]{:S(2)}) collective-permute-start(f32[32,16,128]{2,1,0:T(8,128)S(1)} %get-tuple-element.43), channel_id=1, source_target_pairs={{0,128},{4,132},{8,136},{12,140},{16,144},{20,148},{24,152},{28,15... | collective-permute-start | bytes 786440 | tf_op jit(solution)/shard_map/ppermute | solution.py:433
  7.0 11.3 %collective-permute-start.2 = (f32[32,16,128]{2,1,0:T(8,128)S(1)}, f32[32,16,128]{2,1,0:T(8,128)S(1)}, u32[]{:S(2)}, u32[]{:S(2)}) collective-permute-start(f32[32,16,128]{2,1,0:T(8,128)S(1)} %get-tuple-element.44), channel_id=1, source_target_pairs={{0,192},{4,196},{8,200},{12,204},{16,208},{20,212},{24,216},{28,22... | collective-permute-start | bytes 786440 | tf_op jit(solution)/shard_map/ppermute | solution.py:433
  19.9 38.0 %all-to-all-start = ((f32[16,128,128]{2,1,0:T(8,128)}), f32[16,128,128]{2,1,0:T(8,128)S(1)}, u32[]{:S(2)}, u32[]{:S(2)}) async-start(f32[16,128,128]{2,1,0:T(8,128)} %spread_a.1), calls=%async_computation | async-start | bytes 2097152 | tf_op jit(solution)/shard_map/all_to_all | solution.py:456
  60.4 118.3 %all-to-all-start.1 = ((f32[64,32,128]{2,1,0:T(8,128)}), f32[64,32,128]{2,1,0:T(8,128)S(1)}, u32[]{:S(2)}, u32[]{:S(2)}) async-start(f32[64,32,128]{2,1,0:T(8,128)} %fft_a.1), calls=%async_computation.1 | async-start | bytes 2097152 | tf_op jit(solution)/shard_map/all_to_all | solution.py:464
  66.5 28.2 %collective-permute-start.3 = (f32[32,8,128]{2,1,0:T(8,128)S(1)}, f32[32,8,128]{2,1,0:T(8,128)S(1)}, u32[]{:S(2)}, u32[]{:S(2)}) collective-permute-start(f32[32,8,128]{2,1,0:T(8,128)S(1)} %get-tuple-element.46), channel_id=1, source_target_pairs={{0,8},{4,12},{8,16},{12,20},{16,24},{20,28},{24,32},{28,36},{32,40... | collective-permute-start | bytes 393224 | tf_op jit(solution)/shard_map/ppermute | solution.py:421
  67.9 31.8 %collective-permute-start.4 = (f32[32,8,128]{2,1,0:T(8,128)S(1)}, f32[32,8,128]{2,1,0:T(8,128)S(1)}, u32[]{:S(2)}, u32[]{:S(2)}) collective-permute-start(f32[32,8,128]{2,1,0:T(8,128)S(1)} %get-tuple-element.47), channel_id=1, source_target_pairs={{0,16},{4,20},{8,24},{12,28},{16,32},{20,36},{24,40},{28,44},{32,4... | collective-permute-start | bytes 393224 | tf_op jit(solution)/shard_map/ppermute | solution.py:421
  70.0 40.9 %collective-permute-start.5 = (f32[32,8,128]{2,1,0:T(8,128)S(1)}, f32[32,8,128]{2,1,0:T(8,128)S(1)}, u32[]{:S(2)}, u32[]{:S(2)}) collective-permute-start(f32[32,8,128]{2,1,0:T(8,128)S(1)} %get-tuple-element.48), channel_id=1, source_target_pairs={{0,24},{4,28},{8,32},{12,36},{16,40},{20,44},{24,48},{28,52},{32,5... | collective-permute-start | bytes 393224 | tf_op jit(solution)/shard_map/ppermute | solution.py:421
  72.4 43.4 %collective-permute-start.6 = (f32[32,8,128]{2,1,0:T(8,128)S(1)}, f32[32,8,128]{2,1,0:T(8,128)S(1)}, u32[]{:S(2)}, u32[]{:S(2)}) collective-permute-start(f32[32,8,128]{2,1,0:T(8,128)S(1)} %get-tuple-element.49), channel_id=1, source_target_pairs={{0,32},{4,36},{8,40},{12,44},{16,48},{20,52},{24,56},{28,60},{32,0... | collective-permute-start | bytes 393224 | tf_op jit(solution)/shard_map/ppermute | solution.py:421
  74.5 41.3 %collective-permute-start.7 = (f32[32,8,128]{2,1,0:T(8,128)S(1)}, f32[32,8,128]{2,1,0:T(8,128)S(1)}, u32[]{:S(2)}, u32[]{:S(2)}) collective-permute-start(f32[32,8,128]{2,1,0:T(8,128)S(1)} %get-tuple-element.50), channel_id=1, source_target_pairs={{0,40},{4,44},{8,48},{12,52},{16,56},{20,60},{24,0},{28,4},{32,8},... | collective-permute-start | bytes 393224 | tf_op jit(solution)/shard_map/ppermute | solution.py:421
  94.7 21.1 %collective-permute-start.8 = (f32[32,8,128]{2,1,0:T(8,128)S(1)}, f32[32,8,128]{2,1,0:T(8,128)S(1)}, u32[]{:S(2)}, u32[]{:S(2)}) collective-permute-start(f32[32,8,128]{2,1,0:T(8,128)S(1)} %get-tuple-element.51), channel_id=1, source_target_pairs={{0,48},{4,52},{8,56},{12,60},{16,0},{20,4},{24,8},{28,12},{32,16},... | collective-permute-start | bytes 393224 | tf_op jit(solution)/shard_map/ppermute | solution.py:421
  99.7 16.0 %collective-permute-start.9 = (f32[32,8,128]{2,1,0:T(8,128)S(1)}, f32[32,8,128]{2,1,0:T(8,128)S(1)}, u32[]{:S(2)}, u32[]{:S(2)}) collective-permute-start(f32[32,8,128]{2,1,0:T(8,128)S(1)} %get-tuple-element.52), channel_id=1, source_target_pairs={{0,56},{4,60},{8,0},{12,4},{16,8},{20,12},{24,16},{28,20},{32,24},... | collective-permute-start | bytes 393224 | tf_op jit(solution)/shard_map/ppermute | solution.py:421
  119.2 14.9 %collective-permute-start.12 = (f32[256,128]{1,0:T(8,128)S(1)}, f32[256,128]{1,0:T(8,128)S(1)}, u32[]{:S(2)}, u32[]{:S(2)}) collective-permute-start(f32[256,128]{1,0:T(8,128)S(1)} %get-tuple-element.56), channel_id=1, source_target_pairs={{0,68},{4,64},{8,76},{12,72},{16,84},{20,80},{24,92},{28,88},{32,1... | collective-permute-start | bytes 393224 | tf_op jit(solution)/shard_map/ppermute | solution.py:444
  120.1 13.9 %collective-permute-start.13 = (f32[256,128]{1,0:T(8,128)S(1)}, f32[256,128]{1,0:T(8,128)S(1)}, u32[]{:S(2)}, u32[]{:S(2)}) collective-permute-start(f32[256,128]{1,0:T(8,128)S(1)} %get-tuple-element.57), channel_id=1, source_target_pairs={{0,128},{4,132},{8,136},{12,140},{16,144},{20,148},{24,152},{28,15... | collective-permute-start | bytes 393224 | tf_op jit(solution)/shard_map/ppermute | solution.py:444
  123.3 10.8 %collective-permute-start.14 = (f32[256,128]{1,0:T(8,128)S(1)}, f32[256,128]{1,0:T(8,128)S(1)}, u32[]{:S(2)}, u32[]{:S(2)}) collective-permute-start(f32[256,128]{1,0:T(8,128)S(1)} %get-tuple-element.58), channel_id=1, source_target_pairs={{0,132},{4,128},{8,140},{12,136},{16,148},{20,144},{24,156},{28,15... | collective-permute-start | bytes 393224 | tf_op jit(solution)/shard_map/ppermute | solution.py:444
  123.4 10.7 %collective-permute-start.15 = (f32[256,128]{1,0:T(8,128)S(1)}, f32[256,128]{1,0:T(8,128)S(1)}, u32[]{:S(2)}, u32[]{:S(2)}) collective-permute-start(f32[256,128]{1,0:T(8,128)S(1)} %get-tuple-element.59), channel_id=1, source_target_pairs={{0,192},{4,196},{8,200},{12,204},{16,208},{20,212},{24,216},{28,22... | collective-permute-start | bytes 393224 | tf_op jit(solution)/shard_map/ppermute | solution.py:444
  137.0 10.0 %collective-permute-start.18 = (f32[256,128]{1,0:T(8,128)S(1)}, f32[256,128]{1,0:T(8,128)S(1)}, u32[]{:S(2)}, u32[]{:S(2)}) collective-permute-start(f32[256,128]{1,0:T(8,128)S(1)} %get-tuple-element.63), channel_id=1, source_target_pairs={{0,16},{4,20},{8,24},{12,28},{16,32},{20,36},{24,40},{28,44},{32,4... | collective-permute-start | bytes 393224 | tf_op jit(solution)/shard_map/ppermute | solution.py:421
  138.9 22.5 %collective-permute-start.19 = (f32[256,128]{1,0:T(8,128)S(1)}, f32[256,128]{1,0:T(8,128)S(1)}, u32[]{:S(2)}, u32[]{:S(2)}) collective-permute-start(f32[256,128]{1,0:T(8,128)S(1)} %get-tuple-element.64), channel_id=1, source_target_pairs={{0,24},{4,28},{8,32},{12,36},{16,40},{20,44},{24,48},{28,52},{32,5... | collective-permute-start | bytes 393224 | tf_op jit(solution)/shard_map/ppermute | solution.py:421
  141.1 20.3 %collective-permute-start.20 = (f32[256,128]{1,0:T(8,128)S(1)}, f32[256,128]{1,0:T(8,128)S(1)}, u32[]{:S(2)}, u32[]{:S(2)}) collective-permute-start(f32[256,128]{1,0:T(8,128)S(1)} %get-tuple-element.65), channel_id=1, source_target_pairs={{0,32},{4,36},{8,40},{12,44},{16,48},{20,52},{24,56},{28,60},{32,0... | collective-permute-start | bytes 393224 | tf_op jit(solution)/shard_map/ppermute | solution.py:421
  144.3 17.1 %collective-permute-start.21 = (f32[256,128]{1,0:T(8,128)S(1)}, f32[256,128]{1,0:T(8,128)S(1)}, u32[]{:S(2)}, u32[]{:S(2)}) collective-permute-start(f32[256,128]{1,0:T(8,128)S(1)} %get-tuple-element.66), channel_id=1, source_target_pairs={{0,40},{4,44},{8,48},{12,52},{16,56},{20,60},{24,0},{28,4},{32,8},... | collective-permute-start | bytes 393224 | tf_op jit(solution)/shard_map/ppermute | solution.py:421
  146.5 19.0 %collective-permute-start.22 = (f32[256,128]{1,0:T(8,128)S(1)}, f32[256,128]{1,0:T(8,128)S(1)}, u32[]{:S(2)}, u32[]{:S(2)}) collective-permute-start(f32[256,128]{1,0:T(8,128)S(1)} %get-tuple-element.67), channel_id=1, source_target_pairs={{0,48},{4,52},{8,56},{12,60},{16,0},{20,4},{24,8},{28,12},{32,16},... | collective-permute-start | bytes 393224 | tf_op jit(solution)/shard_map/ppermute | solution.py:421
  147.0 21.2 %collective-permute-start.23 = (f32[256,128]{1,0:T(8,128)S(1)}, f32[256,128]{1,0:T(8,128)S(1)}, u32[]{:S(2)}, u32[]{:S(2)}) collective-permute-start(f32[256,128]{1,0:T(8,128)S(1)} %get-tuple-element.68), channel_id=1, source_target_pairs={{0,56},{4,60},{8,0},{12,4},{16,8},{20,12},{24,16},{28,20},{32,24},... | collective-permute-start | bytes 393224 | tf_op jit(solution)/shard_map/ppermute | solution.py:421
  172.3 9.9 %collective-permute-start.27 = (f32[256,128]{1,0:T(8,128)S(1)}, f32[256,128]{1,0:T(8,128)S(1)}, u32[]{:S(2)}, u32[]{:S(2)}) collective-permute-start(f32[256,128]{1,0:T(8,128)S(1)} %get-tuple-element.73), channel_id=1, source_target_pairs={{0,128},{4,132},{8,136},{12,140},{16,144},{20,148},{24,152},{28,15... | collective-permute-start | bytes 393224 | tf_op jit(solution)/shard_map/ppermute | solution.py:444
  173.8 11.6 %collective-permute-start.28 = (f32[256,128]{1,0:T(8,128)S(1)}, f32[256,128]{1,0:T(8,128)S(1)}, u32[]{:S(2)}, u32[]{:S(2)}) collective-permute-start(f32[256,128]{1,0:T(8,128)S(1)} %get-tuple-element.74), channel_id=1, source_target_pairs={{0,132},{4,128},{8,140},{12,136},{16,148},{20,144},{24,156},{28,15... | collective-permute-start | bytes 393224 | tf_op jit(solution)/shard_map/ppermute | solution.py:444
  175.4 10.0 %collective-permute-start.29 = (f32[256,128]{1,0:T(8,128)S(1)}, f32[256,128]{1,0:T(8,128)S(1)}, u32[]{:S(2)}, u32[]{:S(2)}) collective-permute-start(f32[256,128]{1,0:T(8,128)S(1)} %get-tuple-element.75), channel_id=1, source_target_pairs={{0,192},{4,196},{8,200},{12,204},{16,208},{20,212},{24,216},{28,22... | collective-permute-start | bytes 393224 | tf_op jit(solution)/shard_map/ppermute | solution.py:444
  (9 other events, 71.7 us)

commit v16 on v13

--- a/solution.py
+++ b/solution.py
@@ -439,12 +439,13 @@
 
 
 X_ORDER = ((1, 0), (3, 0), (2, 0), (2, 1), (1, 1), (3, 1), (0, 1))
-
-
-def exchange_xc(blocks):
+X_OUT = ((2, 0), (2, 1), (1, 0), (3, 0), (1, 1), (3, 1), (0, 1))
+
+
+def exchange_xc(blocks, order):
     out = [None] * (NX * NC)
     out[0] = blocks[0]
-    for dx, dc in X_ORDER:
+    for dx, dc in order:
         out[dx * NC + dc] = lax.ppermute(blocks[dx * NC + dc], "lon", shifts(dx, 0, dc))
     return out
 
@@ -461,13 +462,13 @@
         sent, "lon", split_axis=0, concat_axis=0, axis_index_groups=GROUPS, tiled=True
     )
     pieces = spread_x(pos, [b.reshape(LON * 8, LANES) for b in pieces])
-    pieces = exchange_xc(pieces)
+    pieces = exchange_xc(pieces, X_ORDER)
     pieces = fft_p(pos, pieces, wh, wl)
     pieces = exchange_z(pieces)
     spectrum = fft_a(gathered.reshape(NLON, LANES), wh, wl)
     shares = lax.all_to_all(spectrum, "lon", split_axis=0, concat_axis=0, tiled=True)
     pieces = spread_out(pos, pieces)
-    pieces = exchange_xc(pieces)
+    pieces = exchange_xc(pieces, X_OUT)
     out = store_a(shares)
     out = store_p(pos, out, pieces)
     return out.reshape(2, RADIX, FIELDS, 2 * LANES)

time: 192 us -> 192 us (level)
  no operation moved by 1% of the time
where the time goes in v16:
time: 192 us; the launch traced here: 191 us
  waiting for transfers between devices  103 us (54%)
  starting transfers between devices  70.4 us (37%)
  Pallas kernels  12.2 us (6%)
  other arithmetic  3.34 us (2%)
  local copies, waits for them, and re-layouts  2.6 us (1%)
    ppermute x14, waiting for transfers between devices, exchange_z(): out[dz] = lax.ppermute(blocks[dz], 'lon', shifts(0, dz, 0))  52.1 us
    ppermute x14, starting transfers between devices, exchange_z(): out[dz] = lax.ppermute(blocks[dz], 'lon', shifts(0, dz, 0))  28.5 us
    all_to_all x1, waiting for transfers between devices, local(): lax.all_to_all(sent, 'lon', split_axis=0, concat_axis=0, axis_index_group...  24.7 us
    ppermute x14, starting transfers between devices, exchange_xc(): lax.ppermute(blocks[dx * NC + dc], 'lon', shifts(dx, 0, dc))  20.2 us
    ppermute x14, waiting for transfers between devices, exchange_xc(): lax.ppermute(blocks[dx * NC + dc], 'lon', shifts(dx, 0, dc))  15.5 us
    ppermute x3, waiting for transfers between devices, exchange_x(): out[dx] = lax.ppermute(blocks[dx], 'lon', shifts(dx, 0, 0))  10.2 us
    all_to_all x1, starting transfers between devices, local(): lax.all_to_all(sent, 'lon', split_axis=0, concat_axis=0, axis_index_group...  10 us
    all_to_all x1, starting transfers between devices, local(): lax.all_to_all(spectrum, 'lon', split_axis=0, concat_axis=0, tiled=True)  6.08 us
  transfers between devices with their start and end apart: 33, of which 16 were waited for; matrix products, arithmetic and copies ran while one was open for 2% of the time, Pallas kernels for 2%

profile of v16, /device:TPU:1, one launch (start us, length us, event | category | flops | bytes accessed | tf_op | source)
XLA Modules:
  0.0 191.4 jit_solution(8010308844559883195)
XLA Ops:
  7.0 2.5 %collective-permute-start.1 = (f32[32,16,128]{2,1,0:T(8,128)S(1)}, f32[32,16,128]{2,1,0:T(8,128)S(1)}, u32[]{:S(2)}, u32[]{:S(2)}) collective-permute-start(f32[32,16,128]{2,1,0:T(8,128)S(1)} %get-tuple-element.43), channel_id=1, source_target_pairs={{0,128},{4,132},{8,136},{12,140},{16,144},{20,148},{24,152},{28,15... | collective-permute-start | bytes 786440 | tf_op jit(solution)/shard_map/ppermute | solution.py:437
  12.1 8.8 %collective-permute-done.1 = f32[32,16,128]{2,1,0:T(8,128)S(1)} collective-permute-done((f32[32,16,128]{2,1,0:T(8,128)S(1)}, f32[32,16,128]{2,1,0:T(8,128)S(1)}, u32[]{:S(2)}, u32[]{:S(2)}) %collective-permute-start.1) | collective-permute-done | bytes 262176 | tf_op jit(solution)/shard_map/ppermute | solution.py:437
  22.5 10.0 %all-to-all-start = ((f32[16,128,128]{2,1,0:T(8,128)}), f32[16,128,128]{2,1,0:T(8,128)S(1)}, u32[]{:S(2)}, u32[]{:S(2)}) async-start(f32[16,128,128]{2,1,0:T(8,128)} %spread_a.1), calls=%async_computation | async-start | bytes 2097152 | tf_op jit(solution)/shard_map/all_to_all | solution.py:461
  32.5 2.5 %select_select_fusion.1 = (f32[8,2,64,128]{3,2,1,0:T(8,128)S(1)}, f32[8,2,64,128]{3,2,1,0:T(8,128)S(1)}, f32[8,2,64,128]{3,2,1,0:T(8,128)S(1)}, f32[8,2,64,128]{3,2,1,0:T(8,128)S(1)}) fusion(pred[2]{0:T(512)(128)(4,1)S(1)} %iota_compare_fusion.1, pred[8]{0:T(512)(128)(4,1)S(1)} %iota_compare_fusion, s32[64]{0:T(128)S(1)} %iota_multiply_fusion, ...), kind=kLoop, calls=%fused_computation.9 | loop fusion | flops 4456448 | bytes 2097450 | tf_op jit(solution)/shard_map/jit(_where)/select_n | solution.py:60
  35.8 24.7 %all-to-all-done = f32[16,128,128]{2,1,0:T(8,128)S(1)} async-done(((f32[16,128,128]{2,1,0:T(8,128)}), f32[16,128,128]{2,1,0:T(8,128)S(1)}, u32[]{:S(2)}, u32[]{:S(2)}) %all-to-all-start) | async-done | bytes 1048608 | tf_op jit(solution)/shard_map/all_to_all | solution.py:461
  62.6 6.1 %all-to-all-start.1 = ((f32[64,32,128]{2,1,0:T(8,128)}), f32[64,32,128]{2,1,0:T(8,128)S(1)}, u32[]{:S(2)}, u32[]{:S(2)}) async-start(f32[64,32,128]{2,1,0:T(8,128)} %fft_a.1), calls=%async_computation.1 | async-start | bytes 2097152 | tf_op jit(solution)/shard_map/all_to_all | solution.py:469
  72.2 2.4 %collective-permute-start.5 = (f32[32,8,128]{2,1,0:T(8,128)}, f32[32,8,128]{2,1,0:T(8,128)S(1)}, u32[]{:S(2)}, u32[]{:S(2)}) collective-permute-start(f32[32,8,128]{2,1,0:T(8,128)} %copy-done.2), channel_id=1, source_target_pairs={{0,24},{4,28},{8,32},{12,36},{16,40},{20,44},{24,48},{28,52},{32,5... | collective-permute-start | bytes 393224 | tf_op jit(solution)/shard_map/ppermute | solution.py:425
  76.7 2.4 %collective-permute-start.7 = (f32[32,8,128]{2,1,0:T(8,128)}, f32[32,8,128]{2,1,0:T(8,128)S(1)}, u32[]{:S(2)}, u32[]{:S(2)}) collective-permute-start(f32[32,8,128]{2,1,0:T(8,128)} %copy-done), channel_id=1, source_target_pairs={{0,40},{4,44},{8,48},{12,52},{16,56},{20,60},{24,0},{28,4},{32,8},... | collective-permute-start | bytes 393224 | tf_op jit(solution)/shard_map/ppermute | solution.py:425
  79.1 17.8 %collective-permute-done.3 = f32[32,8,128]{2,1,0:T(8,128)S(1)} collective-permute-done((f32[32,8,128]{2,1,0:T(8,128)}, f32[32,8,128]{2,1,0:T(8,128)S(1)}, u32[]{:S(2)}, u32[]{:S(2)}) %collective-permute-start.3) | collective-permute-done | bytes 131104 | tf_op jit(solution)/shard_map/ppermute | solution.py:425
  99.2 2.8 %collective-permute-done.4 = f32[32,8,128]{2,1,0:T(8,128)S(1)} collective-permute-done((f32[32,8,128]{2,1,0:T(8,128)}, f32[32,8,128]{2,1,0:T(8,128)S(1)}, u32[]{:S(2)}, u32[]{:S(2)}) %collective-permute-start.4) | collective-permute-done | bytes 131104 | tf_op jit(solution)/shard_map/ppermute | solution.py:425
  102.0 2.3 %collective-permute-start.9 = (f32[32,8,128]{2,1,0:T(8,128)S(1)}, f32[32,8,128]{2,1,0:T(8,128)S(1)}, u32[]{:S(2)}, u32[]{:S(2)}) collective-permute-start(f32[32,8,128]{2,1,0:T(8,128)S(1)} %get-tuple-element.52), channel_id=1, source_target_pairs={{0,56},{4,60},{8,0},{12,4},{16,8},{20,12},{24,16},{28,20},{32,24},... | collective-permute-start | bytes 393224 | tf_op jit(solution)/shard_map/ppermute | solution.py:425
  104.3 8.8 %collective-permute-done.5 = f32[32,8,128]{2,1,0:T(8,128)S(1)} collective-permute-done((f32[32,8,128]{2,1,0:T(8,128)}, f32[32,8,128]{2,1,0:T(8,128)S(1)}, u32[]{:S(2)}, u32[]{:S(2)}) %collective-permute-start.5) | collective-permute-done | bytes 131104 | tf_op jit(solution)/shard_map/ppermute | solution.py:425
  113.1 4.9 %collective-permute-done.6 = f32[32,8,128]{2,1,0:T(8,128)S(1)} collective-permute-done((f32[32,8,128]{2,1,0:T(8,128)}, f32[32,8,128]{2,1,0:T(8,128)S(1)}, u32[]{:S(2)}, u32[]{:S(2)}) %collective-permute-start.6) | collective-permute-done | bytes 131104 | tf_op jit(solution)/shard_map/ppermute | solution.py:425
  118.9 2.5 %collective-permute-start.10 = (f32[256,128]{1,0:T(8,128)S(1)}, f32[256,128]{1,0:T(8,128)S(1)}, u32[]{:S(2)}, u32[]{:S(2)}) collective-permute-start(f32[256,128]{1,0:T(8,128)S(1)} %get-tuple-element.54), channel_id=1, source_target_pairs={{0,4},{4,0},{8,12},{12,8},{16,20},{20,16},{24,28},{28,24},{32,36},... | collective-permute-start | bytes 393224 | tf_op jit(solution)/shard_map/ppermute | solution.py:449
  122.4 3.2 %collective-permute-start.13 = (f32[256,128]{1,0:T(8,128)S(1)}, f32[256,128]{1,0:T(8,128)S(1)}, u32[]{:S(2)}, u32[]{:S(2)}) collective-permute-start(f32[256,128]{1,0:T(8,128)S(1)} %get-tuple-element.57), channel_id=1, source_target_pairs={{0,128},{4,132},{8,136},{12,140},{16,144},{20,148},{24,152},{28,15... | collective-permute-start | bytes 393224 | tf_op jit(solution)/shard_map/ppermute | solution.py:449
  129.4 6.9 %collective-permute-done.12.refs_3_ = f32[256,128]{1,0:T(8,128)S(1)} collective-permute-done((f32[256,128]{1,0:T(8,128)S(1)}, f32[256,128]{1,0:T(8,128)S(1)}, u32[]{:S(2)}, u32[]{:S(2)}) %collective-permute-start.12) | collective-permute-done | bytes 131104 | tf_op jit(solution)/shard_map/ppermute | solution.py:449
  143.0 3.3 %collective-permute-start.20 = (f32[256,128]{1,0:T(8,128)S(1)}, f32[256,128]{1,0:T(8,128)S(1)}, u32[]{:S(2)}, u32[]{:S(2)}) collective-permute-start(f32[256,128]{1,0:T(8,128)S(1)} %get-tuple-element.65), channel_id=1, source_target_pairs={{0,32},{4,36},{8,40},{12,44},{16,48},{20,52},{24,56},{28,60},{32,0... | collective-permute-start | bytes 393224 | tf_op jit(solution)/shard_map/ppermute | solution.py:425
  149.0 4.6 %collective-permute-start.23 = (f32[256,128]{1,0:T(8,128)S(1)}, f32[256,128]{1,0:T(8,128)S(1)}, u32[]{:S(2)}, u32[]{:S(2)}) collective-permute-start(f32[256,128]{1,0:T(8,128)S(1)} %get-tuple-element.68), channel_id=1, source_target_pairs={{0,56},{4,60},{8,0},{12,4},{16,8},{20,12},{24,16},{28,20},{32,24},... | collective-permute-start | bytes 393224 | tf_op jit(solution)/shard_map/ppermute | solution.py:425
  153.5 9.8 %collective-permute-done.19.refs_3_ = f32[256,128]{1,0:T(8,128)S(1)} collective-permute-done((f32[256,128]{1,0:T(8,128)S(1)}, f32[256,128]{1,0:T(8,128)S(1)}, u32[]{:S(2)}, u32[]{:S(2)}) %collective-permute-start.19) | collective-permute-done | bytes 131104 | tf_op jit(solution)/shard_map/ppermute | solution.py:425
  163.3 4.1 %collective-permute-done.22.refs_6_ = f32[256,128]{1,0:T(8,128)S(1)} collective-permute-done((f32[256,128]{1,0:T(8,128)S(1)}, f32[256,128]{1,0:T(8,128)S(1)}, u32[]{:S(2)}, u32[]{:S(2)}) %collective-permute-start.22) | collective-permute-done | bytes 131104 | tf_op jit(solution)/shard_map/ppermute | solution.py:425
  167.5 2.7 %collective-permute-done.23.refs_7_ = f32[256,128]{1,0:T(8,128)S(1)} collective-permute-done((f32[256,128]{1,0:T(8,128)S(1)}, f32[256,128]{1,0:T(8,128)S(1)}, u32[]{:S(2)}, u32[]{:S(2)}) %collective-permute-start.23) | collective-permute-done | bytes 131104 | tf_op jit(solution)/shard_map/ppermute | solution.py:425
  177.5 2.6 %collective-permute-start.29 = (f32[256,128]{1,0:T(8,128)S(1)}, f32[256,128]{1,0:T(8,128)S(1)}, u32[]{:S(2)}, u32[]{:S(2)}) collective-permute-start(f32[256,128]{1,0:T(8,128)S(1)} %get-tuple-element.75), channel_id=1, source_target_pairs={{0,192},{4,196},{8,200},{12,204},{16,208},{20,212},{24,216},{28,22... | collective-permute-start | bytes 393224 | tf_op jit(solution)/shard_map/ppermute | solution.py:449
  181.7 2.9 %collective-permute-done.27.refs_4_ = f32[256,128]{1,0:T(8,128)S(1)} collective-permute-done((f32[256,128]{1,0:T(8,128)S(1)}, f32[256,128]{1,0:T(8,128)S(1)}, u32[]{:S(2)}, u32[]{:S(2)}) %collective-permute-start.27) | collective-permute-done | bytes 131104 | tf_op jit(solution)/shard_map/ppermute | solution.py:449
  184.6 3.1 %collective-permute-done.28.refs_5_ = f32[256,128]{1,0:T(8,128)S(1)} collective-permute-done((f32[256,128]{1,0:T(8,128)S(1)}, f32[256,128]{1,0:T(8,128)S(1)}, u32[]{:S(2)}, u32[]{:S(2)}) %collective-permute-start.28) | collective-permute-done | bytes 131104 | tf_op jit(solution)/shard_map/ppermute | solution.py:449
  (69 shorter events, 49.5 us)
Async XLA Ops:
  7.0 13.8 %collective-permute-start.1 = (f32[32,16,128]{2,1,0:T(8,128)S(1)}, f32[32,16,128]{2,1,0:T(8,128)S(1)}, u32[]{:S(2)}, u32[]{:S(2)}) collective-permute-start(f32[32,16,128]{2,1,0:T(8,128)S(1)} %get-tuple-element.43), channel_id=1, source_target_pairs={{0,128},{4,132},{8,136},{12,140},{16,144},{20,148},{24,152},{28,15... | collective-permute-start | bytes 786440 | tf_op jit(solution)/shard_map/ppermute | solution.py:437
  9.5 11.3 %collective-permute-start.2 = (f32[32,16,128]{2,1,0:T(8,128)S(1)}, f32[32,16,128]{2,1,0:T(8,128)S(1)}, u32[]{:S(2)}, u32[]{:S(2)}) collective-permute-start(f32[32,16,128]{2,1,0:T(8,128)S(1)} %get-tuple-element.44), channel_id=1, source_target_pairs={{0,192},{4,196},{8,200},{12,204},{16,208},{20,212},{24,216},{28,22... | collective-permute-start | bytes 786440 | tf_op jit(solution)/shard_map/ppermute | solution.py:437
  22.5 38.0 %all-to-all-start = ((f32[16,128,128]{2,1,0:T(8,128)}), f32[16,128,128]{2,1,0:T(8,128)S(1)}, u32[]{:S(2)}, u32[]{:S(2)}) async-start(f32[16,128,128]{2,1,0:T(8,128)} %spread_a.1), calls=%async_computation | async-start | bytes 2097152 | tf_op jit(solution)/shard_map/all_to_all | solution.py:461
  62.6 118.0 %all-to-all-start.1 = ((f32[64,32,128]{2,1,0:T(8,128)}), f32[64,32,128]{2,1,0:T(8,128)S(1)}, u32[]{:S(2)}, u32[]{:S(2)}) async-start(f32[64,32,128]{2,1,0:T(8,128)} %fft_a.1), calls=%async_computation.1 | async-start | bytes 2097152 | tf_op jit(solution)/shard_map/all_to_all | solution.py:469
  68.7 28.2 %collective-permute-start.3 = (f32[32,8,128]{2,1,0:T(8,128)}, f32[32,8,128]{2,1,0:T(8,128)S(1)}, u32[]{:S(2)}, u32[]{:S(2)}) collective-permute-start(f32[32,8,128]{2,1,0:T(8,128)} %copy-done.4), channel_id=1, source_target_pairs={{0,8},{4,12},{8,16},{12,20},{16,24},{20,28},{24,32},{28,36},{32,40... | collective-permute-start | bytes 393224 | tf_op jit(solution)/shard_map/ppermute | solution.py:425
  70.2 31.8 %collective-permute-start.4 = (f32[32,8,128]{2,1,0:T(8,128)}, f32[32,8,128]{2,1,0:T(8,128)S(1)}, u32[]{:S(2)}, u32[]{:S(2)}) collective-permute-start(f32[32,8,128]{2,1,0:T(8,128)} %copy-done.3), channel_id=1, source_target_pairs={{0,16},{4,20},{8,24},{12,28},{16,32},{20,36},{24,40},{28,44},{32,4... | collective-permute-start | bytes 393224 | tf_op jit(solution)/shard_map/ppermute | solution.py:425
  72.2 40.9 %collective-permute-start.5 = (f32[32,8,128]{2,1,0:T(8,128)}, f32[32,8,128]{2,1,0:T(8,128)S(1)}, u32[]{:S(2)}, u32[]{:S(2)}) collective-permute-start(f32[32,8,128]{2,1,0:T(8,128)} %copy-done.2), channel_id=1, source_target_pairs={{0,24},{4,28},{8,32},{12,36},{16,40},{20,44},{24,48},{28,52},{32,5... | collective-permute-start | bytes 393224 | tf_op jit(solution)/shard_map/ppermute | solution.py:425
  74.6 43.4 %collective-permute-start.6 = (f32[32,8,128]{2,1,0:T(8,128)}, f32[32,8,128]{2,1,0:T(8,128)S(1)}, u32[]{:S(2)}, u32[]{:S(2)}) collective-permute-start(f32[32,8,128]{2,1,0:T(8,128)} %copy-done.1), channel_id=1, source_target_pairs={{0,32},{4,36},{8,40},{12,44},{16,48},{20,52},{24,56},{28,60},{32,0... | collective-permute-start | bytes 393224 | tf_op jit(solution)/shard_map/ppermute | solution.py:425
  76.7 41.3 %collective-permute-start.7 = (f32[32,8,128]{2,1,0:T(8,128)}, f32[32,8,128]{2,1,0:T(8,128)S(1)}, u32[]{:S(2)}, u32[]{:S(2)}) collective-permute-start(f32[32,8,128]{2,1,0:T(8,128)} %copy-done), channel_id=1, source_target_pairs={{0,40},{4,44},{8,48},{12,52},{16,56},{20,60},{24,0},{28,4},{32,8},... | collective-permute-start | bytes 393224 | tf_op jit(solution)/shard_map/ppermute | solution.py:425
  96.9 21.1 %collective-permute-start.8 = (f32[32,8,128]{2,1,0:T(8,128)S(1)}, f32[32,8,128]{2,1,0:T(8,128)S(1)}, u32[]{:S(2)}, u32[]{:S(2)}) collective-permute-start(f32[32,8,128]{2,1,0:T(8,128)S(1)} %get-tuple-element.51), channel_id=1, source_target_pairs={{0,48},{4,52},{8,56},{12,60},{16,0},{20,4},{24,8},{28,12},{32,16},... | collective-permute-start | bytes 393224 | tf_op jit(solution)/shard_map/ppermute | solution.py:425
  102.0 16.0 %collective-permute-start.9 = (f32[32,8,128]{2,1,0:T(8,128)S(1)}, f32[32,8,128]{2,1,0:T(8,128)S(1)}, u32[]{:S(2)}, u32[]{:S(2)}) collective-permute-start(f32[32,8,128]{2,1,0:T(8,128)S(1)} %get-tuple-element.52), channel_id=1, source_target_pairs={{0,56},{4,60},{8,0},{12,4},{16,8},{20,12},{24,16},{28,20},{32,24},... | collective-permute-start | bytes 393224 | tf_op jit(solution)/shard_map/ppermute | solution.py:425
  121.5 14.9 %collective-permute-start.12 = (f32[256,128]{1,0:T(8,128)S(1)}, f32[256,128]{1,0:T(8,128)S(1)}, u32[]{:S(2)}, u32[]{:S(2)}) collective-permute-start(f32[256,128]{1,0:T(8,128)S(1)} %get-tuple-element.56), channel_id=1, source_target_pairs={{0,68},{4,64},{8,76},{12,72},{16,84},{20,80},{24,92},{28,88},{32,1... | collective-permute-start | bytes 393224 | tf_op jit(solution)/shard_map/ppermute | solution.py:449
  122.4 13.9 %collective-permute-start.13 = (f32[256,128]{1,0:T(8,128)S(1)}, f32[256,128]{1,0:T(8,128)S(1)}, u32[]{:S(2)}, u32[]{:S(2)}) collective-permute-start(f32[256,128]{1,0:T(8,128)S(1)} %get-tuple-element.57), channel_id=1, source_target_pairs={{0,128},{4,132},{8,136},{12,140},{16,144},{20,148},{24,152},{28,15... | collective-permute-start | bytes 393224 | tf_op jit(solution)/shard_map/ppermute | solution.py:449
  125.6 10.8 %collective-permute-start.14 = (f32[256,128]{1,0:T(8,128)S(1)}, f32[256,128]{1,0:T(8,128)S(1)}, u32[]{:S(2)}, u32[]{:S(2)}) collective-permute-start(f32[256,128]{1,0:T(8,128)S(1)} %get-tuple-element.58), channel_id=1, source_target_pairs={{0,132},{4,128},{8,140},{12,136},{16,148},{20,144},{24,156},{28,15... | collective-permute-start | bytes 393224 | tf_op jit(solution)/shard_map/ppermute | solution.py:449
  125.6 10.7 %collective-permute-start.15 = (f32[256,128]{1,0:T(8,128)S(1)}, f32[256,128]{1,0:T(8,128)S(1)}, u32[]{:S(2)}, u32[]{:S(2)}) collective-permute-start(f32[256,128]{1,0:T(8,128)S(1)} %get-tuple-element.59), channel_id=1, source_target_pairs={{0,192},{4,196},{8,200},{12,204},{16,208},{20,212},{24,216},{28,22... | collective-permute-start | bytes 393224 | tf_op jit(solution)/shard_map/ppermute | solution.py:449
  139.0 10.0 %collective-permute-start.18 = (f32[256,128]{1,0:T(8,128)S(1)}, f32[256,128]{1,0:T(8,128)S(1)}, u32[]{:S(2)}, u32[]{:S(2)}) collective-permute-start(f32[256,128]{1,0:T(8,128)S(1)} %get-tuple-element.63), channel_id=1, source_target_pairs={{0,16},{4,20},{8,24},{12,28},{16,32},{20,36},{24,40},{28,44},{32,4... | collective-permute-start | bytes 393224 | tf_op jit(solution)/shard_map/ppermute | solution.py:425
  140.9 22.5 %collective-permute-start.19 = (f32[256,128]{1,0:T(8,128)S(1)}, f32[256,128]{1,0:T(8,128)S(1)}, u32[]{:S(2)}, u32[]{:S(2)}) collective-permute-start(f32[256,128]{1,0:T(8,128)S(1)} %get-tuple-element.64), channel_id=1, source_target_pairs={{0,24},{4,28},{8,32},{12,36},{16,40},{20,44},{24,48},{28,52},{32,5... | collective-permute-start | bytes 393224 | tf_op jit(solution)/shard_map/ppermute | solution.py:425
  143.0 20.3 %collective-permute-start.20 = (f32[256,128]{1,0:T(8,128)S(1)}, f32[256,128]{1,0:T(8,128)S(1)}, u32[]{:S(2)}, u32[]{:S(2)}) collective-permute-start(f32[256,128]{1,0:T(8,128)S(1)} %get-tuple-element.65), channel_id=1, source_target_pairs={{0,32},{4,36},{8,40},{12,44},{16,48},{20,52},{24,56},{28,60},{32,0... | collective-permute-start | bytes 393224 | tf_op jit(solution)/shard_map/ppermute | solution.py:425
  146.3 17.0 %collective-permute-start.21 = (f32[256,128]{1,0:T(8,128)S(1)}, f32[256,128]{1,0:T(8,128)S(1)}, u32[]{:S(2)}, u32[]{:S(2)}) collective-permute-start(f32[256,128]{1,0:T(8,128)S(1)} %get-tuple-element.66), channel_id=1, source_target_pairs={{0,40},{4,44},{8,48},{12,52},{16,56},{20,60},{24,0},{28,4},{32,8},... | collective-permute-start | bytes 393224 | tf_op jit(solution)/shard_map/ppermute | solution.py:425
  148.5 19.0 %collective-permute-start.22 = (f32[256,128]{1,0:T(8,128)S(1)}, f32[256,128]{1,0:T(8,128)S(1)}, u32[]{:S(2)}, u32[]{:S(2)}) collective-permute-start(f32[256,128]{1,0:T(8,128)S(1)} %get-tuple-element.67), channel_id=1, source_target_pairs={{0,48},{4,52},{8,56},{12,60},{16,0},{20,4},{24,8},{28,12},{32,16},... | collective-permute-start | bytes 393224 | tf_op jit(solution)/shard_map/ppermute | solution.py:425
  149.0 21.2 %collective-permute-start.23 = (f32[256,128]{1,0:T(8,128)S(1)}, f32[256,128]{1,0:T(8,128)S(1)}, u32[]{:S(2)}, u32[]{:S(2)}) collective-permute-start(f32[256,128]{1,0:T(8,128)S(1)} %get-tuple-element.68), channel_id=1, source_target_pairs={{0,56},{4,60},{8,0},{12,4},{16,8},{20,12},{24,16},{28,20},{32,24},... | collective-permute-start | bytes 393224 | tf_op jit(solution)/shard_map/ppermute | solution.py:425
  174.2 10.3 %collective-permute-start.27 = (f32[256,128]{1,0:T(8,128)S(1)}, f32[256,128]{1,0:T(8,128)S(1)}, u32[]{:S(2)}, u32[]{:S(2)}) collective-permute-start(f32[256,128]{1,0:T(8,128)S(1)} %get-tuple-element.73), channel_id=1, source_target_pairs={{0,128},{4,132},{8,136},{12,140},{16,144},{20,148},{24,152},{28,15... | collective-permute-start | bytes 393224 | tf_op jit(solution)/shard_map/ppermute | solution.py:449
  175.8 11.8 %collective-permute-start.28 = (f32[256,128]{1,0:T(8,128)S(1)}, f32[256,128]{1,0:T(8,128)S(1)}, u32[]{:S(2)}, u32[]{:S(2)}) collective-permute-start(f32[256,128]{1,0:T(8,128)S(1)} %get-tuple-element.74), channel_id=1, source_target_pairs={{0,132},{4,128},{8,140},{12,136},{16,148},{20,144},{24,156},{28,15... | collective-permute-start | bytes 393224 | tf_op jit(solution)/shard_map/ppermute | solution.py:449
  177.5 10.1 %collective-permute-start.29 = (f32[256,128]{1,0:T(8,128)S(1)}, f32[256,128]{1,0:T(8,128)S(1)}, u32[]{:S(2)}, u32[]{:S(2)}) collective-permute-start(f32[256,128]{1,0:T(8,128)S(1)} %get-tuple-element.75), channel_id=1, source_target_pairs={{0,192},{4,196},{8,200},{12,204},{16,208},{20,212},{24,216},{28,22... | collective-permute-start | bytes 393224 | tf_op jit(solution)/shard_map/ppermute | solution.py:449
  (14 other events, 91.4 us)
